TPU v7x, 32 devices: a whole 2x2x4 slice. The times are simulated.
32 devices in a mesh: blk: 8 (over z, y), sp: 4 (over x, core).
Axes of the slice: x: 2, y: 2, z: 4, core: 2. Of those that a mesh axis runs over, the one named last changes fastest.
Arguments:
- tokens: bfloat16 [4096, 2304], P(('blk', 'sp')), may hold values from -6 to 6
- w_qkv: bfloat16 [4096, 2304], replicated, may hold values from -5 to 5
- w_out: bfloat16 [2048, 2304], replicated, may hold values from -0.125 to 0.125
- gains: float32 [4, 2304], replicated, may hold values from 0.1 to 1.9
- w_ffn: bfloat16 [9216, 3, 2304], P('blk'), may hold values from -0.125 to 0.125
- cotangent: bfloat16 [4096, 2304], P(('blk', 'sp')), may hold values from -6 to 6
Outputs:
- block_out: bfloat16 [4096, 2304], P(('blk', 'sp'))
- tokens_grad: bfloat16 [4096, 2304], P(('blk', 'sp'))
- qkv_grad: float32 [4096, 2304], P(('sp', 'blk'))
- out_grad: float32 [2048, 2304], P(('sp', 'blk'))
- gains_grad: float32 [4, 2304], P(None, ('sp', 'blk'))
- ffn_grad: float32 [9216, 3, 2304], P(('blk', 'sp'))
All inputs are finite; a program needn't handle non-finite values.
Results may differ from a plain program's by a relative error of at most 0.025.
Values may be sent and summed in bfloat16 or wider, within the bound.
A program may use at most 320 MiB of HBM per device.

v0:
```python
import math

import jax
import jax.numpy as jnp
from jax import lax
from jax.sharding import PartitionSpec as P

HEADS = 8
KV_HEADS = 4
HEAD = 256


NORM_EPSILON = 1e-06
CAP_VALUE = 50.0
GELU_SCALE = 0.7978845608028654
GELU_CUBIC = 0.044715


def norm_parts(values):
    inverse = lax.rsqrt(jnp.mean(values * values, axis=-1, keepdims=True) + NORM_EPSILON)
    return (values * inverse, inverse)


def norm_back(grad_y, normed, inverse, gain):
    grad_n = grad_y * gain
    grad_v = inverse * (grad_n - normed * jnp.mean(grad_n * normed, axis=-1, keepdims=True))
    return (grad_v, jnp.sum(grad_y * normed, axis=0))


def gelu_value(values):
    return (
        0.5
        * values
        * (1.0 + jnp.tanh(GELU_SCALE * (values + GELU_CUBIC * values * values * values)))
    )


def gelu_slope(values):
    bent = jnp.tanh(GELU_SCALE * (values + GELU_CUBIC * values * values * values))
    return 0.5 * (1.0 + bent) + 0.5 * values * (1.0 - bent * bent) * GELU_SCALE * (
        1.0 + 3.0 * GELU_CUBIC * values * values
    )


def contract_last(left, right):
    return lax.dot_general(
        left, right, (((1,), (1,)), ((), ())), preferred_element_type=jnp.float32
    )


def body(tokens, w_qkv, w_out, gains, w_ffn, cotangent):
    row_count = tokens.shape[0]
    groups = lax.axis_size("sp")
    cycle_size = lax.axis_size("blk")
    heads_here = HEADS // groups
    kv_here = KV_HEADS // groups
    group_ratio = HEADS // KV_HEADS
    query_width = HEADS * HEAD
    score_scale = HEAD ** (-0.5)
    source = tokens.astype(jnp.float32)
    normed_in, inverse_in = norm_parts(source)
    act_in = (normed_in * gains[0]).astype(jnp.bfloat16)
    projected = (
        contract_last(act_in, w_qkv)
        .astype(jnp.bfloat16)
        .reshape(row_count, KV_HEADS, group_ratio + 2, HEAD)
    )
    head_data = lax.all_to_all(projected, "sp", split_axis=1, concat_axis=0, tiled=True)
    block_rows = head_data.shape[0]
    query_group = head_data[:, :, :group_ratio]
    key_heads = head_data[:, :, group_ratio]
    value_heads = head_data[:, :, group_ratio + 1]
    first_query = lax.axis_index("blk") * block_rows
    last_query = first_query + block_rows - 1
    query_places = first_query + jnp.arange(block_rows, dtype=jnp.int32)

    def tile_scores(key_tile, tile_first):
        tile_rows = key_tile.shape[0]
        raw = jnp.einsum(
            "qkgd,rkd->kgqr", query_group, key_tile, preferred_element_type=jnp.float32
        )
        squashed = jnp.tanh(raw * score_scale / CAP_VALUE)
        allowed = (tile_first + jnp.arange(tile_rows, dtype=jnp.int32))[None, :] <= query_places[
            :, None
        ]
        weights = jnp.where(allowed, jnp.exp(CAP_VALUE * squashed), 0.0)
        return (weights, squashed)

    def run_tiles(state_now, pieces, tile_step):
        key_piece, value_piece = pieces
        piece_rows = key_piece.shape[0]
        tile_rows = math.gcd(piece_rows, block_rows)
        tile_count = piece_rows // tile_rows
        key_tiles = key_piece.reshape(tile_count, tile_rows, kv_here, HEAD)
        value_tiles = value_piece.reshape(tile_count, tile_rows, kv_here, HEAD)

        def one_tile(state_in, items):
            key_tile, value_tile, tile_index = items
            return (tile_step(state_in, key_tile, value_tile, tile_index * tile_rows), None)

        state_out, unused = lax.scan(
            one_tile, state_now, (key_tiles, value_tiles, jnp.arange(tile_count, dtype=jnp.int32))
        )
        return state_out

    def forward_step(state_in, key_tile, value_tile, tile_first):

        def forward_compute(state_old):
            totals_old, summed_old = state_old
            weights, squashed = tile_scores(key_tile, tile_first)
            totals_new = totals_old + jnp.sum(weights, axis=-1)
            summed_new = summed_old + jnp.einsum(
                "kgqr,rkd->qkgd",
                weights.astype(jnp.bfloat16),
                value_tile,
                preferred_element_type=jnp.float32,
            )
            return (totals_new, summed_new)

        return lax.cond(
            tile_first <= last_query, forward_compute, lambda state_old: state_old, state_in
        )

    zero_totals = jnp.zeros((kv_here, group_ratio, block_rows), jnp.float32)
    zero_summed = jnp.zeros((block_rows, kv_here, group_ratio, HEAD), jnp.float32)
    totals, summed = run_tiles(
        (zero_totals, zero_summed),
        (
            lax.all_gather(key_heads, "blk", axis=0, tiled=True),
            lax.all_gather(value_heads, "blk", axis=0, tiled=True),
        ),
        forward_step,
    )
    totals_rows = jnp.transpose(totals, (2, 0, 1))[..., None]
    attended = summed / totals_rows
    attended_low = attended.reshape(block_rows, heads_here, HEAD).astype(jnp.bfloat16)
    attended_tokens = lax.all_to_all(
        attended_low, "sp", split_axis=0, concat_axis=1, tiled=True
    ).reshape(row_count, query_width)
    attn = jnp.dot(attended_tokens, w_out, preferred_element_type=jnp.float32)
    normed_attn, inverse_attn = norm_parts(attn)
    middle = source + normed_attn * gains[1]
    normed_mid, inverse_mid = norm_parts(middle)
    act_ffn = (normed_mid * gains[2]).astype(jnp.bfloat16)
    w_in = w_ffn[:, :2, :]
    w_down = w_ffn[:, 2, :]
    gate_up = jnp.einsum(
        "td,fkd->tkf",
        lax.all_gather(act_ffn, "blk", axis=0, tiled=True),
        w_in,
        preferred_element_type=jnp.float32,
    )
    hidden = (gelu_value(gate_up[:, 0]) * gate_up[:, 1]).astype(jnp.bfloat16)
    hidden_all = hidden
    part = hidden_all
    ffn_out = lax.psum_scatter(
        jnp.dot(part, w_down, preferred_element_type=jnp.float32).astype(jnp.bfloat16),
        "blk",
        scatter_dimension=0,
        tiled=True,
    ).astype(jnp.float32)
    normed_ffn, inverse_ffn = norm_parts(ffn_out)
    result = middle + normed_ffn * gains[3]
    grad_out = cotangent.astype(jnp.float32)
    grad_ffn_f, gain_grad3 = norm_back(grad_out, normed_ffn, inverse_ffn, gains[3])
    grad_ffn = grad_ffn_f.astype(jnp.bfloat16)
    act_piece = lax.all_gather(act_ffn, "blk", axis=0, tiled=True)
    grad_piece = lax.all_gather(grad_ffn, "blk", axis=0, tiled=True)
    gate_up = jnp.einsum("td,fkd->tkf", act_piece, w_in, preferred_element_type=jnp.float32)
    hidden = (gelu_value(gate_up[:, 0]) * gate_up[:, 1]).astype(jnp.bfloat16)
    grad_hidden = contract_last(grad_piece, w_down)
    grad_gate = grad_hidden * gate_up[:, 1] * gelu_slope(gate_up[:, 0])
    grad_up = grad_hidden * gelu_value(gate_up[:, 0])
    grad_pair = jnp.stack([grad_gate, grad_up], axis=1).astype(jnp.bfloat16)
    in_part = jnp.einsum("tkf,td->fkd", grad_pair, act_piece, preferred_element_type=jnp.float32)
    down_part = jnp.einsum("tf,td->fd", hidden, grad_piece, preferred_element_type=jnp.float32)
    weight_sum = jnp.concatenate([in_part, down_part[:, None, :]], axis=1)
    part = grad_pair
    grad_act_ffn = lax.psum_scatter(
        jnp.einsum("tkf,fkd->td", part, w_in, preferred_element_type=jnp.float32).astype(
            jnp.bfloat16
        ),
        "blk",
        scatter_dimension=0,
        tiled=True,
    ).astype(jnp.float32)
    grad_norm_mid, gain_grad2 = norm_back(grad_act_ffn, normed_mid, inverse_mid, gains[2])
    grad_middle = grad_out + grad_norm_mid
    grad_attn_f, gain_grad1 = norm_back(grad_middle, normed_attn, inverse_attn, gains[1])
    grad_attn = grad_attn_f.astype(jnp.bfloat16)
    out_term = jnp.einsum(
        "tc,td->cd", attended_tokens, grad_attn, preferred_element_type=jnp.float32
    )
    grad_attended = (
        contract_last(grad_attn, w_out).astype(jnp.bfloat16).reshape(row_count, HEADS, HEAD)
    )
    grad_heads = lax.all_to_all(
        grad_attended, "sp", split_axis=1, concat_axis=0, tiled=True
    ).reshape(block_rows, kv_here, group_ratio, HEAD)
    grad_heads_f = grad_heads.astype(jnp.float32)
    scaled = (grad_heads_f / totals_rows).astype(jnp.bfloat16)
    row_delta = jnp.transpose(
        jnp.sum(grad_heads_f * attended, axis=-1) / totals_rows[..., 0], (1, 2, 0)
    )

    def backward_step(state_in, key_tile, value_tile, tile_first):
        tile_rows = key_tile.shape[0]

        def backward_compute(state_old):
            grad_query, grad_keys, grad_values = state_old
            weights, squashed = tile_scores(key_tile, tile_first)
            grad_weights = (
                jnp.einsum("qkgd,rkd->kgqr", scaled, value_tile, preferred_element_type=jnp.float32)
                - row_delta[..., None]
            )
            grad_raw = (weights * grad_weights * (1.0 - squashed * squashed) * score_scale).astype(
                jnp.bfloat16
            )
            grad_query = grad_query + jnp.einsum(
                "kgqr,rkd->qkgd", grad_raw, key_tile, preferred_element_type=jnp.float32
            )
            key_part = jnp.einsum(
                "kgqr,qkgd->rkd", grad_raw, query_group, preferred_element_type=jnp.float32
            )
            value_part = jnp.einsum(
                "kgqr,qkgd->rkd",
                weights.astype(jnp.bfloat16),
                scaled,
                preferred_element_type=jnp.float32,
            )
            old_keys = lax.dynamic_slice_in_dim(grad_keys, tile_first, tile_rows, 0)
            grad_keys = lax.dynamic_update_slice_in_dim(
                grad_keys, old_keys + key_part, tile_first, 0
            )
            old_values = lax.dynamic_slice_in_dim(grad_values, tile_first, tile_rows, 0)
            grad_values = lax.dynamic_update_slice_in_dim(
                grad_values, old_values + value_part, tile_first, 0
            )
            return (grad_query, grad_keys, grad_values)

        return lax.cond(
            tile_first <= last_query, backward_compute, lambda state_old: state_old, state_in
        )

    start_back = (
        jnp.zeros((block_rows, kv_here, group_ratio, HEAD), jnp.float32),
        jnp.zeros((cycle_size * block_rows, kv_here, HEAD), jnp.float32),
        jnp.zeros((cycle_size * block_rows, kv_here, HEAD), jnp.float32),
    )
    grad_query, grad_keys_all, grad_values_all = run_tiles(
        start_back,
        (
            lax.all_gather(key_heads, "blk", axis=0, tiled=True),
            lax.all_gather(value_heads, "blk", axis=0, tiled=True),
        ),
        backward_step,
    )
    grad_keys, grad_values = (
        lax.psum_scatter(
            grad_keys_all.astype(jnp.bfloat16), "blk", scatter_dimension=0, tiled=True
        ).astype(jnp.float32),
        lax.psum_scatter(
            grad_values_all.astype(jnp.bfloat16), "blk", scatter_dimension=0, tiled=True
        ).astype(jnp.float32),
    )
    grad_proj_heads = jnp.concatenate(
        [grad_query, grad_keys[:, :, None], grad_values[:, :, None]], axis=2
    ).astype(jnp.bfloat16)
    grad_proj_tokens = lax.all_to_all(
        grad_proj_heads, "sp", split_axis=0, concat_axis=1, tiled=True
    )
    grad_projected = grad_proj_tokens.reshape(row_count, w_qkv.shape[0])
    grad_act_in = jnp.dot(grad_projected, w_qkv, preferred_element_type=jnp.float32)
    grad_source, gain_grad0 = norm_back(grad_act_in, normed_in, inverse_in, gains[0])
    tokens_grad = (grad_middle + grad_source).astype(jnp.bfloat16)
    gains_term = jnp.stack([gain_grad0, gain_grad1, gain_grad2, gain_grad3], axis=0)
    qkv_term = jnp.einsum("tc,td->cd", grad_projected, act_in, preferred_element_type=jnp.float32)
    ffn_grad, qkv_part, out_part, gains_part = (
        lax.psum_scatter(
            weight_sum.astype(jnp.bfloat16), "sp", scatter_dimension=0, tiled=True
        ).astype(jnp.float32),
        lax.psum_scatter(
            qkv_term.astype(jnp.bfloat16), "sp", scatter_dimension=0, tiled=True
        ).astype(jnp.float32),
        lax.psum_scatter(
            out_term.astype(jnp.bfloat16), "sp", scatter_dimension=0, tiled=True
        ).astype(jnp.float32),
        lax.psum_scatter(
            gains_term.astype(jnp.bfloat16), "sp", scatter_dimension=1, tiled=True
        ).astype(jnp.float32),
    )
    qkv_grad, out_grad, gains_grad = (
        lax.psum_scatter(
            qkv_part.astype(jnp.bfloat16), "blk", scatter_dimension=0, tiled=True
        ).astype(jnp.float32),
        lax.psum_scatter(
            out_part.astype(jnp.bfloat16), "blk", scatter_dimension=0, tiled=True
        ).astype(jnp.float32),
        lax.psum_scatter(
            gains_part.astype(jnp.bfloat16), "blk", scatter_dimension=1, tiled=True
        ).astype(jnp.float32),
    )
    return (result.astype(jnp.bfloat16), tokens_grad, qkv_grad, out_grad, gains_grad, ffn_grad)


def solution(mesh):
    return jax.shard_map(
        body,
        mesh=mesh,
        in_specs=(
            P(("blk", "sp"), None),
            P(),
            P(),
            P(),
            P("blk", None, None),
            P(("blk", "sp"), None),
        ),
        out_specs=(
            P(("blk", "sp"), None),
            P(("blk", "sp"), None),
            P(("sp", "blk"), None),
            P(("sp", "blk"), None),
            P(None, ("sp", "blk")),
            P(("blk", "sp"), None, None),
        ),
        check_vma=False,
    )
```

profile of v0, /device:TPU:26, one launch (start us, length us, event | category | flops | bytes accessed | tf_op | source)
XLA Modules:
  0.0 1480.2 jit_solution(1569440908455529645)
XLA Ops:
  9.5 12.8 convolution_convert_fusion.5
  23.5 15.9 %all_to_all.57 = bf16[128,4,4,256]{3,2,0,1:T(4,128)(2,1)S(1)} all-to-all(bf16[128,4,4,256]{3,2,0,1:T(4,128)(2,1)S(1)} %copy.95), channel_id=1, replica_groups=mesh['blk'=8,'sp'=4] {'sp'}, dimensions={1} | all-to-all | bytes 2097152 | tf_op jit(solution)/shard_map/all_to_all | solution.py:68
  41.3 48.0 %all-gather.13.cloned.1.call-done = bf16[4096,1,1,256]{3,0,2,1:T(8,128)(2,1)} async-done(((bf16[512,1,1,256]{3,0,2,1:T(8,128)(2,1)}), bf16[4096,1,1,256]{3,0,2,1:T(8,128)(2,1)}) %all-gather.13.cloned.1.call-update) | async-done | bytes 2097168 | tf_op jit(solution)/shard_map/all_gather | solution.py:130
  89.3 3.9 copy.98
  93.3 46.4 %all-gather.11.cloned.1.call-done = bf16[4096,1,1,256]{3,0,2,1:T(8,128)(2,1)} async-done(((bf16[512,1,1,256]{3,0,2,1:T(8,128)(2,1)}), bf16[4096,1,1,256]{3,0,2,1:T(8,128)(2,1)}) %all-gather.11.cloned.1.call-update) | async-done | bytes 2097168 | tf_op jit(solution)/shard_map/all_gather | solution.py:129
  139.8 35.6 %while.28 = (s32[]{:T(128)}, f32[1,2,512]{2,1,0:T(2,128)S(1)}, f32[512,1,2,256]{0,3,2,1:T(8,128)S(1)}, s32[8]{0:T(128)S(1)}, s32[]{:T(128)}, /*index=5*/bf16[8,5...) while((s32[]{:T(128)}, f32[1,2,512]{2,1,0:T(2,128)S(1)}, ...), condition=%wide.region_5.6_spmd.clone, body=%wide.region_1.5_spmd.clone.sunk | while | flops 540017664 | bytes 5797131 | solution.py:101
  141.1 3.6 conditional.6
  146.0 3.6 conditional.6
  150.9 3.6 conditional.6
  155.8 3.6 conditional.6
  160.7 3.6 conditional.6
  165.6 3.6 conditional.6
  170.5 3.6 conditional.6
  177.8 10.3 all_to_all.58
  188.5 5.4 multiply_reduce_fusion.3
  195.6 81.3 %all-gather.7.cloned.1.call-done = bf16[1024,2304]{1,0:T(8,128)(2,1)} async-done(((bf16[128,2304]{1,0:T(8,128)(2,1)}), bf16[1024,2304]{1,0:T(8,128)(2,1)}) %all-gather.7.cloned.1.call-update) | async-done | bytes 4718608 | tf_op jit(solution)/shard_map/all_gather | solution.py:149
  276.9 16.6 %fusion.51 = f32[1024,2,1152]{2,0,1:T(8,128)S(1)} fusion(bf16[1152,3,2304]{2,0,1:T(8,128)(2,1)} %param.18, bf16[1024,2304]{1,0:T(8,128)(2,1)} %all-gather.7.cloned.1.call-done), kind=kOutput, calls=%fused_computation.73 | convolution fusion | flops 10871635968 | bytes 24772608 | tf_op jit(solution)/shard_map/td,fkd->tkf/dot_general | solution.py:147
  293.5 3.7 copy-done.20
  297.2 11.3 convolution_convert_fusion.4
  308.5 94.5 %reduce-scatter.16.cloned.1.call-done = bf16[128,2304]{1,0:T(8,128)(2,1)} async-done(((bf16[1024,2304]{1,0:T(8,128)(2,1)}), bf16[128,2304]{1,0:T(8,128)(2,1)}) %reduce-scatter.16.cloned.1.call-update) | async-done | bytes 589840 | tf_op jit(solution)/shard_map/reduce_scatter | solution.py:156
  408.6 78.3 %all-gather.9.cloned.1.call-done = bf16[1024,2304]{1,0:T(8,128)(2,1)} async-done(((bf16[128,2304]{1,0:T(8,128)(2,1)}), bf16[1024,2304]{1,0:T(8,128)(2,1)}) %all-gather.9.cloned.1.call-update) | async-done | bytes 4718608 | tf_op jit(solution)/shard_map/all_gather | solution.py:168
  486.9 14.7 fusion.85
  503.7 14.7 bitcast_convert_fusion
  518.5 94.5 %reduce-scatter.18.cloned.1.call-done = bf16[128,2304]{1,0:T(8,128)(2,1)} async-done(((bf16[1024,2304]{1,0:T(8,128)(2,1)}), bf16[128,2304]{1,0:T(8,128)(2,1)}) %reduce-scatter.18.cloned.1.call-update) | async-done | bytes 589840 | tf_op jit(solution)/shard_map/reduce_scatter | solution.py:179
  618.8 7.0 convolution_convert_fusion.6
  626.6 4.0 all-to-all-start.2
  631.0 6.9 all-to-all-done.2
  645.8 127.8 %while.29 = (s32[]{:T(128)}, f32[512,1,2,256]{0,3,2,1:T(8,128)S(1)}, f32[4096,1,256]{2,0,1:T(8,128)}, f32[4096,1,256]{2,0,1:T(8,128)}, s32[8]{0:T(128)S(1)}, /*i...) while((s32[]{:T(128)}, ...), condition=%wide.region_18.19_spmd.clone, body=%wide.region_15.18_spmd.clone.sunk | while | flops 1350304768 | bytes 27805592 | solution.py:101
  647.1 16.7 %conditional.7 = ((f32[512,1,2,256]{0,3,2,1:T(8,128)S(1)}, f32[4096,1,256]{2,0,1:T(8,128)}, f32[4096,1,256]{2,0,1:T(8,128)})) conditional(s32[]{:T(128)} %convert_element_type.314, (f32[512,1,2,256]{0,3,2,1:T(8,128)S(1)}, f32[4096,1,256]{2,0,1:T(8,128)}, f32[4096,1,256]{2,0,1:T(8,128)}) %tuple.108, (bf16[8,512,1,256]{3,1,2,0:T(8,128)(2,1)}, ...), branch_computations={%region_16.16_spmd, %region_17.17_spmd} | conditional | flops 1350304768 | bytes 27803254 | solution.py:241
  654.0 3.0 dynamic_update_slice.8
  665.2 16.8 %conditional.7 = ((f32[512,1,2,256]{0,3,2,1:T(8,128)S(1)}, f32[4096,1,256]{2,0,1:T(8,128)}, f32[4096,1,256]{2,0,1:T(8,128)})) conditional(s32[]{:T(128)} %convert_element_type.314, (f32[512,1,2,256]{0,3,2,1:T(8,128)S(1)}, f32[4096,1,256]{2,0,1:T(8,128)}, f32[4096,1,256]{2,0,1:T(8,128)}) %tuple.108, (bf16[8,512,1,256]{3,1,2,0:T(8,128)(2,1)}, ...), branch_computations={%region_16.16_spmd, %region_17.17_spmd} | conditional | flops 1350304768 | bytes 27803254 | solution.py:241
  672.0 3.0 dynamic_update_slice.8
  677.6 3.0 dynamic_update_slice.9
  683.3 16.8 %conditional.7 = ((f32[512,1,2,256]{0,3,2,1:T(8,128)S(1)}, f32[4096,1,256]{2,0,1:T(8,128)}, f32[4096,1,256]{2,0,1:T(8,128)})) conditional(s32[]{:T(128)} %convert_element_type.314, (f32[512,1,2,256]{0,3,2,1:T(8,128)S(1)}, f32[4096,1,256]{2,0,1:T(8,128)}, f32[4096,1,256]{2,0,1:T(8,128)}) %tuple.108, (bf16[8,512,1,256]{3,1,2,0:T(8,128)(2,1)}, ...), branch_computations={%region_16.16_spmd, %region_17.17_spmd} | conditional | flops 1350304768 | bytes 27803254 | solution.py:241
  690.1 3.0 dynamic_update_slice.8
  695.6 3.0 dynamic_update_slice.9
  701.3 16.7 %conditional.7 = ((f32[512,1,2,256]{0,3,2,1:T(8,128)S(1)}, f32[4096,1,256]{2,0,1:T(8,128)}, f32[4096,1,256]{2,0,1:T(8,128)})) conditional(s32[]{:T(128)} %convert_element_type.314, (f32[512,1,2,256]{0,3,2,1:T(8,128)S(1)}, f32[4096,1,256]{2,0,1:T(8,128)}, f32[4096,1,256]{2,0,1:T(8,128)}) %tuple.108, (bf16[8,512,1,256]{3,1,2,0:T(8,128)(2,1)}, ...), branch_computations={%region_16.16_spmd, %region_17.17_spmd} | conditional | flops 1350304768 | bytes 27803254 | solution.py:241
  708.2 3.0 dynamic_update_slice.8
  719.4 16.8 %conditional.7 = ((f32[512,1,2,256]{0,3,2,1:T(8,128)S(1)}, f32[4096,1,256]{2,0,1:T(8,128)}, f32[4096,1,256]{2,0,1:T(8,128)})) conditional(s32[]{:T(128)} %convert_element_type.314, (f32[512,1,2,256]{0,3,2,1:T(8,128)S(1)}, f32[4096,1,256]{2,0,1:T(8,128)}, f32[4096,1,256]{2,0,1:T(8,128)}) %tuple.108, (bf16[8,512,1,256]{3,1,2,0:T(8,128)(2,1)}, ...), branch_computations={%region_16.16_spmd, %region_17.17_spmd} | conditional | flops 1350304768 | bytes 27803254 | solution.py:241
  731.7 3.0 dynamic_update_slice.9
  737.4 16.8 %conditional.7 = ((f32[512,1,2,256]{0,3,2,1:T(8,128)S(1)}, f32[4096,1,256]{2,0,1:T(8,128)}, f32[4096,1,256]{2,0,1:T(8,128)})) conditional(s32[]{:T(128)} %convert_element_type.314, (f32[512,1,2,256]{0,3,2,1:T(8,128)S(1)}, f32[4096,1,256]{2,0,1:T(8,128)}, f32[4096,1,256]{2,0,1:T(8,128)}) %tuple.108, (bf16[8,512,1,256]{3,1,2,0:T(8,128)(2,1)}, ...), branch_computations={%region_16.16_spmd, %region_17.17_spmd} | conditional | flops 1350304768 | bytes 27803254 | solution.py:241
  749.8 3.0 dynamic_update_slice.9
  755.5 16.8 %conditional.7 = ((f32[512,1,2,256]{0,3,2,1:T(8,128)S(1)}, f32[4096,1,256]{2,0,1:T(8,128)}, f32[4096,1,256]{2,0,1:T(8,128)})) conditional(s32[]{:T(128)} %convert_element_type.314, (f32[512,1,2,256]{0,3,2,1:T(8,128)S(1)}, f32[4096,1,256]{2,0,1:T(8,128)}, f32[4096,1,256]{2,0,1:T(8,128)}) %tuple.108, (bf16[8,512,1,256]{3,1,2,0:T(8,128)(2,1)}, ...), branch_computations={%region_16.16_spmd, %region_17.17_spmd} | conditional | flops 1350304768 | bytes 27803254 | solution.py:241
  767.9 3.0 dynamic_update_slice.9
  773.6 3.7 convert_element_type.179
  777.4 3.7 convert_element_type.180
  782.3 5.0 convolution_convert_fusion.3
  788.0 72.2 %reduce-scatter.20.cloned.1.call-done = bf16[512,1,256]{2,0,1:T(8,128)(2,1)} async-done(((bf16[4096,1,256]{2,0,1:T(8,128)(2,1)}), bf16[512,1,256]{2,0,1:T(8,128)(2,1)}) %reduce-scatter.20.cloned.1.call-update) | async-done | bytes 262160 | tf_op jit(solution)/shard_map/reduce_scatter | solution.py:259
  861.6 70.3 %reduce-scatter.22.cloned.1.call-done = bf16[512,1,256]{2,0,1:T(8,128)(2,1)} async-done(((bf16[4096,1,256]{2,0,1:T(8,128)(2,1)}), bf16[512,1,256]{2,0,1:T(8,128)(2,1)}) %reduce-scatter.22.cloned.1.call-update) | async-done | bytes 262160 | tf_op jit(solution)/shard_map/reduce_scatter | solution.py:262
  935.0 16.1 %all_to_all.59 = bf16[512,1,4,256]{3,2,1,0:T(4,128)(2,1)S(1)} all-to-all(bf16[512,1,4,256]{3,2,1,0:T(4,128)(2,1)S(1)} %pad_maximum_fusion.4), channel_id=1, replica_groups=mesh['blk'=8,'sp'=4] {'sp'}, dimensions={0} | all-to-all | bytes 2097152 | tf_op jit(solution)/shard_map/all_to_all | solution.py:269
  953.9 9.5 convolution_convert_fusion
  963.5 12.9 fusion.46
  976.4 17.3 %fusion.45 = bf16[1152,2,2304]{0,2,1:T(8,128)(2,1)} fusion(bf16[1024,2304]{1,0:T(8,128)(2,1)} %all-gather.7.cloned.1.call-done, bf16[1024,1,1152]{2,0,1:T(8,128)(2,1)} %copy-done.22, bf16[1024,1,1152]{2,0,1:T(8,128)(2,1)} %copy-done.21), kind=kOutput, calls=%fused_computation.61 | convolution fusion | flops 10886381568 | bytes 20054016 | tf_op jit(solution)/shard_map/tkf,td->fkd/dot_general | solution.py:175
  993.8 5.1 fusion.112
  1000.2 13.4 pad_maximum_fusion
  1013.6 21.5 %copy.131 = bf16[1152,6912]{1,0:T(8,128)(2,1)} copy(bf16[1152,6912]{0,1:T(8,128)(2,1)} %bitcast.253) | data formatting | bytes 31850496
  1035.9 116.4 %reduce-scatter.24.cloned.1.call-done = bf16[1024,2304]{1,0:T(8,128)(2,1)} async-done(((bf16[4096,2304]{1,0:T(8,128)(2,1)}), bf16[1024,2304]{1,0:T(8,128)(2,1)}) %reduce-scatter.24.cloned.1.call-update) | async-done | bytes 4718608 | tf_op jit(solution)/shard_map/reduce_scatter | solution.py:282
  1156.7 20.8 %reduce-scatter.32.cloned.1.call-done = bf16[576,4]{1,0:T(8,128)(2,1)} async-done(((bf16[2304,4]{1,0:T(8,128)(2,1)}), bf16[576,4]{1,0:T(8,128)(2,1)}) %reduce-scatter.32.cloned.1.call-update) | async-done | bytes 4624
  1178.4 17.1 %all-reduce = bf16[4,576]{1,0:T(4,128)(2,1)S(1)} all-reduce(bf16[4,576]{1,0:T(4,128)(2,1)S(1)} %copy.126), channel_id=13, replica_groups=mesh['blk'=8,'sp'=4] {'blk'}, use_global_device_ids=true, to_apply=%region_31.32.clone | all-reduce | flops 2304 | bytes 9216
  1196.2 103.8 %reduce-scatter.34.cloned.1.call-done = bf16[288,6912]{1,0:T(8,128)(2,1)} async-done(((bf16[1152,6912]{1,0:T(8,128)(2,1)}), bf16[288,6912]{1,0:T(8,128)(2,1)}) %reduce-scatter.34.cloned.1.call-update) | async-done | bytes 3981328
  1300.0 6.6 copy.132
  1306.6 7.4 copy.117
  1313.9 58.7 %reduce-scatter.30.cloned.1.call-done = bf16[64,2304]{1,0:T(8,128)(2,1)} async-done(((bf16[512,2304]{1,0:T(8,128)(2,1)}), bf16[64,2304]{1,0:T(8,128)(2,1)}) %reduce-scatter.30.cloned.1.call-update) | async-done | bytes 294928 | tf_op jit(solution)/shard_map/reduce_scatter | solution.py:296
  1374.4 96.7 %reduce-scatter.26.cloned.1.call-done = bf16[128,2304]{1,0:T(8,128)(2,1)} async-done(((bf16[1024,2304]{1,0:T(8,128)(2,1)}), bf16[128,2304]{1,0:T(8,128)(2,1)}) %reduce-scatter.26.cloned.1.call-update) | async-done | bytes 589840 | tf_op jit(solution)/shard_map/reduce_scatter | solution.py:293
  (280 shorter events, 178.1 us)
Async XLA Ops:
  7.2 82.2 %all-gather.13.cloned.1.call-start = ((), (), s32[]{:S(2)}) async-start(), calls=%async_computation.25 | async-start | bytes 2359296 | tf_op jit(solution)/shard_map/all_gather | solution.py:130
  8.2 14.1 copy-start.15
  9.5 12.8 copy-start.17
  40.5 99.2 %all-gather.11.cloned.1.call-start = ((), (), s32[]{:S(2)}) async-start(), calls=%async_computation.24 | async-start | bytes 2359296 | tf_op jit(solution)/shard_map/all_gather | solution.py:129
  41.2 235.7 %all-gather.7.cloned.1.call-start = ((), (), s32[]{:S(2)}) async-start(), calls=%async_computation.14 | async-start | bytes 5308416 | tf_op jit(solution)/shard_map/all_gather | solution.py:149
  175.6 2.2 copy-start.13
  188.4 5.4 copy-start.7
  188.5 5.4 copy-start.1
  195.3 207.7 %reduce-scatter.16.cloned.1.call-start = ((), (), s32[]{:S(2)}) async-start(), calls=%async_computation.15 | async-start | bytes 5308416 | tf_op jit(solution)/shard_map/reduce_scatter | solution.py:156
  293.5 3.7 copy-start.20
  308.4 95.9 %copy-start.11 = (bf16[128,2304]{1,0:T(8,128)(2,1)S(1)}, bf16[128,2304]{1,0:T(8,128)(2,1)}, u32[]{:S(2)}) copy-start(bf16[128,2304]{1,0:T(8,128)(2,1)} %param.19) | copy-start | bytes 1769476
  308.5 178.4 %all-gather.9.cloned.1.call-start = ((), (), s32[]{:S(2)}) async-start(), calls=%async_computation.16 | async-start | bytes 5308416 | tf_op jit(solution)/shard_map/all_gather | solution.py:168
  408.1 204.8 %reduce-scatter.18.cloned.1.call-start = ((), (), s32[]{:S(2)}) async-start(), calls=%async_computation.17 | async-start | bytes 5308416 | tf_op jit(solution)/shard_map/reduce_scatter | solution.py:179
  501.6 1.4 copy-start.21
  501.6 2.1 copy-start.22
  518.4 96.0 %copy-start.6 = (bf16[128,2304]{1,0:T(8,128)(2,1)S(1)}, bf16[128,2304]{1,0:T(8,128)(2,1)}, u32[]{:S(2)}) copy-start(bf16[128,2304]{1,0:T(8,128)(2,1)} %reduce-scatter.16.cloned.1.call-done) | copy-start | bytes 1769476
  617.4 1.0 copy-start.4
  618.7 7.0 copy-start.9
  625.8 12.6 copy-start.12
  625.8 12.6 copy-start.14
  626.6 11.2 all-to-all-start.2
  630.6 229.6 %reduce-scatter.20.cloned.1.call-start = ((), (), s32[]{:S(2)}) async-start(), calls=%async_computation.18 | async-start | bytes 2359296 | tf_op jit(solution)/shard_map/reduce_scatter | solution.py:259
  648.8 1.4 copy-start
  666.8 1.4 copy-start
  684.9 1.4 copy-start
  703.0 1.4 copy-start
  721.1 1.4 copy-start
  739.1 1.4 copy-start
  757.2 1.4 copy-start
  777.3 154.6 %reduce-scatter.22.cloned.1.call-start = ((), (), s32[]{:S(2)}) async-start(), calls=%async_computation.19 | async-start | bytes 2359296 | tf_op jit(solution)/shard_map/reduce_scatter | solution.py:262
  781.1 1.0 copy-start.8
  781.1 1.2 copy-start.10
  781.1 254.1 %reduce-scatter.28.cloned.1.call-start = ((), (), s32[]{:S(2)}) async-start(), calls=%async_computation.22 | async-start | bytes 11796480 | tf_op jit(solution)/shard_map/reduce_scatter | solution.py:285
  787.3 364.9 %reduce-scatter.24.cloned.1.call-start = ((), (), s32[]{:S(2)}) async-start(), calls=%async_computation.20 | async-start | bytes 23592960 | tf_op jit(solution)/shard_map/reduce_scatter | solution.py:282
  951.1 2.8 copy-start.2
  951.1 2.8 copy-start.16
  951.1 2.8 copy-start.18
  953.8 9.5 copy-start.3
  963.4 214.0 %reduce-scatter.32.cloned.1.call-start = ((), (), s32[]{:S(2)}) async-start(), calls=%async_computation.26 | async-start | bytes 737280
  963.4 30.3 %slice-start = ((s8[18874368]{0:T(1024)(128)(4,1)}), s8[4194304]{0:T(1024)(128)(4,1)S(1)}, s32[]{:S(2)}) async-start(s8[18874368]{0:T(1024)(128)(4,1)} %bitcast.251), calls=%async_computation.28 | async-start | bytes 8388608
  963.5 30.3 %slice-start.1 = ((s8[18874368]{0:T(1024)(128)(4,1)}), s8[4194304]{0:T(1024)(128)(4,1)S(1)}, s32[]{:S(2)}) async-start(s8[18874368]{0:T(1024)(128)(4,1)} %bitcast.251), calls=%async_computation.29 | async-start | bytes 8388608
  976.4 17.4 %slice-start.2 = ((s8[18874368]{0:T(1024)(128)(4,1)}), s8[4194304]{0:T(1024)(128)(4,1)S(1)}, s32[]{:S(2)}) async-start(s8[18874368]{0:T(1024)(128)(4,1)} %bitcast.251), calls=%async_computation.30 | async-start | bytes 8388608
  976.4 17.4 %slice-start.3 = ((s8[18874368]{0:T(1024)(128)(4,1)}), s8[4194304]{0:T(1024)(128)(4,1)S(1)}, s32[]{:S(2)}) async-start(s8[18874368]{0:T(1024)(128)(4,1)} %bitcast.251), calls=%async_computation.31 | async-start | bytes 8388608
  976.4 17.4 %slice-start.4 = ((s8[18874368]{0:T(1024)(128)(4,1)}), s8[2097152]{0:T(1024)(128)(4,1)S(1)}, s32[]{:S(2)}) async-start(s8[18874368]{0:T(1024)(128)(4,1)} %bitcast.251), calls=%async_computation.32 | async-start | bytes 4194304
  1000.1 299.8 %reduce-scatter.34.cloned.1.call-start = ((), (), s32[]{:S(2)}) async-start(), calls=%async_computation.27 | async-start | bytes 19906560
  1035.1 337.5 %reduce-scatter.30.cloned.1.call-start = ((), (), s32[]{:S(2)}) async-start(), calls=%async_computation.23 | async-start | bytes 2654208 | tf_op jit(solution)/shard_map/reduce_scatter | solution.py:296
  1035.8 435.3 %reduce-scatter.26.cloned.1.call-start = ((), (), s32[]{:S(2)}) async-start(), calls=%async_computation.21 | async-start | bytes 5308416 | tf_op jit(solution)/shard_map/reduce_scatter | solution.py:293
  1152.2 0.7 copy-start.19
  1152.3 1.9 copy-start.5
Sparse Core Ops, SparseCore 0:
  40.6 48.7 all-gather.12
  92.0 47.6 all-gather.10
  195.4 81.4 all-gather.6
  308.6 94.3 reduce-scatter.15
  408.2 78.5 all-gather.8
  518.6 94.3 reduce-scatter.17
  777.4 82.7 reduce-scatter.19
  864.3 67.5 reduce-scatter.21
  934.5 77.3 reduce-scatter.27
  1014.4 137.8 reduce-scatter.23
  1155.3 22.0 reduce-scatter.31
  1179.9 120.0 reduce-scatter.33
  1303.5 69.0 reduce-scatter.29
  1376.1 94.9 reduce-scatter.25
where the time goes:
time: 1490 us; the launch traced here: 1480 us
  waiting for transfers between devices  990 us (66%)
  matrix products  220 us (15%)
  local copies, waits for them, and re-layouts  129 us (9%)
  blocking collectives  59.4 us (4%)
  other arithmetic  48.8 us (3%)
  between operations  15.6 us (1%)
    unnamed x16, waiting for transfers between devices  126 us
    reduce_scatter x1, waiting for transfers between devices, body(): lax.psum_scatter(qkv_term.astype(jnp.bfloat16), 'sp', scatter_dimension=0...  116 us
    reduce_scatter x1, waiting for transfers between devices, body(): lax.psum_scatter(qkv_part.astype(jnp.bfloat16), 'blk', scatter_dimension=...  96.7 us
    reduce_scatter x1, waiting for transfers between devices, body(): lax.psum_scatter(jnp.dot(part, w_down, preferred_element_type=jnp.float32...  94.5 us
    reduce_scatter x1, waiting for transfers between devices, body(): lax.psum_scatter(jnp.einsum('tkf,fkd->td', part, w_in, preferred_element_...  94.5 us
    all_gather x1, waiting for transfers between devices, body(): lax.all_gather(act_ffn, 'blk', axis=0, tiled=True)  81.3 us
    all_gather x1, waiting for transfers between devices, body(): grad_piece = lax.all_gather(grad_ffn, 'blk', axis=0, tiled=True)  78.3 us
    reduce_scatter x1, waiting for transfers between devices, body(): lax.psum_scatter(grad_keys_all.astype(jnp.bfloat16), 'blk', scatter_dimen...  72.2 us
  transfers between devices with their start and end apart: 15, of which 14 were waited for; matrix products, arithmetic and copies ran while one was open for 8% of the time, Pallas kernels for 0%

commit v1 on v0

--- a/solution.py
+++ b/solution.py
@@ -60,12 +60,15 @@
     source = tokens.astype(jnp.float32)
     normed_in, inverse_in = norm_parts(source)
     act_in = (normed_in * gains[0]).astype(jnp.bfloat16)
-    projected = (
-        contract_last(act_in, w_qkv)
+    act_block = lax.all_gather(act_in, "sp", axis=0, tiled=True)
+    group_cols = (group_ratio + 2) * HEAD * kv_here
+    sp_at = lax.axis_index("sp")
+    w_group = lax.dynamic_slice_in_dim(w_qkv, sp_at * group_cols, group_cols, 0)
+    head_data = (
+        contract_last(act_block, w_group)
         .astype(jnp.bfloat16)
-        .reshape(row_count, KV_HEADS, group_ratio + 2, HEAD)
-    )
-    head_data = lax.all_to_all(projected, "sp", split_axis=1, concat_axis=0, tiled=True)
+        .reshape(act_block.shape[0], kv_here, group_ratio + 2, HEAD)
+    )
     block_rows = head_data.shape[0]
     query_group = head_data[:, :, :group_ratio]
     key_heads = head_data[:, :, group_ratio]
@@ -188,15 +191,20 @@
     grad_middle = grad_out + grad_norm_mid
     grad_attn_f, gain_grad1 = norm_back(grad_middle, normed_attn, inverse_attn, gains[1])
     grad_attn = grad_attn_f.astype(jnp.bfloat16)
+    grad_block = lax.all_gather(grad_attn, "sp", axis=0, tiled=True)
+    attended_cols = attended_low.reshape(block_rows, heads_here * HEAD)
     out_term = jnp.einsum(
-        "tc,td->cd", attended_tokens, grad_attn, preferred_element_type=jnp.float32
-    )
-    grad_attended = (
-        contract_last(grad_attn, w_out).astype(jnp.bfloat16).reshape(row_count, HEADS, HEAD)
-    )
-    grad_heads = lax.all_to_all(
-        grad_attended, "sp", split_axis=1, concat_axis=0, tiled=True
-    ).reshape(block_rows, kv_here, group_ratio, HEAD)
+        "tc,td->cd", attended_cols, grad_block, preferred_element_type=jnp.float32
+    )
+    out_grad = lax.psum_scatter(
+        out_term.astype(jnp.bfloat16), "blk", scatter_dimension=0, tiled=True
+    ).astype(jnp.float32)
+    w_out_group = lax.dynamic_slice_in_dim(w_out, sp_at * heads_here * HEAD, heads_here * HEAD, 0)
+    grad_heads = (
+        contract_last(grad_block, w_out_group)
+        .astype(jnp.bfloat16)
+        .reshape(block_rows, kv_here, group_ratio, HEAD)
+    )
     grad_heads_f = grad_heads.astype(jnp.float32)
     scaled = (grad_heads_f / totals_rows).astype(jnp.bfloat16)
     row_delta = jnp.transpose(
@@ -266,40 +274,22 @@
     grad_proj_heads = jnp.concatenate(
         [grad_query, grad_keys[:, :, None], grad_values[:, :, None]], axis=2
     ).astype(jnp.bfloat16)
-    grad_proj_tokens = lax.all_to_all(
-        grad_proj_heads, "sp", split_axis=0, concat_axis=1, tiled=True
-    )
+    grad_cols = grad_proj_heads.reshape(block_rows, group_cols)
+    qkv_term = jnp.einsum("tc,td->cd", grad_cols, act_block, preferred_element_type=jnp.float32)
+    qkv_grad = lax.psum_scatter(
+        qkv_term.astype(jnp.bfloat16), "blk", scatter_dimension=0, tiled=True
+    ).astype(jnp.float32)
+    grad_proj_tokens = lax.all_to_all(grad_proj_heads, "sp", split_axis=0, concat_axis=1, tiled=True)
     grad_projected = grad_proj_tokens.reshape(row_count, w_qkv.shape[0])
     grad_act_in = jnp.dot(grad_projected, w_qkv, preferred_element_type=jnp.float32)
     grad_source, gain_grad0 = norm_back(grad_act_in, normed_in, inverse_in, gains[0])
     tokens_grad = (grad_middle + grad_source).astype(jnp.bfloat16)
     gains_term = jnp.stack([gain_grad0, gain_grad1, gain_grad2, gain_grad3], axis=0)
-    qkv_term = jnp.einsum("tc,td->cd", grad_projected, act_in, preferred_element_type=jnp.float32)
-    ffn_grad, qkv_part, out_part, gains_part = (
-        lax.psum_scatter(
-            weight_sum.astype(jnp.bfloat16), "sp", scatter_dimension=0, tiled=True
-        ).astype(jnp.float32),
-        lax.psum_scatter(
-            qkv_term.astype(jnp.bfloat16), "sp", scatter_dimension=0, tiled=True
-        ).astype(jnp.float32),
-        lax.psum_scatter(
-            out_term.astype(jnp.bfloat16), "sp", scatter_dimension=0, tiled=True
-        ).astype(jnp.float32),
-        lax.psum_scatter(
-            gains_term.astype(jnp.bfloat16), "sp", scatter_dimension=1, tiled=True
-        ).astype(jnp.float32),
-    )
-    qkv_grad, out_grad, gains_grad = (
-        lax.psum_scatter(
-            qkv_part.astype(jnp.bfloat16), "blk", scatter_dimension=0, tiled=True
-        ).astype(jnp.float32),
-        lax.psum_scatter(
-            out_part.astype(jnp.bfloat16), "blk", scatter_dimension=0, tiled=True
-        ).astype(jnp.float32),
-        lax.psum_scatter(
-            gains_part.astype(jnp.bfloat16), "blk", scatter_dimension=1, tiled=True
-        ).astype(jnp.float32),
-    )
+    ffn_grad = lax.psum_scatter(
+        weight_sum.astype(jnp.bfloat16), "sp", scatter_dimension=0, tiled=True
+    ).astype(jnp.float32)
+    gains_part = lax.psum_scatter(gains_term, "sp", scatter_dimension=1, tiled=True)
+    gains_grad = lax.psum_scatter(gains_part, "blk", scatter_dimension=1, tiled=True)
     return (result.astype(jnp.bfloat16), tokens_grad, qkv_grad, out_grad, gains_grad, ffn_grad)
 
 

time: 1490 us -> 1310 us (0.88)
  waiting for transfers between devices: 990 us -> 839 us
  other arithmetic: 48.8 us -> 33.1 us
  blocking collectives: 59.4 us -> 44.4 us
    reduce_scatter x4 -> x2, waiting for transfers between devices: 272 us -> 64.1 us  [the longest x1 64.1 us: body(): lax.psum_scatter(qkv_term.astype(jnp.bfloat16), 'blk', scatter_dimension=...]
    all_gather x0 -> x2, waiting for transfers between devices: none -> 47.9 us  [the longest x1 24.2 us: body(): act_block = lax.all_gather(act_in, 'sp', axis=0, tiled=True)]
    all_to_all x2 -> x0, blocking collectives: 32 us -> none  [the longest x1 16.1 us: body(): lax.all_to_all(grad_proj_heads, 'sp', split_axis=0, concat_axis=1, tiled=...]
    unnamed x1, blocking collectives: 17.1 us -> 34.1 us
    unnamed x63 -> x50, local copies, waits for them, and re-layouts: 51.7 us -> 54.9 us
  transfers between devices with their start and end apart: 15 -> 15, of which waited for: 14 -> 14; matrix products, arithmetic and copies ran while one was open for 8% -> 7% of each run, Pallas kernels for 0% -> 0%
where the time goes in v1:
time: 1310 us; the launch traced here: 1300 us
  waiting for transfers between devices  839 us (64%)
  matrix products  213 us (16%)
  local copies, waits for them, and re-layouts  137 us (10%)
  blocking collectives  44.4 us (3%)
  other arithmetic  33.1 us (3%)
  between operations  15.2 us (1%)
    unnamed x16, waiting for transfers between devices  124 us
    reduce_scatter x1, waiting for transfers between devices, body(): lax.psum_scatter(jnp.dot(part, w_down, preferred_element_type=jnp.float32...  94.5 us
    reduce_scatter x1, waiting for transfers between devices, body(): lax.psum_scatter(jnp.einsum('tkf,fkd->td', part, w_in, preferred_element_...  94.5 us
    all_gather x1, waiting for transfers between devices, body(): lax.all_gather(act_ffn, 'blk', axis=0, tiled=True)  81.4 us
    all_gather x1, waiting for transfers between devices, body(): grad_piece = lax.all_gather(grad_ffn, 'blk', axis=0, tiled=True)  78.5 us
    reduce_scatter x1, waiting for transfers between devices, body(): lax.psum_scatter(grad_values_all.astype(jnp.bfloat16), 'blk', scatter_dim...  75.5 us
    reduce_scatter x1, waiting for transfers between devices, body(): lax.psum_scatter(grad_keys_all.astype(jnp.bfloat16), 'blk', scatter_dimen...  71.3 us
    reduce_scatter x1, waiting for transfers between devices, body(): lax.psum_scatter(qkv_term.astype(jnp.bfloat16), 'blk', scatter_dimension=...  64.1 us
  transfers between devices with their start and end apart: 15, of which 14 were waited for; matrix products, arithmetic and copies ran while one was open for 7% of the time, Pallas kernels for 0%

profile of v1, /device:TPU:26, one launch (start us, length us, event | category | flops | bytes accessed | tf_op | source)
XLA Modules:
  0.0 1298.2 jit_solution(2162536864589294923)
XLA Ops:
  12.2 24.2 %all-gather.9.cloned.1.call-done = bf16[512,2304]{1,0:T(8,128)(2,1)} async-done(((bf16[128,2304]{1,0:T(8,128)(2,1)}), bf16[512,2304]{1,0:T(8,128)(2,1)}) %all-gather.9.cloned.1.call-update) | async-done | bytes 2359312 | tf_op jit(solution)/shard_map/all_gather | solution.py:63
  36.4 5.7 fusion.95
  45.9 47.4 %all-gather.19.cloned.1.call-done = bf16[4096,1,1,256]{3,0,2,1:T(8,128)(2,1)} async-done(((bf16[512,1,1,256]{3,0,2,1:T(8,128)(2,1)}), bf16[4096,1,1,256]{3,0,2,1:T(8,128)(2,1)}) %all-gather.19.cloned.1.call-update) | async-done | bytes 2097168 | tf_op jit(solution)/shard_map/all_gather | solution.py:133
  93.3 3.9 copy.89
  97.2 46.4 %all-gather.17.cloned.1.call-done = bf16[4096,1,1,256]{3,0,2,1:T(8,128)(2,1)} async-done(((bf16[512,1,1,256]{3,0,2,1:T(8,128)(2,1)}), bf16[4096,1,1,256]{3,0,2,1:T(8,128)(2,1)}) %all-gather.17.cloned.1.call-update) | async-done | bytes 2097168 | tf_op jit(solution)/shard_map/all_gather | solution.py:132
  143.8 35.6 %while.28 = (s32[]{:T(128)}, f32[1,2,512]{2,1,0:T(2,128)S(1)}, f32[512,1,2,256]{0,3,2,1:T(8,128)S(1)}, s32[8]{0:T(128)S(1)}, s32[]{:T(128)}, /*index=5*/bf16[8,5...) while((s32[]{:T(128)}, f32[1,2,512]{2,1,0:T(2,128)S(1)}, ...), condition=%wide.region_5.6_spmd.clone, body=%wide.region_1.5_spmd.clone.sunk | while | flops 540017664 | bytes 5797131 | solution.py:104
  145.1 3.6 conditional.6
  150.0 3.6 conditional.6
  154.9 3.6 conditional.6
  159.8 3.6 conditional.6
  164.7 3.6 conditional.6
  169.6 3.6 conditional.6
  174.5 3.6 conditional.6
  180.0 10.3 all_to_all.30
  190.6 5.2 multiply_reduce_fusion.3
  198.6 81.4 %all-gather.11.cloned.1.call-done = bf16[1024,2304]{1,0:T(8,128)(2,1)} async-done(((bf16[128,2304]{1,0:T(8,128)(2,1)}), bf16[1024,2304]{1,0:T(8,128)(2,1)}) %all-gather.11.cloned.1.call-update) | async-done | bytes 4718608 | tf_op jit(solution)/shard_map/all_gather | solution.py:152
  279.9 16.6 %fusion.51 = f32[1024,2,1152]{2,0,1:T(8,128)S(1)} fusion(bf16[1152,3,2304]{2,0,1:T(8,128)(2,1)} %param.18, bf16[1024,2304]{1,0:T(8,128)(2,1)} %all-gather.11.cloned.1.call-done), kind=kOutput, calls=%fused_computation.71 | convolution fusion | flops 10871635968 | bytes 24772608 | tf_op jit(solution)/shard_map/td,fkd->tkf/dot_general | solution.py:150
  296.5 3.6 copy-done.17
  300.1 11.3 convolution_convert_fusion.3
  311.5 94.5 %reduce-scatter.14.cloned.1.call-done = bf16[128,2304]{1,0:T(8,128)(2,1)} async-done(((bf16[1024,2304]{1,0:T(8,128)(2,1)}), bf16[128,2304]{1,0:T(8,128)(2,1)}) %reduce-scatter.14.cloned.1.call-update) | async-done | bytes 589840 | tf_op jit(solution)/shard_map/reduce_scatter | solution.py:159
  411.4 78.5 %all-gather.13.cloned.1.call-done = bf16[1024,2304]{1,0:T(8,128)(2,1)} async-done(((bf16[128,2304]{1,0:T(8,128)(2,1)}), bf16[1024,2304]{1,0:T(8,128)(2,1)}) %all-gather.13.cloned.1.call-update) | async-done | bytes 4718608 | tf_op jit(solution)/shard_map/all_gather | solution.py:171
  489.9 14.7 %fusion.89 = (bf16[1024,1,1152]{2,0,1:T(8,128)(2,1)S(1)}, bf16[1024,1,1152]{2,0,1:T(8,128)(2,1)S(1)}) fusion(f32[1024,2,1152]{2,0,1:T(8,128)} %copy-done.17, bf16[1024,2304]{1,0:T(8,128)(2,1)} %all-gather.13.cloned.1.call-done, bf16[1152,3,2304]{2,0,1:T(8,128)(2,1)} %param.18), kind=kOutput, calls=%fused_computation.111 | convolution fusion | flops 5462949888 | bytes 24182784 | tf_op jit(solution)/shard_map/dot_general | solution.py:46
  506.7 14.7 %bitcast_convert_fusion = bf16[1024,2304]{1,0:T(8,128)(2,1)} fusion(bf16[1152,3,2304]{2,0,1:T(8,128)(2,1)} %param.18, bf16[1024,1,1152]{2,0,1:T(8,128)(2,1)S(1)} %get-tuple-element.539, bf16[1024,1,1152]{2,0,1:T(8,128)(2,1)S(1)} %get-tuple-element.538), kind=kOutput, calls=%fused_computation.63 | convolution fusion | flops 10876354560 | bytes 20054016 | tf_op jit(solution)/shard_map/tkf,fkd->td/dot_general | solution.py:183
  521.5 94.5 %reduce-scatter.16.cloned.1.call-done = bf16[128,2304]{1,0:T(8,128)(2,1)} async-done(((bf16[1024,2304]{1,0:T(8,128)(2,1)}), bf16[128,2304]{1,0:T(8,128)(2,1)}) %reduce-scatter.16.cloned.1.call-update) | async-done | bytes 589840 | tf_op jit(solution)/shard_map/reduce_scatter | solution.py:182
  623.6 23.7 %all-gather.15.cloned.1.call-done = bf16[512,2304]{1,0:T(8,128)(2,1)} async-done(((bf16[128,2304]{1,0:T(8,128)(2,1)}), bf16[512,2304]{1,0:T(8,128)(2,1)}) %all-gather.15.cloned.1.call-update) | async-done | bytes 2359312 | tf_op jit(solution)/shard_map/all_gather | solution.py:194
  647.4 3.8 fusion.104
  658.1 136.3 %while.29 = (s32[]{:T(128)}, f32[512,1,2,256]{0,3,2,1:T(8,128)}, f32[4096,1,256]{2,0,1:T(8,128)}, f32[4096,1,256]{2,0,1:T(8,128)}, s32[8]{0:T(128)S(1)}, /*index...) while((s32[]{:T(128)}, f32[512,1,2,256]{0,3,2,1:T(8,128)}, ...), condition=%wide.region_18.19_spmd.clone, body=%wide.region_15.18_spmd.clone.sunk | while | flops 1350304768 | bytes 27805592 | solution.py:104
  659.4 18.0 %conditional.7 = ((f32[512,1,2,256]{0,3,2,1:T(8,128)}, f32[4096,1,256]{2,0,1:T(8,128)}, f32[4096,1,256]{2,0,1:T(8,128)})) conditional(s32[]{:T(128)} %convert_element_type.304, (f32[512,1,2,256]{0,3,2,1:T(8,128)}, f32[4096,1,256]{2,0,1:T(8,128)}, f32[4096,1,256]{2,0,1:T(8,128)}) %tuple.106, (bf16[8,512,1,256]{3,1,2,0:T(8,128)(2,1)}, s32[]{:T(128)}, ...), branch_computations={%region_16.16_spmd, %region_17.17_spmd} | conditional | flops 1350304768 | bytes 27803254 | solution.py:249
  666.2 3.0 dynamic_update_slice.8
  671.7 3.0 dynamic_update_slice.9
  678.7 18.0 %conditional.7 = ((f32[512,1,2,256]{0,3,2,1:T(8,128)}, f32[4096,1,256]{2,0,1:T(8,128)}, f32[4096,1,256]{2,0,1:T(8,128)})) conditional(s32[]{:T(128)} %convert_element_type.304, (f32[512,1,2,256]{0,3,2,1:T(8,128)}, f32[4096,1,256]{2,0,1:T(8,128)}, f32[4096,1,256]{2,0,1:T(8,128)}) %tuple.106, (bf16[8,512,1,256]{3,1,2,0:T(8,128)(2,1)}, s32[]{:T(128)}, ...), branch_computations={%region_16.16_spmd, %region_17.17_spmd} | conditional | flops 1350304768 | bytes 27803254 | solution.py:249
  685.5 3.0 dynamic_update_slice.8
  691.0 3.0 dynamic_update_slice.9
  698.0 18.0 %conditional.7 = ((f32[512,1,2,256]{0,3,2,1:T(8,128)}, f32[4096,1,256]{2,0,1:T(8,128)}, f32[4096,1,256]{2,0,1:T(8,128)})) conditional(s32[]{:T(128)} %convert_element_type.304, (f32[512,1,2,256]{0,3,2,1:T(8,128)}, f32[4096,1,256]{2,0,1:T(8,128)}, f32[4096,1,256]{2,0,1:T(8,128)}) %tuple.106, (bf16[8,512,1,256]{3,1,2,0:T(8,128)(2,1)}, s32[]{:T(128)}, ...), branch_computations={%region_16.16_spmd, %region_17.17_spmd} | conditional | flops 1350304768 | bytes 27803254 | solution.py:249
  704.8 3.0 dynamic_update_slice.8
  717.2 18.0 %conditional.7 = ((f32[512,1,2,256]{0,3,2,1:T(8,128)}, f32[4096,1,256]{2,0,1:T(8,128)}, f32[4096,1,256]{2,0,1:T(8,128)})) conditional(s32[]{:T(128)} %convert_element_type.304, (f32[512,1,2,256]{0,3,2,1:T(8,128)}, f32[4096,1,256]{2,0,1:T(8,128)}, f32[4096,1,256]{2,0,1:T(8,128)}) %tuple.106, (bf16[8,512,1,256]{3,1,2,0:T(8,128)(2,1)}, s32[]{:T(128)}, ...), branch_computations={%region_16.16_spmd, %region_17.17_spmd} | conditional | flops 1350304768 | bytes 27803254 | solution.py:249
  724.1 3.0 dynamic_update_slice.8
  729.6 3.0 dynamic_update_slice.9
  736.5 18.1 %conditional.7 = ((f32[512,1,2,256]{0,3,2,1:T(8,128)}, f32[4096,1,256]{2,0,1:T(8,128)}, f32[4096,1,256]{2,0,1:T(8,128)})) conditional(s32[]{:T(128)} %convert_element_type.304, (f32[512,1,2,256]{0,3,2,1:T(8,128)}, f32[4096,1,256]{2,0,1:T(8,128)}, f32[4096,1,256]{2,0,1:T(8,128)}) %tuple.106, (bf16[8,512,1,256]{3,1,2,0:T(8,128)(2,1)}, s32[]{:T(128)}, ...), branch_computations={%region_16.16_spmd, %region_17.17_spmd} | conditional | flops 1350304768 | bytes 27803254 | solution.py:249
  743.4 3.0 dynamic_update_slice.8
  748.9 3.0 dynamic_update_slice.9
  755.8 18.0 %conditional.7 = ((f32[512,1,2,256]{0,3,2,1:T(8,128)}, f32[4096,1,256]{2,0,1:T(8,128)}, f32[4096,1,256]{2,0,1:T(8,128)})) conditional(s32[]{:T(128)} %convert_element_type.304, (f32[512,1,2,256]{0,3,2,1:T(8,128)}, f32[4096,1,256]{2,0,1:T(8,128)}, f32[4096,1,256]{2,0,1:T(8,128)}) %tuple.106, (bf16[8,512,1,256]{3,1,2,0:T(8,128)(2,1)}, s32[]{:T(128)}, ...), branch_computations={%region_16.16_spmd, %region_17.17_spmd} | conditional | flops 1350304768 | bytes 27803254 | solution.py:249
  762.7 3.0 dynamic_update_slice.8
  775.1 18.0 %conditional.7 = ((f32[512,1,2,256]{0,3,2,1:T(8,128)}, f32[4096,1,256]{2,0,1:T(8,128)}, f32[4096,1,256]{2,0,1:T(8,128)})) conditional(s32[]{:T(128)} %convert_element_type.304, (f32[512,1,2,256]{0,3,2,1:T(8,128)}, f32[4096,1,256]{2,0,1:T(8,128)}, f32[4096,1,256]{2,0,1:T(8,128)}) %tuple.106, (bf16[8,512,1,256]{3,1,2,0:T(8,128)(2,1)}, s32[]{:T(128)}, ...), branch_computations={%region_16.16_spmd, %region_17.17_spmd} | conditional | flops 1350304768 | bytes 27803254 | solution.py:249
  782.0 3.0 dynamic_update_slice.8
  787.5 3.0 dynamic_update_slice.9
  794.4 4.7 copy.97
  799.2 4.7 copy.96
  808.4 75.5 %reduce-scatter.20.cloned.1.call-done = bf16[512,1,256]{0,2,1:T(8,128)(2,1)} async-done(((bf16[4096,1,256]{0,2,1:T(8,128)(2,1)}), bf16[512,1,256]{0,2,1:T(8,128)(2,1)}) %reduce-scatter.20.cloned.1.call-update) | async-done | bytes 262160 | tf_op jit(solution)/shard_map/reduce_scatter | solution.py:270
  883.9 71.3 %reduce-scatter.18.cloned.1.call-done = bf16[512,1,256]{0,2,1:T(8,128)(2,1)} async-done(((bf16[4096,1,256]{0,2,1:T(8,128)(2,1)}), bf16[512,1,256]{0,2,1:T(8,128)(2,1)}) %reduce-scatter.18.cloned.1.call-update) | async-done | bytes 262160 | tf_op jit(solution)/shard_map/reduce_scatter | solution.py:267
  958.2 4.0 all-to-all-start.1
  962.3 12.7 all-to-all-done.1
  975.9 9.6 fusion.122
  987.2 5.9 convolution_convert_fusion.2
  993.1 11.3 fusion.46
  1004.5 14.6 %fusion.45 = bf16[1152,2,2304]{0,2,1:T(8,128)(2,1)S(1)} fusion(bf16[1024,2304]{1,0:T(8,128)(2,1)} %all-gather.11.cloned.1.call-done, bf16[1024,1,1152]{2,0,1:T(8,128)(2,1)} %copy-done.19, bf16[1024,1,1152]{2,0,1:T(8,128)(2,1)} %copy-done.18), kind=kOutput, calls=%fused_computation.60 | convolution fusion | flops 10886381568 | bytes 20054016 | tf_op jit(solution)/shard_map/tkf,td->fkd/dot_general | solution.py:178
  1019.1 6.8 pad_maximum_fusion
  1025.9 20.5 %copy.117 = bf16[1152,6912]{1,0:T(8,128)(2,1)} copy(bf16[1152,6912]{0,1:T(8,128)(2,1)} %bitcast.242) | data formatting | bytes 31850496
  1051.3 3.8 reduce-scatter.26.cloned.1.call-done
  1056.2 34.1 %all-reduce = f32[4,576]{1,0:T(4,128)S(1)} all-reduce(f32[4,576]{1,0:T(4,128)S(1)} %copy.112), channel_id=11, replica_groups=mesh['blk'=8,'sp'=4] {'blk'}, use_global_device_ids=true, to_apply=%region_29.30.clone | all-reduce | flops 2304 | bytes 18432
  1090.9 64.1 %reduce-scatter.22.cloned.1.call-done = bf16[128,2304]{1,0:T(8,128)(2,1)} async-done(((bf16[1024,2304]{1,0:T(8,128)(2,1)}), bf16[128,2304]{1,0:T(8,128)(2,1)}) %reduce-scatter.22.cloned.1.call-update) | async-done | bytes 589840 | tf_op jit(solution)/shard_map/reduce_scatter | solution.py:279
  1157.2 120.4 %reduce-scatter.28.cloned.1.call-done = bf16[288,6912]{1,0:T(8,128)(2,1)} async-done(((bf16[1152,6912]{1,0:T(8,128)(2,1)}), bf16[288,6912]{1,0:T(8,128)(2,1)}) %reduce-scatter.28.cloned.1.call-update) | async-done | bytes 3981328
  1277.6 6.6 copy.118
  1284.1 7.3 copy.103
  (257 shorter events, 177.6 us)
Async XLA Ops:
  7.2 29.2 %all-gather.9.cloned.1.call-start = ((), (), s32[]{:S(2)}) async-start(), calls=%async_computation.10 | async-start | bytes 2949120 | tf_op jit(solution)/shard_map/all_gather | solution.py:63
  8.3 1.3 copy-start.11
  9.5 0.5 copy-start.13
  12.2 81.1 %all-gather.19.cloned.1.call-start = ((), (), s32[]{:S(2)}) async-start(), calls=%async_computation.21 | async-start | bytes 2359296 | tf_op jit(solution)/shard_map/all_gather | solution.py:133
  44.6 99.0 %all-gather.17.cloned.1.call-start = ((), (), s32[]{:S(2)}) async-start(), calls=%async_computation.20 | async-start | bytes 2359296 | tf_op jit(solution)/shard_map/all_gather | solution.py:132
  45.4 234.5 %all-gather.11.cloned.1.call-start = ((), (), s32[]{:S(2)}) async-start(), calls=%async_computation.11 | async-start | bytes 5308416 | tf_op jit(solution)/shard_map/all_gather | solution.py:152
  190.6 5.3 copy-start.3
  196.3 1.0 copy-start.1
  198.3 207.7 %reduce-scatter.14.cloned.1.call-start = ((), (), s32[]{:S(2)}) async-start(), calls=%async_computation.12 | async-start | bytes 5308416 | tf_op jit(solution)/shard_map/reduce_scatter | solution.py:159
  296.5 3.6 copy-start.17
  311.4 95.9 %copy-start.8 = (bf16[128,2304]{1,0:T(8,128)(2,1)S(1)}, bf16[128,2304]{1,0:T(8,128)(2,1)}, u32[]{:S(2)}) copy-start(bf16[128,2304]{1,0:T(8,128)(2,1)} %param.19) | copy-start | bytes 1769476
  311.4 178.4 %all-gather.13.cloned.1.call-start = ((), (), s32[]{:S(2)}) async-start(), calls=%async_computation.13 | async-start | bytes 5308416 | tf_op jit(solution)/shard_map/all_gather | solution.py:171
  411.1 204.9 %reduce-scatter.16.cloned.1.call-start = ((), (), s32[]{:S(2)}) async-start(), calls=%async_computation.14 | async-start | bytes 5308416 | tf_op jit(solution)/shard_map/reduce_scatter | solution.py:182
  504.5 1.5 copy-start.18
  504.5 2.2 copy-start.19
  521.5 96.6 %copy-start.7 = (bf16[128,2304]{1,0:T(8,128)(2,1)S(1)}, bf16[128,2304]{1,0:T(8,128)(2,1)}, u32[]{:S(2)}) copy-start(bf16[128,2304]{1,0:T(8,128)(2,1)} %reduce-scatter.14.cloned.1.call-done) | copy-start | bytes 1769476
  521.5 125.9 %all-gather.15.cloned.1.call-start = ((), (), s32[]{:S(2)}) async-start(), calls=%async_computation.15 | async-start | bytes 2949120 | tf_op jit(solution)/shard_map/all_gather | solution.py:194
  616.1 2.0 copy-start.2
  621.0 1.0 copy-start.5
  623.2 260.8 %reduce-scatter.20.cloned.1.call-start = ((), (), s32[]{:S(2)}) async-start(), calls=%async_computation.17 | async-start | bytes 2359296 | tf_op jit(solution)/shard_map/reduce_scatter | solution.py:270
  661.1 1.4 copy-start
  680.3 1.4 copy-start
  699.6 1.4 copy-start
  718.9 1.4 copy-start
  738.2 1.4 copy-start
  757.5 1.4 copy-start
  776.8 1.4 copy-start
  799.2 156.1 %reduce-scatter.18.cloned.1.call-start = ((), (), s32[]{:S(2)}) async-start(), calls=%async_computation.16 | async-start | bytes 2359296 | tf_op jit(solution)/shard_map/reduce_scatter | solution.py:267
  803.9 1.7 copy-start.15
  803.9 244.3 %reduce-scatter.24.cloned.1.call-start = ((), (), s32[]{:S(2)}) async-start(), calls=%async_computation.19 | async-start | bytes 2654208 | tf_op jit(solution)/shard_map/reduce_scatter | solution.py:199
  956.8 1.4 copy-start.9
  958.2 16.8 %all-to-all-start.1 = ((bf16[512,1,4,256]{3,2,1,0:T(4,128)(2,1)}), bf16[512,1,4,256]{3,2,1,0:T(4,128)(2,1)S(1)}, u32[]{:S(2)}, u32[]{:S(2)}) async-start(bf16[512,1,4,256]{3,2,1,0:T(4,128)(2,1)} %copy.98), calls=%async_computation.5 | async-start | bytes 2097152 | tf_op jit(solution)/shard_map/all_to_all | solution.py:282
  962.2 13.6 %copy-start.4 = (bf16[128,2304]{1,0:T(8,128)(2,1)S(1)}, bf16[128,2304]{1,0:T(8,128)(2,1)}, u32[]{:S(2)}) copy-start(bf16[128,2304]{1,0:T(8,128)(2,1)} %param.14) | copy-start | bytes 1769476
  962.2 13.6 %copy-start.12 = (f32[2304]{0:T(1024)S(1)}, f32[2304]{0:T(1024)}, u32[]{:S(2)}) copy-start(f32[2304]{0:T(1024)} %copy-done.11) | copy-start | bytes 27652
  962.2 13.6 %copy-start.14 = (f32[128]{0:T(128)S(1)}, f32[128]{0:T(128)}, u32[]{:S(2)}) copy-start(f32[128]{0:T(128)} %copy-done.13) | copy-start | bytes 1540
  962.2 92.9 %reduce-scatter.26.cloned.1.call-start = ((), (), s32[]{:S(2)}) async-start(), calls=%async_computation.22 | async-start | bytes 1474560
  985.4 1.7 copy-start.10
  986.9 168.1 %reduce-scatter.22.cloned.1.call-start = ((), (), s32[]{:S(2)}) async-start(), calls=%async_computation.18 | async-start | bytes 5308416 | tf_op jit(solution)/shard_map/reduce_scatter | solution.py:279
  993.1 284.5 %reduce-scatter.28.cloned.1.call-start = ((), (), s32[]{:S(2)}) async-start(), calls=%async_computation.23 | async-start | bytes 19906560
  1046.3 0.7 copy-start.16
  1046.3 3.7 copy-start.6
Sparse Core Ops, SparseCore 0:
  12.3 24.0 all-gather.8
  44.7 48.5 all-gather.18
  96.0 47.6 all-gather.16
  198.5 81.4 all-gather.10
  311.6 94.3 reduce-scatter.13
  411.2 78.5 all-gather.12
  521.6 94.3 reduce-scatter.15
  623.3 24.0 all-gather.14
  799.3 84.5 reduce-scatter.19
  887.3 67.8 reduce-scatter.17
  958.7 68.6 reduce-scatter.23
  1029.8 25.2 reduce-scatter.25
  1059.3 95.6 reduce-scatter.21
  1157.5 120.0 reduce-scatter.27

commit v2 on v1

v2 whole, which is shorter than its diff:
```python
import functools

import jax
import jax.numpy as jnp
from jax import lax
from jax.experimental import pallas as pl
from jax.experimental.pallas import tpu as pltpu
from jax.sharding import PartitionSpec as P

HEADS = 8
KV_HEADS = 4
HEAD = 256


VMEM_BYTES = 62 * 1024 * 1024
NORM_EPSILON = 1e-06
CAP_VALUE = 50.0
GELU_SCALE = 0.7978845608028654
GELU_CUBIC = 0.044715


def norm_parts(values):
    inverse = lax.rsqrt(jnp.mean(values * values, axis=-1, keepdims=True) + NORM_EPSILON)
    return (values * inverse, inverse)


def norm_back(grad_y, normed, inverse, gain):
    grad_n = grad_y * gain
    grad_v = inverse * (grad_n - normed * jnp.mean(grad_n * normed, axis=-1, keepdims=True))
    return (grad_v, jnp.sum(grad_y * normed, axis=0))


def gelu_value(values):
    return (
        0.5
        * values
        * (1.0 + jnp.tanh(GELU_SCALE * (values + GELU_CUBIC * values * values * values)))
    )


def gelu_slope(values):
    bent = jnp.tanh(GELU_SCALE * (values + GELU_CUBIC * values * values * values))
    return 0.5 * (1.0 + bent) + 0.5 * values * (1.0 - bent * bent) * GELU_SCALE * (
        1.0 + 3.0 * GELU_CUBIC * values * values
    )


def contract_last(left, right):
    return lax.dot_general(
        left, right, (((1,), (1,)), ((), ())), preferred_element_type=jnp.float32
    )


def push(source, target, sent, landed, block):
    return pltpu.make_async_remote_copy(
        src_ref=source,
        dst_ref=target,
        send_sem=sent,
        recv_sem=landed,
        device_id={"blk": block},
        device_id_type=pl.DeviceIdType.MESH,
    )


def greet(at, line, rows):
    barrier = pltpu.get_barrier_semaphore()

    def tell(block):
        pl.semaphore_signal(
            barrier, inc=1, device_id={"blk": block}, device_id_type=pl.DeviceIdType.MESH
        )

    tell(at + 1 - 2 * (at % 2))
    pl.when(line > 0)(lambda: tell(at - 2))
    pl.when(line < rows - 1)(lambda: tell(at + 2))
    pl.semaphore_wait(barrier, 1 + jnp.minimum(line, 1) + jnp.minimum(rows - 1 - line, 1))


def both(*terms):
    result = terms[0]
    for term in terms[1:]:
        result = jnp.logical_and(result, term)
    return result


def attend_kernel(
    heads,
    x_ref,
    low_ref,
    att_ref,
    tot_ref,
    kv_ref,
    kv,
    acc,
    part,
    up_sent,
    up_landed,
    side_sent,
    side_landed,
    own_done,
    save_done,
):
    at = lax.axis_index("blk")
    blocks = lax.axis_size("blk")
    rows = blocks // 2
    line, column = at // 2, at % 2
    partner = at + 1 - 2 * column
    size = x_ref.shape[0]
    first = heads * HEAD
    own = x_ref.at[:, pl.ds(first, 2 * HEAD)]
    greet(at, line, rows)

    def up_copy(index, source):
        return push(source, kv.at[index], up_sent.at[index // 2], up_landed.at[index // 2], at + 2)

    def side_copy(index, source):
        return push(
            source, kv.at[index], side_sent.at[index // 2], side_landed.at[index // 2], partner
        )

    def save(index):
        return pltpu.make_async_copy(kv.at[index], kv_ref.at[index], save_done.at[index])

    pl.when(line < rows - 1)(lambda: up_copy(at, own).start())
    pl.when(column == 0)(lambda: side_copy(at, own).start())
    keep = pltpu.make_async_copy(own, kv.at[at], own_done)
    keep.start()
    acc[...] = jnp.zeros_like(acc)
    part[...] = jnp.zeros_like(part)
    keep.wait()
    ahead = lax.broadcasted_iota(jnp.int32, (size, size), 1) - lax.broadcasted_iota(
        jnp.int32, (size, size), 0
    )

    def compute(index):
        save(index).start()
        span = (at - index) * size
        for head in range(heads):
            raw = lax.dot_general(
                x_ref[:, head * HEAD : (head + 1) * HEAD],
                kv[index, :, :HEAD],
                (((1,), (1,)), ((), ())),
                preferred_element_type=jnp.float32,
            )
            weights = jnp.exp(CAP_VALUE * jnp.tanh(raw * (HEAD ** (-0.5) / CAP_VALUE)))
            weights = jnp.where(ahead <= span, weights, 0.0)
            total = weights[:, :128]
            for piece in range(1, size // 128):
                total = total + weights[:, piece * 128 : (piece + 1) * 128]
            part[head] += total
            acc[:, head * HEAD : (head + 1) * HEAD] += jnp.dot(
                weights.astype(jnp.bfloat16),
                kv[index, :, HEAD:],
                preferred_element_type=jnp.float32,
            )

    @pl.loop(0, rows + 1)
    def _(step):
        source = line - step
        index = 2 * source + column

        @pl.when(both(step > 0, source >= 0))
        def _():
            up_copy(index, kv.at[index]).wait_recv()
            pl.when(line < rows - 1)(lambda: up_copy(index, kv.at[index]).start())
            side_copy(index, kv.at[index]).start()

        pl.when(source >= 0)(lambda: compute(index))
        other = 2 * (source + 1) + 1 - column

        @pl.when(both(step > 0, source + 1 >= 0, jnp.logical_or(step > 1, column == 1)))
        def _():
            side_copy(other, kv.at[other]).wait_recv()
            compute(other)

    for head in range(heads):
        columns = slice(head * HEAD, (head + 1) * HEAD)
        total = jnp.sum(part[head], axis=1, keepdims=True)
        value = acc[:, columns] / total
        att_ref[:, columns] = value
        low_ref[:, columns] = value.astype(jnp.bfloat16)
        tot_ref[head] = jnp.sum(part[head].T, axis=0, keepdims=True)

    @pl.loop(0, rows)
    def _(source):
        index = 2 * source + column

        @pl.when(source <= line)
        def _():
            pl.when(line < rows - 1)(lambda: up_copy(index, kv.at[index]).wait_send())
            pl.when(jnp.logical_or(source < line, column == 0))(
                lambda: side_copy(index, kv.at[index]).wait_send()
            )

    @pl.loop(0, blocks)
    def _(index):
        pl.when(index <= at)(lambda: save(index).wait())


def attend(projected, heads):
    size = projected.shape[0]
    blocks = lax.axis_size("blk")
    whole = pl.BlockSpec(memory_space=pltpu.VMEM)
    return pl.pallas_call(
        functools.partial(attend_kernel, heads),
        out_shape=(
            jax.ShapeDtypeStruct((size, heads * HEAD), jnp.bfloat16),
            jax.ShapeDtypeStruct((size, heads * HEAD), jnp.float32),
            jax.ShapeDtypeStruct((heads, 1, size), jnp.float32),
            jax.ShapeDtypeStruct((blocks, size, 2 * HEAD), jnp.bfloat16),
        ),
        in_specs=[whole],
        out_specs=(whole, whole, whole, pl.BlockSpec(memory_space=pl.ANY)),
        scratch_shapes=[
            pltpu.VMEM((blocks, size, 2 * HEAD), jnp.bfloat16),
            pltpu.VMEM((size, heads * HEAD), jnp.float32),
            pltpu.VMEM((heads, size, 128), jnp.float32),
            pltpu.SemaphoreType.DMA((blocks // 2,)),
            pltpu.SemaphoreType.DMA((blocks // 2,)),
            pltpu.SemaphoreType.DMA((blocks // 2,)),
            pltpu.SemaphoreType.DMA((blocks // 2,)),
            pltpu.SemaphoreType.DMA,
            pltpu.SemaphoreType.DMA((blocks,)),
        ],
        compiler_params=pltpu.CompilerParams(
            collective_id=0, has_side_effects=True, vmem_limit_bytes=VMEM_BYTES
        ),
        name="attend",
    )(projected)


def attend_back_kernel(
    heads,
    x_ref,
    scaled_ref,
    delta_ref,
    kv_ref,
    out_ref,
    kv,
    part,
    side,
    down,
    dq,
    dk,
    dv,
    load_done,
    side_sent,
    side_landed,
    down_sent,
    down_landed,
):
    at = lax.axis_index("blk")
    blocks = lax.axis_size("blk")
    rows = blocks // 2
    line, column = at // 2, at % 2
    partner = at + 1 - 2 * column
    size = x_ref.shape[0]

    def load(index):
        return pltpu.make_async_copy(kv_ref.at[index], kv.at[index], load_done.at[index])

    @pl.loop(0, blocks)
    def _(index):
        pl.when(index <= at)(lambda: load(index).start())

    greet(at, line, rows)

    def side_copy(target):
        return push(
            part.at[target, 1 - column],
            side.at[target],
            side_sent.at[target],
            side_landed.at[target],
            partner,
        )

    def down_copy(target):
        return push(
            part.at[target, column],
            down.at[target],
            down_sent.at[target],
            down_landed.at[target],
            at - 2,
        )

    dq[...] = jnp.zeros_like(dq)
    ahead = lax.broadcasted_iota(jnp.int32, (size, size), 0) - lax.broadcasted_iota(
        jnp.int32, (size, size), 1
    )

    def compute(target, half):
        index = 2 * target + half
        load(index).wait()
        span = (at - index) * size
        for head in range(heads):
            columns = slice(head * HEAD, (head + 1) * HEAD)
            query = x_ref[:, columns]
            scaled = scaled_ref[:, columns]
            key = kv[index, :, :HEAD]
            raw = lax.dot_general(
                key, query, (((1,), (1,)), ((), ())), preferred_element_type=jnp.float32
            )
            squashed = jnp.tanh(raw * (HEAD ** (-0.5) / CAP_VALUE))
            weights = jnp.exp(CAP_VALUE * squashed)
            weights = jnp.where(ahead <= span, weights, 0.0)
            inner = lax.dot_general(
                kv[index, :, HEAD:],
                scaled,
                (((1,), (1,)), ((), ())),
                preferred_element_type=jnp.float32,
            )
            grad_raw = (
                weights * (inner - delta_ref[head]) * (1.0 - squashed * squashed)
            ).astype(jnp.bfloat16)
            dv_now = jnp.dot(
                weights.astype(jnp.bfloat16), scaled, preferred_element_type=jnp.float32
            )
            dk_now = jnp.dot(grad_raw, query, preferred_element_type=jnp.float32)
            dq[:, columns] += lax.dot_general(
                grad_raw, key, (((0,), (0,)), ((), ())), preferred_element_type=jnp.float32
            )
            if head == 0:
                dv[...] = dv_now
                dk[...] = dk_now
            else:
                dv[...] += dv_now
                dk[...] += dk_now
        part[target, half, :, :HEAD] = (dk[...] * HEAD ** (-0.5)).astype(jnp.bfloat16)
        part[target, half, :, HEAD:] = dv[...].astype(jnp.bfloat16)

    def merge(target):
        last = target == line

        @pl.when(jnp.logical_or(target < line, column == 0))
        def _():
            side_copy(target).wait_recv()
            part[target, column] = (
                part[target, column].astype(jnp.float32) + side[target].astype(jnp.float32)
            ).astype(jnp.bfloat16)

        @pl.when(line < rows - 1)
        def _():
            down_copy(target).wait_recv()
            part[target, column] = (
                part[target, column].astype(jnp.float32) + down[target].astype(jnp.float32)
            ).astype(jnp.bfloat16)

        pl.when(target < line)(lambda: down_copy(target).start())

        @pl.when(last)
        def _():
            out_ref[:, heads * HEAD :] = part[target, column]

    @pl.loop(0, rows)
    def _(target):
        @pl.when(jnp.logical_or(target < line, both(target == line, column == 1)))
        def _():
            compute(target, 1 - column)
            side_copy(target).start()

        pl.when(target <= line)(lambda: compute(target, column))
        pl.when(both(line == rows - 1, target > 0))(lambda: merge(target - 1))

    out_ref[:, : heads * HEAD] = (dq[...] * HEAD ** (-0.5)).astype(jnp.bfloat16)

    @pl.loop(0, rows)
    def _(target):
        pl.when(both(target <= line, jnp.logical_or(line < rows - 1, target == rows - 1)))(
            lambda: merge(target)
        )

    @pl.loop(0, rows)
    def _(target):
        pl.when(jnp.logical_or(target < line, both(target == line, column == 1)))(
            lambda: side_copy(target).wait_send()
        )
        pl.when(target < line)(lambda: down_copy(target).wait_send())


def attend_back(projected, scaled, delta, kv_all):
    size = projected.shape[0]
    blocks = lax.axis_size("blk")
    rows = blocks // 2
    heads = scaled.shape[1] // HEAD
    whole = pl.BlockSpec(memory_space=pltpu.VMEM)
    return pl.pallas_call(
        functools.partial(attend_back_kernel, heads),
        out_shape=jax.ShapeDtypeStruct(projected.shape, jnp.bfloat16),
        in_specs=[whole, whole, whole, pl.BlockSpec(memory_space=pl.ANY)],
        out_specs=whole,
        scratch_shapes=[
            pltpu.VMEM((blocks, size, 2 * HEAD), jnp.bfloat16),
            pltpu.VMEM((rows, 2, size, 2 * HEAD), jnp.bfloat16),
            pltpu.VMEM((rows, size, 2 * HEAD), jnp.bfloat16),
            pltpu.VMEM((rows, size, 2 * HEAD), jnp.bfloat16),
            pltpu.VMEM((size, heads * HEAD), jnp.float32),
            pltpu.VMEM((size, HEAD), jnp.float32),
            pltpu.VMEM((size, HEAD), jnp.float32),
            pltpu.SemaphoreType.DMA((blocks,)),
            pltpu.SemaphoreType.DMA((rows,)),
            pltpu.SemaphoreType.DMA((rows,)),
            pltpu.SemaphoreType.DMA((rows,)),
            pltpu.SemaphoreType.DMA((rows,)),
        ],
        compiler_params=pltpu.CompilerParams(
            collective_id=1, has_side_effects=True, vmem_limit_bytes=VMEM_BYTES
        ),
        name="attend_back",
    )(projected, scaled, delta, kv_all)


def body(tokens, w_qkv, w_out, gains, w_ffn, cotangent):
    row_count = tokens.shape[0]
    groups = lax.axis_size("sp")
    heads_here = HEADS // groups
    kv_here = KV_HEADS // groups
    group_ratio = HEADS // KV_HEADS
    query_width = HEADS * HEAD
    score_scale = HEAD ** (-0.5)
    source = tokens.astype(jnp.float32)
    normed_in, inverse_in = norm_parts(source)
    act_in = (normed_in * gains[0]).astype(jnp.bfloat16)
    act_block = lax.all_gather(act_in, "sp", axis=0, tiled=True)
    group_cols = (group_ratio + 2) * HEAD * kv_here
    sp_at = lax.axis_index("sp")
    w_group = lax.dynamic_slice_in_dim(w_qkv, sp_at * group_cols, group_cols, 0)
    projected = contract_last(act_block, w_group).astype(jnp.bfloat16)
    block_rows = projected.shape[0]
    attended_cols, attended, totals, kv_all = attend(projected, heads_here)
    attended_low = attended_cols.reshape(block_rows, heads_here, HEAD)
    attended_tokens = lax.all_to_all(
        attended_low, "sp", split_axis=0, concat_axis=1, tiled=True
    ).reshape(row_count, query_width)
    attn = jnp.dot(attended_tokens, w_out, preferred_element_type=jnp.float32)
    normed_attn, inverse_attn = norm_parts(attn)
    middle = source + normed_attn * gains[1]
    normed_mid, inverse_mid = norm_parts(middle)
    act_ffn = (normed_mid * gains[2]).astype(jnp.bfloat16)
    w_in = w_ffn[:, :2, :]
    w_down = w_ffn[:, 2, :]
    gate_up = jnp.einsum(
        "td,fkd->tkf",
        lax.all_gather(act_ffn, "blk", axis=0, tiled=True),
        w_in,
        preferred_element_type=jnp.float32,
    )
    hidden = (gelu_value(gate_up[:, 0]) * gate_up[:, 1]).astype(jnp.bfloat16)
    hidden_all = hidden
    part = hidden_all
    ffn_out = lax.psum_scatter(
        jnp.dot(part, w_down, preferred_element_type=jnp.float32).astype(jnp.bfloat16),
        "blk",
        scatter_dimension=0,
        tiled=True,
    ).astype(jnp.float32)
    normed_ffn, inverse_ffn = norm_parts(ffn_out)
    result = middle + normed_ffn * gains[3]
    grad_out = cotangent.astype(jnp.float32)
    grad_ffn_f, gain_grad3 = norm_back(grad_out, normed_ffn, inverse_ffn, gains[3])
    grad_ffn = grad_ffn_f.astype(jnp.bfloat16)
    act_piece = lax.all_gather(act_ffn, "blk", axis=0, tiled=True)
    grad_piece = lax.all_gather(grad_ffn, "blk", axis=0, tiled=True)
    gate_up = jnp.einsum("td,fkd->tkf", act_piece, w_in, preferred_element_type=jnp.float32)
    hidden = (gelu_value(gate_up[:, 0]) * gate_up[:, 1]).astype(jnp.bfloat16)
    grad_hidden = contract_last(grad_piece, w_down)
    grad_gate = grad_hidden * gate_up[:, 1] * gelu_slope(gate_up[:, 0])
    grad_up = grad_hidden * gelu_value(gate_up[:, 0])
    grad_pair = jnp.stack([grad_gate, grad_up], axis=1).astype(jnp.bfloat16)
    in_part = jnp.einsum("tkf,td->fkd", grad_pair, act_piece, preferred_element_type=jnp.float32)
    down_part = jnp.einsum("tf,td->fd", hidden, grad_piece, preferred_element_type=jnp.float32)
    weight_sum = jnp.concatenate([in_part, down_part[:, None, :]], axis=1)
    part = grad_pair
    grad_act_ffn = lax.psum_scatter(
        jnp.einsum("tkf,fkd->td", part, w_in, preferred_element_type=jnp.float32).astype(
            jnp.bfloat16
        ),
        "blk",
        scatter_dimension=0,
        tiled=True,
    ).astype(jnp.float32)
    grad_norm_mid, gain_grad2 = norm_back(grad_act_ffn, normed_mid, inverse_mid, gains[2])
    grad_middle = grad_out + grad_norm_mid
    grad_attn_f, gain_grad1 = norm_back(grad_middle, normed_attn, inverse_attn, gains[1])
    grad_attn = grad_attn_f.astype(jnp.bfloat16)
    grad_block = lax.all_gather(grad_attn, "sp", axis=0, tiled=True)
    out_term = jnp.einsum(
        "tc,td->cd", attended_cols, grad_block, preferred_element_type=jnp.float32
    )
    out_grad = lax.psum_scatter(
        out_term.astype(jnp.bfloat16), "blk", scatter_dimension=0, tiled=True
    ).astype(jnp.float32)
    w_out_group = lax.dynamic_slice_in_dim(w_out, sp_at * heads_here * HEAD, heads_here * HEAD, 0)
    grad_heads = (
        contract_last(grad_block, w_out_group).astype(jnp.bfloat16).astype(jnp.float32)
    ).reshape(block_rows, heads_here, HEAD)
    totals_rows = jnp.transpose(totals.reshape(heads_here, block_rows))
    scaled = (grad_heads / totals_rows[..., None]).astype(jnp.bfloat16)
    row_delta = (
        jnp.sum(grad_heads * attended.reshape(block_rows, heads_here, HEAD), axis=-1) / totals_rows
    )
    grad_cols = attend_back(
        projected,
        scaled.reshape(block_rows, heads_here * HEAD),
        jnp.transpose(row_delta).reshape(heads_here, 1, block_rows),
        kv_all,
    )
    grad_proj_heads = grad_cols.reshape(block_rows, kv_here, group_ratio + 2, HEAD)
    qkv_term = jnp.einsum("tc,td->cd", grad_cols, act_block, preferred_element_type=jnp.float32)
    qkv_grad = lax.psum_scatter(
        qkv_term.astype(jnp.bfloat16), "blk", scatter_dimension=0, tiled=True
    ).astype(jnp.float32)
    grad_proj_tokens = lax.all_to_all(grad_proj_heads, "sp", split_axis=0, concat_axis=1, tiled=True)
    grad_projected = grad_proj_tokens.reshape(row_count, w_qkv.shape[0])
    grad_act_in = jnp.dot(grad_projected, w_qkv, preferred_element_type=jnp.float32)
    grad_source, gain_grad0 = norm_back(grad_act_in, normed_in, inverse_in, gains[0])
    tokens_grad = (grad_middle + grad_source).astype(jnp.bfloat16)
    gains_term = jnp.stack([gain_grad0, gain_grad1, gain_grad2, gain_grad3], axis=0)
    ffn_grad = lax.psum_scatter(
        weight_sum.astype(jnp.bfloat16), "sp", scatter_dimension=0, tiled=True
    ).astype(jnp.float32)
    gains_part = lax.psum_scatter(gains_term, "sp", scatter_dimension=1, tiled=True)
    gains_grad = lax.psum_scatter(gains_part, "blk", scatter_dimension=1, tiled=True)
    return (result.astype(jnp.bfloat16), tokens_grad, qkv_grad, out_grad, gains_grad, ffn_grad)


def solution(mesh):
    return jax.shard_map(
        body,
        mesh=mesh,
        in_specs=(
            P(("blk", "sp"), None),
            P(),
            P(),
            P(),
            P("blk", None, None),
            P(("blk", "sp"), None),
        ),
        out_specs=(
            P(("blk", "sp"), None),
            P(("blk", "sp"), None),
            P(("sp", "blk"), None),
            P(("sp", "blk"), None),
            P(None, ("sp", "blk")),
            P(("blk", "sp"), None, None),
        ),
        check_vma=False,
    )
```

time: 1310 us -> 1010 us (0.77)
  waiting for transfers between devices: 839 us -> 621 us
  Pallas kernels: 0 us -> 107 us
  matrix products: 213 us -> 119 us
  local copies, waits for them, and re-layouts: 137 us -> 55 us
    reduce_scatter x2 -> x0, waiting for transfers between devices: 147 us -> none  [the longest x1 75.5 us: body(): lax.psum_scatter(grad_values_all.astype(jnp.bfloat16), 'blk', scatter_dim...]
    pallas_call x0 -> x2, Pallas kernels: none -> 107 us  [the longest x1 53.7 us: attend(): pl.pallas_call(functools.partial(attend_kernel, heads), out_shape=(jax.Sh...]
    dot_general x49 -> x0, matrix products: 96.8 us -> none  [the longest x14 23 us: tile_scores(): jnp.einsum('qkgd,rkd->kgqr', query_group, key_tile, preferred_element_typ...]
    all_gather x2 -> x0, waiting for transfers between devices: 93.8 us -> none  [the longest x1 47.4 us: body(): lax.all_gather(value_heads, 'blk', axis=0, tiled=True)]
    dynamic_update_slice x14 -> x0, local copies, waits for them, and re-layouts: 41.4 us -> none  [the longest x7 20.7 us: backward_compute(): lax.dynamic_update_slice_in_dim(grad_values, old_values + value_part, til...]
    reduce_scatter x1, waiting for transfers between devices: 64.1 us -> 95.7 us  [body(): lax.psum_scatter(qkv_term.astype(jnp.bfloat16), 'blk', scatter_dimension=...]
    unnamed x50 -> x59, local copies, waits for them, and re-layouts: 54.9 us -> 45.6 us
    unnamed x16 -> x12, waiting for transfers between devices: 124 us -> 121 us
  transfers between devices with their start and end apart: 15 -> 11, of which waited for: 14 -> 9; matrix products, arithmetic and copies ran while one was open for 7% -> 7% of each run, Pallas kernels for 0% -> 0%
where the time goes in v2:
time: 1010 us; the launch traced here: 998 us
  waiting for transfers between devices  621 us (61%)
  matrix products  119 us (12%)
  Pallas kernels  107 us (11%)
  local copies, waits for them, and re-layouts  55 us (5%)
  blocking collectives  43.6 us (4%)
  other arithmetic  30.5 us (3%)
  between operations  15.4 us (2%)
    unnamed x12, waiting for transfers between devices  121 us
    reduce_scatter x1, waiting for transfers between devices, body(): lax.psum_scatter(qkv_term.astype(jnp.bfloat16), 'blk', scatter_dimension=...  95.7 us
    reduce_scatter x1, waiting for transfers between devices, body(): lax.psum_scatter(jnp.einsum('tkf,fkd->td', part, w_in, preferred_element_...  94.5 us
    reduce_scatter x1, waiting for transfers between devices, body(): lax.psum_scatter(jnp.dot(part, w_down, preferred_element_type=jnp.float32...  94.5 us
    all_gather x1, waiting for transfers between devices, body(): grad_piece = lax.all_gather(grad_ffn, 'blk', axis=0, tiled=True)  78.5 us
    all_gather x1, waiting for transfers between devices, body(): lax.all_gather(act_ffn, 'blk', axis=0, tiled=True)  77.7 us
    pallas_call x1, Pallas kernels, attend(): pl.pallas_call(functools.partial(attend_kernel, heads), out_shape=(jax.Sh...  53.7 us
    pallas_call x1, Pallas kernels, attend_back(): pl.pallas_call(functools.partial(attend_back_kernel, heads), out_shape=ja...  53.1 us
  transfers between devices with their start and end apart: 11, of which 9 were waited for; matrix products, arithmetic and copies ran while one was open for 7% of the time, Pallas kernels for 0%

profile of v2, /device:TPU:26, one launch (start us, length us, event | category | flops | bytes accessed | tf_op | source)
XLA Modules:
  0.0 997.7 jit_solution(18436251584608283023)
XLA Ops:
  7.2 1.6 slice_reduce_fusion
  8.9 1.3 fusion.78
  10.1 2.1 fusion.71
  12.3 24.2 %all-gather.5.cloned.1.call-done = bf16[512,2304]{1,0:T(8,128)(2,1)} async-done(((bf16[128,2304]{1,0:T(8,128)(2,1)}), bf16[512,2304]{1,0:T(8,128)(2,1)}) %all-gather.5.cloned.1.call-update) | async-done | bytes 2359312 | tf_op jit(solution)/shard_map/all_gather | solution.py:423
  36.5 6.7 fusion.50.x_ref
  43.2 53.7 %attend.1 = (bf16[512,512]{1,0:T(8,128)(2,1)}, f32[512,512]{1,0:T(8,128)}, f32[2,1,512]{2,1,0:T(1,128)}, bf16[8,512,512]{2,1,0:T(8,128)(2,1)}) custom-call(bf16[512,1024]{1,0:T(8,128)(2,1)} %fusion.50.x_ref), custom_call_target="tpu_custom_call" | custom-call | tf_op jit(solution)/shard_map/attend/pallas_call | solution.py:204
  96.9 1.2 reshape.87
  98.0 11.0 %all_to_all.30 = bf16[512,2,256]{2,1,0:T(2,128)(2,1)S(1)} all-to-all(bf16[512,2,256]{2,1,0:T(2,128)(2,1)S(1)} %reshape.87), channel_id=1, replica_groups=mesh['blk'=8,'sp'=4] {'sp'}, dimensions={0} | all-to-all | bytes 1048576 | tf_op jit(solution)/shard_map/all_to_all | solution.py:431
  109.2 0.3 copy.32
  109.5 5.2 multiply_reduce_fusion.3
  114.7 0.4 multiply_reduce_fusion.2
  115.2 1.0 multiply_convert_fusion.2
  116.2 0.3 reduce-scatter.12.cloned.1.call-start
  116.4 77.7 %all-gather.7.cloned.1.call-done = bf16[1024,2304]{1,0:T(8,128)(2,1)} async-done(((bf16[128,2304]{1,0:T(8,128)(2,1)}), bf16[1024,2304]{1,0:T(8,128)(2,1)}) %all-gather.7.cloned.1.call-update) | async-done | bytes 4718608 | tf_op jit(solution)/shard_map/all_gather | solution.py:443
  194.2 16.6 %fusion.6 = f32[1024,2,1152]{2,0,1:T(8,128)S(1)} fusion(bf16[1152,3,2304]{2,0,1:T(8,128)(2,1)} %param.10, bf16[1024,2304]{1,0:T(8,128)(2,1)} %all-gather.7.cloned.1.call-done), kind=kOutput, calls=%fused_computation.13 | convolution fusion | flops 10871635968 | bytes 24772608 | tf_op jit(solution)/shard_map/td,fkd->tkf/dot_general | solution.py:441
  210.8 3.6 copy-done.21
  214.4 11.3 %convolution_convert_fusion.3 = bf16[1024,2304]{1,0:T(8,128)(2,1)} fusion(bf16[1152,3,2304]{2,0,1:T(8,128)(2,1)} %param.10, f32[1024,2,1152]{2,0,1:T(8,128)S(1)} %fusion.6), kind=kOutput, calls=%fused_computation.15 | convolution fusion | flops 5449973760 | bytes 19464192 | tf_op jit(solution)/shard_map/dot_general | solution.py:451
  225.7 94.5 %reduce-scatter.12.cloned.1.call-done = bf16[128,2304]{1,0:T(8,128)(2,1)} async-done(((bf16[1024,2304]{1,0:T(8,128)(2,1)}), bf16[128,2304]{1,0:T(8,128)(2,1)}) %reduce-scatter.12.cloned.1.call-update) | async-done | bytes 589840 | tf_op jit(solution)/shard_map/reduce_scatter | solution.py:450
  320.2 1.3 fusion.69
  321.5 2.1 fusion.79
  323.6 2.3 fusion.63
  325.9 0.3 reduce-scatter.14.cloned.1.call-start
  326.2 78.5 %all-gather.9.cloned.1.call-done = bf16[1024,2304]{1,0:T(8,128)(2,1)} async-done(((bf16[128,2304]{1,0:T(8,128)(2,1)}), bf16[1024,2304]{1,0:T(8,128)(2,1)}) %all-gather.9.cloned.1.call-update) | async-done | bytes 4718608 | tf_op jit(solution)/shard_map/all_gather | solution.py:462
  404.7 14.7 %fusion.44 = (bf16[1024,1,1152]{2,0,1:T(8,128)(2,1)S(1)}, bf16[1024,1,1152]{2,0,1:T(8,128)(2,1)S(1)}) fusion(f32[1024,2,1152]{2,0,1:T(8,128)} %copy-done.21, bf16[1024,2304]{1,0:T(8,128)(2,1)} %all-gather.9.cloned.1.call-done, bf16[1152,3,2304]{2,0,1:T(8,128)(2,1)} %param.10), kind=kOutput, calls=%fused_computation.53 | convolution fusion | flops 5462949888 | bytes 24182784 | tf_op jit(solution)/shard_map/dot_general | solution.py:49
  419.4 1.5 copy-done.22
  420.9 0.7 copy-done.24
  421.6 14.7 %bitcast_convert_fusion = bf16[1024,2304]{1,0:T(8,128)(2,1)} fusion(bf16[1152,3,2304]{2,0,1:T(8,128)(2,1)} %param.10, bf16[1024,1,1152]{2,0,1:T(8,128)(2,1)S(1)} %get-tuple-element.54, bf16[1024,1,1152]{2,0,1:T(8,128)(2,1)S(1)} %get-tuple-element.53), kind=kOutput, calls=%fused_computation.5 | convolution fusion | flops 10876354560 | bytes 20054016 | tf_op jit(solution)/shard_map/tkf,fkd->td/dot_general | solution.py:474
  436.4 94.5 %reduce-scatter.14.cloned.1.call-done = bf16[128,2304]{1,0:T(8,128)(2,1)} async-done(((bf16[1024,2304]{1,0:T(8,128)(2,1)}), bf16[128,2304]{1,0:T(8,128)(2,1)}) %reduce-scatter.14.cloned.1.call-update) | async-done | bytes 589840 | tf_op jit(solution)/shard_map/reduce_scatter | solution.py:473
  530.9 2.1 fusion.70
  533.0 3.5 multiply_reduce_fusion
  536.6 1.0 copy-done.1
  537.6 1.8 multiply_convert_fusion.1
  539.5 0.6 div.46
  540.2 23.3 %all-gather.11.cloned.1.call-done = bf16[512,2304]{1,0:T(8,128)(2,1)} async-done(((bf16[128,2304]{1,0:T(8,128)(2,1)}), bf16[512,2304]{1,0:T(8,128)(2,1)}) %all-gather.11.cloned.1.call-update) | async-done | bytes 2359312 | tf_op jit(solution)/shard_map/all_gather | solution.py:485
  563.6 4.8 convert_multiply_fusion.8
  568.4 0.7 mul.360
  569.1 0.6 reduce_sum.126
  569.9 0.6 reshape.90.delta_ref
  570.5 53.1 %attend_back.1 = bf16[512,1024]{1,0:T(8,128)(2,1)} custom-call(bf16[512,1024]{1,0:T(8,128)(2,1)} %fusion.50.x_ref, bf16[512,512]{1,0:T(8,128)(2,1)} %get-tuple-element.57.scaled_ref, f32[2,1,512]{2,1,0:T(1,128)} %reshape.90.delta_ref, bf16[8,512,512]{2,1,0:T(8,128)(2,1)} %get-tuple-element.13.kv_ref), custom_call_target="tpu_custom_call" | custom-call | tf_op jit(solution)/shard_map/attend_back/pallas_call | solution.py:386
  623.6 2.6 reshape.91
  626.3 4.9 all-to-all-start.1
  631.3 0.6 stack.31
  631.9 12.1 %all-to-all-done.1 = bf16[512,1,4,256]{3,2,1,0:T(4,128)(2,1)S(1)} async-done(((bf16[512,1,4,256]{3,2,1,0:T(4,128)(2,1)}), bf16[512,1,4,256]{3,2,1,0:T(4,128)(2,1)S(1)}, u32[]{:S(2)}, u32[]{:S(2)}) %all-to-all-start.1) | async-done | bytes 1048608 | tf_op jit(solution)/shard_map/all_to_all | solution.py:512
  644.2 0.7 copy.38
  644.9 9.3 fusion.77
  654.2 1.5 copy.46
  655.8 4.6 convolution_convert_fusion.4
  660.4 6.0 convolution_convert_fusion.2
  666.7 11.4 %fusion.1 = bf16[1152,1,2304]{0,2,1:T(8,128)(2,1)S(1)} fusion(bf16[1024,2304]{1,0:T(8,128)(2,1)} %all-gather.9.cloned.1.call-done, f32[1024,2,1152]{2,0,1:T(8,128)} %copy-done.21), kind=kOutput, calls=%fused_computation.4 | convolution fusion | flops 5450268672 | bytes 19464192 | tf_op jit(solution)/shard_map/tf,td->fd/dot_general | solution.py:470
  678.1 14.0 %fusion = bf16[1152,2,2304]{0,2,1:T(8,128)(2,1)S(1)} fusion(bf16[1024,2304]{1,0:T(8,128)(2,1)} %all-gather.7.cloned.1.call-done, bf16[1024,1,1152]{2,0,1:T(8,128)(2,1)} %copy-done.24, bf16[1024,1,1152]{2,0,1:T(8,128)(2,1)S(1)} %copy-done.23), kind=kOutput, calls=%fused_computation.2 | convolution fusion | flops 10886381568 | bytes 20054016 | tf_op jit(solution)/shard_map/tkf,td->fkd/dot_general | solution.py:469
  692.1 6.8 pad_maximum_fusion
  698.9 20.4 %copy.52 = bf16[1152,6912]{1,0:T(8,128)(2,1)} copy(bf16[1152,6912]{0,1:T(8,128)(2,1)} %bitcast.96) | data formatting | bytes 31850496
  719.4 0.6 copy-done.20
  720.0 0.6 dynamic-slice
  721.3 1.2 fusion.76
  722.5 1.1 copy.47
  723.6 32.5 %all-reduce = f32[4,576]{1,0:T(4,128)S(1)} all-reduce(f32[4,576]{1,0:T(4,128)S(1)} %copy.47), channel_id=7, replica_groups=mesh['blk'=8,'sp'=4] {'blk'}, use_global_device_ids=true, to_apply=%region_18.0.clone | all-reduce | flops 2304 | bytes 18432
  756.1 0.6 constant_dynamic-slice_fusion
  756.7 1.8 convert_element_type.96
  758.6 95.7 %reduce-scatter.16.cloned.1.call-done = bf16[128,2304]{1,0:T(8,128)(2,1)} async-done(((bf16[1024,2304]{1,0:T(8,128)(2,1)}), bf16[128,2304]{1,0:T(8,128)(2,1)}) %reduce-scatter.16.cloned.1.call-update) | async-done | bytes 589840 | tf_op jit(solution)/shard_map/reduce_scatter | solution.py:509
  854.3 2.2 convert_element_type.94
  856.4 120.4 %reduce-scatter.22.cloned.1.call-done = bf16[288,6912]{1,0:T(8,128)(2,1)} async-done(((bf16[1152,6912]{1,0:T(8,128)(2,1)}), bf16[288,6912]{1,0:T(8,128)(2,1)}) %reduce-scatter.22.cloned.1.call-update) | async-done | bytes 3981328
  976.8 6.6 copy.53
  983.4 7.3 copy.41
  (84 shorter events, 1.4 us)
Async XLA Ops:
  7.2 29.3 %all-gather.5.cloned.1.call-start = ((), (), s32[]{:S(2)}) async-start(), calls=%async_computation.8 | async-start | bytes 2949120 | tf_op jit(solution)/shard_map/all_gather | solution.py:423
  8.8 105.9 %copy-start.7 = (f32[2304]{0:T(1024)}, f32[2304]{0:T(1024)S(1)}, u32[]{:S(2)}) copy-start(f32[2304]{0:T(1024)S(1)} %get-tuple-element.47) | copy-start | bytes 27652
  8.9 106.3 %copy-start.9 = (f32[2304]{0:T(1024)}, f32[2304]{0:T(1024)S(1)}, u32[]{:S(2)}) copy-start(f32[2304]{0:T(1024)S(1)} %get-tuple-element.49) | copy-start | bytes 27652
  10.1 33.0 %copy-start.15 = (f32[128]{0:T(128)}, f32[128]{0:T(128)S(1)}, u32[]{:S(2)}) copy-start(f32[128]{0:T(128)S(1)} %add_rsqrt_fusion.3) | copy-start | bytes 1540
  12.3 181.9 %all-gather.7.cloned.1.call-start = ((), (), s32[]{:S(2)}) async-start(), calls=%async_computation.9 | async-start | bytes 5308416 | tf_op jit(solution)/shard_map/all_gather | solution.py:443
  109.4 5.3 copy-start
  114.7 96.0 %copy-start.19 = (f32[128]{0:T(128)}, f32[128]{0:T(128)S(1)}, u32[]{:S(2)}) copy-start(f32[128]{0:T(128)S(1)} %add_rsqrt_fusion.2) | copy-start | bytes 1540
  115.1 415.8 %copy-start.18 = (f32[128]{0:T(128)}, f32[128]{0:T(128)S(1)}, u32[]{:S(2)}) copy-start(f32[128]{0:T(128)S(1)} %add_rsqrt_fusion.1) | copy-start | bytes 1540
  116.2 204.1 %reduce-scatter.12.cloned.1.call-start = ((), (), s32[]{:S(2)}) async-start(), calls=%async_computation.10 | async-start | bytes 5308416 | tf_op jit(solution)/shard_map/reduce_scatter | solution.py:450
  210.7 3.6 copy-start.21
  225.6 95.9 %copy-start.4 = (bf16[128,2304]{1,0:T(8,128)(2,1)S(1)}, bf16[128,2304]{1,0:T(8,128)(2,1)}, u32[]{:S(2)}) copy-start(bf16[128,2304]{1,0:T(8,128)(2,1)} %param.11) | copy-start | bytes 1769476
  225.7 179.0 %all-gather.9.cloned.1.call-start = ((), (), s32[]{:S(2)}) async-start(), calls=%async_computation.11 | async-start | bytes 5308416 | tf_op jit(solution)/shard_map/all_gather | solution.py:462
  321.5 2.1 copy-start.17
  325.9 205.0 %reduce-scatter.14.cloned.1.call-start = ((), (), s32[]{:S(2)}) async-start(), calls=%async_computation.12 | async-start | bytes 5308416 | tf_op jit(solution)/shard_map/reduce_scatter | solution.py:473
  419.4 1.5 copy-start.22
  419.4 2.2 copy-start.24
  436.3 96.7 %copy-start.3 = (bf16[128,2304]{1,0:T(8,128)(2,1)S(1)}, bf16[128,2304]{1,0:T(8,128)(2,1)}, u32[]{:S(2)}) copy-start(bf16[128,2304]{1,0:T(8,128)(2,1)} %reduce-scatter.12.cloned.1.call-done) | copy-start | bytes 1769476
  436.3 127.3 %all-gather.11.cloned.1.call-start = ((), (), s32[]{:S(2)}) async-start(), calls=%async_computation.13 | async-start | bytes 2949120 | tf_op jit(solution)/shard_map/all_gather | solution.py:485
  530.9 6.7 copy-start.8
  533.0 6.3 copy-start.14
  536.5 1.0 copy-start.1
  570.5 60.8 %copy-start.10 = (f32[2304]{0:T(1024)S(1)}, f32[2304]{0:T(1024)}, u32[]{:S(2)}) copy-start(f32[2304]{0:T(1024)} %get-tuple-element.44) | copy-start | bytes 27652
  570.5 60.8 %copy-start.11 = (f32[2304]{0:T(1024)S(1)}, f32[2304]{0:T(1024)}, u32[]{:S(2)}) copy-start(f32[2304]{0:T(1024)} %get-tuple-element.42) | copy-start | bytes 27652
  570.5 60.8 %copy-start.12 = (f32[2304]{0:T(1024)S(1)}, f32[2304]{0:T(1024)}, u32[]{:S(2)}) copy-start(f32[2304]{0:T(1024)} %get-tuple-element.38) | copy-start | bytes 27652
  623.6 21.2 %copy-start.16 = (f32[128]{0:T(128)S(1)}, f32[128]{0:T(128)}, u32[]{:S(2)}) copy-start(f32[128]{0:T(128)} %copy-done.15) | copy-start | bytes 1540
  626.3 17.7 %all-to-all-start.1 = ((bf16[512,1,4,256]{3,2,1,0:T(4,128)(2,1)}), bf16[512,1,4,256]{3,2,1,0:T(4,128)(2,1)S(1)}, u32[]{:S(2)}, u32[]{:S(2)}) async-start(bf16[512,1,4,256]{3,2,1,0:T(4,128)(2,1)} %bitcast.14), calls=%async_computation.3 | async-start | bytes 2097152 | tf_op jit(solution)/shard_map/all_to_all | solution.py:512
  631.2 91.3 %reduce-scatter.20.cloned.1.call-start = ((), (), s32[]{:S(2)}) async-start(), calls=%async_computation.16 | async-start | bytes 1474560
  644.8 9.3 copy-start.13
  644.9 10.9 %copy-start.6 = (bf16[512,512]{1,0:T(8,128)(2,1)S(1)}, bf16[512,512]{1,0:T(8,128)(2,1)}, u32[]{:S(2)}) copy-start(bf16[512,512]{1,0:T(8,128)(2,1)} %get-tuple-element.10) | copy-start | bytes 1572868
  655.7 4.7 copy-start.5
  655.7 101.0 %reduce-scatter.18.cloned.1.call-start = ((), (), s32[]{:S(2)}) async-start(), calls=%async_computation.15 | async-start | bytes 2654208 | tf_op jit(solution)/shard_map/reduce_scatter | solution.py:489
  660.4 193.9 %reduce-scatter.16.cloned.1.call-start = ((), (), s32[]{:S(2)}) async-start(), calls=%async_computation.14 | async-start | bytes 5308416 | tf_op jit(solution)/shard_map/reduce_scatter | solution.py:509
  666.4 310.4 %reduce-scatter.22.cloned.1.call-start = ((), (), s32[]{:S(2)}) async-start(), calls=%async_computation.17 | async-start | bytes 19906560
  666.6 11.5 %copy-start.23 = (bf16[1024,1,1152]{2,0,1:T(8,128)(2,1)S(1)}, bf16[1024,1,1152]{2,0,1:T(8,128)(2,1)}, u32[]{:S(2)}) copy-start(bf16[1024,1,1152]{2,0,1:T(8,128)(2,1)} %copy-done.22) | copy-start | bytes 7077892
  719.4 0.7 copy-start.20
  719.4 1.9 copy-start.2
Sparse Core Ops, SparseCore 0:
  12.4 24.0 all-gather.4
  116.3 77.8 all-gather.6
  225.8 94.3 reduce-scatter.11
  326.1 78.5 all-gather.8
  436.4 94.4 reduce-scatter.13
  539.5 24.0 all-gather.10
  655.8 26.1 reduce-scatter.19
  685.5 69.5 reduce-scatter.17
  759.3 94.9 reduce-scatter.15
  856.7 120.0 reduce-scatter.21

commit v3 on v2

--- a/solution.py
+++ b/solution.py
@@ -409,6 +409,450 @@
     )(projected, scaled, delta, kv_all)
 
 
+def line_gather(own_ref, full, line_sent, line_landed, side_sent, side_landed, own_done, work):
+    at = lax.axis_index("blk")
+    rows = lax.axis_size("blk") // 2
+    line, column = at // 2, at % 2
+    size = own_ref.shape[0]
+
+    def spot(source, side):
+        start = pl.multiple_of((2 * source + side) * size, size)
+        return full.at[pl.ds(start, size), :]
+
+    def line_copy(source, sign, first=False):
+        return push(
+            own_ref if first else spot(source, column),
+            spot(source, column),
+            line_sent.at[(sign + 1) // 2, source],
+            line_landed.at[source],
+            at + 2 * sign,
+        )
+
+    def side_copy(source, side, first=False):
+        return push(
+            own_ref if first else spot(source, side),
+            spot(source, side),
+            side_sent.at[source],
+            side_landed.at[source],
+            at + 1 - 2 * column,
+        )
+
+    def inside(row):
+        return jnp.logical_and(row >= 0, row < rows)
+
+    pl.when(line < rows - 1)(lambda: line_copy(line, 1, True).start())
+    pl.when(line > 0)(lambda: line_copy(line, -1, True).start())
+    side_copy(line, column, True).start()
+    keep = pltpu.make_async_copy(own_ref, spot(line, column), own_done)
+    keep.start()
+    keep.wait()
+
+    @pl.loop(0, rows + 1)
+    def _(step):
+        for sign in (-1, 1):
+            source = line - sign * step
+
+            @pl.when(both(step > 0, inside(source)))
+            def _():
+                line_copy(source, sign).wait_recv()
+                pl.when(inside(line + sign))(lambda: line_copy(source, sign).start())
+                side_copy(source, column).start()
+
+        for sign in (-1, 1):
+            source = line - sign * (step - 1)
+            once = step > 0 if sign == -1 else step > 1
+
+            @pl.when(both(once, inside(source)))
+            def _():
+                side_copy(source, 1 - column).wait_recv()
+                work(source)
+
+    @pl.loop(0, rows)
+    def _(source):
+        pl.when(both(source <= line, line < rows - 1))(lambda: line_copy(source, 1).wait_send())
+        pl.when(both(source >= line, line > 0))(lambda: line_copy(source, -1).wait_send())
+        side_copy(source, column).wait_send()
+
+
+def line_scatter(part, side, lane, out_ref, side_sent, side_landed, lane_sent, lane_landed, work, fill):
+    at = lax.axis_index("blk")
+    rows = lax.axis_size("blk") // 2
+    line, column = at // 2, at % 2
+    size = out_ref.shape[0]
+
+    def spot(target, half):
+        start = pl.multiple_of((2 * target + half) * size, size)
+        return pl.ds(start, size)
+
+    def side_copy(target):
+        return push(
+            part.at[spot(target, 1 - column), :],
+            side.at[target],
+            side_sent.at[target],
+            side_landed.at[target],
+            at + 1 - 2 * column,
+        )
+
+    def lane_copy(target, sign):
+        slot = target if sign == 1 else jnp.where(target == line - 1, rows, target)
+        return push(
+            part.at[spot(target, column), :],
+            lane.at[slot],
+            lane_sent.at[target],
+            lane_landed.at[slot],
+            at + 2 * sign,
+        )
+
+    def lane_wait(slot):
+        push(
+            lane.at[slot], lane.at[slot], lane_sent.at[0], lane_landed.at[slot], at + 1 - 2 * column
+        ).wait_recv()
+
+    def inside(row):
+        return jnp.logical_and(row >= 0, row < rows)
+
+    @pl.loop(0, rows)
+    def _(step):
+        for sign in (-1, 1):
+            target = line + sign * (rows - 1 - step)
+            once = step >= 0 if sign == -1 else step < rows - 1
+
+            @pl.when(both(once, inside(target)))
+            def _():
+                work(target)
+                side_copy(target).start()
+
+    def merge(target):
+        mine = spot(target, column)
+        side_copy(target).wait_recv()
+        part[mine, :] = (
+            part[mine, :].astype(jnp.float32) + side[target].astype(jnp.float32)
+        ).astype(jnp.bfloat16)
+
+        def pass_on(sign):
+            @pl.when(inside(line - sign))
+            def _():
+                lane_wait(target)
+                part[mine, :] = (
+                    part[mine, :].astype(jnp.float32) + lane[target].astype(jnp.float32)
+                ).astype(jnp.bfloat16)
+
+            lane_copy(target, sign).start()
+
+        pl.when(target > line)(lambda: pass_on(1))
+        pl.when(target < line)(lambda: pass_on(-1))
+
+    @pl.loop(0, rows)
+    def _(step):
+        fill(step)
+        for sign in (-1, 1):
+            target = line + sign * (rows - 1 - step)
+            once = step >= 0 if sign == -1 else step < rows - 1
+            pl.when(both(once, inside(target)))(lambda: merge(target))
+
+    mine = spot(line, column)
+    out_ref[...] = part[mine, :].astype(jnp.float32)
+
+    @pl.when(line > 0)
+    def _():
+        lane_wait(line)
+        out_ref[...] += lane[line].astype(jnp.float32)
+
+    @pl.when(line < rows - 1)
+    def _():
+        lane_wait(rows)
+        out_ref[...] += lane[rows].astype(jnp.float32)
+
+    @pl.loop(0, rows)
+    def _(target):
+        side_copy(target).wait_send()
+        pl.when(target > line)(lambda: lane_copy(target, 1).wait_send())
+        pl.when(target < line)(lambda: lane_copy(target, -1).wait_send())
+
+
+def line_sems(rows):
+    dma = pltpu.SemaphoreType.DMA
+    return [dma((2, rows)), dma((rows,)), dma((rows,)), dma((rows,)), dma]
+
+
+def lane_sems(rows):
+    dma = pltpu.SemaphoreType.DMA
+    return [dma((rows,)), dma((rows,)), dma((rows,)), dma((rows + 1,))]
+
+
+def ffn_kernel(
+    act_ref,
+    w_ref,
+    out_ref,
+    acts_ref,
+    w,
+    acts,
+    hidden,
+    part,
+    side,
+    lane,
+    w_done,
+    save_done,
+    *sems,
+):
+    at = lax.axis_index("blk")
+    rows = lax.axis_size("blk") // 2
+    pair = 2 * act_ref.shape[0]
+
+    def load(which):
+        return pltpu.make_async_copy(w_ref.at[which], w.at[which], w_done.at[which])
+
+    def pair_rows(source):
+        return pl.ds(pl.multiple_of(source * pair, pair), pair)
+
+    def save(source):
+        return pltpu.make_async_copy(
+            acts.at[pair_rows(source), :], acts_ref.at[pair_rows(source), :], save_done.at[source]
+        )
+
+    for which in range(3):
+        load(which).start()
+    greet(at, at // 2, rows)
+    for which in range(3):
+        load(which).wait()
+
+    def expand(source):
+        save(source).start()
+        rows_now = acts[pair_rows(source), :]
+        gate = contract_last(w[0], rows_now)
+        up = contract_last(w[1], rows_now)
+        hidden[source] = (gelu_value(gate) * up).astype(jnp.bfloat16)
+
+    def reduce(target):
+        part[pair_rows(target), :] = lax.dot_general(
+            hidden[target], w[2], (((0,), (0,)), ((), ())), preferred_element_type=jnp.float32
+        ).astype(jnp.bfloat16)
+
+    line_gather(act_ref, acts, *sems[:5], expand)
+    line_scatter(part, side, lane, out_ref, *sems[5:], reduce, lambda step: None)
+    pl.loop(0, rows)(lambda source: save(source).wait())
+
+
+def ffn_forward(act_ffn, w_parts):
+    size, width = act_ffn.shape
+    units = w_parts.shape[1]
+    blocks = lax.axis_size("blk")
+    rows = blocks // 2
+    whole = pl.BlockSpec(memory_space=pltpu.VMEM)
+    far = pl.BlockSpec(memory_space=pl.ANY)
+    return pl.pallas_call(
+        ffn_kernel,
+        out_shape=(
+            jax.ShapeDtypeStruct((size, width), jnp.float32),
+            jax.ShapeDtypeStruct((blocks * size, width), jnp.bfloat16),
+        ),
+        in_specs=[whole, far],
+        out_specs=(whole, far),
+        scratch_shapes=[
+            pltpu.VMEM(w_parts.shape, jnp.bfloat16),
+            pltpu.VMEM((blocks * size, width), jnp.bfloat16),
+            pltpu.VMEM((rows, units, 2 * size), jnp.bfloat16),
+            pltpu.VMEM((blocks * size, width), jnp.bfloat16),
+            pltpu.VMEM((rows, size, width), jnp.bfloat16),
+            pltpu.VMEM((rows + 1, size, width), jnp.bfloat16),
+            pltpu.SemaphoreType.DMA((3,)),
+            pltpu.SemaphoreType.DMA((rows,)),
+            *line_sems(rows),
+            *lane_sems(rows),
+        ],
+        compiler_params=pltpu.CompilerParams(
+            collective_id=2, has_side_effects=True, vmem_limit_bytes=VMEM_BYTES
+        ),
+        name="ffn_forward",
+    )(act_ffn, w_parts)
+
+
+FILL_COLUMNS = 256
+FILL_FIRST = 3
+
+
+def ffn_back_kernel(
+    owners,
+    grad_ref,
+    acts_ref,
+    w_ref,
+    out_ref,
+    sum_ref,
+    w,
+    rights,
+    lefts,
+    part,
+    side,
+    lane,
+    stage,
+    w_done,
+    acts_done,
+    stage_done,
+    *sems,
+):
+    at = lax.axis_index("blk")
+    rows = lax.axis_size("blk") // 2
+    size, width = grad_ref.shape
+    pair = 2 * size
+    units = w.shape[1]
+    acts, grads = rights.at[0], rights.at[1]
+
+    def load(which):
+        return pltpu.make_async_copy(w_ref.at[which], w.at[which], w_done.at[which])
+
+    def pair_rows(source):
+        return pl.ds(pl.multiple_of(source * pair, pair), pair)
+
+    acts_copy = pltpu.make_async_copy(acts_ref, acts, acts_done)
+    acts_copy.start()
+    for which in range(3):
+        load(which).start()
+    greet(at, at // 2, rows)
+    acts_copy.wait()
+    for which in range(3):
+        load(which).wait()
+
+    def expand(source):
+        columns = pair_rows(source)
+        rows_now = acts[pair_rows(source), :]
+        gate = contract_last(w[0], rows_now)
+        up = contract_last(w[1], rows_now)
+        grad_hidden = contract_last(w[2], grads[pair_rows(source), :])
+        bent = jnp.tanh(GELU_SCALE * (gate + GELU_CUBIC * gate * gate * gate))
+        value = 0.5 * gate * (1.0 + bent)
+        slope = 0.5 * (1.0 + bent) + 0.5 * gate * (1.0 - bent * bent) * GELU_SCALE * (
+            1.0 + 3.0 * GELU_CUBIC * gate * gate
+        )
+        lefts[2, :, columns] = (value * up).astype(jnp.bfloat16)
+        lefts[0, :, columns] = (grad_hidden * up * slope).astype(jnp.bfloat16)
+        lefts[1, :, columns] = (grad_hidden * value).astype(jnp.bfloat16)
+
+    def reduce(target):
+        columns = pair_rows(target)
+        dims = (((0,), (0,)), ((), ()))
+        total = lax.dot_general(
+            lefts[0, :, columns], w[0], dims, preferred_element_type=jnp.float32
+        ) + lax.dot_general(lefts[1, :, columns], w[1], dims, preferred_element_type=jnp.float32)
+        part[pair_rows(target), :] = total.astype(jnp.bfloat16)
+
+    pieces = width // FILL_COLUMNS
+    total_pieces = 3 * pieces
+
+    def piece_columns(item):
+        return pl.ds(pl.multiple_of((item % pieces) * FILL_COLUMNS, FILL_COLUMNS), FILL_COLUMNS)
+
+    def stage_copy(item):
+        return pltpu.make_async_copy(
+            stage.at[item % 2],
+            sum_ref.at[:, item // pieces, :, piece_columns(item)],
+            stage_done.at[item % 2],
+        )
+
+    def fill_one(item):
+        which = item // pieces
+        total = jnp.dot(
+            lefts[which],
+            rights[which // 2, :, piece_columns(item)],
+            preferred_element_type=jnp.float32,
+        )
+        pl.when(item > 1)(lambda: stage_copy(item - 2).wait())
+        stage[item % 2] = total.astype(jnp.bfloat16).reshape(
+            owners, units // owners, FILL_COLUMNS
+        )
+        stage_copy(item).start()
+
+    each = pl.cdiv(total_pieces - FILL_FIRST, rows - 1)
+
+    def fill(step):
+        first = jnp.maximum(FILL_FIRST + (step - 1) * each, 0)
+        last = jnp.minimum(FILL_FIRST + step * each, total_pieces)
+
+        @pl.loop(0, each)
+        def _(item):
+            pl.when(first + item < last)(lambda: fill_one(first + item))
+
+    line_gather(grad_ref, grads, *sems[:5], expand)
+    line_scatter(part, side, lane, out_ref, *sems[5:], reduce, fill)
+    stage_copy(total_pieces - 2).wait()
+    stage_copy(total_pieces - 1).wait()
+
+
+def ffn_back(grad_ffn, acts, w_parts, owners):
+    size, width = grad_ffn.shape
+    units = w_parts.shape[1]
+    blocks = lax.axis_size("blk")
+    rows = blocks // 2
+    tokens = blocks * size
+    whole = pl.BlockSpec(memory_space=pltpu.VMEM)
+    far = pl.BlockSpec(memory_space=pl.ANY)
+    return pl.pallas_call(
+        functools.partial(ffn_back_kernel, owners),
+        out_shape=(
+            jax.ShapeDtypeStruct((size, width), jnp.float32),
+            jax.ShapeDtypeStruct((owners, 3, units // owners, width), jnp.bfloat16),
+        ),
+        in_specs=[whole, far, far],
+        out_specs=(whole, far),
+        scratch_shapes=[
+            pltpu.VMEM(w_parts.shape, jnp.bfloat16),
+            pltpu.VMEM((2, tokens, width), jnp.bfloat16),
+            pltpu.VMEM((3, units, tokens), jnp.bfloat16),
+            pltpu.VMEM((tokens, width), jnp.bfloat16),
+            pltpu.VMEM((rows, size, width), jnp.bfloat16),
+            pltpu.VMEM((rows + 1, size, width), jnp.bfloat16),
+            pltpu.VMEM((2, owners, units // owners, FILL_COLUMNS), jnp.bfloat16),
+            pltpu.SemaphoreType.DMA((3,)),
+            pltpu.SemaphoreType.DMA,
+            pltpu.SemaphoreType.DMA((2,)),
+            *line_sems(rows),
+            *lane_sems(rows),
+        ],
+        compiler_params=pltpu.CompilerParams(
+            collective_id=3, has_side_effects=True, vmem_limit_bytes=VMEM_BYTES
+        ),
+        name="ffn_back",
+    )(grad_ffn, acts, w_parts)
+
+
+def ffn_hidden(acts, w_parts):
+    gate = contract_last(acts, w_parts[0])
+    up = contract_last(acts, w_parts[1])
+    return (gate, up, (gelu_value(gate) * up).astype(jnp.bfloat16))
+
+
+def scatter_tokens(partial):
+    return lax.psum_scatter(
+        partial.astype(jnp.bfloat16), "blk", scatter_dimension=0, tiled=True
+    ).astype(jnp.float32)
+
+
+def ffn_forward_wide(act_ffn, w_parts):
+    acts = lax.all_gather(act_ffn, "blk", axis=0, tiled=True)
+    hidden = ffn_hidden(acts, w_parts)[2]
+    partial = jnp.dot(hidden, w_parts[2], preferred_element_type=jnp.float32)
+    return (scatter_tokens(partial), acts)
+
+
+def ffn_back_wide(grad_ffn, acts, w_parts, owners):
+    grads = lax.all_gather(grad_ffn, "blk", axis=0, tiled=True)
+    gate, up, hidden = ffn_hidden(acts, w_parts)
+    grad_hidden = contract_last(grads, w_parts[2])
+    grad_gate = (grad_hidden * up * gelu_slope(gate)).astype(jnp.bfloat16)
+    grad_up = (grad_hidden * gelu_value(gate)).astype(jnp.bfloat16)
+    partial = jnp.dot(grad_gate, w_parts[0], preferred_element_type=jnp.float32) + jnp.dot(
+        grad_up, w_parts[1], preferred_element_type=jnp.float32
+    )
+    sums = jnp.stack(
+        [
+            jnp.einsum("tf,td->fd", left, right, preferred_element_type=jnp.float32)
+            for left, right in ((grad_gate, acts), (grad_up, acts), (hidden, grads))
+        ]
+    ).astype(jnp.bfloat16)
+    units = w_parts.shape[1]
+    owned = sums.reshape(3, owners, units // owners, sums.shape[2])
+    return (scatter_tokens(partial), jnp.transpose(owned, (1, 0, 2, 3)))
+
+
 def body(tokens, w_qkv, w_out, gains, w_ffn, cotangent):
     row_count = tokens.shape[0]
     groups = lax.axis_size("sp")
@@ -436,48 +880,17 @@
     middle = source + normed_attn * gains[1]
     normed_mid, inverse_mid = norm_parts(middle)
     act_ffn = (normed_mid * gains[2]).astype(jnp.bfloat16)
-    w_in = w_ffn[:, :2, :]
-    w_down = w_ffn[:, 2, :]
-    gate_up = jnp.einsum(
-        "td,fkd->tkf",
-        lax.all_gather(act_ffn, "blk", axis=0, tiled=True),
-        w_in,
-        preferred_element_type=jnp.float32,
-    )
-    hidden = (gelu_value(gate_up[:, 0]) * gate_up[:, 1]).astype(jnp.bfloat16)
-    hidden_all = hidden
-    part = hidden_all
-    ffn_out = lax.psum_scatter(
-        jnp.dot(part, w_down, preferred_element_type=jnp.float32).astype(jnp.bfloat16),
-        "blk",
-        scatter_dimension=0,
-        tiled=True,
-    ).astype(jnp.float32)
+    wide = lax.axis_size("blk") > 8
+    w_parts = jnp.transpose(w_ffn, (1, 0, 2))
+    ffn_out, act_all = (ffn_forward_wide if wide else ffn_forward)(act_ffn, w_parts)
     normed_ffn, inverse_ffn = norm_parts(ffn_out)
     result = middle + normed_ffn * gains[3]
     grad_out = cotangent.astype(jnp.float32)
     grad_ffn_f, gain_grad3 = norm_back(grad_out, normed_ffn, inverse_ffn, gains[3])
     grad_ffn = grad_ffn_f.astype(jnp.bfloat16)
-    act_piece = lax.all_gather(act_ffn, "blk", axis=0, tiled=True)
-    grad_piece = lax.all_gather(grad_ffn, "blk", axis=0, tiled=True)
-    gate_up = jnp.einsum("td,fkd->tkf", act_piece, w_in, preferred_element_type=jnp.float32)
-    hidden = (gelu_value(gate_up[:, 0]) * gate_up[:, 1]).astype(jnp.bfloat16)
-    grad_hidden = contract_last(grad_piece, w_down)
-    grad_gate = grad_hidden * gate_up[:, 1] * gelu_slope(gate_up[:, 0])
-    grad_up = grad_hidden * gelu_value(gate_up[:, 0])
-    grad_pair = jnp.stack([grad_gate, grad_up], axis=1).astype(jnp.bfloat16)
-    in_part = jnp.einsum("tkf,td->fkd", grad_pair, act_piece, preferred_element_type=jnp.float32)
-    down_part = jnp.einsum("tf,td->fd", hidden, grad_piece, preferred_element_type=jnp.float32)
-    weight_sum = jnp.concatenate([in_part, down_part[:, None, :]], axis=1)
-    part = grad_pair
-    grad_act_ffn = lax.psum_scatter(
-        jnp.einsum("tkf,fkd->td", part, w_in, preferred_element_type=jnp.float32).astype(
-            jnp.bfloat16
-        ),
-        "blk",
-        scatter_dimension=0,
-        tiled=True,
-    ).astype(jnp.float32)
+    grad_act_ffn, ffn_sums = (ffn_back_wide if wide else ffn_back)(
+        grad_ffn, act_all, w_parts, groups
+    )
     grad_norm_mid, gain_grad2 = norm_back(grad_act_ffn, normed_mid, inverse_mid, gains[2])
     grad_middle = grad_out + grad_norm_mid
     grad_attn_f, gain_grad1 = norm_back(grad_middle, normed_attn, inverse_attn, gains[1])
@@ -515,9 +928,8 @@
     grad_source, gain_grad0 = norm_back(grad_act_in, normed_in, inverse_in, gains[0])
     tokens_grad = (grad_middle + grad_source).astype(jnp.bfloat16)
     gains_term = jnp.stack([gain_grad0, gain_grad1, gain_grad2, gain_grad3], axis=0)
-    ffn_grad = lax.psum_scatter(
-        weight_sum.astype(jnp.bfloat16), "sp", scatter_dimension=0, tiled=True
-    ).astype(jnp.float32)
+    ffn_part = lax.psum_scatter(ffn_sums, "sp", scatter_dimension=0, tiled=True)
+    ffn_grad = jnp.transpose(ffn_part[0].astype(jnp.float32), (1, 0, 2))
     gains_part = lax.psum_scatter(gains_term, "sp", scatter_dimension=1, tiled=True)
     gains_grad = lax.psum_scatter(gains_part, "blk", scatter_dimension=1, tiled=True)
     return (result.astype(jnp.bfloat16), tokens_grad, qkv_grad, out_grad, gains_grad, ffn_grad)

time: 1010 us -> 824 us (0.82)
  waiting for transfers between devices: 621 us -> 327 us
  Pallas kernels: 107 us -> 343 us
  matrix products: 119 us -> 36.5 us
  local copies, waits for them, and re-layouts: 55 us -> 17.1 us
    pallas_call x0 -> x2, Pallas kernels: none -> 236 us  [the longest x1 118 us: ffn_back(): pl.pallas_call(functools.partial(ffn_back_kernel, owners), out_shape=(jax...]
    all_gather x2 -> x0, waiting for transfers between devices: 156 us -> none  [the longest x1 78.5 us: body(): grad_piece = lax.all_gather(grad_ffn, 'blk', axis=0, tiled=True)]
    unnamed x12 -> x7, waiting for transfers between devices: 121 us -> 12 us
    reduce_scatter x2 -> x1, waiting for transfers between devices: 189 us -> 120 us  [body(): ffn_part = lax.psum_scatter(ffn_sums, 'sp', scatter_dimension=0, tiled=True)]
    dot_general x5 -> x0, matrix products: 68 us -> none  [the longest x1 16.6 us: body(): jnp.einsum('td,fkd->tkf', lax.all_gather(act_ffn, 'blk', axis=0, tiled=Tr...]
    unnamed x59 -> x30, local copies, waits for them, and re-layouts: 45.6 us -> 6.84 us
    reduce_scatter x1, waiting for transfers between devices: 0.01 us -> 38.2 us  [body(): lax.psum_scatter(out_term.astype(jnp.bfloat16), 'blk', scatter_dimension=...]
    dot_general x3 -> x2, matrix products: 26.2 us -> 11.5 us  [contract_last(): lax.dot_general(left, right, (((1,), (1,)), ((), ())), preferred_element_...]
  transfers between devices with their start and end apart: 11 -> 7, of which waited for: 9 -> 7; matrix products, arithmetic and copies ran while one was open for 7% -> 2% of each run, Pallas kernels for 0% -> 0%
where the time goes in v3:
time: 824 us; the launch traced here: 815 us
  Pallas kernels  343 us (42%)
  waiting for transfers between devices  327 us (40%)
  blocking collectives  44 us (5%)
  matrix products  36.5 us (4%)
  other arithmetic  26.1 us (3%)
  local copies, waits for them, and re-layouts  17.1 us (2%)
  between operations  15.3 us (2%)
    reduce_scatter x1, waiting for transfers between devices, body(): ffn_part = lax.psum_scatter(ffn_sums, 'sp', scatter_dimension=0, tiled=True)  120 us
    pallas_call x1, Pallas kernels, ffn_back(): pl.pallas_call(functools.partial(ffn_back_kernel, owners), out_shape=(jax...  118 us
    pallas_call x1, Pallas kernels, ffn_forward(): pl.pallas_call(ffn_kernel, out_shape=(jax.ShapeDtypeStruct((size, width),...  118 us
    reduce_scatter x1, waiting for transfers between devices, body(): lax.psum_scatter(qkv_term.astype(jnp.bfloat16), 'blk', scatter_dimension=...  97.2 us
    pallas_call x1, Pallas kernels, attend(): pl.pallas_call(functools.partial(attend_kernel, heads), out_shape=(jax.Sh...  53.7 us
    pallas_call x1, Pallas kernels, attend_back(): pl.pallas_call(functools.partial(attend_back_kernel, heads), out_shape=ja...  53.1 us
    reduce_scatter x1, waiting for transfers between devices, body(): lax.psum_scatter(out_term.astype(jnp.bfloat16), 'blk', scatter_dimension=...  38.2 us
    unnamed x1, blocking collectives  33 us
  transfers between devices with their start and end apart: 7, of which 7 were waited for; matrix products, arithmetic and copies ran while one was open for 2% of the time, Pallas kernels for 0%

profile of v3, /device:TPU:26, one launch (start us, length us, event | category | flops | bytes accessed | tf_op | source)
XLA Modules:
  0.0 814.7 jit_solution(9205207329256270283)
XLA Ops:
  7.2 0.0 all-gather.3.cloned.1.call-start
  7.2 1.0 slice_reduce_fusion
  8.2 1.3 fusion.26
  9.5 2.1 fusion.19
  11.6 0.0 all-gather.3.cloned.1.call-update
  11.6 0.0 all-gather.5.cloned.1.call-start
  11.7 24.2 %all-gather.3.cloned.1.call-done = bf16[512,2304]{1,0:T(8,128)(2,1)} async-done(((bf16[128,2304]{1,0:T(8,128)(2,1)}), bf16[512,2304]{1,0:T(8,128)(2,1)}) %all-gather.3.cloned.1.call-update) | async-done | bytes 2359312 | tf_op jit(solution)/shard_map/all_gather | solution.py:867
  35.9 6.7 fusion.8.x_ref
  42.5 53.7 %attend.1 = (bf16[512,512]{1,0:T(8,128)(2,1)}, f32[512,512]{1,0:T(8,128)}, f32[2,1,512]{2,1,0:T(1,128)}, bf16[8,512,512]{2,1,0:T(8,128)(2,1)}) custom-call(bf16[512,1024]{1,0:T(8,128)(2,1)} %fusion.8.x_ref), custom_call_target="tpu_custom_call" | custom-call | tf_op jit(solution)/shard_map/attend/pallas_call | solution.py:204
  96.3 1.2 reshape.88
  97.4 11.0 %all_to_all.30 = bf16[512,2,256]{2,1,0:T(2,128)(2,1)S(1)} all-to-all(bf16[512,2,256]{2,1,0:T(2,128)(2,1)S(1)} %reshape.88), channel_id=1, replica_groups=mesh['blk'=8,'sp'=4] {'sp'}, dimensions={0} | all-to-all | bytes 1048576 | tf_op jit(solution)/shard_map/all_to_all | solution.py:875
  108.5 0.1 copy.22
  108.6 0.3 copy.23
  108.9 5.2 multiply_reduce_fusion.6
  114.1 0.4 multiply_reduce_fusion.5
  114.5 0.6 copy-done
  115.1 1.0 multiply_convert_fusion.1.act_ref
  116.1 118.1 %ffn_forward.1 = (f32[128,2304]{1,0:T(8,128)}, bf16[1024,2304]{1,0:T(8,128)(2,1)}) custom-call(bf16[128,2304]{1,0:T(8,128)(2,1)} %multiply_convert_fusion.1.act_ref, bf16[3,1152,2304]{2,1,0:T(8,128)(2,1)} %bitcast.40), custom_call_target="tpu_custom_call" | custom-call | tf_op jit(solution)/shard_map/ffn_forward/pallas_call | solution.py:643
  234.3 1.5 multiply_reduce_fusion.4
  235.8 0.1 copy-done.5
  235.9 1.6 fusion.27
  237.5 1.4 fusion.18
  238.9 118.4 %ffn_back.1 = (f32[128,2304]{1,0:T(8,128)}, bf16[4,3,288,2304]{3,2,1,0:T(8,128)(2,1)}) custom-call(bf16[128,2304]{1,0:T(8,128)(2,1)} %get-tuple-element.37.grad_ref, bf16[1024,2304]{1,0:T(8,128)(2,1)} %get-tuple-element.16.acts_ref, bf16[3,1152,2304]{2,1,0:T(8,128)(2,1)} %bitcast.41), custom_call_target="tpu_custom_call" | custom-call | tf_op jit(solution)/shard_map/ffn_back/pallas_call | solution.py:788
  357.3 1.8 multiply_reduce_fusion
  359.1 2.0 multiply_reduce_fusion.1
  361.1 1.0 copy-done.3
  362.1 1.1 multiply_convert_fusion
  363.3 0.1 copy.25
  363.4 0.6 div.46
  364.0 0.1 copy.36
  364.1 22.5 %all-gather.5.cloned.1.call-done = bf16[512,2304]{1,0:T(8,128)(2,1)} async-done(((bf16[128,2304]{1,0:T(8,128)(2,1)}), bf16[512,2304]{1,0:T(8,128)(2,1)}) %all-gather.5.cloned.1.call-update) | async-done | bytes 2359312 | tf_op jit(solution)/shard_map/all_gather | solution.py:898
  386.6 4.9 convert_multiply_fusion.4
  391.5 0.7 mul.243
  392.2 0.6 reduce_sum.126
  392.8 0.1 copy.26
  392.9 0.6 reshape.91.delta_ref
  393.5 53.1 %attend_back.1 = bf16[512,1024]{1,0:T(8,128)(2,1)} custom-call(bf16[512,1024]{1,0:T(8,128)(2,1)} %fusion.8.x_ref, bf16[512,512]{1,0:T(8,128)(2,1)} %get-tuple-element.40.scaled_ref, f32[2,1,512]{2,1,0:T(1,128)} %reshape.91.delta_ref, bf16[8,512,512]{2,1,0:T(8,128)(2,1)} %get-tuple-element.20.kv_ref), custom_call_target="tpu_custom_call" | custom-call | tf_op jit(solution)/shard_map/attend_back/pallas_call | solution.py:386
  446.6 2.6 reshape.92
  449.3 5.0 all-to-all-start.1
  454.3 12.8 %all-to-all-done.1 = bf16[512,1,4,256]{3,2,1,0:T(4,128)(2,1)S(1)} async-done(((bf16[512,1,4,256]{3,2,1,0:T(4,128)(2,1)}), bf16[512,1,4,256]{3,2,1,0:T(4,128)(2,1)S(1)}, u32[]{:S(2)}, u32[]{:S(2)}) %all-to-all-start.1) | async-done | bytes 1048608 | tf_op jit(solution)/shard_map/all_to_all | solution.py:925
  467.0 1.1 copy.28
  468.1 1.8 copy.29
  469.9 9.2 %fusion.25 = (f32[2304]{0:T(1024)S(1)}, f32[128]{0:T(128)S(1)}, f32[128,2304]{1,0:T(8,128)S(1)}) fusion(bf16[128,2304]{1,0:T(8,128)(2,1)S(1)} %copy-done.2, f32[128]{0:T(128)S(1)} %add_rsqrt_fusion.3, f32[2304]{0:T(1024)S(1)} %get-tuple-element.32, bf16[128,4096]{0,1:T(8,128)(2,1)S(1)} %bitcast.42, bf16[4096,2304]{1,0:T(8,128)(2,1)} %param.7), kind=kOutput, calls=%fused_computation.32 | convolution fusion | flops 2417980928 | bytes 21711872 | tf_op jit(solution)/shard_map/dot_general | solution.py:927
  479.3 1.5 copy.31
  480.8 0.0 reduce-scatter.10.cloned.1.call-start
  480.8 4.5 convolution_convert_fusion.1
  485.4 0.0 reduce-scatter.8.cloned.1.call-start
  485.4 1.1 copy-done.8
  486.6 6.0 convolution_convert_fusion
  492.6 0.0 reduce-scatter.12.cloned.1.call-start
  492.6 0.5 reduce-scatter.12.cloned.1.call-update
  493.1 0.1 copy-done.11
  493.3 0.6 dynamic-slice
  494.5 1.2 fusion.24
  495.7 11.4 %reduce-scatter.14.cloned.1.call-done = f32[576,4]{1,0:T(8,128)} async-done(((f32[2304,4]{1,0:T(8,128)}), f32[576,4]{1,0:T(8,128)}) %reduce-scatter.14.cloned.1.call-update) | async-done | bytes 9232
  507.1 1.1 copy.32
  508.2 33.0 %all-reduce = f32[4,576]{1,0:T(4,128)S(1)} all-reduce(f32[4,576]{1,0:T(4,128)S(1)} %copy.32), channel_id=5, replica_groups=mesh['blk'=8,'sp'=4] {'blk'}, use_global_device_ids=true, to_apply=%region_16.0.clone | all-reduce | flops 2304 | bytes 18432
  541.2 0.6 constant_dynamic-slice_fusion
  541.8 38.2 %reduce-scatter.10.cloned.1.call-done = bf16[64,2304]{1,0:T(8,128)(2,1)} async-done(((bf16[512,2304]{1,0:T(8,128)(2,1)}), bf16[64,2304]{1,0:T(8,128)(2,1)}) %reduce-scatter.10.cloned.1.call-update) | async-done | bytes 294928 | tf_op jit(solution)/shard_map/reduce_scatter | solution.py:902
  580.0 1.8 convert_element_type.68
  581.8 97.2 %reduce-scatter.8.cloned.1.call-done = bf16[128,2304]{1,0:T(8,128)(2,1)} async-done(((bf16[1024,2304]{1,0:T(8,128)(2,1)}), bf16[128,2304]{1,0:T(8,128)(2,1)}) %reduce-scatter.8.cloned.1.call-update) | async-done | bytes 589840 | tf_op jit(solution)/shard_map/reduce_scatter | solution.py:922
  679.1 2.2 convert_element_type.66
  681.2 120.4 %reduce-scatter.12.cloned.1.call-done = bf16[1,3,288,2304]{3,2,1,0:T(8,128)(2,1)} async-done(((bf16[4,3,288,2304]{3,2,1,0:T(8,128)(2,1)}), bf16[1,3,288,2304]{3,2,1,0:T(8,128)(2,1)}) %reduce-scatter.12.cloned.1.call-update) | async-done | bytes 3981328 | tf_op jit(solution)/shard_map/reduce_scatter | solution.py:931
  801.6 6.0 convert_bitcast_fusion
  (39 shorter events, 0.2 us)
Async XLA Ops:
  7.2 28.7 %all-gather.3.cloned.1.call-start = ((), (), s32[]{:S(2)}) async-start(), calls=%async_computation.6 | async-start | bytes 2949120 | tf_op jit(solution)/shard_map/all_gather | solution.py:867
  11.6 375.0 %all-gather.5.cloned.1.call-start = ((), (), s32[]{:S(2)}) async-start(), calls=%async_computation.7 | async-start | bytes 2949120 | tf_op jit(solution)/shard_map/all_gather | solution.py:898
  108.8 5.3 copy-start.2
  114.1 1.0 copy-start
  234.3 1.6 copy-start.5
  235.8 1.7 copy-start.6
  357.3 1.8 copy-start.1
  357.3 1.8 copy-start.7
  361.1 1.0 copy-start.3
  362.1 1.1 copy-start.10
  449.3 17.8 %all-to-all-start.1 = ((bf16[512,1,4,256]{3,2,1,0:T(4,128)(2,1)}), bf16[512,1,4,256]{3,2,1,0:T(4,128)(2,1)S(1)}, u32[]{:S(2)}, u32[]{:S(2)}) async-start(bf16[512,1,4,256]{3,2,1,0:T(4,128)(2,1)} %bitcast.6), calls=%async_computation.1 | async-start | bytes 2097152 | tf_op jit(solution)/shard_map/all_to_all | solution.py:925
  454.2 52.9 %reduce-scatter.14.cloned.1.call-start = ((), (), s32[]{:S(2)}) async-start(), calls=%async_computation.11 | async-start | bytes 1474560
  479.3 1.6 copy-start.9
  480.8 99.3 %reduce-scatter.10.cloned.1.call-start = ((), (), s32[]{:S(2)}) async-start(), calls=%async_computation.9 | async-start | bytes 2654208 | tf_op jit(solution)/shard_map/reduce_scatter | solution.py:902
  485.3 1.2 copy-start.8
  485.4 193.7 %reduce-scatter.8.cloned.1.call-start = ((), (), s32[]{:S(2)}) async-start(), calls=%async_computation.8 | async-start | bytes 5308416 | tf_op jit(solution)/shard_map/reduce_scatter | solution.py:922
  492.6 309.1 %reduce-scatter.12.cloned.1.call-start = ((), (), s32[]{:S(2)}) async-start(), calls=%async_computation.10 | async-start | bytes 19906560 | tf_op jit(solution)/shard_map/reduce_scatter | solution.py:931
  492.6 0.7 copy-start.11
  492.6 1.9 copy-start.4
Sparse Core Ops, SparseCore 0:
  11.7 24.0 all-gather.2
  363.4 23.2 all-gather.4
  480.9 26.1 reduce-scatter.13
  510.5 69.5 reduce-scatter.9
  584.1 94.9 reduce-scatter.7
  681.5 120.0 reduce-scatter.11

commit v4 on v3

--- a/solution.py
+++ b/solution.py
@@ -225,6 +225,7 @@
         compiler_params=pltpu.CompilerParams(
             collective_id=0, has_side_effects=True, vmem_limit_bytes=VMEM_BYTES
         ),
+        cost_estimate=cost_of(50),
         name="attend",
     )(projected)
 
@@ -405,6 +406,7 @@
         compiler_params=pltpu.CompilerParams(
             collective_id=1, has_side_effects=True, vmem_limit_bytes=VMEM_BYTES
         ),
+        cost_estimate=cost_of(50),
         name="attend_back",
     )(projected, scaled, delta, kv_all)
 
@@ -663,6 +665,7 @@
         compiler_params=pltpu.CompilerParams(
             collective_id=2, has_side_effects=True, vmem_limit_bytes=VMEM_BYTES
         ),
+        cost_estimate=cost_of(115),
         name="ffn_forward",
     )(act_ffn, w_parts)
 
@@ -810,6 +813,7 @@
         compiler_params=pltpu.CompilerParams(
             collective_id=3, has_side_effects=True, vmem_limit_bytes=VMEM_BYTES
         ),
+        cost_estimate=cost_of(115),
         name="ffn_back",
     )(grad_ffn, acts, w_parts)
 
@@ -853,29 +857,222 @@
     return (scatter_tokens(partial), jnp.transpose(owned, (1, 0, 2, 3)))
 
 
+def cost_of(microseconds):
+    return pl.CostEstimate(
+        flops=int(microseconds * 1e9), bytes_accessed=int(microseconds * 3e6), transcendentals=0
+    )
+
+
+def push_sp(source, target, sent, landed, peer):
+    return pltpu.make_async_remote_copy(
+        src_ref=source,
+        dst_ref=target,
+        send_sem=sent,
+        recv_sem=landed,
+        device_id={"sp": peer},
+        device_id_type=pl.DeviceIdType.MESH,
+    )
+
+
+def greet_sp(me, groups):
+    barrier = pltpu.get_barrier_semaphore()
+    for step in range(1, groups):
+        pl.semaphore_signal(
+            barrier,
+            inc=1,
+            device_id={"sp": (me + step) % groups},
+            device_id_type=pl.DeviceIdType.MESH,
+        )
+    pl.semaphore_wait(barrier, groups - 1)
+
+
+def gather_project_kernel(x_ref, w_ref, full_ref, out_ref, w, w_done, own_done, sent, landed):
+    me = lax.axis_index("sp")
+    size = x_ref.shape[0]
+    units = w.shape[0]
+    mate = me + 1 - 2 * (me % 2)
+    across = (me + 2) % 4
+
+    def spot(member):
+        return full_ref.at[pl.ds(pl.multiple_of(member * size, size), size), :]
+
+    load = pltpu.make_async_copy(
+        w_ref.at[pl.ds(pl.multiple_of(me * units, units), units), :], w, w_done
+    )
+    load.start()
+    greet_sp(me, 4)
+    over = push_sp(x_ref, spot(me), sent.at[0], landed.at[0], across)
+    over.start()
+    beside = push_sp(x_ref, spot(me), sent.at[1], landed.at[1], mate)
+    beside.start()
+    keep = pltpu.make_async_copy(x_ref, spot(me), own_done)
+    keep.start()
+    keep.wait()
+    load.wait()
+
+    def project(chip):
+        rows = pl.ds(pl.multiple_of(chip * 2 * size, 2 * size), 2 * size)
+        out_ref[rows, :] = contract_last(full_ref[rows, :], w[...]).astype(jnp.bfloat16)
+
+    beside.wait_recv()
+    project(me // 2)
+    over.wait_recv()
+    onward = push_sp(spot(across), spot(across), sent.at[2], landed.at[2], mate)
+    onward.start()
+    onward.wait_recv()
+    project(across // 2)
+    over.wait_send()
+    beside.wait_send()
+    onward.wait_send()
+
+
+def gather_project(rows, weights, identity):
+    size, width = rows.shape
+    units = weights.shape[0] // 4
+    whole = pl.BlockSpec(memory_space=pltpu.VMEM)
+    return pl.pallas_call(
+        gather_project_kernel,
+        out_shape=(
+            jax.ShapeDtypeStruct((4 * size, width), jnp.bfloat16),
+            jax.ShapeDtypeStruct((4 * size, units), jnp.bfloat16),
+        ),
+        in_specs=[whole, pl.BlockSpec(memory_space=pl.ANY)],
+        out_specs=(whole, whole),
+        scratch_shapes=[
+            pltpu.VMEM((units, width), jnp.bfloat16),
+            pltpu.SemaphoreType.DMA,
+            pltpu.SemaphoreType.DMA,
+            pltpu.SemaphoreType.DMA((3,)),
+            pltpu.SemaphoreType.DMA((3,)),
+        ],
+        compiler_params=pltpu.CompilerParams(
+            collective_id=identity, has_side_effects=True, vmem_limit_bytes=VMEM_BYTES
+        ),
+        cost_estimate=cost_of(18),
+        name="gather_project",
+    )(rows, weights)
+
+
+def exchange_project_kernel(x_ref, w_ref, out_ref, w, got, w_done, own_done, sent, landed):
+    me = lax.axis_index("sp")
+    size = out_ref.shape[0]
+    units = x_ref.shape[1]
+
+    def rows_of(member):
+        return x_ref.at[pl.ds(pl.multiple_of(member * size, size), size), :]
+
+    def load(member):
+        rows = pl.ds(pl.multiple_of(member * units, units), units)
+        return pltpu.make_async_copy(w_ref.at[rows, :], w.at[rows, :], w_done.at[member])
+
+    def send(step):
+        peer = (me + step) % 4
+        return push_sp(rows_of(peer), got.at[4 - step], sent.at[step], landed.at[4 - step], peer)
+
+    greet_sp(me, 4)
+    for step in (2, 1, 3):
+        send(step).start()
+    keep = pltpu.make_async_copy(rows_of(me), got.at[0], own_done)
+    keep.start()
+    for step in range(4):
+        load((me + step) % 4).start()
+    keep.wait()
+    for step in (0, 1, 3, 2):
+        member = (me + step) % 4
+        load(member).wait()
+        if step > 0:
+            send(4 - step).wait_recv()
+        rows = pl.ds(pl.multiple_of(member * units, units), units)
+        term = jnp.dot(got[step], w[rows, :], preferred_element_type=jnp.float32)
+        if step == 0:
+            out_ref[...] = term
+        else:
+            out_ref[...] += term
+    for step in (1, 2, 3):
+        send(step).wait_send()
+
+
+def exchange_project(columns, weights, identity):
+    size = columns.shape[0] // 4
+    whole = pl.BlockSpec(memory_space=pltpu.VMEM)
+    return pl.pallas_call(
+        exchange_project_kernel,
+        out_shape=jax.ShapeDtypeStruct((size, weights.shape[1]), jnp.float32),
+        in_specs=[whole, pl.BlockSpec(memory_space=pl.ANY)],
+        out_specs=whole,
+        scratch_shapes=[
+            pltpu.VMEM(weights.shape, jnp.bfloat16),
+            pltpu.VMEM((4, size, columns.shape[1]), jnp.bfloat16),
+            pltpu.SemaphoreType.DMA((4,)),
+            pltpu.SemaphoreType.DMA,
+            pltpu.SemaphoreType.DMA((4,)),
+            pltpu.SemaphoreType.DMA((4,)),
+        ],
+        compiler_params=pltpu.CompilerParams(
+            collective_id=identity, has_side_effects=True, vmem_limit_bytes=VMEM_BYTES
+        ),
+        cost_estimate=cost_of(16),
+        name="exchange_project",
+    )(columns, weights)
+
+
+def weight_kernel(left_ref, right_ref, out_ref, part, side, lane, *sems):
+    at = lax.axis_index("blk")
+    rows = lax.axis_size("blk") // 2
+    pair = 2 * out_ref.shape[0]
+    greet(at, at // 2, rows)
+
+    def reduce(target):
+        span = pl.ds(pl.multiple_of(target * pair, pair), pair)
+        part[span, :] = lax.dot_general(
+            left_ref[:, span],
+            right_ref[...],
+            (((0,), (0,)), ((), ())),
+            preferred_element_type=jnp.float32,
+        ).astype(jnp.bfloat16)
+
+    line_scatter(part, side, lane, out_ref, *sems, reduce, lambda step: None)
+
+
+def weight_sums(left, right, identity):
+    blocks = lax.axis_size("blk")
+    rows = blocks // 2
+    size, width = left.shape[1] // blocks, right.shape[1]
+    whole = pl.BlockSpec(memory_space=pltpu.VMEM)
+    return pl.pallas_call(
+        weight_kernel,
+        out_shape=jax.ShapeDtypeStruct((size, width), jnp.float32),
+        in_specs=[whole, whole],
+        out_specs=whole,
+        scratch_shapes=[
+            pltpu.VMEM((blocks * size, width), jnp.bfloat16),
+            pltpu.VMEM((rows, size, width), jnp.bfloat16),
+            pltpu.VMEM((rows + 1, size, width), jnp.bfloat16),
+            *lane_sems(rows),
+        ],
+        compiler_params=pltpu.CompilerParams(
+            collective_id=identity, has_side_effects=True, vmem_limit_bytes=VMEM_BYTES
+        ),
+        cost_estimate=cost_of(60),
+        name="weight_sums",
+    )(left, right)
+
+
+def weight_sums_wide(left, right):
+    term = jnp.einsum("tc,td->cd", left, right, preferred_element_type=jnp.float32)
+    return scatter_tokens(term)
+
+
 def body(tokens, w_qkv, w_out, gains, w_ffn, cotangent):
-    row_count = tokens.shape[0]
     groups = lax.axis_size("sp")
     heads_here = HEADS // groups
-    kv_here = KV_HEADS // groups
-    group_ratio = HEADS // KV_HEADS
-    query_width = HEADS * HEAD
-    score_scale = HEAD ** (-0.5)
     source = tokens.astype(jnp.float32)
     normed_in, inverse_in = norm_parts(source)
     act_in = (normed_in * gains[0]).astype(jnp.bfloat16)
-    act_block = lax.all_gather(act_in, "sp", axis=0, tiled=True)
-    group_cols = (group_ratio + 2) * HEAD * kv_here
-    sp_at = lax.axis_index("sp")
-    w_group = lax.dynamic_slice_in_dim(w_qkv, sp_at * group_cols, group_cols, 0)
-    projected = contract_last(act_block, w_group).astype(jnp.bfloat16)
+    act_block, projected = gather_project(act_in, w_qkv, 4)
     block_rows = projected.shape[0]
     attended_cols, attended, totals, kv_all = attend(projected, heads_here)
-    attended_low = attended_cols.reshape(block_rows, heads_here, HEAD)
-    attended_tokens = lax.all_to_all(
-        attended_low, "sp", split_axis=0, concat_axis=1, tiled=True
-    ).reshape(row_count, query_width)
-    attn = jnp.dot(attended_tokens, w_out, preferred_element_type=jnp.float32)
+    attn = exchange_project(attended_cols, w_out, 5)
     normed_attn, inverse_attn = norm_parts(attn)
     middle = source + normed_attn * gains[1]
     normed_mid, inverse_mid = norm_parts(middle)
@@ -895,17 +1092,14 @@
     grad_middle = grad_out + grad_norm_mid
     grad_attn_f, gain_grad1 = norm_back(grad_middle, normed_attn, inverse_attn, gains[1])
     grad_attn = grad_attn_f.astype(jnp.bfloat16)
-    grad_block = lax.all_gather(grad_attn, "sp", axis=0, tiled=True)
+    grad_block, grad_attended = gather_project(grad_attn, w_out, 6)
     out_term = jnp.einsum(
         "tc,td->cd", attended_cols, grad_block, preferred_element_type=jnp.float32
     )
     out_grad = lax.psum_scatter(
         out_term.astype(jnp.bfloat16), "blk", scatter_dimension=0, tiled=True
     ).astype(jnp.float32)
-    w_out_group = lax.dynamic_slice_in_dim(w_out, sp_at * heads_here * HEAD, heads_here * HEAD, 0)
-    grad_heads = (
-        contract_last(grad_block, w_out_group).astype(jnp.bfloat16).astype(jnp.float32)
-    ).reshape(block_rows, heads_here, HEAD)
+    grad_heads = grad_attended.astype(jnp.float32).reshape(block_rows, heads_here, HEAD)
     totals_rows = jnp.transpose(totals.reshape(heads_here, block_rows))
     scaled = (grad_heads / totals_rows[..., None]).astype(jnp.bfloat16)
     row_delta = (
@@ -917,21 +1111,19 @@
         jnp.transpose(row_delta).reshape(heads_here, 1, block_rows),
         kv_all,
     )
-    grad_proj_heads = grad_cols.reshape(block_rows, kv_here, group_ratio + 2, HEAD)
-    qkv_term = jnp.einsum("tc,td->cd", grad_cols, act_block, preferred_element_type=jnp.float32)
-    qkv_grad = lax.psum_scatter(
-        qkv_term.astype(jnp.bfloat16), "blk", scatter_dimension=0, tiled=True
-    ).astype(jnp.float32)
-    grad_proj_tokens = lax.all_to_all(grad_proj_heads, "sp", split_axis=0, concat_axis=1, tiled=True)
-    grad_projected = grad_proj_tokens.reshape(row_count, w_qkv.shape[0])
-    grad_act_in = jnp.dot(grad_projected, w_qkv, preferred_element_type=jnp.float32)
+    grad_act_in = exchange_project(grad_cols, w_qkv, 7)
+    qkv_grad = (
+        weight_sums_wide(grad_cols, act_block) if wide else weight_sums(grad_cols, act_block, 8)
+    )
     grad_source, gain_grad0 = norm_back(grad_act_in, normed_in, inverse_in, gains[0])
     tokens_grad = (grad_middle + grad_source).astype(jnp.bfloat16)
     gains_term = jnp.stack([gain_grad0, gain_grad1, gain_grad2, gain_grad3], axis=0)
     ffn_part = lax.psum_scatter(ffn_sums, "sp", scatter_dimension=0, tiled=True)
     ffn_grad = jnp.transpose(ffn_part[0].astype(jnp.float32), (1, 0, 2))
-    gains_part = lax.psum_scatter(gains_term, "sp", scatter_dimension=1, tiled=True)
-    gains_grad = lax.psum_scatter(gains_part, "blk", scatter_dimension=1, tiled=True)
+    gains_all = lax.psum(gains_term, ("blk", "sp"))
+    share = gains_all.shape[1] // (groups * lax.axis_size("blk"))
+    place = lax.axis_index("sp") * lax.axis_size("blk") + lax.axis_index("blk")
+    gains_grad = lax.dynamic_slice_in_dim(gains_all, place * share, share, 1)
     return (result.astype(jnp.bfloat16), tokens_grad, qkv_grad, out_grad, gains_grad, ffn_grad)
 
 

time: 824 us -> 616 us (0.75)
  waiting for transfers between devices: 327 us -> 2.37 us
  Pallas kernels: 343 us -> 507 us
  matrix products: 36.5 us -> 4.49 us
  local copies, waits for them, and re-layouts: 17.1 us -> 8.75 us
    pallas_call x0 -> x5, Pallas kernels: none -> 139 us  [the longest x1 57.5 us: weight_sums(): pl.pallas_call(weight_kernel, out_shape=jax.ShapeDtypeStruct((size, width...]
    reduce_scatter x1, waiting for transfers between devices: 120 us -> 1.67 us  [body(): ffn_part = lax.psum_scatter(ffn_sums, 'sp', scatter_dimension=0, tiled=True)]
    reduce_scatter x1 -> x0, waiting for transfers between devices: 97.2 us -> none  [body(): lax.psum_scatter(qkv_term.astype(jnp.bfloat16), 'blk', scatter_dimension=...]
    all_gather x2 -> x0, waiting for transfers between devices: 46.7 us -> none  [the longest x1 24.2 us: body(): act_block = lax.all_gather(act_in, 'sp', axis=0, tiled=True)]
    psum x0 -> x1, blocking collectives: none -> 42.3 us  [body(): gains_all = lax.psum(gains_term, ('blk', 'sp'))]
    reduce_scatter x1, waiting for transfers between devices: 38.2 us -> 0.01 us  [body(): lax.psum_scatter(out_term.astype(jnp.bfloat16), 'blk', scatter_dimension=...]
    unnamed x1 -> x0, blocking collectives: 33 us -> none
    dot_general x5 -> x0, matrix products: 32 us -> none  [the longest x2 11.5 us: contract_last(): lax.dot_general(left, right, (((1,), (1,)), ((), ())), preferred_element_...]
  transfers between devices with their start and end apart: 7 -> 2, of which waited for: 7 -> 1; matrix products, arithmetic and copies ran while one was open for 2% -> 2% of each run, Pallas kernels for 0% -> 26%
where the time goes in v4:
time: 616 us; the launch traced here: 607 us
  Pallas kernels  507 us (82%)
  blocking collectives  42.3 us (7%)
  other arithmetic  27.7 us (4%)
  between operations  14.7 us (2%)
  local copies, waits for them, and re-layouts  8.75 us (1%)
    pallas_call x1, Pallas kernels, ffn_forward(): pl.pallas_call(ffn_kernel, out_shape=(jax.ShapeDtypeStruct((size, width),...  122 us
    pallas_call x1, Pallas kernels, ffn_back(): pl.pallas_call(functools.partial(ffn_back_kernel, owners), out_shape=(jax...  119 us
    pallas_call x1, Pallas kernels, attend_back(): pl.pallas_call(functools.partial(attend_back_kernel, heads), out_shape=ja...  71 us
    pallas_call x1, Pallas kernels, weight_sums(): pl.pallas_call(weight_kernel, out_shape=jax.ShapeDtypeStruct((size, width...  57.5 us
    pallas_call x1, Pallas kernels, attend(): pl.pallas_call(functools.partial(attend_kernel, heads), out_shape=(jax.Sh...  56.1 us
    psum x1, blocking collectives, body(): gains_all = lax.psum(gains_term, ('blk', 'sp'))  42.3 us
    pallas_call x2, Pallas kernels, gather_project(): pl.pallas_call(gather_project_kernel, out_shape=(jax.ShapeDtypeStruct((4...  41.2 us
    pallas_call x2, Pallas kernels, exchange_project(): pl.pallas_call(exchange_project_kernel, out_shape=jax.ShapeDtypeStruct((s...  40.6 us
  transfers between devices with their start and end apart: 2, of which 1 were waited for; matrix products, arithmetic and copies ran while one was open for 2% of the time, Pallas kernels for 26%

profile of v4, /device:TPU:26, one launch (start us, length us, event | category | flops | bytes accessed | tf_op | source)
XLA Modules:
  0.0 606.9 jit_solution(12997009020122993826)
XLA Ops:
  7.2 0.0 reduce-scatter.3.cloned.1.call-start
  7.2 1.6 slice_reduce_fusion
  8.8 1.3 fusion.16
  10.1 0.0 copy-done.12
  10.1 0.5 copy-done.21
  10.7 2.1 fusion.9.x_ref
  12.7 21.0 %gather_project.2 = (bf16[512,2304]{1,0:T(8,128)(2,1)}, bf16[512,1024]{1,0:T(8,128)(2,1)}) custom-call(bf16[128,2304]{1,0:T(8,128)(2,1)} %fusion.9.x_ref, bf16[4096,2304]{1,0:T(8,128)(2,1)} %w_ref.7), custom_call_target="tpu_custom_call" | custom-call | flops 17999998976 | bytes 54000000 | tf_op jit(solution)/shard_map/gather_project/pallas_call | solution.py:933
  33.7 56.1 %attend.1 = (bf16[512,512]{1,0:T(8,128)(2,1)}, f32[512,512]{1,0:T(8,128)}, f32[2,1,512]{2,1,0:T(1,128)}, bf16[8,512,512]{2,1,0:T(8,128)(2,1)}) custom-call(bf16[512,1024]{1,0:T(8,128)(2,1)} %get-tuple-element.18.x_ref), custom_call_target="tpu_custom_call" | custom-call | flops 49999998976 | bytes 150000000 | tf_op jit(solution)/shard_map/attend/pallas_call | solution.py:204
  89.9 0.0 copy-start.2
  89.9 11.2 %exchange_project.2 = f32[128,2304]{1,0:T(8,128)} custom-call(bf16[512,512]{1,0:T(8,128)(2,1)} %get-tuple-element.19.x_ref, bf16[2048,2304]{1,0:T(8,128)(2,1)} %w_ref.6), custom_call_target="tpu_custom_call" | custom-call | flops 16000000000 | bytes 48000000 | tf_op jit(solution)/shard_map/exchange_project/pallas_call | solution.py:998
  101.1 0.0 copy-start
  101.1 1.5 multiply_reduce_fusion.6
  102.6 0.0 copy-done.14
  102.6 0.0 copy-done.2
  102.7 0.0 copy-done
  102.7 0.4 multiply_reduce_fusion.5
  103.1 0.1 copy-done.25
  103.2 0.0 copy-done.16
  103.2 1.0 multiply_convert_fusion.1.act_ref
  104.2 121.6 %ffn_forward.1 = (f32[128,2304]{1,0:T(8,128)}, bf16[1024,2304]{1,0:T(8,128)(2,1)}) custom-call(bf16[128,2304]{1,0:T(8,128)(2,1)} %multiply_convert_fusion.1.act_ref, bf16[3,1152,2304]{2,1,0:T(8,128)(2,1)} %bitcast.21), custom_call_target="tpu_custom_call" | custom-call | flops 115000000512 | bytes 345000000 | tf_op jit(solution)/shard_map/ffn_forward/pallas_call | solution.py:645
  225.8 1.5 multiply_reduce_fusion.4
  227.4 0.1 copy-done.6
  227.4 1.0 fusion.17
  228.4 1.4 fusion.8
  229.9 118.5 %ffn_back.1 = (f32[128,2304]{1,0:T(8,128)}, bf16[4,3,288,2304]{3,2,1,0:T(8,128)(2,1)}) custom-call(bf16[128,2304]{1,0:T(8,128)(2,1)} %get-tuple-element.45.grad_ref, bf16[1024,2304]{1,0:T(8,128)(2,1)} %get-tuple-element.21.acts_ref, bf16[3,1152,2304]{2,1,0:T(8,128)(2,1)} %bitcast.22), custom_call_target="tpu_custom_call" | custom-call | flops 115000000512 | bytes 345000000 | tf_op jit(solution)/shard_map/ffn_back/pallas_call | solution.py:791
  348.4 0.0 copy-start.15
  348.4 0.0 copy-start.26
  348.4 1.8 multiply_reduce_fusion
  350.2 0.1 copy-done.8
  350.4 0.7 multiply_reduce_fusion.1
  351.1 1.0 copy-done.4
  352.1 1.1 multiply_convert_fusion.x_ref
  353.2 20.2 %gather_project.3 = (bf16[512,2304]{1,0:T(8,128)(2,1)}, bf16[512,512]{1,0:T(8,128)(2,1)}) custom-call(bf16[128,2304]{1,0:T(8,128)(2,1)} %multiply_convert_fusion.x_ref, bf16[2048,2304]{1,0:T(8,128)(2,1)} %w_ref.6), custom_call_target="tpu_custom_call" | custom-call | flops 17999998976 | bytes 54000000 | tf_op jit(solution)/shard_map/gather_project/pallas_call | solution.py:933
  373.4 4.5 convolution_convert_fusion
  377.9 0.0 reduce-scatter.3.cloned.1.call-update
  377.9 0.0 reduce-scatter.5.cloned.1.call-start
  378.0 0.7 reduce-scatter.5.cloned.1.call-update
  378.7 0.1 copy.13
  378.9 0.6 div.46
  379.5 0.1 copy.16
  379.6 1.1 copy-done.10
  380.7 0.1 copy-done.11
  380.8 1.1 convert_multiply_fusion.4
  382.0 0.7 mul.240
  382.6 0.6 reduce_sum.126
  383.2 0.1 copy.14
  383.4 0.6 reshape.75.delta_ref
  384.0 71.0 %attend_back.1.x_ref.left_ref = bf16[512,1024]{1,0:T(8,128)(2,1)} custom-call(bf16[512,1024]{1,0:T(8,128)(2,1)} %get-tuple-element.18.x_ref, bf16[512,512]{1,0:T(8,128)(2,1)} %get-tuple-element.48.scaled_ref, f32[2,1,512]{2,1,0:T(1,128)} %reshape.75.delta_ref, bf16[8,512,512]{2,1,0:T(8,128)(2,1)} %get-tuple-element.26.kv_ref), custom_call_target="tpu_custom_call" | custom-call | flops 49999998976 | bytes 150000000 | tf_op jit(solution)/shard_map/attend_back/pallas_call | solution.py:387
  455.0 0.0 copy-start.19
  455.0 57.5 %weight_sums.1 = f32[128,2304]{1,0:T(8,128)} custom-call(bf16[512,1024]{1,0:T(8,128)(2,1)} %attend_back.1.x_ref.left_ref, bf16[512,2304]{1,0:T(8,128)(2,1)} %get-tuple-element.27.right_ref), custom_call_target="tpu_custom_call" | custom-call | flops 60000002048 | bytes 180000000 | tf_op jit(solution)/shard_map/weight_sums/pallas_call | solution.py:1042
  512.5 0.0 copy-done.19
  512.6 0.0 copy-start.3
  512.6 29.4 %exchange_project.3 = f32[128,2304]{1,0:T(8,128)} custom-call(bf16[512,1024]{1,0:T(8,128)(2,1)} %attend_back.1.x_ref.left_ref, bf16[4096,2304]{1,0:T(8,128)(2,1)} %w_ref.7), custom_call_target="tpu_custom_call" | custom-call | flops 16000000000 | bytes 48000000 | tf_op jit(solution)/shard_map/exchange_project/pallas_call | solution.py:998
  542.1 0.0 copy-start.5
  542.1 1.8 fusion.15
  543.9 42.3 %psum.7 = f32[4,2304]{1,0:T(4,128)S(1)} all-reduce(f32[4,2304]{1,0:T(4,128)S(1)} %pad_maximum_fusion), channel_id=1, replica_groups=mesh['blk'=8,'sp'=4] {'blk','sp'}, use_global_device_ids=true, to_apply=%region_14.0 | all-reduce | flops 9216 | bytes 73728 | tf_op jit(solution)/shard_map/psum | solution.py:1123
  586.2 0.6 constant_dynamic-slice_fusion
  586.9 0.0 copy-done.5
  586.9 2.5 fusion.14
  589.4 1.8 convert_element_type.52
  591.2 1.7 reduce-scatter.5.cloned.1.call-done
  592.9 6.0 convert_bitcast_fusion
  598.9 0.0 copy-done.9
  598.9 1.0 copy.21
  (50 shorter events, 0.2 us)
Async XLA Ops:
  7.2 582.2 %reduce-scatter.3.cloned.1.call-start = ((), (), s32[]{:S(2)}) async-start(), calls=%async_computation.2 | async-start | bytes 2654208 | tf_op jit(solution)/shard_map/reduce_scatter | solution.py:1099
  8.8 1.3 copy-start.12
  8.8 93.8 %copy-start.14 = (f32[2304]{0:T(1024)}, f32[2304]{0:T(1024)S(1)}, u32[]{:S(2)}) copy-start(f32[2304]{0:T(1024)S(1)} %get-tuple-element.39) | copy-start | bytes 27652
  8.8 94.3 %copy-start.16 = (f32[2304]{0:T(1024)}, f32[2304]{0:T(1024)S(1)}, u32[]{:S(2)}) copy-start(f32[2304]{0:T(1024)S(1)} %get-tuple-element.41) | copy-start | bytes 27652
  10.1 0.5 copy-start.21
  89.9 12.8 %copy-start.2 = (bf16[128,2304]{1,0:T(8,128)(2,1)S(1)}, bf16[128,2304]{1,0:T(8,128)(2,1)}, u32[]{:S(2)}) copy-start(bf16[128,2304]{1,0:T(8,128)(2,1)} %param.6) | copy-start | bytes 1769476
  101.1 1.6 copy-start
  102.6 0.5 copy-start.25
  103.2 1.0 copy-start.23
  104.2 123.2 %copy-start.7 = (bf16[128,2304]{1,0:T(8,128)(2,1)S(1)}, bf16[128,2304]{1,0:T(8,128)(2,1)}, u32[]{:S(2)}) copy-start(bf16[128,2304]{1,0:T(8,128)(2,1)} %param.11) | copy-start | bytes 1769476
  104.2 123.2 %copy-start.18 = (f32[2304]{0:T(1024)S(1)}, f32[2304]{0:T(1024)}, u32[]{:S(2)}) copy-start(f32[2304]{0:T(1024)} %get-tuple-element.38) | copy-start | bytes 27652
  225.8 1.6 copy-start.6
  229.8 118.5 %copy-start.17 = (f32[2304]{0:T(1024)S(1)}, f32[2304]{0:T(1024)}, u32[]{:S(2)}) copy-start(f32[2304]{0:T(1024)} %copy-done.16) | copy-start | bytes 27652
  229.9 118.5 %copy-start.24 = (f32[128]{0:T(128)S(1)}, f32[128]{0:T(128)}, u32[]{:S(2)}) copy-start(f32[128]{0:T(128)} %copy-done.23) | copy-start | bytes 1540
  348.4 1.8 copy-start.1
  348.4 2.0 copy-start.8
  348.4 2.0 copy-start.15
  348.4 2.0 copy-start.26
  351.1 1.0 copy-start.4
  353.2 20.2 %copy-start.27 = (bf16[512,512]{1,0:T(8,128)(2,1)S(1)}, bf16[512,512]{1,0:T(8,128)(2,1)}, u32[]{:S(2)}) copy-start(bf16[512,512]{1,0:T(8,128)(2,1)} %get-tuple-element.19.x_ref) | copy-start | bytes 1572868
  377.9 214.9 %reduce-scatter.5.cloned.1.call-start = ((), (), s32[]{:S(2)}) async-start(), calls=%async_computation.3 | async-start | bytes 19906560 | tf_op jit(solution)/shard_map/reduce_scatter | solution.py:1121
  378.0 0.7 copy-start.20
  379.5 1.2 copy-start.10
  379.5 1.3 copy-start.11
  455.0 57.5 %copy-start.19 = (f32[2304]{0:T(1024)S(1)}, f32[2304]{0:T(1024)}, u32[]{:S(2)}) copy-start(f32[2304]{0:T(1024)} %get-tuple-element.36) | copy-start | bytes 27652
  512.6 29.5 %copy-start.3 = (bf16[128,2304]{1,0:T(8,128)(2,1)S(1)}, bf16[128,2304]{1,0:T(8,128)(2,1)}, u32[]{:S(2)}) copy-start(bf16[128,2304]{1,0:T(8,128)(2,1)} %param.6) | copy-start | bytes 1769476
  512.6 29.5 %copy-start.13 = (f32[2304]{0:T(1024)S(1)}, f32[2304]{0:T(1024)}, u32[]{:S(2)}) copy-start(f32[2304]{0:T(1024)} %copy-done.12) | copy-start | bytes 27652
  512.6 29.5 %copy-start.22 = (f32[128]{0:T(128)S(1)}, f32[128]{0:T(128)}, u32[]{:S(2)}) copy-start(f32[128]{0:T(128)} %copy-done.21) | copy-start | bytes 1540
  542.1 44.8 %copy-start.5 = (f32[128,2304]{1,0:T(8,128)S(1)}, f32[128,2304]{1,0:T(8,128)}, u32[]{:S(2)}) copy-start(f32[128,2304]{1,0:T(8,128)} %copy-done.4) | copy-start | bytes 3538948
  591.2 7.7 %copy-start.9 = (f32[128,2304]{1,0:T(8,128)S(1)}, f32[128,2304]{1,0:T(8,128)}, u32[]{:S(2)}) copy-start(f32[128,2304]{1,0:T(8,128)} %weight_sums.1) | copy-start | bytes 3538948
Sparse Core Ops, SparseCore 0:
  378.1 79.9 reduce-scatter.2
  460.6 132.1 reduce-scatter.4

commit v5 on v4

--- a/solution.py
+++ b/solution.py
@@ -1016,51 +1016,237 @@
     )(columns, weights)
 
 
-def weight_kernel(left_ref, right_ref, out_ref, part, side, lane, *sems):
+def finish_kernel(
+    cols_ref,
+    act_ref,
+    att_ref,
+    grad_ref,
+    w_ref,
+    tokens_ref,
+    middle_ref,
+    gain_ref,
+    rows_ref,
+    sum_ref,
+    tokens_grad_ref,
+    gains_ref,
+    w,
+    got,
+    grad_in,
+    part,
+    side,
+    lane,
+    mine,
+    from_sp,
+    from_side,
+    from_line,
+    w_done,
+    own_done,
+    swap_sent,
+    swap_landed,
+    sp_sent,
+    sp_landed,
+    gain_side,
+    line_sent,
+    line_landed,
+    *sems,
+):
     at = lax.axis_index("blk")
+    me = lax.axis_index("sp")
     rows = lax.axis_size("blk") // 2
-    pair = 2 * out_ref.shape[0]
-    greet(at, at // 2, rows)
+    line, column = at // 2, at % 2
+    partner = at + 1 - 2 * column
+    block = sum_ref.shape[0]
+    size = tokens_ref.shape[0]
+    units = cols_ref.shape[1]
+    extra = block - size
+
+    barrier = pltpu.get_barrier_semaphore()
+    for step in range(1, 4):
+        pl.semaphore_signal(
+            barrier, inc=1, device_id={"sp": (me + step) % 4}, device_id_type=pl.DeviceIdType.MESH
+        )
+
+    def line_peer(step):
+        return 2 * ((line + step) % rows) + column
+
+    for peer in [partner] + [line_peer(step) for step in range(1, rows)]:
+        pl.semaphore_signal(
+            barrier, inc=1, device_id={"blk": peer}, device_id_type=pl.DeviceIdType.MESH
+        )
+
+    def load(member):
+        span = pl.ds(pl.multiple_of(member * units, units), units)
+        return pltpu.make_async_copy(w_ref.at[span, :], w.at[span, :], w_done.at[member])
+
+    def rows_of(member):
+        return cols_ref.at[pl.ds(pl.multiple_of(member * size, size), size), :]
+
+    def swap(step):
+        peer = (me + step) % 4
+        return push_sp(
+            rows_of(peer), got.at[4 - step], swap_sent.at[step], swap_landed.at[4 - step], peer
+        )
+
+    for step in range(4):
+        load((me + step) % 4).start()
+    keep = pltpu.make_async_copy(rows_of(me), got.at[0], own_done)
+    keep.start()
+    pl.semaphore_wait(barrier, 3 + rows)
+    for step in (2, 1, 3):
+        swap(step).start()
+    keep.wait()
+
+    def sp_gains(step):
+        return push_sp(
+            mine, from_sp.at[4 - step], sp_sent.at[step], sp_landed.at[4 - step], (me + step) % 4
+        )
+
+    def side_gains():
+        return push(from_sp.at[0], from_side, gain_side.at[0], gain_side.at[1], partner)
+
+    def line_gains(step):
+        return push(
+            from_line.at[0],
+            from_line.at[rows - step],
+            line_sent.at[step],
+            line_landed.at[rows - step],
+            line_peer(step),
+        )
 
     def reduce(target):
-        span = pl.ds(pl.multiple_of(target * pair, pair), pair)
-        part[span, :] = lax.dot_general(
-            left_ref[:, span],
-            right_ref[...],
-            (((0,), (0,)), ((), ())),
-            preferred_element_type=jnp.float32,
+        dims = (((0,), (0,)), ((), ()))
+        wide_columns = pl.ds(pl.multiple_of(target * 2 * size, 2 * size), 2 * size)
+        term = lax.dot_general(
+            cols_ref[:, wide_columns], act_ref[...], dims, preferred_element_type=jnp.float32
         ).astype(jnp.bfloat16)
-
-    line_scatter(part, side, lane, out_ref, *sems, reduce, lambda step: None)
-
-
-def weight_sums(left, right, identity):
+        columns = pl.ds(pl.multiple_of(target * 2 * extra, 2 * extra), 2 * extra)
+        more = lax.dot_general(
+            att_ref[:, columns], grad_ref[...], dims, preferred_element_type=jnp.float32
+        ).astype(jnp.bfloat16)
+        for half in range(2):
+            start = pl.multiple_of((2 * target + half) * block, block)
+            part[pl.ds(start, size), :] = term[half * size : (half + 1) * size]
+            start = pl.multiple_of((2 * target + half) * block + size, extra)
+            part[pl.ds(start, extra), :] = more[half * extra : (half + 1) * extra]
+
+    def inputs_back():
+        for step in (0, 1, 3, 2):
+            member = (me + step) % 4
+            load(member).wait()
+            if step > 0:
+                swap(4 - step).wait_recv()
+            span = pl.ds(pl.multiple_of(member * units, units), units)
+            term = jnp.dot(got[step], w[span, :], preferred_element_type=jnp.float32)
+            if step == 0:
+                grad_in[...] = term
+            else:
+                grad_in[...] += term
+        normed, inverse = norm_parts(tokens_ref[...].astype(jnp.float32))
+        grad_v, gain_row = norm_back(grad_in[...], normed, inverse, gain_ref[...])
+        tokens_grad_ref[...] = (middle_ref[...] + grad_v).astype(jnp.bfloat16)
+        mine[...] = rows_ref[...]
+        mine[0:1, :] = gain_row[None, :]
+        for step in range(1, 4):
+            sp_gains(step).start()
+
+    def fill(step):
+        pl.when(step == 0)(inputs_back)
+
+        @pl.when(step == 1)
+        def _():
+            total = mine[...]
+            for other in range(1, 4):
+                sp_gains(4 - other).wait_recv()
+                total = total + from_sp[other]
+            from_sp[0] = total
+            side_gains().start()
+
+        @pl.when(step == 2)
+        def _():
+            side_gains().wait_recv()
+            from_line[0] = from_sp[0] + from_side[...]
+            for other in range(1, rows):
+                line_gains(other).start()
+
+    line_scatter(part, side, lane, sum_ref, *sems, reduce, fill)
+    total = from_line[0]
+    for other in range(1, rows):
+        line_gains(rows - other).wait_recv()
+        total = total + from_line[other]
+    gains_ref[...] = total
+    for step in (1, 2, 3):
+        swap(step).wait_send()
+        sp_gains(step).wait_send()
+    side_gains().wait_send()
+    for step in range(1, rows):
+        line_gains(step).wait_send()
+
+
+def finish(cols, act_block, attended, grad_block, w_qkv, tokens, grad_middle, gain, gain_rows):
     blocks = lax.axis_size("blk")
     rows = blocks // 2
-    size, width = left.shape[1] // blocks, right.shape[1]
+    size, width = tokens.shape
+    block = (cols.shape[1] + attended.shape[1]) // blocks
     whole = pl.BlockSpec(memory_space=pltpu.VMEM)
-    return pl.pallas_call(
-        weight_kernel,
-        out_shape=jax.ShapeDtypeStruct((size, width), jnp.float32),
-        in_specs=[whole, whole],
-        out_specs=whole,
+    dma = pltpu.SemaphoreType.DMA
+    small = gain_rows.shape
+    total, tokens_grad, gains_all = pl.pallas_call(
+        finish_kernel,
+        out_shape=(
+            jax.ShapeDtypeStruct((block, width), jnp.float32),
+            jax.ShapeDtypeStruct((size, width), jnp.bfloat16),
+            jax.ShapeDtypeStruct(small, jnp.float32),
+        ),
+        in_specs=[whole] * 4 + [pl.BlockSpec(memory_space=pl.ANY)] + [whole] * 4,
+        out_specs=(whole,) * 3,
         scratch_shapes=[
-            pltpu.VMEM((blocks * size, width), jnp.bfloat16),
-            pltpu.VMEM((rows, size, width), jnp.bfloat16),
-            pltpu.VMEM((rows + 1, size, width), jnp.bfloat16),
+            pltpu.VMEM(w_qkv.shape, jnp.bfloat16),
+            pltpu.VMEM((4, size, cols.shape[1]), jnp.bfloat16),
+            pltpu.VMEM((size, width), jnp.float32),
+            pltpu.VMEM((blocks * block, width), jnp.bfloat16),
+            pltpu.VMEM((rows, block, width), jnp.bfloat16),
+            pltpu.VMEM((rows + 1, block, width), jnp.bfloat16),
+            pltpu.VMEM(small, jnp.float32),
+            pltpu.VMEM((4, *small), jnp.float32),
+            pltpu.VMEM(small, jnp.float32),
+            pltpu.VMEM((rows, *small), jnp.float32),
+            dma((4,)),
+            dma,
+            dma((4,)),
+            dma((4,)),
+            dma((4,)),
+            dma((4,)),
+            dma((2,)),
+            dma((rows,)),
+            dma((rows,)),
             *lane_sems(rows),
         ],
         compiler_params=pltpu.CompilerParams(
-            collective_id=identity, has_side_effects=True, vmem_limit_bytes=VMEM_BYTES
+            collective_id=8, has_side_effects=True, vmem_limit_bytes=VMEM_BYTES
         ),
-        cost_estimate=cost_of(60),
-        name="weight_sums",
-    )(left, right)
+        cost_estimate=cost_of(85),
+        name="finish",
+    )(cols, act_block, attended, grad_block, w_qkv, tokens, grad_middle, gain, gain_rows)
+    shared = cols.shape[1] // blocks
+    return (total[:shared], total[shared:], tokens_grad, gains_all)
 
 
 def weight_sums_wide(left, right):
     term = jnp.einsum("tc,td->cd", left, right, preferred_element_type=jnp.float32)
     return scatter_tokens(term)
+
+
+def finish_wide(cols, act_block, attended, grad_block, w_qkv, tokens, grad_middle, gain, gain_rows):
+    grad_act_in = exchange_project(cols, w_qkv, 7)
+    normed, inverse = norm_parts(tokens.astype(jnp.float32))
+    grad_v, gain_row = norm_back(grad_act_in, normed, inverse, gain)
+    gains_all = lax.psum(jnp.concatenate([gain_row[None], gain_rows[1:]]), ("blk", "sp"))
+    return (
+        weight_sums_wide(cols, act_block),
+        weight_sums_wide(attended, grad_block),
+        (grad_middle + grad_v).astype(jnp.bfloat16),
+        gains_all,
+    )
 
 
 def body(tokens, w_qkv, w_out, gains, w_ffn, cotangent):
@@ -1093,12 +1279,6 @@
     grad_attn_f, gain_grad1 = norm_back(grad_middle, normed_attn, inverse_attn, gains[1])
     grad_attn = grad_attn_f.astype(jnp.bfloat16)
     grad_block, grad_attended = gather_project(grad_attn, w_out, 6)
-    out_term = jnp.einsum(
-        "tc,td->cd", attended_cols, grad_block, preferred_element_type=jnp.float32
-    )
-    out_grad = lax.psum_scatter(
-        out_term.astype(jnp.bfloat16), "blk", scatter_dimension=0, tiled=True
-    ).astype(jnp.float32)
     grad_heads = grad_attended.astype(jnp.float32).reshape(block_rows, heads_here, HEAD)
     totals_rows = jnp.transpose(totals.reshape(heads_here, block_rows))
     scaled = (grad_heads / totals_rows[..., None]).astype(jnp.bfloat16)
@@ -1111,19 +1291,26 @@
         jnp.transpose(row_delta).reshape(heads_here, 1, block_rows),
         kv_all,
     )
-    grad_act_in = exchange_project(grad_cols, w_qkv, 7)
-    qkv_grad = (
-        weight_sums_wide(grad_cols, act_block) if wide else weight_sums(grad_cols, act_block, 8)
-    )
-    grad_source, gain_grad0 = norm_back(grad_act_in, normed_in, inverse_in, gains[0])
-    tokens_grad = (grad_middle + grad_source).astype(jnp.bfloat16)
-    gains_term = jnp.stack([gain_grad0, gain_grad1, gain_grad2, gain_grad3], axis=0)
+    gain_rows = jnp.stack(
+        [jnp.zeros_like(gain_grad1), gain_grad1, gain_grad2, gain_grad3]
+        + [jnp.zeros_like(gain_grad1)] * 4
+    )
+    qkv_grad, out_grad, tokens_grad, gains_all = (finish_wide if wide else finish)(
+        grad_cols,
+        act_block,
+        attended_cols,
+        grad_block,
+        w_qkv,
+        tokens,
+        grad_middle,
+        gains[0][None],
+        gain_rows,
+    )
     ffn_part = lax.psum_scatter(ffn_sums, "sp", scatter_dimension=0, tiled=True)
     ffn_grad = jnp.transpose(ffn_part[0].astype(jnp.float32), (1, 0, 2))
-    gains_all = lax.psum(gains_term, ("blk", "sp"))
     share = gains_all.shape[1] // (groups * lax.axis_size("blk"))
     place = lax.axis_index("sp") * lax.axis_size("blk") + lax.axis_index("blk")
-    gains_grad = lax.dynamic_slice_in_dim(gains_all, place * share, share, 1)
+    gains_grad = lax.dynamic_slice_in_dim(gains_all[:4], place * share, share, 1)
     return (result.astype(jnp.bfloat16), tokens_grad, qkv_grad, out_grad, gains_grad, ffn_grad)
 
 

time: 616 us -> 581 us (0.943)
  blocking collectives: 42.3 us -> 0 us
  Pallas kernels: 507 us -> 518 us
  local copies, waits for them, and re-layouts: 8.75 us -> 16.4 us
  other arithmetic: 27.7 us -> 21.4 us
    pallas_call x1, Pallas kernels: 57.5 us -> 116 us  [finish(): pl.pallas_call(finish_kernel, out_shape=(jax.ShapeDtypeStruct((block, wid...]
    psum x1 -> x0, blocking collectives: 42.3 us -> none  [body(): gains_all = lax.psum(gains_term, ('blk', 'sp'))]
    pallas_call x2 -> x1, Pallas kernels: 40.6 us -> 11.2 us  [exchange_project(): pl.pallas_call(exchange_project_kernel, out_shape=jax.ShapeDtypeStruct((s...]
    pallas_call x1, Pallas kernels: 71 us -> 54.4 us  [attend_back(): pl.pallas_call(functools.partial(attend_back_kernel, heads), out_shape=ja...]
  transfers between devices with their start and end apart: 2 -> 1, of which waited for: 1 -> 0; matrix products, arithmetic and copies ran while one was open for 2% -> 3% of each run, Pallas kernels for 26% -> 33%
where the time goes in v5:
time: 581 us; the launch traced here: 571 us
  Pallas kernels  518 us (89%)
  other arithmetic  21.4 us (4%)
  local copies, waits for them, and re-layouts  16.4 us (3%)
  between operations  14.5 us (2%)
    pallas_call x1, Pallas kernels, ffn_forward(): pl.pallas_call(ffn_kernel, out_shape=(jax.ShapeDtypeStruct((size, width),...  122 us
    pallas_call x1, Pallas kernels, ffn_back(): pl.pallas_call(functools.partial(ffn_back_kernel, owners), out_shape=(jax...  118 us
    pallas_call x1, Pallas kernels, finish(): pl.pallas_call(finish_kernel, out_shape=(jax.ShapeDtypeStruct((block, wid...  116 us
    pallas_call x1, Pallas kernels, attend(): pl.pallas_call(functools.partial(attend_kernel, heads), out_shape=(jax.Sh...  56.1 us
    pallas_call x1, Pallas kernels, attend_back(): pl.pallas_call(functools.partial(attend_back_kernel, heads), out_shape=ja...  54.4 us
    pallas_call x2, Pallas kernels, gather_project(): pl.pallas_call(gather_project_kernel, out_shape=(jax.ShapeDtypeStruct((4...  41.2 us
  transfers between devices with their start and end apart: 1, of which 0 were waited for; matrix products, arithmetic and copies ran while one was open for 3% of the time, Pallas kernels for 33%

profile of v5, /device:TPU:26, one launch (start us, length us, event | category | flops | bytes accessed | tf_op | source)
XLA Modules:
  0.0 570.9 jit_solution(3369597115675000801)
XLA Ops:
  7.2 0.0 reduce-scatter.2.cloned.1.call-start
  7.2 2.1 slice_reduce_fusion
  9.4 1.3 fusion.5
  10.6 2.1 fusion.7.x_ref
  12.7 21.0 %gather_project.2 = (bf16[512,2304]{1,0:T(8,128)(2,1)}, bf16[512,1024]{1,0:T(8,128)(2,1)}) custom-call(bf16[128,2304]{1,0:T(8,128)(2,1)} %fusion.7.x_ref, bf16[4096,2304]{1,0:T(8,128)(2,1)} %w_ref.7), custom_call_target="tpu_custom_call" | custom-call | flops 17999998976 | bytes 54000000 | tf_op jit(solution)/shard_map/gather_project/pallas_call | solution.py:933
  33.7 56.1 %attend.1 = (bf16[512,512]{1,0:T(8,128)(2,1)}, f32[512,512]{1,0:T(8,128)}, f32[2,1,512]{2,1,0:T(1,128)}, bf16[8,512,512]{2,1,0:T(8,128)(2,1)}) custom-call(bf16[512,1024]{1,0:T(8,128)(2,1)} %get-tuple-element.21.x_ref), custom_call_target="tpu_custom_call" | custom-call | flops 49999998976 | bytes 150000000 | tf_op jit(solution)/shard_map/attend/pallas_call | solution.py:204
  89.9 0.0 copy-start.4
  89.9 11.2 %exchange_project.1 = f32[128,2304]{1,0:T(8,128)} custom-call(bf16[512,512]{1,0:T(8,128)(2,1)} %get-tuple-element.22.x_ref.att_ref, bf16[2048,2304]{1,0:T(8,128)(2,1)} %w_ref.6), custom_call_target="tpu_custom_call" | custom-call | flops 16000000000 | bytes 48000000 | tf_op jit(solution)/shard_map/exchange_project/pallas_call | solution.py:998
  101.1 0.0 copy-start
  101.1 1.5 multiply_reduce_fusion.6
  102.6 0.0 copy-done.9
  102.6 0.0 copy-done.4
  102.6 0.0 copy-done
  102.7 0.4 multiply_reduce_fusion.5
  103.1 0.1 copy-done.18
  103.2 0.0 copy-done.11
  103.2 1.0 multiply_convert_fusion.1.act_ref
  104.1 0.0 copy-done.16
  104.2 121.6 %ffn_forward.1 = (f32[128,2304]{1,0:T(8,128)}, bf16[1024,2304]{1,0:T(8,128)(2,1)}) custom-call(bf16[128,2304]{1,0:T(8,128)(2,1)} %multiply_convert_fusion.1.act_ref, bf16[3,1152,2304]{2,1,0:T(8,128)(2,1)} %bitcast.19), custom_call_target="tpu_custom_call" | custom-call | flops 115000000512 | bytes 345000000 | tf_op jit(solution)/shard_map/ffn_forward/pallas_call | solution.py:645
  225.8 0.0 copy-start.2
  225.8 1.5 multiply_reduce_fusion.4
  227.4 0.0 copy-done.3
  227.4 0.0 copy-done.13
  227.4 0.1 copy-done.2
  227.4 0.5 fusion.8
  227.9 1.4 fusion.4
  229.3 118.5 %ffn_back.1 = (f32[128,2304]{1,0:T(8,128)}, bf16[4,3,288,2304]{3,2,1,0:T(8,128)(2,1)}) custom-call(bf16[128,2304]{1,0:T(8,128)(2,1)} %get-tuple-element.49.grad_ref, bf16[1024,2304]{1,0:T(8,128)(2,1)} %get-tuple-element.24.acts_ref, bf16[3,1152,2304]{2,1,0:T(8,128)(2,1)} %bitcast.20), custom_call_target="tpu_custom_call" | custom-call | flops 115000000512 | bytes 345000000 | tf_op jit(solution)/shard_map/ffn_back/pallas_call | solution.py:791
  347.8 0.0 copy-start.15
  347.8 0.0 reduce-scatter.2.cloned.1.call-update
  347.9 0.6 copy-done.15
  348.5 0.1 copy.13
  348.7 0.6 div.43
  349.3 0.0 copy-start.5
  349.3 0.0 copy-start.12
  349.3 0.0 copy-start.17
  349.3 1.0 copy.16
  350.3 0.6 copy-done.5
  350.9 0.0 copy-done.12
  350.9 0.0 copy-done.17
  350.9 0.0 copy-start.19
  350.9 0.4 multiply_reduce_fusion
  351.3 0.8 copy-done.1
  352.2 0.0 copy-done.10
  352.2 0.0 copy-done.19
  352.2 0.7 multiply_reduce_fusion.1
  352.9 1.0 copy-done.6
  353.9 1.1 multiply_convert_fusion.x_ref
  355.0 20.2 %gather_project.3 = (bf16[512,2304]{1,0:T(8,128)(2,1)}, bf16[512,512]{1,0:T(8,128)(2,1)}) custom-call(bf16[128,2304]{1,0:T(8,128)(2,1)} %multiply_convert_fusion.x_ref, bf16[2048,2304]{1,0:T(8,128)(2,1)} %w_ref.6), custom_call_target="tpu_custom_call" | custom-call | flops 17999998976 | bytes 54000000 | tf_op jit(solution)/shard_map/gather_project/pallas_call | solution.py:933
  375.3 0.0 copy-done.7
  375.3 2.8 convert_multiply_fusion.4
  378.1 1.9 mul.214
  380.0 0.6 reduce_sum.108
  380.6 0.1 copy.14
  380.7 0.6 reshape.71.delta_ref
  381.4 0.7 stack.19.rows_ref
  382.1 54.4 %attend_back.1.cols_ref = bf16[512,1024]{1,0:T(8,128)(2,1)} custom-call(bf16[512,1024]{1,0:T(8,128)(2,1)} %get-tuple-element.21.x_ref, bf16[512,512]{1,0:T(8,128)(2,1)} %get-tuple-element.52.scaled_ref, f32[2,1,512]{2,1,0:T(1,128)} %reshape.71.delta_ref, bf16[8,512,512]{2,1,0:T(8,128)(2,1)} %get-tuple-element.29.kv_ref), custom_call_target="tpu_custom_call" | custom-call | flops 49999998976 | bytes 150000000 | tf_op jit(solution)/shard_map/attend_back/pallas_call | solution.py:387
  436.4 115.5 %finish.1 = (f32[192,2304]{1,0:T(8,128)}, bf16[128,2304]{1,0:T(8,128)(2,1)}, f32[8,2304]{1,0:T(8,128)}) custom-call(bf16[512,1024]{1,0:T(8,128)(2,1)} %attend_back.1.cols_ref, bf16[512,2304]{1,0:T(8,128)(2,1)} %get-tuple-element.30.act_ref, bf16[512,512]{1,0:T(8,128)(2,1)} %get-tuple-element.22.x_ref.att_ref, bf16[512,2304]{1,0:T(8,128)(2,1)} %get-tuple-element.31.grad_ref, ...), custom_call_target="tpu_custom_call" | custom-call | flops 85000003584 | bytes 255000000 | tf_op jit(solution)/shard_map/finish/pallas_call | solution.py:1193
  552.0 2.4 slice.29
  554.3 1.9 slice.30
  556.3 0.0 copy-done.14
  556.3 0.7 constant_dynamic-slice_fusion
  556.9 6.1 %convert_bitcast_fusion = f32[288,3,2304]{2,0,1:T(8,128)} fusion(bf16[1,3,288,2304]{3,2,1,0:T(8,128)(2,1)} %reduce-scatter.2.cloned.1.call-done), kind=kLoop, calls=%fused_computation | loop fusion | flops 1990656 | bytes 11943936 | tf_op jit(solution)/shard_map/transpose | solution.py:1310
  563.0 0.0 copy-done.8
  563.0 0.8 copy.21
  (28 shorter events, 0.1 us)
Async XLA Ops:
  7.2 549.8 %reduce-scatter.2.cloned.1.call-start = ((), (), s32[]{:S(2)}) async-start(), calls=%async_computation.1 | async-start | bytes 19906560 | tf_op jit(solution)/shard_map/reduce_scatter | solution.py:1309
  9.4 93.3 %copy-start.9 = (f32[2304]{0:T(1024)}, f32[2304]{0:T(1024)S(1)}, u32[]{:S(2)}) copy-start(f32[2304]{0:T(1024)S(1)} %get-tuple-element.44) | copy-start | bytes 27652
  9.4 93.8 %copy-start.11 = (f32[2304]{0:T(1024)}, f32[2304]{0:T(1024)S(1)}, u32[]{:S(2)}) copy-start(f32[2304]{0:T(1024)S(1)} %get-tuple-element.45) | copy-start | bytes 27652
  89.9 12.8 %copy-start.4 = (bf16[128,2304]{1,0:T(8,128)(2,1)S(1)}, bf16[128,2304]{1,0:T(8,128)(2,1)}, u32[]{:S(2)}) copy-start(bf16[128,2304]{1,0:T(8,128)(2,1)} %tokens_ref.1) | copy-start | bytes 1769476
  101.1 1.6 copy-start
  102.6 0.5 copy-start.18
  103.2 1.0 copy-start.16
  104.1 123.2 %copy-start.3 = (bf16[128,2304]{1,0:T(8,128)(2,1)S(1)}, bf16[128,2304]{1,0:T(8,128)(2,1)}, u32[]{:S(2)}) copy-start(bf16[128,2304]{1,0:T(8,128)(2,1)} %param.11) | copy-start | bytes 1769476
  104.2 123.2 %copy-start.13 = (f32[2304]{0:T(1024)S(1)}, f32[2304]{0:T(1024)}, u32[]{:S(2)}) copy-start(f32[2304]{0:T(1024)} %get-tuple-element.42) | copy-start | bytes 27652
  225.8 1.6 copy-start.2
  347.8 0.7 copy-start.15
  349.3 1.6 copy-start.5
  349.3 1.6 copy-start.12
  349.3 1.6 copy-start.17
  350.9 1.3 copy-start.1
  350.9 1.3 copy-start.10
  350.9 1.3 copy-start.19
  352.9 1.0 copy-start.6
  355.0 20.2 %copy-start.7 = (f32[64,8,2,256]{3,1,2,0:T(8,128)S(1)}, f32[64,8,2,256]{3,1,2,0:T(8,128)}, u32[]{:S(2)}) copy-start(f32[64,8,2,256]{3,1,2,0:T(8,128)} %copy.16) | copy-start | bytes 3145732
  554.3 2.0 copy-start.14
  556.9 6.1 %copy-start.8 = (bf16[128,2304]{1,0:T(8,128)(2,1)S(1)}, bf16[128,2304]{1,0:T(8,128)(2,1)}, u32[]{:S(2)}) copy-start(bf16[128,2304]{1,0:T(8,128)(2,1)} %get-tuple-element.61) | copy-start | bytes 1769476
Sparse Core Ops, SparseCore 0:
  348.0 134.3 reduce-scatter.1

commit v6 on v5

--- a/solution.py
+++ b/solution.py
@@ -62,8 +62,14 @@
     )
 
 
-def greet(at, line, rows):
+def greet(at, line, rows, sp_peer=None):
     barrier = pltpu.get_barrier_semaphore()
+    others = 1
+    if sp_peer is not None:
+        others = 2
+        pl.semaphore_signal(
+            barrier, inc=1, device_id={"sp": sp_peer}, device_id_type=pl.DeviceIdType.MESH
+        )
 
     def tell(block):
         pl.semaphore_signal(
@@ -73,7 +79,7 @@
     tell(at + 1 - 2 * (at % 2))
     pl.when(line > 0)(lambda: tell(at - 2))
     pl.when(line < rows - 1)(lambda: tell(at + 2))
-    pl.semaphore_wait(barrier, 1 + jnp.minimum(line, 1) + jnp.minimum(rows - 1 - line, 1))
+    pl.semaphore_wait(barrier, others + jnp.minimum(line, 1) + jnp.minimum(rows - 1 - line, 1))
 
 
 def both(*terms):
@@ -230,8 +236,33 @@
     )(projected)
 
 
-def attend_back_kernel(
+def carry(cross_ref, far_ref, first, sent, landed, across):
+    return push_sp(
+        cross_ref.at[:, pl.ds(first, far_ref.shape[1]), :], far_ref, sent, landed, across
+    )
+
+
+def attend_back_kernel(heads, carried, *refs):
+    if carried:
+        x_ref, scaled_ref, delta_ref, kv_ref, cross_ref, out_ref, far_ref, *scratch = refs
+        *scratch, cross_sent, cross_landed = scratch
+        across = (lax.axis_index("sp") + 2) % 4
+        over = carry(cross_ref, far_ref, 0, cross_sent, cross_landed, across)
+        after = over.start
+    else:
+        x_ref, scaled_ref, delta_ref, kv_ref, out_ref, *scratch = refs
+        across, after = None, lambda: None
+    attend_back_steps(
+        heads, across, after, x_ref, scaled_ref, delta_ref, kv_ref, out_ref, *scratch
+    )
+    if carried:
+        over.wait()
+
+
+def attend_back_steps(
     heads,
+    across,
+    after_greeting,
     x_ref,
     scaled_ref,
     delta_ref,
@@ -264,7 +295,8 @@
     def _(index):
         pl.when(index <= at)(lambda: load(index).start())
 
-    greet(at, line, rows)
+    greet(at, line, rows, across)
+    after_greeting()
 
     def side_copy(target):
         return push(
@@ -378,17 +410,28 @@
         pl.when(target < line)(lambda: down_copy(target).wait_send())
 
 
-def attend_back(projected, scaled, delta, kv_all):
+def half_of(cross):
+    kinds, units, width = cross.shape
+    return jax.ShapeDtypeStruct((kinds, units // 2, width), cross.dtype)
+
+
+def attend_back(projected, scaled, delta, kv_all, cross=None):
     size = projected.shape[0]
     blocks = lax.axis_size("blk")
     rows = blocks // 2
     heads = scaled.shape[1] // HEAD
     whole = pl.BlockSpec(memory_space=pltpu.VMEM)
+    far = pl.BlockSpec(memory_space=pl.ANY)
+    carried = cross is not None
+    far_shape, operands = [], [projected, scaled, delta, kv_all]
+    if carried:
+        far_shape = [half_of(cross)]
+        operands.append(cross)
     return pl.pallas_call(
-        functools.partial(attend_back_kernel, heads),
-        out_shape=jax.ShapeDtypeStruct(projected.shape, jnp.bfloat16),
-        in_specs=[whole, whole, whole, pl.BlockSpec(memory_space=pl.ANY)],
-        out_specs=whole,
+        functools.partial(attend_back_kernel, heads, carried),
+        out_shape=[jax.ShapeDtypeStruct(projected.shape, jnp.bfloat16)] + far_shape,
+        in_specs=[whole, whole, whole, far] + [far] * carried,
+        out_specs=[whole] + [far] * carried,
         scratch_shapes=[
             pltpu.VMEM((blocks, size, 2 * HEAD), jnp.bfloat16),
             pltpu.VMEM((rows, 2, size, 2 * HEAD), jnp.bfloat16),
@@ -402,13 +445,14 @@
             pltpu.SemaphoreType.DMA((rows,)),
             pltpu.SemaphoreType.DMA((rows,)),
             pltpu.SemaphoreType.DMA((rows,)),
-        ],
+        ]
+        + [pltpu.SemaphoreType.DMA, pltpu.SemaphoreType.DMA] * carried,
         compiler_params=pltpu.CompilerParams(
             collective_id=1, has_side_effects=True, vmem_limit_bytes=VMEM_BYTES
         ),
         cost_estimate=cost_of(50),
         name="attend_back",
-    )(projected, scaled, delta, kv_all)
+    )(*operands)
 
 
 def line_gather(own_ref, full, line_sent, line_landed, side_sent, side_landed, own_done, work):
@@ -680,7 +724,8 @@
     acts_ref,
     w_ref,
     out_ref,
-    sum_ref,
+    keep_ref,
+    cross_ref,
     w,
     rights,
     lefts,
@@ -688,12 +733,19 @@
     side,
     lane,
     stage,
+    mate_part,
+    summed,
     w_done,
     acts_done,
-    stage_done,
+    mate_sent,
+    mate_landed,
+    summed_done,
     *sems,
 ):
     at = lax.axis_index("blk")
+    me = lax.axis_index("sp")
+    chip, core = me // 2, me % 2
+    mate = me + 1 - 2 * core
     rows = lax.axis_size("blk") // 2
     size, width = grad_ref.shape
     pair = 2 * size
@@ -710,7 +762,7 @@
     acts_copy.start()
     for which in range(3):
         load(which).start()
-    greet(at, at // 2, rows)
+    greet(at, at // 2, rows, mate)
     acts_copy.wait()
     for which in range(3):
         load(which).wait()
@@ -744,12 +796,34 @@
     def piece_columns(item):
         return pl.ds(pl.multiple_of((item % pieces) * FILL_COLUMNS, FILL_COLUMNS), FILL_COLUMNS)
 
-    def stage_copy(item):
+    def mate_copy(item):
+        return push_sp(
+            stage.at[item % 3, :, 1 - core],
+            mate_part.at[item],
+            mate_sent.at[item % 3],
+            mate_landed.at[item],
+            mate,
+        )
+
+    def put(item, side_chip, target):
         return pltpu.make_async_copy(
-            stage.at[item % 2],
-            sum_ref.at[:, item // pieces, :, piece_columns(item)],
-            stage_done.at[item % 2],
-        )
+            summed.at[item % 2, side_chip],
+            target.at[item // pieces, :, piece_columns(item)],
+            summed_done.at[item % 2, side_chip],
+        )
+
+    def put_wait(item):
+        put(item, chip, keep_ref).wait()
+        put(item, 1 - chip, cross_ref).wait()
+
+    def sum_one(item):
+        pl.when(item > 1)(lambda: put_wait(item - 2))
+        mate_copy(item).wait_recv()
+        summed[item % 2] = (
+            stage[item % 3, :, core].astype(jnp.float32) + mate_part[item].astype(jnp.float32)
+        ).astype(jnp.bfloat16)
+        put(item, chip, keep_ref).start()
+        put(item, 1 - chip, cross_ref).start()
 
     def fill_one(item):
         which = item // pieces
@@ -758,11 +832,12 @@
             rights[which // 2, :, piece_columns(item)],
             preferred_element_type=jnp.float32,
         )
-        pl.when(item > 1)(lambda: stage_copy(item - 2).wait())
-        stage[item % 2] = total.astype(jnp.bfloat16).reshape(
-            owners, units // owners, FILL_COLUMNS
-        )
-        stage_copy(item).start()
+        pl.when(item > 2)(lambda: mate_copy(item - 3).wait_send())
+        stage[item % 3] = total.astype(jnp.bfloat16).reshape(
+            2, 2, units // owners, FILL_COLUMNS
+        )
+        mate_copy(item).start()
+        pl.when(item > 0)(lambda: sum_one(item - 1))
 
     each = pl.cdiv(total_pieces - FILL_FIRST, rows - 1)
 
@@ -776,8 +851,11 @@
 
     line_gather(grad_ref, grads, *sems[:5], expand)
     line_scatter(part, side, lane, out_ref, *sems[5:], reduce, fill)
-    stage_copy(total_pieces - 2).wait()
-    stage_copy(total_pieces - 1).wait()
+    sum_one(total_pieces - 1)
+    put_wait(total_pieces - 2)
+    put_wait(total_pieces - 1)
+    for item in range(total_pieces - 3, total_pieces):
+        mate_copy(item).wait_send()
 
 
 def ffn_back(grad_ffn, acts, w_parts, owners):
@@ -786,16 +864,18 @@
     blocks = lax.axis_size("blk")
     rows = blocks // 2
     tokens = blocks * size
+    items = 3 * width // FILL_COLUMNS
     whole = pl.BlockSpec(memory_space=pltpu.VMEM)
     far = pl.BlockSpec(memory_space=pl.ANY)
     return pl.pallas_call(
         functools.partial(ffn_back_kernel, owners),
         out_shape=(
             jax.ShapeDtypeStruct((size, width), jnp.float32),
-            jax.ShapeDtypeStruct((owners, 3, units // owners, width), jnp.bfloat16),
+            jax.ShapeDtypeStruct((3, units // owners, width), jnp.bfloat16),
+            jax.ShapeDtypeStruct((3, units // owners, width), jnp.bfloat16),
         ),
         in_specs=[whole, far, far],
-        out_specs=(whole, far),
+        out_specs=(whole, far, far),
         scratch_shapes=[
             pltpu.VMEM(w_parts.shape, jnp.bfloat16),
             pltpu.VMEM((2, tokens, width), jnp.bfloat16),
@@ -803,10 +883,14 @@
             pltpu.VMEM((tokens, width), jnp.bfloat16),
             pltpu.VMEM((rows, size, width), jnp.bfloat16),
             pltpu.VMEM((rows + 1, size, width), jnp.bfloat16),
-            pltpu.VMEM((2, owners, units // owners, FILL_COLUMNS), jnp.bfloat16),
+            pltpu.VMEM((3, 2, 2, units // owners, FILL_COLUMNS), jnp.bfloat16),
+            pltpu.VMEM((items, 2, units // owners, FILL_COLUMNS), jnp.bfloat16),
+            pltpu.VMEM((2, 2, units // owners, FILL_COLUMNS), jnp.bfloat16),
             pltpu.SemaphoreType.DMA((3,)),
             pltpu.SemaphoreType.DMA,
-            pltpu.SemaphoreType.DMA((2,)),
+            pltpu.SemaphoreType.DMA((3,)),
+            pltpu.SemaphoreType.DMA((items,)),
+            pltpu.SemaphoreType.DMA((2, 2)),
             *line_sems(rows),
             *lane_sems(rows),
         ],
@@ -854,7 +938,10 @@
     ).astype(jnp.bfloat16)
     units = w_parts.shape[1]
     owned = sums.reshape(3, owners, units // owners, sums.shape[2])
-    return (scatter_tokens(partial), jnp.transpose(owned, (1, 0, 2, 3)))
+    mine = lax.psum_scatter(
+        jnp.transpose(owned, (1, 0, 2, 3)), "sp", scatter_dimension=0, tiled=True
+    )
+    return (scatter_tokens(partial), mine[0], None)
 
 
 def cost_of(microseconds):
@@ -1026,9 +1113,11 @@
     middle_ref,
     gain_ref,
     rows_ref,
+    cross_ref,
     sum_ref,
     tokens_grad_ref,
     gains_ref,
+    far_ref,
     w,
     got,
     grad_in,
@@ -1048,6 +1137,8 @@
     gain_side,
     line_sent,
     line_landed,
+    cross_sent,
+    cross_landed,
     *sems,
 ):
     at = lax.axis_index("blk")
@@ -1094,6 +1185,10 @@
     pl.semaphore_wait(barrier, 3 + rows)
     for step in (2, 1, 3):
         swap(step).start()
+    over = carry(
+        cross_ref, far_ref, far_ref.shape[1], cross_sent, cross_landed, (me + 2) % 4
+    )
+    over.start()
     keep.wait()
 
     def sp_gains(step):
@@ -1177,28 +1272,33 @@
     for step in (1, 2, 3):
         swap(step).wait_send()
         sp_gains(step).wait_send()
+    over.wait()
     side_gains().wait_send()
     for step in range(1, rows):
         line_gains(step).wait_send()
 
 
-def finish(cols, act_block, attended, grad_block, w_qkv, tokens, grad_middle, gain, gain_rows):
+def finish(
+    cols, act_block, attended, grad_block, w_qkv, tokens, grad_middle, gain, gain_rows, cross
+):
     blocks = lax.axis_size("blk")
     rows = blocks // 2
     size, width = tokens.shape
     block = (cols.shape[1] + attended.shape[1]) // blocks
     whole = pl.BlockSpec(memory_space=pltpu.VMEM)
+    any_space = pl.BlockSpec(memory_space=pl.ANY)
     dma = pltpu.SemaphoreType.DMA
     small = gain_rows.shape
-    total, tokens_grad, gains_all = pl.pallas_call(
+    total, tokens_grad, gains_all, far = pl.pallas_call(
         finish_kernel,
         out_shape=(
             jax.ShapeDtypeStruct((block, width), jnp.float32),
             jax.ShapeDtypeStruct((size, width), jnp.bfloat16),
             jax.ShapeDtypeStruct(small, jnp.float32),
+            half_of(cross),
         ),
-        in_specs=[whole] * 4 + [pl.BlockSpec(memory_space=pl.ANY)] + [whole] * 4,
-        out_specs=(whole,) * 3,
+        in_specs=[whole] * 4 + [any_space] + [whole] * 4 + [any_space],
+        out_specs=(whole, whole, whole, any_space),
         scratch_shapes=[
             pltpu.VMEM(w_qkv.shape, jnp.bfloat16),
             pltpu.VMEM((4, size, cols.shape[1]), jnp.bfloat16),
@@ -1219,6 +1319,8 @@
             dma((2,)),
             dma((rows,)),
             dma((rows,)),
+            dma,
+            dma,
             *lane_sems(rows),
         ],
         compiler_params=pltpu.CompilerParams(
@@ -1226,9 +1328,9 @@
         ),
         cost_estimate=cost_of(85),
         name="finish",
-    )(cols, act_block, attended, grad_block, w_qkv, tokens, grad_middle, gain, gain_rows)
+    )(cols, act_block, attended, grad_block, w_qkv, tokens, grad_middle, gain, gain_rows, cross)
     shared = cols.shape[1] // blocks
-    return (total[:shared], total[shared:], tokens_grad, gains_all)
+    return (total[:shared], total[shared:], tokens_grad, gains_all, far)
 
 
 def weight_sums_wide(left, right):
@@ -1236,7 +1338,9 @@
     return scatter_tokens(term)
 
 
-def finish_wide(cols, act_block, attended, grad_block, w_qkv, tokens, grad_middle, gain, gain_rows):
+def finish_wide(
+    cols, act_block, attended, grad_block, w_qkv, tokens, grad_middle, gain, gain_rows, cross
+):
     grad_act_in = exchange_project(cols, w_qkv, 7)
     normed, inverse = norm_parts(tokens.astype(jnp.float32))
     grad_v, gain_row = norm_back(grad_act_in, normed, inverse, gain)
@@ -1246,6 +1350,7 @@
         weight_sums_wide(attended, grad_block),
         (grad_middle + grad_v).astype(jnp.bfloat16),
         gains_all,
+        None,
     )
 
 
@@ -1271,7 +1376,7 @@
     grad_out = cotangent.astype(jnp.float32)
     grad_ffn_f, gain_grad3 = norm_back(grad_out, normed_ffn, inverse_ffn, gains[3])
     grad_ffn = grad_ffn_f.astype(jnp.bfloat16)
-    grad_act_ffn, ffn_sums = (ffn_back_wide if wide else ffn_back)(
+    grad_act_ffn, ffn_part, cross = (ffn_back_wide if wide else ffn_back)(
         grad_ffn, act_all, w_parts, groups
     )
     grad_norm_mid, gain_grad2 = norm_back(grad_act_ffn, normed_mid, inverse_mid, gains[2])
@@ -1285,17 +1390,18 @@
     row_delta = (
         jnp.sum(grad_heads * attended.reshape(block_rows, heads_here, HEAD), axis=-1) / totals_rows
     )
-    grad_cols = attend_back(
+    grad_cols, *far_first = attend_back(
         projected,
         scaled.reshape(block_rows, heads_here * HEAD),
         jnp.transpose(row_delta).reshape(heads_here, 1, block_rows),
         kv_all,
+        cross,
     )
     gain_rows = jnp.stack(
         [jnp.zeros_like(gain_grad1), gain_grad1, gain_grad2, gain_grad3]
         + [jnp.zeros_like(gain_grad1)] * 4
     )
-    qkv_grad, out_grad, tokens_grad, gains_all = (finish_wide if wide else finish)(
+    qkv_grad, out_grad, tokens_grad, gains_all, far_last = (finish_wide if wide else finish)(
         grad_cols,
         act_block,
         attended_cols,
@@ -1305,9 +1411,12 @@
         grad_middle,
         gains[0][None],
         gain_rows,
-    )
-    ffn_part = lax.psum_scatter(ffn_sums, "sp", scatter_dimension=0, tiled=True)
-    ffn_grad = jnp.transpose(ffn_part[0].astype(jnp.float32), (1, 0, 2))
+        cross,
+    )
+    ffn_sum = ffn_part.astype(jnp.float32)
+    if not wide:
+        ffn_sum = ffn_sum + jnp.concatenate([*far_first, far_last], axis=1).astype(jnp.float32)
+    ffn_grad = jnp.transpose(ffn_sum, (1, 0, 2))
     share = gains_all.shape[1] // (groups * lax.axis_size("blk"))
     place = lax.axis_index("sp") * lax.axis_size("blk") + lax.axis_index("blk")
     gains_grad = lax.dynamic_slice_in_dim(gains_all[:4], place * share, share, 1)

time: 581 us -> 569 us (0.979)
  between operations: 14.5 us -> 1.16 us
  transfers between devices with their start and end apart: 1 -> 0, of which waited for: 0 -> 0; matrix products, arithmetic and copies ran while one was open for 3% -> 0% of each run, Pallas kernels for 33% -> 0%
where the time goes in v6:
time: 569 us; the launch traced here: 559 us
  Pallas kernels  523 us (92%)
  other arithmetic  21.1 us (4%)
  local copies, waits for them, and re-layouts  13.8 us (2%)
    pallas_call x1, Pallas kernels, ffn_back(): pl.pallas_call(functools.partial(ffn_back_kernel, owners), out_shape=(jax...  123 us
    pallas_call x1, Pallas kernels, ffn_forward(): pl.pallas_call(ffn_kernel, out_shape=(jax.ShapeDtypeStruct((size, width),...  122 us
    pallas_call x1, Pallas kernels, finish(): pl.pallas_call(finish_kernel, out_shape=(jax.ShapeDtypeStruct((block, wid...  115 us
    pallas_call x1, Pallas kernels, attend(): pl.pallas_call(functools.partial(attend_kernel, heads), out_shape=(jax.Sh...  56.1 us
    pallas_call x1, Pallas kernels, attend_back(): pl.pallas_call(functools.partial(attend_back_kernel, heads, carried), out...  54.6 us
    pallas_call x2, Pallas kernels, gather_project(): pl.pallas_call(gather_project_kernel, out_shape=(jax.ShapeDtypeStruct((4...  41.2 us

profile of v6, /device:TPU:26, one launch (start us, length us, event | category | flops | bytes accessed | tf_op | source)
XLA Modules:
  0.0 559.3 jit_solution(15397702740907544642)
XLA Ops:
  0.6 2.2 slice_reduce_fusion
  2.8 1.3 fusion.5
  4.1 2.1 fusion.7.x_ref
  6.2 21.0 %gather_project.2 = (bf16[512,2304]{1,0:T(8,128)(2,1)}, bf16[512,1024]{1,0:T(8,128)(2,1)}) custom-call(bf16[128,2304]{1,0:T(8,128)(2,1)} %fusion.7.x_ref, bf16[4096,2304]{1,0:T(8,128)(2,1)} %w_ref.7), custom_call_target="tpu_custom_call" | custom-call | flops 17999998976 | bytes 54000000 | tf_op jit(solution)/shard_map/gather_project/pallas_call | solution.py:1020
  27.2 56.1 %attend.1 = (bf16[512,512]{1,0:T(8,128)(2,1)}, f32[512,512]{1,0:T(8,128)}, f32[2,1,512]{2,1,0:T(1,128)}, bf16[8,512,512]{2,1,0:T(8,128)(2,1)}) custom-call(bf16[512,1024]{1,0:T(8,128)(2,1)} %get-tuple-element.25.x_ref.refs_0_), custom_call_target="tpu_custom_call" | custom-call | flops 49999998976 | bytes 150000000 | tf_op jit(solution)/shard_map/attend/pallas_call | solution.py:210
  83.3 0.0 copy-start.4
  83.3 11.2 %exchange_project.1 = f32[128,2304]{1,0:T(8,128)} custom-call(bf16[512,512]{1,0:T(8,128)(2,1)} %get-tuple-element.26.x_ref.att_ref, bf16[2048,2304]{1,0:T(8,128)(2,1)} %w_ref.6), custom_call_target="tpu_custom_call" | custom-call | flops 16000000000 | bytes 48000000 | tf_op jit(solution)/shard_map/exchange_project/pallas_call | solution.py:1085
  94.5 0.0 copy-start
  94.5 1.5 multiply_reduce_fusion.6
  96.1 0.0 copy-done.11
  96.1 0.0 copy-done.4
  96.1 0.1 copy-done
  96.2 0.4 multiply_reduce_fusion.5
  96.5 0.1 copy-done.21
  96.7 0.0 copy-done.13
  96.7 1.0 multiply_convert_fusion.1.act_ref
  97.7 0.0 copy-done.19
  97.7 121.7 %ffn_forward.1 = (f32[128,2304]{1,0:T(8,128)}, bf16[1024,2304]{1,0:T(8,128)(2,1)}) custom-call(bf16[128,2304]{1,0:T(8,128)(2,1)} %multiply_convert_fusion.1.act_ref, bf16[3,1152,2304]{2,1,0:T(8,128)(2,1)} %bitcast.16), custom_call_target="tpu_custom_call" | custom-call | flops 115000000512 | bytes 345000000 | tf_op jit(solution)/shard_map/ffn_forward/pallas_call | solution.py:689
  219.4 0.0 copy-start.2
  219.4 1.5 multiply_reduce_fusion.4
  220.9 0.0 copy-done.3
  220.9 0.0 copy-done.15
  220.9 0.1 copy-done.2
  221.0 1.0 fusion.8
  222.0 1.4 fusion.4
  223.4 123.2 %ffn_back.1 = (f32[128,2304]{1,0:T(8,128)}, bf16[3,288,2304]{2,1,0:T(8,128)(2,1)}, bf16[3,288,2304]{2,1,0:T(8,128)(2,1)}) custom-call(bf16[128,2304]{1,0:T(8,128)(2,1)} %get-tuple-element.57.grad_ref, bf16[1024,2304]{1,0:T(8,128)(2,1)} %get-tuple-element.28.acts_ref, bf16[3,1152,2304]{2,1,0:T(8,128)(2,1)} %bitcast.17), custom_call_target="tpu_custom_call" | custom-call | flops 115000000512 | bytes 345000000 | tf_op jit(solution)/shard_map/ffn_back/pallas_call | solution.py:870
  346.6 0.0 copy-done.14
  346.6 0.0 copy-done.20
  346.6 0.0 copy-start.1
  346.7 0.0 copy-start.5
  346.7 0.0 copy-start.12
  346.7 0.0 copy-start.22
  346.7 1.8 multiply_reduce_fusion
  348.5 0.0 copy-done.1
  348.5 0.1 copy-done.5
  348.6 0.0 copy-done.12
  348.6 0.0 copy-done.22
  348.6 0.7 multiply_reduce_fusion.1
  349.4 1.0 copy-done.6
  350.4 1.1 multiply_convert_fusion.x_ref
  351.4 20.2 %gather_project.3 = (bf16[512,2304]{1,0:T(8,128)(2,1)}, bf16[512,512]{1,0:T(8,128)(2,1)}) custom-call(bf16[128,2304]{1,0:T(8,128)(2,1)} %multiply_convert_fusion.x_ref, bf16[2048,2304]{1,0:T(8,128)(2,1)} %w_ref.6), custom_call_target="tpu_custom_call" | custom-call | flops 17999998976 | bytes 54000000 | tf_op jit(solution)/shard_map/gather_project/pallas_call | solution.py:1020
  371.6 0.0 copy-done.18
  371.7 0.1 copy.13
  371.8 0.6 div.43
  372.4 0.0 copy-start.8
  372.4 0.0 copy-start.10
  372.4 0.1 copy.16
  372.5 1.1 copy-done.8
  373.7 0.1 copy-done.10
  373.8 1.1 convert_multiply_fusion.4
  374.9 0.7 mul.214
  375.6 0.6 reduce_sum.108
  376.2 0.1 copy.14
  376.3 0.6 reshape.69.refs_2_
  376.9 54.6 %attend_back.1 = (bf16[512,1024]{1,0:T(8,128)(2,1)}, bf16[3,144,2304]{2,1,0:T(8,128)(2,1)}) custom-call(bf16[512,1024]{1,0:T(8,128)(2,1)} %get-tuple-element.25.x_ref.refs_0_, bf16[512,512]{1,0:T(8,128)(2,1)} %get-tuple-element.60.refs_1_, f32[2,1,512]{2,1,0:T(1,128)} %reshape.69.refs_2_, bf16[8,512,512]{2,1,0:T(8,128)(2,1)} %get-tuple-element.33.refs_3_, ...), custom_call_target="tpu_custom_call" | custom-call | flops 49999998976 | bytes 150000000 | tf_op jit(solution)/shard_map/attend_back/pallas_call | solution.py:430
  431.6 0.0 copy-done.16
  431.6 0.7 stack.19.rows_ref
  432.3 115.3 %finish.1 = (f32[192,2304]{1,0:T(8,128)}, bf16[128,2304]{1,0:T(8,128)(2,1)}, f32[8,2304]{1,0:T(8,128)}, bf16[3,144,2304]{2,1,0:T(8,128)(2,1)}) custom-call(bf16[512,1024]{1,0:T(8,128)(2,1)} %get-tuple-element.35.cols_ref, bf16[512,2304]{1,0:T(8,128)(2,1)} %get-tuple-element.36.act_ref, bf16[512,512]{1,0:T(8,128)(2,1)} %get-tuple-element.26.x_ref.att_ref, ...), custom_call_target="tpu_custom_call" | custom-call | flops 85000003584 | bytes 255000000 | tf_op jit(solution)/shard_map/finish/pallas_call | solution.py:1292
  547.7 0.0 copy-start.7
  547.7 2.5 slice.29
  550.2 1.9 slice.30
  552.1 0.7 constant_dynamic-slice_fusion
  552.8 5.5 add_bitcast_fusion
  558.3 0.8 copy.21
  (31 shorter events, 0.1 us)
Async XLA Ops:
  2.8 93.3 %copy-start.11 = (f32[2304]{0:T(1024)}, f32[2304]{0:T(1024)S(1)}, u32[]{:S(2)}) copy-start(f32[2304]{0:T(1024)S(1)} %get-tuple-element.52) | copy-start | bytes 27652
  2.8 93.9 %copy-start.13 = (f32[2304]{0:T(1024)}, f32[2304]{0:T(1024)S(1)}, u32[]{:S(2)}) copy-start(f32[2304]{0:T(1024)S(1)} %get-tuple-element.53) | copy-start | bytes 27652
  83.3 12.8 %copy-start.4 = (bf16[128,2304]{1,0:T(8,128)(2,1)S(1)}, bf16[128,2304]{1,0:T(8,128)(2,1)}, u32[]{:S(2)}) copy-start(bf16[128,2304]{1,0:T(8,128)(2,1)} %tokens_ref.1) | copy-start | bytes 1769476
  94.5 1.6 copy-start
  96.2 0.5 copy-start.21
  96.7 1.0 copy-start.19
  97.7 123.3 %copy-start.3 = (bf16[128,2304]{1,0:T(8,128)(2,1)S(1)}, bf16[128,2304]{1,0:T(8,128)(2,1)}, u32[]{:S(2)}) copy-start(bf16[128,2304]{1,0:T(8,128)(2,1)} %param.11) | copy-start | bytes 1769476
  97.7 123.3 %copy-start.15 = (f32[2304]{0:T(1024)S(1)}, f32[2304]{0:T(1024)}, u32[]{:S(2)}) copy-start(f32[2304]{0:T(1024)} %get-tuple-element.50) | copy-start | bytes 27652
  219.4 1.6 copy-start.2
  223.4 123.2 %copy-start.14 = (f32[2304]{0:T(1024)S(1)}, f32[2304]{0:T(1024)}, u32[]{:S(2)}) copy-start(f32[2304]{0:T(1024)} %copy-done.13) | copy-start | bytes 27652
  223.4 123.2 %copy-start.20 = (f32[128]{0:T(128)S(1)}, f32[128]{0:T(128)}, u32[]{:S(2)}) copy-start(f32[128]{0:T(128)} %copy-done.19) | copy-start | bytes 1540
  346.6 1.8 copy-start.1
  346.7 2.0 copy-start.5
  346.7 2.0 copy-start.12
  346.7 2.0 copy-start.22
  349.3 1.0 copy-start.6
  351.4 20.2 %copy-start.18 = (f32[2,1,512]{2,1,0:T(1,128)S(1)}, f32[2,1,512]{2,1,0:T(1,128)}, u32[]{:S(2)}) copy-start(f32[2,1,512]{2,1,0:T(1,128)} %get-tuple-element.31) | copy-start | bytes 12292
  372.4 1.2 copy-start.8
  372.4 1.3 copy-start.10
  376.9 54.6 %copy-start.16 = (f32[2304]{0:T(1024)S(1)}, f32[2304]{0:T(1024)}, u32[]{:S(2)}) copy-start(f32[2304]{0:T(1024)} %get-tuple-element.48) | copy-start | bytes 27652
  547.7 5.1 copy-start.7
  550.2 2.0 copy-start.17
  552.8 5.5 copy-start.9

commit v7 on v6

--- a/solution.py
+++ b/solution.py
@@ -171,13 +171,16 @@
             pl.when(line < rows - 1)(lambda: up_copy(index, kv.at[index]).start())
             side_copy(index, kv.at[index]).start()
 
-        pl.when(source >= 0)(lambda: compute(index))
-        other = 2 * (source + 1) + 1 - column
-
-        @pl.when(both(step > 0, source + 1 >= 0, jnp.logical_or(step > 1, column == 1)))
-        def _():
-            side_copy(other, kv.at[other]).wait_recv()
-            compute(other)
+        @pl.loop(0, 2)
+        def _(way):
+            found = source + way
+            here = 2 * found + jnp.where(way == 0, column, 1 - column)
+            due = jnp.logical_or(way == 0, both(step > 0, jnp.logical_or(step > 1, column == 1)))
+
+            @pl.when(both(found >= 0, due))
+            def _():
+                pl.when(way == 1)(lambda: side_copy(here, kv.at[here]).wait_recv())
+                compute(here)
 
     for head in range(heads):
         columns = slice(head * HEAD, (head + 1) * HEAD)
@@ -386,12 +389,15 @@
 
     @pl.loop(0, rows)
     def _(target):
-        @pl.when(jnp.logical_or(target < line, both(target == line, column == 1)))
-        def _():
-            compute(target, 1 - column)
-            side_copy(target).start()
-
-        pl.when(target <= line)(lambda: compute(target, column))
+        away = jnp.logical_or(target < line, both(target == line, column == 1))
+
+        @pl.loop(0, 2)
+        def _(way):
+            @pl.when(jnp.logical_or(both(way == 0, away), both(way == 1, target <= line)))
+            def _():
+                compute(target, jnp.where(way == 0, 1 - column, column))
+                pl.when(way == 0)(lambda: side_copy(target).start())
+
         pl.when(both(line == rows - 1, target > 0))(lambda: merge(target - 1))
 
     out_ref[:, : heads * HEAD] = (dq[...] * HEAD ** (-0.5)).astype(jnp.bfloat16)
@@ -455,7 +461,7 @@
     )(*operands)
 
 
-def line_gather(own_ref, full, line_sent, line_landed, side_sent, side_landed, own_done, work):
+def line_gather(own_ref, full, line_sent, line_landed, side_sent, side_landed, own_done, ready, work):
     at = lax.axis_index("blk")
     rows = lax.axis_size("blk") // 2
     line, column = at // 2, at % 2
@@ -492,10 +498,13 @@
     keep = pltpu.make_async_copy(own_ref, spot(line, column), own_done)
     keep.start()
     keep.wait()
+    ready()
 
     @pl.loop(0, rows + 1)
     def _(step):
-        for sign in (-1, 1):
+        @pl.loop(0, 2)
+        def _(way):
+            sign = 2 * way - 1
             source = line - sign * step
 
             @pl.when(both(step > 0, inside(source)))
@@ -504,9 +513,11 @@
                 pl.when(inside(line + sign))(lambda: line_copy(source, sign).start())
                 side_copy(source, column).start()
 
-        for sign in (-1, 1):
+        @pl.loop(0, 2)
+        def _(way):
+            sign = 2 * way - 1
             source = line - sign * (step - 1)
-            once = step > 0 if sign == -1 else step > 1
+            once = step > way
 
             @pl.when(both(once, inside(source)))
             def _():
@@ -559,9 +570,10 @@
 
     @pl.loop(0, rows)
     def _(step):
-        for sign in (-1, 1):
-            target = line + sign * (rows - 1 - step)
-            once = step >= 0 if sign == -1 else step < rows - 1
+        @pl.loop(0, 2)
+        def _(way):
+            target = line + (2 * way - 1) * (rows - 1 - step)
+            once = step < rows - way
 
             @pl.when(both(once, inside(target)))
             def _():
@@ -591,9 +603,10 @@
     @pl.loop(0, rows)
     def _(step):
         fill(step)
-        for sign in (-1, 1):
-            target = line + sign * (rows - 1 - step)
-            once = step >= 0 if sign == -1 else step < rows - 1
+        @pl.loop(0, 2)
+        def _(way):
+            target = line + (2 * way - 1) * (rows - 1 - step)
+            once = step < rows - way
             pl.when(both(once, inside(target)))(lambda: merge(target))
 
     mine = spot(line, column)
@@ -659,8 +672,10 @@
     for which in range(3):
         load(which).start()
     greet(at, at // 2, rows)
-    for which in range(3):
-        load(which).wait()
+
+    def ready():
+        for which in range(3):
+            load(which).wait()
 
     def expand(source):
         save(source).start()
@@ -674,7 +689,7 @@
             hidden[target], w[2], (((0,), (0,)), ((), ())), preferred_element_type=jnp.float32
         ).astype(jnp.bfloat16)
 
-    line_gather(act_ref, acts, *sems[:5], expand)
+    line_gather(act_ref, acts, *sems[:5], ready, expand)
     line_scatter(part, side, lane, out_ref, *sems[5:], reduce, lambda step: None)
     pl.loop(0, rows)(lambda source: save(source).wait())
 
@@ -763,9 +778,11 @@
     for which in range(3):
         load(which).start()
     greet(at, at // 2, rows, mate)
-    acts_copy.wait()
-    for which in range(3):
-        load(which).wait()
+
+    def ready():
+        acts_copy.wait()
+        for which in range(3):
+            load(which).wait()
 
     def expand(source):
         columns = pair_rows(source)
@@ -849,7 +866,7 @@
         def _(item):
             pl.when(first + item < last)(lambda: fill_one(first + item))
 
-    line_gather(grad_ref, grads, *sems[:5], expand)
+    line_gather(grad_ref, grads, *sems[:5], ready, expand)
     line_scatter(part, side, lane, out_ref, *sems[5:], reduce, fill)
     sum_one(total_pieces - 1)
     put_wait(total_pieces - 2)
@@ -1114,13 +1131,15 @@
     gain_ref,
     rows_ref,
     cross_ref,
-    sum_ref,
+    qkv_ref,
+    out_ref,
     tokens_grad_ref,
     gains_ref,
     far_ref,
     w,
     got,
     grad_in,
+    total,
     part,
     side,
     lane,
@@ -1146,7 +1165,7 @@
     rows = lax.axis_size("blk") // 2
     line, column = at // 2, at % 2
     partner = at + 1 - 2 * column
-    block = sum_ref.shape[0]
+    block = total.shape[0]
     size = tokens_ref.shape[0]
     units = cols_ref.shape[1]
     extra = block - size
@@ -1245,30 +1264,32 @@
             sp_gains(step).start()
 
     def fill(step):
-        pl.when(step == 0)(inputs_back)
-
-        @pl.when(step == 1)
+        pl.when(step == 1)(inputs_back)
+
+        @pl.when(step == 2)
         def _():
-            total = mine[...]
+            gains = mine[...]
             for other in range(1, 4):
                 sp_gains(4 - other).wait_recv()
-                total = total + from_sp[other]
-            from_sp[0] = total
+                gains = gains + from_sp[other]
+            from_sp[0] = gains
             side_gains().start()
 
-        @pl.when(step == 2)
+        @pl.when(step == 3)
         def _():
             side_gains().wait_recv()
             from_line[0] = from_sp[0] + from_side[...]
             for other in range(1, rows):
                 line_gains(other).start()
 
-    line_scatter(part, side, lane, sum_ref, *sems, reduce, fill)
-    total = from_line[0]
+    line_scatter(part, side, lane, total, *sems, reduce, fill)
+    qkv_ref[...] = total[:size]
+    out_ref[...] = total[size:]
+    gains = from_line[0]
     for other in range(1, rows):
         line_gains(rows - other).wait_recv()
-        total = total + from_line[other]
-    gains_ref[...] = total
+        gains = gains + from_line[other]
+    gains_ref[...] = gains
     for step in (1, 2, 3):
         swap(step).wait_send()
         sp_gains(step).wait_send()
@@ -1289,20 +1310,22 @@
     any_space = pl.BlockSpec(memory_space=pl.ANY)
     dma = pltpu.SemaphoreType.DMA
     small = gain_rows.shape
-    total, tokens_grad, gains_all, far = pl.pallas_call(
+    return pl.pallas_call(
         finish_kernel,
         out_shape=(
-            jax.ShapeDtypeStruct((block, width), jnp.float32),
+            jax.ShapeDtypeStruct((cols.shape[1] // blocks, width), jnp.float32),
+            jax.ShapeDtypeStruct((attended.shape[1] // blocks, width), jnp.float32),
             jax.ShapeDtypeStruct((size, width), jnp.bfloat16),
             jax.ShapeDtypeStruct(small, jnp.float32),
             half_of(cross),
         ),
         in_specs=[whole] * 4 + [any_space] + [whole] * 4 + [any_space],
-        out_specs=(whole, whole, whole, any_space),
+        out_specs=(whole, whole, whole, whole, any_space),
         scratch_shapes=[
             pltpu.VMEM(w_qkv.shape, jnp.bfloat16),
             pltpu.VMEM((4, size, cols.shape[1]), jnp.bfloat16),
             pltpu.VMEM((size, width), jnp.float32),
+            pltpu.VMEM((block, width), jnp.float32),
             pltpu.VMEM((blocks * block, width), jnp.bfloat16),
             pltpu.VMEM((rows, block, width), jnp.bfloat16),
             pltpu.VMEM((rows + 1, block, width), jnp.bfloat16),
@@ -1329,8 +1352,6 @@
         cost_estimate=cost_of(85),
         name="finish",
     )(cols, act_block, attended, grad_block, w_qkv, tokens, grad_middle, gain, gain_rows, cross)
-    shared = cols.shape[1] // blocks
-    return (total[:shared], total[shared:], tokens_grad, gains_all, far)
 
 
 def weight_sums_wide(left, right):

time: 569 us -> 536 us (0.942); the launches traced: 559 us -> 535 us
  Pallas kernels: 523 us -> 500 us
    pallas_call x1, Pallas kernels: 115 us -> 101 us  [finish(): pl.pallas_call(finish_kernel, out_shape=(jax.ShapeDtypeStruct((cols.shape...]
where the time goes in v7:
time: 536 us; the launch traced here: 535 us
  Pallas kernels  500 us (93%)
  other arithmetic  21.2 us (4%)
  local copies, waits for them, and re-layouts  13.1 us (2%)
    pallas_call x1, Pallas kernels, ffn_back(): pl.pallas_call(functools.partial(ffn_back_kernel, owners), out_shape=(jax...  121 us
    pallas_call x1, Pallas kernels, ffn_forward(): pl.pallas_call(ffn_kernel, out_shape=(jax.ShapeDtypeStruct((size, width),...  116 us
    pallas_call x1, Pallas kernels, finish(): pl.pallas_call(finish_kernel, out_shape=(jax.ShapeDtypeStruct((cols.shape...  101 us
    pallas_call x1, Pallas kernels, attend(): pl.pallas_call(functools.partial(attend_kernel, heads), out_shape=(jax.Sh...  56.2 us
    pallas_call x1, Pallas kernels, attend_back(): pl.pallas_call(functools.partial(attend_back_kernel, heads, carried), out...  53.8 us
    pallas_call x2, Pallas kernels, gather_project(): pl.pallas_call(gather_project_kernel, out_shape=(jax.ShapeDtypeStruct((4...  41.2 us
    pallas_call x1, Pallas kernels, exchange_project(): pl.pallas_call(exchange_project_kernel, out_shape=jax.ShapeDtypeStruct((s...  11.2 us

profile of v7, /device:TPU:26, one launch (start us, length us, event | category | flops | bytes accessed | tf_op | source)
XLA Modules:
  0.0 535.3 jit_solution(11153547362595840615)
XLA Ops:
  0.6 2.2 slice_reduce_fusion
  2.8 1.3 fusion.5
  4.1 2.1 fusion.7.x_ref
  6.2 21.0 %gather_project.2 = (bf16[512,2304]{1,0:T(8,128)(2,1)}, bf16[512,1024]{1,0:T(8,128)(2,1)}) custom-call(bf16[128,2304]{1,0:T(8,128)(2,1)} %fusion.7.x_ref, bf16[4096,2304]{1,0:T(8,128)(2,1)} %w_ref.7), custom_call_target="tpu_custom_call" | custom-call | flops 17999998976 | bytes 54000000 | tf_op jit(solution)/shard_map/gather_project/pallas_call | solution.py:1037
  27.2 56.2 %attend.1 = (bf16[512,512]{1,0:T(8,128)(2,1)}, f32[512,512]{1,0:T(8,128)}, f32[2,1,512]{2,1,0:T(1,128)}, bf16[8,512,512]{2,1,0:T(8,128)(2,1)}) custom-call(bf16[512,1024]{1,0:T(8,128)(2,1)} %get-tuple-element.26.x_ref.refs_0_), custom_call_target="tpu_custom_call" | custom-call | flops 49999998976 | bytes 150000000 | tf_op jit(solution)/shard_map/attend/pallas_call | solution.py:213
  83.3 0.0 copy-start.4
  83.4 11.2 %exchange_project.1 = f32[128,2304]{1,0:T(8,128)} custom-call(bf16[512,512]{1,0:T(8,128)(2,1)} %get-tuple-element.27.x_ref.att_ref, bf16[2048,2304]{1,0:T(8,128)(2,1)} %w_ref.6), custom_call_target="tpu_custom_call" | custom-call | flops 16000000000 | bytes 48000000 | tf_op jit(solution)/shard_map/exchange_project/pallas_call | solution.py:1102
  94.6 0.0 copy-start
  94.6 1.5 multiply_reduce_fusion.6
  96.1 0.0 copy-done.13
  96.1 0.0 copy-done.4
  96.1 0.1 copy-done
  96.2 0.4 multiply_reduce_fusion.5
  96.6 0.1 copy-done.22
  96.7 0.0 copy-done.15
  96.7 1.0 multiply_convert_fusion.1.act_ref
  97.7 116.3 %ffn_forward.1 = (f32[128,2304]{1,0:T(8,128)}, bf16[1024,2304]{1,0:T(8,128)(2,1)}) custom-call(bf16[128,2304]{1,0:T(8,128)(2,1)} %multiply_convert_fusion.1.act_ref, bf16[3,1152,2304]{2,1,0:T(8,128)(2,1)} %bitcast.16), custom_call_target="tpu_custom_call" | custom-call | flops 115000000512 | bytes 345000000 | tf_op jit(solution)/shard_map/ffn_forward/pallas_call | solution.py:704
  214.0 0.0 copy-done.20
  214.1 0.0 copy-start.2
  214.1 1.5 multiply_reduce_fusion.4
  215.6 0.0 copy-done.3
  215.6 0.0 copy-done.17
  215.6 0.1 copy-done.2
  215.7 1.0 fusion.8
  216.7 1.4 fusion.4
  218.1 120.5 %ffn_back.1 = (f32[128,2304]{1,0:T(8,128)}, bf16[3,288,2304]{2,1,0:T(8,128)(2,1)}, bf16[3,288,2304]{2,1,0:T(8,128)(2,1)}) custom-call(bf16[128,2304]{1,0:T(8,128)(2,1)} %get-tuple-element.59.grad_ref, bf16[1024,2304]{1,0:T(8,128)(2,1)} %get-tuple-element.29.acts_ref, bf16[3,1152,2304]{2,1,0:T(8,128)(2,1)} %bitcast.17), custom_call_target="tpu_custom_call" | custom-call | flops 115000000512 | bytes 345000000 | tf_op jit(solution)/shard_map/ffn_back/pallas_call | solution.py:887
  338.6 0.0 copy-done.16
  338.6 0.0 copy-done.21
  338.6 0.0 copy-start.1
  338.7 0.0 copy-start.5
  338.7 0.0 copy-start.14
  338.7 0.0 copy-start.23
  338.7 1.8 multiply_reduce_fusion
  340.5 0.0 copy-done.1
  340.5 0.1 copy-done.5
  340.6 0.0 copy-done.14
  340.6 0.0 copy-done.23
  340.6 0.7 multiply_reduce_fusion.1
  341.4 1.0 copy-done.6
  342.4 1.1 multiply_convert_fusion.x_ref
  343.5 20.2 %gather_project.3 = (bf16[512,2304]{1,0:T(8,128)(2,1)}, bf16[512,512]{1,0:T(8,128)(2,1)}) custom-call(bf16[128,2304]{1,0:T(8,128)(2,1)} %multiply_convert_fusion.x_ref, bf16[2048,2304]{1,0:T(8,128)(2,1)} %w_ref.6), custom_call_target="tpu_custom_call" | custom-call | flops 17999998976 | bytes 54000000 | tf_op jit(solution)/shard_map/gather_project/pallas_call | solution.py:1037
  363.7 0.0 copy-done.19
  363.7 0.1 copy.13
  363.9 0.6 div.43
  364.5 0.0 copy-start.9
  364.5 0.1 copy.16
  364.6 1.1 copy-done.9
  365.7 0.1 copy-done.12
  365.9 1.1 convert_multiply_fusion.4
  367.0 0.7 mul.214
  367.6 0.6 reduce_sum.108
  368.3 0.1 copy.14
  368.4 0.6 reshape.69.refs_2_
  369.0 53.8 %attend_back.1 = (bf16[512,1024]{1,0:T(8,128)(2,1)}, bf16[3,144,2304]{2,1,0:T(8,128)(2,1)}) custom-call(bf16[512,1024]{1,0:T(8,128)(2,1)} %get-tuple-element.26.x_ref.refs_0_, bf16[512,512]{1,0:T(8,128)(2,1)} %get-tuple-element.62.refs_1_, f32[2,1,512]{2,1,0:T(1,128)} %reshape.69.refs_2_, bf16[8,512,512]{2,1,0:T(8,128)(2,1)} %get-tuple-element.34.refs_3_, ...), custom_call_target="tpu_custom_call" | custom-call | flops 49999998976 | bytes 150000000 | tf_op jit(solution)/shard_map/attend_back/pallas_call | solution.py:436
  422.9 0.7 stack.19.rows_ref
  423.6 100.9 %finish.1 = (f32[128,2304]{1,0:T(8,128)}, f32[64,2304]{1,0:T(8,128)}, bf16[128,2304]{1,0:T(8,128)(2,1)}, f32[8,2304]{1,0:T(8,128)}, bf16[3,144,2304]{2,1,0:T(8,128)(2,1)}) custom-call(bf16[512,1024]{1,0:T(8,128)(2,1)} %get-tuple-element.36.cols_ref, bf16[512,2304]{1,0:T(8,128)(2,1)} %get-tuple-element.37.act_ref, ...), custom_call_target="tpu_custom_call" | custom-call | flops 85000003584 | bytes 255000000 | tf_op jit(solution)/shard_map/finish/pallas_call | solution.py:1313
  524.5 0.9 slice.23
  525.4 0.6 constant_dynamic-slice_fusion
  526.0 5.5 %add_bitcast_fusion = f32[288,3,2304]{2,0,1:T(8,128)} fusion(bf16[3,288,2304]{2,1,0:T(8,128)(2,1)} %get-tuple-element.43, bf16[3,144,2304]{2,1,0:T(8,128)(2,1)} %get-tuple-element.45, bf16[3,144,2304]{2,1,0:T(8,128)(2,1)S(1)} %copy-done.7), kind=kLoop, calls=%fused_computation | loop fusion | flops 11943936 | bytes 15925248 | tf_op jit(solution)/shard_map/transpose | solution.py:1440
  531.5 0.8 copy.23
  532.3 0.7 copy-done.8
  533.0 1.0 copy.24
  534.0 0.5 copy-done.10
  534.5 0.8 copy.25
  (33 shorter events, 0.1 us)
Async XLA Ops:
  2.8 93.3 %copy-start.13 = (f32[2304]{0:T(1024)}, f32[2304]{0:T(1024)S(1)}, u32[]{:S(2)}) copy-start(f32[2304]{0:T(1024)S(1)} %get-tuple-element.54) | copy-start | bytes 27652
  2.8 93.9 %copy-start.15 = (f32[2304]{0:T(1024)}, f32[2304]{0:T(1024)S(1)}, u32[]{:S(2)}) copy-start(f32[2304]{0:T(1024)S(1)} %get-tuple-element.55) | copy-start | bytes 27652
  83.3 12.8 %copy-start.4 = (bf16[128,2304]{1,0:T(8,128)(2,1)S(1)}, bf16[128,2304]{1,0:T(8,128)(2,1)}, u32[]{:S(2)}) copy-start(bf16[128,2304]{1,0:T(8,128)(2,1)} %tokens_ref.1) | copy-start | bytes 1769476
  94.6 1.6 copy-start
  96.2 0.5 copy-start.22
  96.7 117.3 %copy-start.20 = (f32[128]{0:T(128)}, f32[128]{0:T(128)S(1)}, u32[]{:S(2)}) copy-start(f32[128]{0:T(128)S(1)} %add_rsqrt_fusion.1) | copy-start | bytes 1540
  97.7 117.9 %copy-start.3 = (bf16[128,2304]{1,0:T(8,128)(2,1)S(1)}, bf16[128,2304]{1,0:T(8,128)(2,1)}, u32[]{:S(2)}) copy-start(bf16[128,2304]{1,0:T(8,128)(2,1)} %param.11) | copy-start | bytes 1769476
  97.7 117.9 %copy-start.17 = (f32[2304]{0:T(1024)S(1)}, f32[2304]{0:T(1024)}, u32[]{:S(2)}) copy-start(f32[2304]{0:T(1024)} %get-tuple-element.52) | copy-start | bytes 27652
  214.1 1.6 copy-start.2
  218.1 120.5 %copy-start.16 = (f32[2304]{0:T(1024)S(1)}, f32[2304]{0:T(1024)}, u32[]{:S(2)}) copy-start(f32[2304]{0:T(1024)} %copy-done.15) | copy-start | bytes 27652
  218.1 120.5 %copy-start.21 = (f32[128]{0:T(128)S(1)}, f32[128]{0:T(128)}, u32[]{:S(2)}) copy-start(f32[128]{0:T(128)} %copy-done.20) | copy-start | bytes 1540
  338.6 1.9 copy-start.1
  338.7 2.0 copy-start.5
  338.7 2.0 copy-start.14
  338.7 2.0 copy-start.23
  341.4 1.0 copy-start.6
  343.5 20.2 %copy-start.19 = (f32[2,1,512]{2,1,0:T(1,128)S(1)}, f32[2,1,512]{2,1,0:T(1,128)}, u32[]{:S(2)}) copy-start(f32[2,1,512]{2,1,0:T(1,128)} %get-tuple-element.32) | copy-start | bytes 12292
  364.5 1.2 copy-start.9
  364.5 1.3 copy-start.12
  369.0 53.9 %copy-start.18 = (f32[2304]{0:T(1024)S(1)}, f32[2304]{0:T(1024)}, u32[]{:S(2)}) copy-start(f32[2304]{0:T(1024)} %get-tuple-element.50) | copy-start | bytes 27652
  423.6 102.4 %copy-start.7 = (bf16[3,144,2304]{2,1,0:T(8,128)(2,1)S(1)}, bf16[3,144,2304]{2,1,0:T(8,128)(2,1)}, u32[]{:S(2)}) copy-start(bf16[3,144,2304]{2,1,0:T(8,128)(2,1)} %get-tuple-element.44) | copy-start | bytes 5971972
  526.0 5.5 %copy-start.11 = (bf16[128,2304]{1,0:T(8,128)(2,1)S(1)}, bf16[128,2304]{1,0:T(8,128)(2,1)}, u32[]{:S(2)}) copy-start(bf16[128,2304]{1,0:T(8,128)(2,1)} %get-tuple-element.71) | copy-start | bytes 1769476
  531.5 1.5 copy-start.8
  533.0 1.5 copy-start.10

commit v8 on v7

--- a/solution.py
+++ b/solution.py
@@ -461,42 +461,92 @@
     )(*operands)
 
 
-def line_gather(own_ref, full, line_sent, line_landed, side_sent, side_landed, own_done, ready, work):
+def line_gather(
+    own_ref,
+    full,
+    line_sent,
+    line_landed,
+    extra_sent,
+    extra_landed,
+    side_sent,
+    side_landed,
+    first_done,
+    own_done,
+    ready,
+    work,
+):
     at = lax.axis_index("blk")
     rows = lax.axis_size("blk") // 2
     line, column = at // 2, at % 2
+    partner = at + 1 - 2 * column
     size = own_ref.shape[0]
-
-    def spot(source, side):
-        start = pl.multiple_of((2 * source + side) * size, size)
-        return full.at[pl.ds(start, size), :]
+    half = size // 2
+
+    def span(source, start, count):
+        return full.at[pl.ds(pl.multiple_of(2 * source * size + start, half), count), :]
 
     def line_copy(source, sign, first=False):
+        target = span(source, column * size, size)
         return push(
-            own_ref if first else spot(source, column),
-            spot(source, column),
+            own_ref if first else target,
+            target,
             line_sent.at[(sign + 1) // 2, source],
             line_landed.at[source],
             at + 2 * sign,
         )
 
-    def side_copy(source, side, first=False):
+    def extra_copy(source, sign):
+        target = span(source, (1 - column) * size + half, half)
         return push(
-            own_ref if first else spot(source, side),
-            spot(source, side),
+            target,
+            target,
+            extra_sent.at[(sign + 1) // 2, source],
+            extra_landed.at[source],
+            at + 2 * sign,
+        )
+
+    def side_copy(source, member, count, first=False):
+        target = span(source, member * size, count)
+        return push(
+            own_ref.at[:count] if first else target,
+            target,
             side_sent.at[source],
             side_landed.at[source],
-            at + 1 - 2 * column,
+            partner,
+        )
+
+    def first_copy(member):
+        return push(
+            own_ref.at[half:],
+            span(line, member * size + half, half),
+            first_done.at[0],
+            first_done.at[1],
+            partner,
         )
 
     def inside(row):
         return jnp.logical_and(row >= 0, row < rows)
 
+    def end(row):
+        return jnp.logical_or(row == 0, row == rows - 1)
+
+    def by_end(source, act):
+        pl.when(end(source))(lambda: act(half))
+        pl.when(jnp.logical_not(end(source)))(lambda: act(size))
+
+    pl.when(end(line))(lambda: first_copy(column).start())
     pl.when(line < rows - 1)(lambda: line_copy(line, 1, True).start())
     pl.when(line > 0)(lambda: line_copy(line, -1, True).start())
-    side_copy(line, column, True).start()
-    keep = pltpu.make_async_copy(own_ref, spot(line, column), own_done)
+    by_end(line, lambda count: side_copy(line, column, count, True).start())
+    keep = pltpu.make_async_copy(own_ref, span(line, column * size, size), own_done)
     keep.start()
+
+    @pl.when(end(line))
+    def _():
+        first_copy(1 - column).wait_recv()
+        pl.when(line < rows - 1)(lambda: extra_copy(line, 1).start())
+        pl.when(line > 0)(lambda: extra_copy(line, -1).start())
+
     keep.wait()
     ready()
 
@@ -511,132 +561,231 @@
             def _():
                 line_copy(source, sign).wait_recv()
                 pl.when(inside(line + sign))(lambda: line_copy(source, sign).start())
-                side_copy(source, column).start()
+                by_end(source, lambda count: side_copy(source, column, count).start())
 
         @pl.loop(0, 2)
         def _(way):
             sign = 2 * way - 1
-            source = line - sign * (step - 1)
-            once = step > way
-
-            @pl.when(both(once, inside(source)))
+            source = line - sign * step
+
+            @pl.when(both(step > 0, inside(source), end(source)))
             def _():
-                side_copy(source, 1 - column).wait_recv()
+                extra_copy(source, sign).wait_recv()
+                pl.when(inside(line + sign))(lambda: extra_copy(source, sign).start())
+
+        @pl.loop(0, 2)
+        def _(way):
+            source = line - (2 * way - 1) * (step - 1)
+
+            @pl.when(both(step > way, inside(source)))
+            def _():
+                by_end(source, lambda count: side_copy(source, 1 - column, count).wait_recv())
                 work(source)
 
     @pl.loop(0, rows)
     def _(source):
-        pl.when(both(source <= line, line < rows - 1))(lambda: line_copy(source, 1).wait_send())
-        pl.when(both(source >= line, line > 0))(lambda: line_copy(source, -1).wait_send())
-        side_copy(source, column).wait_send()
-
-
-def line_scatter(part, side, lane, out_ref, side_sent, side_landed, lane_sent, lane_landed, work, fill):
+        @pl.when(both(source <= line, line < rows - 1))
+        def _():
+            line_copy(source, 1).wait_send()
+            pl.when(end(source))(lambda: extra_copy(source, 1).wait_send())
+
+        @pl.when(both(source >= line, line > 0))
+        def _():
+            line_copy(source, -1).wait_send()
+            pl.when(end(source))(lambda: extra_copy(source, -1).wait_send())
+
+        by_end(source, lambda count: side_copy(source, column, count).wait_send())
+
+    pl.when(end(line))(lambda: first_copy(column).wait_send())
+
+
+def line_scatter(
+    part,
+    side,
+    lane,
+    tail,
+    out_ref,
+    side_sent,
+    side_landed,
+    lane_sent,
+    lane_landed,
+    tail_done,
+    work,
+    fill,
+):
     at = lax.axis_index("blk")
     rows = lax.axis_size("blk") // 2
     line, column = at // 2, at % 2
+    partner = at + 1 - 2 * column
     size = out_ref.shape[0]
-
-    def spot(target, half):
-        start = pl.multiple_of((2 * target + half) * size, size)
-        return pl.ds(start, size)
-
-    def side_copy(target):
+    half = size // 2
+
+    def span(target, start, count):
+        return pl.ds(pl.multiple_of(2 * target * size + start, half), count)
+
+    def piece(target, which):
+        start = ((0, 0), (0, half), (size, half))[which]
+        return span(target, column * (size - 2 * start[0]) + start[0] + start[1], half)
+
+    def side_copy(target, count):
         return push(
-            part.at[spot(target, 1 - column), :],
-            side.at[target],
+            part.at[span(target, (1 - column) * size, count), :],
+            side.at[target, :count],
             side_sent.at[target],
             side_landed.at[target],
-            at + 1 - 2 * column,
-        )
-
-    def lane_copy(target, sign):
+            partner,
+        )
+
+    def lane_copy(target, which, sign):
         slot = target if sign == 1 else jnp.where(target == line - 1, rows, target)
         return push(
-            part.at[spot(target, column), :],
-            lane.at[slot],
-            lane_sent.at[target],
-            lane_landed.at[slot],
+            part.at[piece(target, which), :],
+            lane.at[slot, which],
+            lane_sent.at[target, which],
+            lane_landed.at[slot, which],
             at + 2 * sign,
         )
 
-    def lane_wait(slot):
+    def lane_wait(slot, which):
         push(
-            lane.at[slot], lane.at[slot], lane_sent.at[0], lane_landed.at[slot], at + 1 - 2 * column
+            lane.at[slot, which],
+            lane.at[slot, which],
+            lane_sent.at[0, which],
+            lane_landed.at[slot, which],
+            partner,
         ).wait_recv()
+
+    def tail_copy():
+        return push(
+            part.at[piece(line, 2), :], tail, tail_done.at[0], tail_done.at[1], partner
+        )
 
     def inside(row):
         return jnp.logical_and(row >= 0, row < rows)
+
+    def end(row):
+        return jnp.logical_or(row == 0, row == rows - 1)
+
+    def by_end(target, act):
+        pl.when(end(target))(lambda: act(half))
+        pl.when(jnp.logical_not(end(target)))(lambda: act(size))
+
+    def add(where, more):
+        part[where, :] = (
+            part[where, :].astype(jnp.float32) + more.astype(jnp.float32)
+        ).astype(jnp.bfloat16)
+
+    def hop(target, which):
+        for sign in (1, -1):
+
+            @pl.when(target > line if sign == 1 else target < line)
+            def _():
+                @pl.when(inside(line - sign))
+                def _():
+                    lane_wait(target, which)
+                    add(piece(target, which), lane[target, which])
+
+                lane_copy(target, which, sign).start()
+
+    def early(target):
+        return both(end(target), end(line), target != line)
 
     @pl.loop(0, rows)
     def _(step):
         @pl.loop(0, 2)
         def _(way):
             target = line + (2 * way - 1) * (rows - 1 - step)
-            once = step < rows - way
-
-            @pl.when(both(once, inside(target)))
+
+            @pl.when(both(step < rows - way, inside(target)))
             def _():
                 work(target)
-                side_copy(target).start()
+                by_end(target, lambda count: side_copy(target, count).start())
+
+                @pl.when(early(target))
+                def _():
+                    hop(target, 1)
+                    hop(target, 2)
+
+    def gather_lanes(which):
+        for slot, present in ((line, line > 0), (rows, line < rows - 1)):
+
+            @pl.when(present)
+            def _():
+                lane_wait(slot, which)
+                add(piece(line, which), lane[slot, which])
 
     def merge(target):
-        mine = spot(target, column)
-        side_copy(target).wait_recv()
-        part[mine, :] = (
-            part[mine, :].astype(jnp.float32) + side[target].astype(jnp.float32)
-        ).astype(jnp.bfloat16)
-
-        def pass_on(sign):
-            @pl.when(inside(line - sign))
-            def _():
-                lane_wait(target)
-                part[mine, :] = (
-                    part[mine, :].astype(jnp.float32) + lane[target].astype(jnp.float32)
-                ).astype(jnp.bfloat16)
-
-            lane_copy(target, sign).start()
-
-        pl.when(target > line)(lambda: pass_on(1))
-        pl.when(target < line)(lambda: pass_on(-1))
+        @pl.when(both(end(target), target != line, jnp.logical_not(early(target))))
+        def _():
+            hop(target, 1)
+            hop(target, 2)
+
+        @pl.when(both(end(line), target == line))
+        def _():
+            gather_lanes(2)
+            tail_copy().start()
+
+        def add_side(count):
+            side_copy(target, count).wait_recv()
+            add(span(target, column * size, count), side[target, :count])
+
+        by_end(target, add_side)
+
+        @pl.when(target != line)
+        def _():
+            hop(target, 0)
+            pl.when(jnp.logical_not(end(target)))(lambda: hop(target, 1))
 
     @pl.loop(0, rows)
     def _(step):
         fill(step)
+
         @pl.loop(0, 2)
         def _(way):
             target = line + (2 * way - 1) * (rows - 1 - step)
-            once = step < rows - way
-            pl.when(both(once, inside(target)))(lambda: merge(target))
-
-    mine = spot(line, column)
-    out_ref[...] = part[mine, :].astype(jnp.float32)
-
-    @pl.when(line > 0)
+            pl.when(both(step < rows - way, inside(target)))(lambda: merge(target))
+
+    gather_lanes(1)
+    gather_lanes(0)
+    out_ref[...] = part[span(line, column * size, size), :].astype(jnp.float32)
+
+    @pl.when(end(line))
     def _():
-        lane_wait(line)
-        out_ref[...] += lane[line].astype(jnp.float32)
-
-    @pl.when(line < rows - 1)
-    def _():
-        lane_wait(rows)
-        out_ref[...] += lane[rows].astype(jnp.float32)
+        tail_copy().wait_recv()
+        out_ref[half:, :] += tail[...].astype(jnp.float32)
+        tail_copy().wait_send()
 
     @pl.loop(0, rows)
     def _(target):
-        side_copy(target).wait_send()
-        pl.when(target > line)(lambda: lane_copy(target, 1).wait_send())
-        pl.when(target < line)(lambda: lane_copy(target, -1).wait_send())
+        by_end(target, lambda count: side_copy(target, count).wait_send())
+
+        def sent(sign):
+            for which in (0, 1):
+                lane_copy(target, which, sign).wait_send()
+            pl.when(end(target))(lambda: lane_copy(target, 2, sign).wait_send())
+
+        pl.when(target > line)(lambda: sent(1))
+        pl.when(target < line)(lambda: sent(-1))
 
 
 def line_sems(rows):
     dma = pltpu.SemaphoreType.DMA
-    return [dma((2, rows)), dma((rows,)), dma((rows,)), dma((rows,)), dma]
+    ways, each = dma((2, rows)), dma((rows,))
+    return [ways, each, ways, each, each, each, dma((2,)), dma]
 
 
 def lane_sems(rows):
     dma = pltpu.SemaphoreType.DMA
-    return [dma((rows,)), dma((rows,)), dma((rows,)), dma((rows + 1,))]
+    return [dma((rows,)), dma((rows,)), dma((rows, 3)), dma((rows + 1, 3)), dma((2,))]
+
+
+def lane_buffers(rows, size, width):
+    return [
+        pltpu.VMEM((2 * rows * size, width), jnp.bfloat16),
+        pltpu.VMEM((rows, size, width), jnp.bfloat16),
+        pltpu.VMEM((rows + 1, 3, size // 2, width), jnp.bfloat16),
+        pltpu.VMEM((size // 2, width), jnp.bfloat16),
+    ]
 
 
 def ffn_kernel(
@@ -644,14 +793,18 @@
     w_ref,
     out_ref,
     acts_ref,
+    factors_ref,
     w,
     acts,
     hidden,
+    factors,
     part,
     side,
     lane,
+    tail,
     w_done,
     save_done,
+    factors_done,
     *sems,
 ):
     at = lax.axis_index("blk")
@@ -689,8 +842,32 @@
             hidden[target], w[2], (((0,), (0,)), ((), ())), preferred_element_type=jnp.float32
         ).astype(jnp.bfloat16)
 
-    line_gather(act_ref, acts, *sems[:5], ready, expand)
-    line_scatter(part, side, lane, out_ref, *sems[5:], reduce, lambda step: None)
+    line_gather(act_ref, acts, *sems[:8], ready, expand)
+    def factors_copy(source):
+        return pltpu.make_async_copy(
+            factors.at[source % 2],
+            factors_ref.at[:, :, pair_rows(source)],
+            factors_done.at[source % 2],
+        )
+
+    def fill(source):
+        rows_now = acts[pair_rows(source), :]
+        gate = contract_last(w[0], rows_now)
+        up = contract_last(w[1], rows_now)
+        bent = jnp.tanh(GELU_SCALE * (gate + GELU_CUBIC * gate * gate * gate))
+        slope = 0.5 * (1.0 + bent) + 0.5 * gate * (1.0 - bent * bent) * GELU_SCALE * (
+            1.0 + 3.0 * GELU_CUBIC * gate * gate
+        )
+        pl.when(source > 1)(lambda: factors_copy(source - 2).wait())
+        slot = source % 2
+        factors[slot, 0] = (up * slope).astype(jnp.bfloat16)
+        factors[slot, 1] = (0.5 * gate * (1.0 + bent)).astype(jnp.bfloat16)
+        factors[slot, 2] = hidden[source]
+        factors_copy(source).start()
+
+    line_scatter(part, side, lane, tail, out_ref, *sems[8:], reduce, fill)
+    factors_copy(rows - 2).wait()
+    factors_copy(rows - 1).wait()
     pl.loop(0, rows)(lambda source: save(source).wait())
 
 
@@ -706,18 +883,19 @@
         out_shape=(
             jax.ShapeDtypeStruct((size, width), jnp.float32),
             jax.ShapeDtypeStruct((blocks * size, width), jnp.bfloat16),
+            jax.ShapeDtypeStruct((3, units, blocks * size), jnp.bfloat16),
         ),
         in_specs=[whole, far],
-        out_specs=(whole, far),
+        out_specs=(whole, far, far),
         scratch_shapes=[
             pltpu.VMEM(w_parts.shape, jnp.bfloat16),
             pltpu.VMEM((blocks * size, width), jnp.bfloat16),
             pltpu.VMEM((rows, units, 2 * size), jnp.bfloat16),
-            pltpu.VMEM((blocks * size, width), jnp.bfloat16),
-            pltpu.VMEM((rows, size, width), jnp.bfloat16),
-            pltpu.VMEM((rows + 1, size, width), jnp.bfloat16),
+            pltpu.VMEM((2, 3, units, 2 * size), jnp.bfloat16),
+            *lane_buffers(rows, size, width),
             pltpu.SemaphoreType.DMA((3,)),
             pltpu.SemaphoreType.DMA((rows,)),
+            pltpu.SemaphoreType.DMA((2,)),
             *line_sems(rows),
             *lane_sems(rows),
         ],
@@ -730,13 +908,14 @@
 
 
 FILL_COLUMNS = 256
-FILL_FIRST = 3
+FILL_FIRST = 0
 
 
 def ffn_back_kernel(
     owners,
     grad_ref,
     acts_ref,
+    factors_ref,
     w_ref,
     out_ref,
     keep_ref,
@@ -747,11 +926,13 @@
     part,
     side,
     lane,
+    tail,
     stage,
     mate_part,
     summed,
     w_done,
     acts_done,
+    factors_done,
     mate_sent,
     mate_landed,
     summed_done,
@@ -774,30 +955,25 @@
         return pl.ds(pl.multiple_of(source * pair, pair), pair)
 
     acts_copy = pltpu.make_async_copy(acts_ref, acts, acts_done)
+    factors_copy = pltpu.make_async_copy(factors_ref, lefts, factors_done)
+    load(2).start()
+    factors_copy.start()
+    load(0).start()
+    load(1).start()
     acts_copy.start()
-    for which in range(3):
-        load(which).start()
     greet(at, at // 2, rows, mate)
 
     def ready():
-        acts_copy.wait()
-        for which in range(3):
-            load(which).wait()
+        load(2).wait()
+        factors_copy.wait()
 
     def expand(source):
         columns = pair_rows(source)
-        rows_now = acts[pair_rows(source), :]
-        gate = contract_last(w[0], rows_now)
-        up = contract_last(w[1], rows_now)
-        grad_hidden = contract_last(w[2], grads[pair_rows(source), :])
-        bent = jnp.tanh(GELU_SCALE * (gate + GELU_CUBIC * gate * gate * gate))
-        value = 0.5 * gate * (1.0 + bent)
-        slope = 0.5 * (1.0 + bent) + 0.5 * gate * (1.0 - bent * bent) * GELU_SCALE * (
-            1.0 + 3.0 * GELU_CUBIC * gate * gate
-        )
-        lefts[2, :, columns] = (value * up).astype(jnp.bfloat16)
-        lefts[0, :, columns] = (grad_hidden * up * slope).astype(jnp.bfloat16)
-        lefts[1, :, columns] = (grad_hidden * value).astype(jnp.bfloat16)
+        grad_hidden = contract_last(w[2], grads[columns, :])
+        for which in range(2):
+            lefts[which, :, columns] = (
+                lefts[which, :, columns].astype(jnp.float32) * grad_hidden
+            ).astype(jnp.bfloat16)
 
     def reduce(target):
         columns = pair_rows(target)
@@ -866,8 +1042,11 @@
         def _(item):
             pl.when(first + item < last)(lambda: fill_one(first + item))
 
-    line_gather(grad_ref, grads, *sems[:5], ready, expand)
-    line_scatter(part, side, lane, out_ref, *sems[5:], reduce, fill)
+    line_gather(grad_ref, grads, *sems[:8], ready, expand)
+    load(0).wait()
+    load(1).wait()
+    acts_copy.wait()
+    line_scatter(part, side, lane, tail, out_ref, *sems[8:], reduce, fill)
     sum_one(total_pieces - 1)
     put_wait(total_pieces - 2)
     put_wait(total_pieces - 1)
@@ -875,7 +1054,7 @@
         mate_copy(item).wait_send()
 
 
-def ffn_back(grad_ffn, acts, w_parts, owners):
+def ffn_back(grad_ffn, kept, w_parts, owners):
     size, width = grad_ffn.shape
     units = w_parts.shape[1]
     blocks = lax.axis_size("blk")
@@ -891,19 +1070,18 @@
             jax.ShapeDtypeStruct((3, units // owners, width), jnp.bfloat16),
             jax.ShapeDtypeStruct((3, units // owners, width), jnp.bfloat16),
         ),
-        in_specs=[whole, far, far],
+        in_specs=[whole, far, far, far],
         out_specs=(whole, far, far),
         scratch_shapes=[
             pltpu.VMEM(w_parts.shape, jnp.bfloat16),
             pltpu.VMEM((2, tokens, width), jnp.bfloat16),
             pltpu.VMEM((3, units, tokens), jnp.bfloat16),
-            pltpu.VMEM((tokens, width), jnp.bfloat16),
-            pltpu.VMEM((rows, size, width), jnp.bfloat16),
-            pltpu.VMEM((rows + 1, size, width), jnp.bfloat16),
+            *lane_buffers(rows, size, width),
             pltpu.VMEM((3, 2, 2, units // owners, FILL_COLUMNS), jnp.bfloat16),
             pltpu.VMEM((items, 2, units // owners, FILL_COLUMNS), jnp.bfloat16),
             pltpu.VMEM((2, 2, units // owners, FILL_COLUMNS), jnp.bfloat16),
             pltpu.SemaphoreType.DMA((3,)),
+            pltpu.SemaphoreType.DMA,
             pltpu.SemaphoreType.DMA,
             pltpu.SemaphoreType.DMA((3,)),
             pltpu.SemaphoreType.DMA((items,)),
@@ -916,7 +1094,7 @@
         ),
         cost_estimate=cost_of(115),
         name="ffn_back",
-    )(grad_ffn, acts, w_parts)
+    )(grad_ffn, *kept, w_parts)
 
 
 def ffn_hidden(acts, w_parts):
@@ -938,7 +1116,8 @@
     return (scatter_tokens(partial), acts)
 
 
-def ffn_back_wide(grad_ffn, acts, w_parts, owners):
+def ffn_back_wide(grad_ffn, kept, w_parts, owners):
+    (acts,) = kept
     grads = lax.all_gather(grad_ffn, "blk", axis=0, tiled=True)
     gate, up, hidden = ffn_hidden(acts, w_parts)
     grad_hidden = contract_last(grads, w_parts[2])
@@ -1143,6 +1322,7 @@
     part,
     side,
     lane,
+    tail,
     mine,
     from_sp,
     from_side,
@@ -1264,9 +1444,9 @@
             sp_gains(step).start()
 
     def fill(step):
-        pl.when(step == 1)(inputs_back)
-
-        @pl.when(step == 2)
+        pl.when(step == 2)(inputs_back)
+
+        @pl.when(step == 3)
         def _():
             gains = mine[...]
             for other in range(1, 4):
@@ -1282,7 +1462,7 @@
             for other in range(1, rows):
                 line_gains(other).start()
 
-    line_scatter(part, side, lane, total, *sems, reduce, fill)
+    line_scatter(part, side, lane, tail, total, *sems, reduce, fill)
     qkv_ref[...] = total[:size]
     out_ref[...] = total[size:]
     gains = from_line[0]
@@ -1326,9 +1506,7 @@
             pltpu.VMEM((4, size, cols.shape[1]), jnp.bfloat16),
             pltpu.VMEM((size, width), jnp.float32),
             pltpu.VMEM((block, width), jnp.float32),
-            pltpu.VMEM((blocks * block, width), jnp.bfloat16),
-            pltpu.VMEM((rows, block, width), jnp.bfloat16),
-            pltpu.VMEM((rows + 1, block, width), jnp.bfloat16),
+            *lane_buffers(rows, block, width),
             pltpu.VMEM(small, jnp.float32),
             pltpu.VMEM((4, *small), jnp.float32),
             pltpu.VMEM(small, jnp.float32),
@@ -1391,14 +1569,14 @@
     act_ffn = (normed_mid * gains[2]).astype(jnp.bfloat16)
     wide = lax.axis_size("blk") > 8
     w_parts = jnp.transpose(w_ffn, (1, 0, 2))
-    ffn_out, act_all = (ffn_forward_wide if wide else ffn_forward)(act_ffn, w_parts)
+    ffn_out, *kept = (ffn_forward_wide if wide else ffn_forward)(act_ffn, w_parts)
     normed_ffn, inverse_ffn = norm_parts(ffn_out)
     result = middle + normed_ffn * gains[3]
     grad_out = cotangent.astype(jnp.float32)
     grad_ffn_f, gain_grad3 = norm_back(grad_out, normed_ffn, inverse_ffn, gains[3])
     grad_ffn = grad_ffn_f.astype(jnp.bfloat16)
     grad_act_ffn, ffn_part, cross = (ffn_back_wide if wide else ffn_back)(
-        grad_ffn, act_all, w_parts, groups
+        grad_ffn, kept, w_parts, groups
     )
     grad_norm_mid, gain_grad2 = norm_back(grad_act_ffn, normed_mid, inverse_mid, gains[2])
     grad_middle = grad_out + grad_norm_mid

time: 536 us -> 529 us (0.987)
  Pallas kernels: 500 us -> 487 us
    pallas_call x1, Pallas kernels: 116 us -> 111 us  [ffn_forward(): pl.pallas_call(ffn_kernel, out_shape=(jax.ShapeDtypeStruct((size, width),...]
where the time goes in v8:
time: 529 us; the launch traced here: 523 us
  Pallas kernels  487 us (92%)
  other arithmetic  21.2 us (4%)
  local copies, waits for them, and re-layouts  13.1 us (2%)
    pallas_call x1, Pallas kernels, ffn_back(): pl.pallas_call(functools.partial(ffn_back_kernel, owners), out_shape=(jax...  117 us
    pallas_call x1, Pallas kernels, ffn_forward(): pl.pallas_call(ffn_kernel, out_shape=(jax.ShapeDtypeStruct((size, width),...  111 us
    pallas_call x1, Pallas kernels, finish(): pl.pallas_call(finish_kernel, out_shape=(jax.ShapeDtypeStruct((cols.shape...  97 us
    pallas_call x1, Pallas kernels, attend(): pl.pallas_call(functools.partial(attend_kernel, heads), out_shape=(jax.Sh...  56.2 us
    pallas_call x1, Pallas kernels, attend_back(): pl.pallas_call(functools.partial(attend_back_kernel, heads, carried), out...  53.8 us
    pallas_call x2, Pallas kernels, gather_project(): pl.pallas_call(gather_project_kernel, out_shape=(jax.ShapeDtypeStruct((4...  41.1 us
    pallas_call x1, Pallas kernels, exchange_project(): pl.pallas_call(exchange_project_kernel, out_shape=jax.ShapeDtypeStruct((s...  11.2 us

profile of v8, /device:TPU:26, one launch (start us, length us, event | category | flops | bytes accessed | tf_op | source)
XLA Modules:
  0.0 523.2 jit_solution(3541696684921542205)
XLA Ops:
  0.6 2.2 slice_reduce_fusion
  2.8 1.3 fusion.5
  4.1 2.1 fusion.7.x_ref
  6.2 21.0 %gather_project.2 = (bf16[512,2304]{1,0:T(8,128)(2,1)}, bf16[512,1024]{1,0:T(8,128)(2,1)}) custom-call(bf16[128,2304]{1,0:T(8,128)(2,1)} %fusion.7.x_ref, bf16[4096,2304]{1,0:T(8,128)(2,1)} %w_ref.7), custom_call_target="tpu_custom_call" | custom-call | flops 17999998976 | bytes 54000000 | tf_op jit(solution)/shard_map/gather_project/pallas_call | solution.py:1216
  27.1 56.2 %attend.1 = (bf16[512,512]{1,0:T(8,128)(2,1)}, f32[512,512]{1,0:T(8,128)}, f32[2,1,512]{2,1,0:T(1,128)}, bf16[8,512,512]{2,1,0:T(8,128)(2,1)}) custom-call(bf16[512,1024]{1,0:T(8,128)(2,1)} %get-tuple-element.27.x_ref.refs_0_), custom_call_target="tpu_custom_call" | custom-call | flops 49999998976 | bytes 150000000 | tf_op jit(solution)/shard_map/attend/pallas_call | solution.py:213
  83.3 0.0 copy-start.4
  83.3 11.2 %exchange_project.1 = f32[128,2304]{1,0:T(8,128)} custom-call(bf16[512,512]{1,0:T(8,128)(2,1)} %get-tuple-element.28.x_ref.att_ref, bf16[2048,2304]{1,0:T(8,128)(2,1)} %w_ref.6), custom_call_target="tpu_custom_call" | custom-call | flops 16000000000 | bytes 48000000 | tf_op jit(solution)/shard_map/exchange_project/pallas_call | solution.py:1281
  94.5 0.0 copy-start
  94.5 1.5 multiply_reduce_fusion.6
  96.1 0.0 copy-done.13
  96.1 0.0 copy-done.4
  96.1 0.1 copy-done
  96.1 0.4 multiply_reduce_fusion.5
  96.5 0.1 copy-done.22
  96.7 0.0 copy-done.15
  96.7 1.0 multiply_convert_fusion.1.act_ref
  97.7 110.8 %ffn_forward.1 = (f32[128,2304]{1,0:T(8,128)}, bf16[1024,2304]{1,0:T(8,128)(2,1)}, bf16[3,1152,1024]{2,1,0:T(8,128)(2,1)}) custom-call(bf16[128,2304]{1,0:T(8,128)(2,1)} %multiply_convert_fusion.1.act_ref, bf16[3,1152,2304]{2,1,0:T(8,128)(2,1)} %bitcast.16), custom_call_target="tpu_custom_call" | custom-call | flops 115000000512 | bytes 345000000 | tf_op jit(solution)/shard_map/ffn_forward/pallas_call | solution.py:881
  208.5 0.0 copy-done.20
  208.5 0.0 copy-start.2
  208.5 1.5 multiply_reduce_fusion.4
  210.0 0.0 copy-done.3
  210.0 0.0 copy-done.17
  210.0 0.1 copy-done.2
  210.1 1.0 fusion.8
  211.1 1.4 fusion.4
  212.5 117.5 %ffn_back.1 = (f32[128,2304]{1,0:T(8,128)}, bf16[3,288,2304]{2,1,0:T(8,128)(2,1)}, bf16[3,288,2304]{2,1,0:T(8,128)(2,1)}) custom-call(bf16[128,2304]{1,0:T(8,128)(2,1)} %get-tuple-element.61.grad_ref, bf16[1024,2304]{1,0:T(8,128)(2,1)} %get-tuple-element.30.acts_ref, bf16[3,1152,1024]{2,1,0:T(8,128)(2,1)} %get-tuple-element.31.factors_ref, ...), custom_call_target="tpu_custom_call" | custom-call | flops 115000000512 | bytes 345000000 | tf_op jit(solution)/shard_map/ffn_back/pallas_call | solution.py:1066
  330.0 0.0 copy-done.16
  330.0 0.0 copy-done.21
  330.0 0.0 copy-start.1
  330.0 0.0 copy-start.5
  330.1 0.0 copy-start.14
  330.1 0.0 copy-start.23
  330.1 1.8 multiply_reduce_fusion
  331.9 0.0 copy-done.1
  331.9 0.1 copy-done.5
  332.0 0.0 copy-done.14
  332.0 0.0 copy-done.23
  332.0 0.7 multiply_reduce_fusion.1
  332.8 1.0 copy-done.6
  333.8 1.1 multiply_convert_fusion.x_ref
  334.9 20.1 %gather_project.3 = (bf16[512,2304]{1,0:T(8,128)(2,1)}, bf16[512,512]{1,0:T(8,128)(2,1)}) custom-call(bf16[128,2304]{1,0:T(8,128)(2,1)} %multiply_convert_fusion.x_ref, bf16[2048,2304]{1,0:T(8,128)(2,1)} %w_ref.6), custom_call_target="tpu_custom_call" | custom-call | flops 17999998976 | bytes 54000000 | tf_op jit(solution)/shard_map/gather_project/pallas_call | solution.py:1216
  355.0 0.0 copy-done.19
  355.1 0.1 copy.13
  355.2 0.6 div.43
  355.8 0.0 copy-start.9
  355.9 0.1 copy.16
  355.9 1.1 copy-done.9
  357.1 0.1 copy-done.12
  357.2 1.1 convert_multiply_fusion.4
  358.3 0.7 mul.214
  359.0 0.6 reduce_sum.108
  359.6 0.1 copy.14
  359.7 0.6 reshape.69.refs_2_
  360.3 53.8 %attend_back.1 = (bf16[512,1024]{1,0:T(8,128)(2,1)}, bf16[3,144,2304]{2,1,0:T(8,128)(2,1)}) custom-call(bf16[512,1024]{1,0:T(8,128)(2,1)} %get-tuple-element.27.x_ref.refs_0_, bf16[512,512]{1,0:T(8,128)(2,1)} %get-tuple-element.64.refs_1_, f32[2,1,512]{2,1,0:T(1,128)} %reshape.69.refs_2_, bf16[8,512,512]{2,1,0:T(8,128)(2,1)} %get-tuple-element.36.refs_3_, ...), custom_call_target="tpu_custom_call" | custom-call | flops 49999998976 | bytes 150000000 | tf_op jit(solution)/shard_map/attend_back/pallas_call | solution.py:436
  414.2 0.7 stack.19.rows_ref
  414.9 97.0 %finish.1 = (f32[128,2304]{1,0:T(8,128)}, f32[64,2304]{1,0:T(8,128)}, bf16[128,2304]{1,0:T(8,128)(2,1)}, f32[8,2304]{1,0:T(8,128)}, bf16[3,144,2304]{2,1,0:T(8,128)(2,1)}) custom-call(bf16[512,1024]{1,0:T(8,128)(2,1)} %get-tuple-element.38.cols_ref, bf16[512,2304]{1,0:T(8,128)(2,1)} %get-tuple-element.39.act_ref, ...), custom_call_target="tpu_custom_call" | custom-call | flops 85000003584 | bytes 255000000 | tf_op jit(solution)/shard_map/finish/pallas_call | solution.py:1493
  511.9 0.9 slice.23
  512.8 0.6 constant_dynamic-slice_fusion
  513.5 5.5 %add_bitcast_fusion = f32[288,3,2304]{2,0,1:T(8,128)} fusion(bf16[3,288,2304]{2,1,0:T(8,128)(2,1)} %get-tuple-element.45, bf16[3,144,2304]{2,1,0:T(8,128)(2,1)} %get-tuple-element.47, bf16[3,144,2304]{2,1,0:T(8,128)(2,1)S(1)} %copy-done.7), kind=kLoop, calls=%fused_computation | loop fusion | flops 11943936 | bytes 15925248 | tf_op jit(solution)/shard_map/transpose | solution.py:1618
  519.0 0.8 copy.23
  519.8 0.7 copy-done.8
  520.5 1.0 copy.24
  521.5 0.5 copy-done.10
  521.9 0.8 copy.25
  (33 shorter events, 0.1 us)
Async XLA Ops:
  2.8 93.3 %copy-start.13 = (f32[2304]{0:T(1024)}, f32[2304]{0:T(1024)S(1)}, u32[]{:S(2)}) copy-start(f32[2304]{0:T(1024)S(1)} %get-tuple-element.56) | copy-start | bytes 27652
  2.8 93.9 %copy-start.15 = (f32[2304]{0:T(1024)}, f32[2304]{0:T(1024)S(1)}, u32[]{:S(2)}) copy-start(f32[2304]{0:T(1024)S(1)} %get-tuple-element.57) | copy-start | bytes 27652
  83.3 12.8 %copy-start.4 = (bf16[128,2304]{1,0:T(8,128)(2,1)S(1)}, bf16[128,2304]{1,0:T(8,128)(2,1)}, u32[]{:S(2)}) copy-start(bf16[128,2304]{1,0:T(8,128)(2,1)} %tokens_ref.1) | copy-start | bytes 1769476
  94.5 1.6 copy-start
  96.1 0.5 copy-start.22
  96.7 111.8 %copy-start.20 = (f32[128]{0:T(128)}, f32[128]{0:T(128)S(1)}, u32[]{:S(2)}) copy-start(f32[128]{0:T(128)S(1)} %add_rsqrt_fusion.1) | copy-start | bytes 1540
  97.7 112.4 %copy-start.3 = (bf16[128,2304]{1,0:T(8,128)(2,1)S(1)}, bf16[128,2304]{1,0:T(8,128)(2,1)}, u32[]{:S(2)}) copy-start(bf16[128,2304]{1,0:T(8,128)(2,1)} %param.11) | copy-start | bytes 1769476
  97.7 112.4 %copy-start.17 = (f32[2304]{0:T(1024)S(1)}, f32[2304]{0:T(1024)}, u32[]{:S(2)}) copy-start(f32[2304]{0:T(1024)} %get-tuple-element.54) | copy-start | bytes 27652
  208.5 1.6 copy-start.2
  212.5 117.5 %copy-start.16 = (f32[2304]{0:T(1024)S(1)}, f32[2304]{0:T(1024)}, u32[]{:S(2)}) copy-start(f32[2304]{0:T(1024)} %copy-done.15) | copy-start | bytes 27652
  212.5 117.5 %copy-start.21 = (f32[128]{0:T(128)S(1)}, f32[128]{0:T(128)}, u32[]{:S(2)}) copy-start(f32[128]{0:T(128)} %copy-done.20) | copy-start | bytes 1540
  330.0 1.9 copy-start.1
  330.0 2.0 copy-start.5
  330.1 2.0 copy-start.14
  330.1 2.0 copy-start.23
  332.8 1.0 copy-start.6
  334.9 20.2 %copy-start.19 = (f32[2,1,512]{2,1,0:T(1,128)S(1)}, f32[2,1,512]{2,1,0:T(1,128)}, u32[]{:S(2)}) copy-start(f32[2,1,512]{2,1,0:T(1,128)} %get-tuple-element.34) | copy-start | bytes 12292
  355.8 1.2 copy-start.9
  355.8 1.3 copy-start.12
  360.3 53.9 %copy-start.18 = (f32[2304]{0:T(1024)S(1)}, f32[2304]{0:T(1024)}, u32[]{:S(2)}) copy-start(f32[2304]{0:T(1024)} %get-tuple-element.52) | copy-start | bytes 27652
  414.9 98.5 %copy-start.7 = (bf16[3,144,2304]{2,1,0:T(8,128)(2,1)S(1)}, bf16[3,144,2304]{2,1,0:T(8,128)(2,1)}, u32[]{:S(2)}) copy-start(bf16[3,144,2304]{2,1,0:T(8,128)(2,1)} %get-tuple-element.46) | copy-start | bytes 5971972
  513.5 5.5 %copy-start.11 = (bf16[128,2304]{1,0:T(8,128)(2,1)S(1)}, bf16[128,2304]{1,0:T(8,128)(2,1)}, u32[]{:S(2)}) copy-start(bf16[128,2304]{1,0:T(8,128)(2,1)} %get-tuple-element.73) | copy-start | bytes 1769476
  519.0 1.5 copy-start.8
  520.5 1.5 copy-start.10

commit v9 on v8

--- a/solution.py
+++ b/solution.py
@@ -95,6 +95,7 @@
     low_ref,
     att_ref,
     tot_ref,
+    by_row_ref,
     kv_ref,
     kv,
     acc,
@@ -185,6 +186,7 @@
     for head in range(heads):
         columns = slice(head * HEAD, (head + 1) * HEAD)
         total = jnp.sum(part[head], axis=1, keepdims=True)
+        by_row_ref[head] = jnp.broadcast_to(total, by_row_ref.shape[1:])
         value = acc[:, columns] / total
         att_ref[:, columns] = value
         low_ref[:, columns] = value.astype(jnp.bfloat16)
@@ -216,10 +218,11 @@
             jax.ShapeDtypeStruct((size, heads * HEAD), jnp.bfloat16),
             jax.ShapeDtypeStruct((size, heads * HEAD), jnp.float32),
             jax.ShapeDtypeStruct((heads, 1, size), jnp.float32),
+            jax.ShapeDtypeStruct((heads, size, 128), jnp.float32),
             jax.ShapeDtypeStruct((blocks, size, 2 * HEAD), jnp.bfloat16),
         ),
         in_specs=[whole],
-        out_specs=(whole, whole, whole, pl.BlockSpec(memory_space=pl.ANY)),
+        out_specs=(whole, whole, whole, whole, pl.BlockSpec(memory_space=pl.ANY)),
         scratch_shapes=[
             pltpu.VMEM((blocks, size, 2 * HEAD), jnp.bfloat16),
             pltpu.VMEM((size, heads * HEAD), jnp.float32),
@@ -624,8 +627,8 @@
         return pl.ds(pl.multiple_of(2 * target * size + start, half), count)
 
     def piece(target, which):
-        start = ((0, 0), (0, half), (size, half))[which]
-        return span(target, column * (size - 2 * start[0]) + start[0] + start[1], half)
+        member = jnp.where(which == 2, 1 - column, column)
+        return span(target, member * size + jnp.where(which == 0, 0, half), half)
 
     def side_copy(target, count):
         return push(
@@ -676,16 +679,15 @@
         ).astype(jnp.bfloat16)
 
     def hop(target, which):
-        for sign in (1, -1):
-
-            @pl.when(target > line if sign == 1 else target < line)
-            def _():
-                @pl.when(inside(line - sign))
-                def _():
-                    lane_wait(target, which)
-                    add(piece(target, which), lane[target, which])
-
-                lane_copy(target, which, sign).start()
+        sign = jnp.where(target > line, 1, -1)
+
+        @pl.when(inside(line - sign))
+        def _():
+            lane_wait(target, which)
+            add(piece(target, which), lane[target, which])
+
+        pl.when(target > line)(lambda: lane_copy(target, which, 1).start())
+        pl.when(target < line)(lambda: lane_copy(target, which, -1).start())
 
     def early(target):
         return both(end(target), end(line), target != line)
@@ -701,15 +703,14 @@
                 work(target)
                 by_end(target, lambda count: side_copy(target, count).start())
 
-                @pl.when(early(target))
-                def _():
-                    hop(target, 1)
-                    hop(target, 2)
+                pl.when(early(target))(lambda: pl.loop(1, 3)(lambda which: hop(target, which)))
 
     def gather_lanes(which):
-        for slot, present in ((line, line > 0), (rows, line < rows - 1)):
-
-            @pl.when(present)
+        @pl.loop(0, 2)
+        def _(above):
+            slot = jnp.where(above == 0, line, rows)
+
+            @pl.when(jnp.where(above == 0, line > 0, line < rows - 1))
             def _():
                 lane_wait(slot, which)
                 add(piece(line, which), lane[slot, which])
@@ -717,24 +718,21 @@
     def merge(target):
         @pl.when(both(end(target), target != line, jnp.logical_not(early(target))))
         def _():
-            hop(target, 1)
-            hop(target, 2)
+            pl.loop(1, 3)(lambda which: hop(target, which))
 
         @pl.when(both(end(line), target == line))
         def _():
             gather_lanes(2)
             tail_copy().start()
 
-        def add_side(count):
-            side_copy(target, count).wait_recv()
-            add(span(target, column * size, count), side[target, :count])
-
-        by_end(target, add_side)
-
-        @pl.when(target != line)
-        def _():
-            hop(target, 0)
-            pl.when(jnp.logical_not(end(target)))(lambda: hop(target, 1))
+        by_end(target, lambda count: side_copy(target, count).wait_recv())
+
+        @pl.loop(0, 2)
+        def _(which):
+            @pl.when(jnp.logical_or(which == 0, jnp.logical_not(end(target))))
+            def _():
+                add(piece(target, which), side[target, pl.ds(which * half, half)])
+                pl.when(target != line)(lambda: hop(target, which))
 
     @pl.loop(0, rows)
     def _(step):
@@ -745,8 +743,7 @@
             target = line + (2 * way - 1) * (rows - 1 - step)
             pl.when(both(step < rows - way, inside(target)))(lambda: merge(target))
 
-    gather_lanes(1)
-    gather_lanes(0)
+    pl.loop(0, 2)(lambda which: gather_lanes(1 - which))
     out_ref[...] = part[span(line, column * size, size), :].astype(jnp.float32)
 
     @pl.when(end(line))
@@ -760,9 +757,9 @@
         by_end(target, lambda count: side_copy(target, count).wait_send())
 
         def sent(sign):
-            for which in (0, 1):
-                lane_copy(target, which, sign).wait_send()
-            pl.when(end(target))(lambda: lane_copy(target, 2, sign).wait_send())
+            pl.loop(0, jnp.where(end(target), 3, 2))(
+                lambda which: lane_copy(target, which, sign).wait_send()
+            )
 
         pl.when(target > line)(lambda: sent(1))
         pl.when(target < line)(lambda: sent(-1))
@@ -791,9 +788,15 @@
 def ffn_kernel(
     act_ref,
     w_ref,
-    out_ref,
+    middle_ref,
+    cotangent_ref,
+    gains_ref,
+    result_ref,
+    grad_ref,
+    row_ref,
     acts_ref,
     factors_ref,
+    out_ref,
     w,
     acts,
     hidden,
@@ -866,12 +869,19 @@
         factors_copy(source).start()
 
     line_scatter(part, side, lane, tail, out_ref, *sems[8:], reduce, fill)
+    normed, inverse = norm_parts(out_ref[...])
+    result_ref[...] = (middle_ref[...] + normed * gains_ref[3:4, :]).astype(jnp.bfloat16)
+    grad_v, gain_row = norm_back(
+        cotangent_ref[...].astype(jnp.float32), normed, inverse, gains_ref[3:4, :]
+    )
+    grad_ref[...] = grad_v.astype(jnp.bfloat16)
+    row_ref[...] = gain_row[None, :]
     factors_copy(rows - 2).wait()
     factors_copy(rows - 1).wait()
     pl.loop(0, rows)(lambda source: save(source).wait())
 
 
-def ffn_forward(act_ffn, w_parts):
+def ffn_forward(act_ffn, w_parts, middle, cotangent, gains):
     size, width = act_ffn.shape
     units = w_parts.shape[1]
     blocks = lax.axis_size("blk")
@@ -881,13 +891,16 @@
     return pl.pallas_call(
         ffn_kernel,
         out_shape=(
-            jax.ShapeDtypeStruct((size, width), jnp.float32),
+            jax.ShapeDtypeStruct((size, width), jnp.bfloat16),
+            jax.ShapeDtypeStruct((size, width), jnp.bfloat16),
+            jax.ShapeDtypeStruct((1, width), jnp.float32),
             jax.ShapeDtypeStruct((blocks * size, width), jnp.bfloat16),
             jax.ShapeDtypeStruct((3, units, blocks * size), jnp.bfloat16),
         ),
-        in_specs=[whole, far],
-        out_specs=(whole, far, far),
+        in_specs=[whole, far, whole, whole, whole],
+        out_specs=(whole, whole, whole, far, far),
         scratch_shapes=[
+            pltpu.VMEM((size, width), jnp.float32),
             pltpu.VMEM(w_parts.shape, jnp.bfloat16),
             pltpu.VMEM((blocks * size, width), jnp.bfloat16),
             pltpu.VMEM((rows, units, 2 * size), jnp.bfloat16),
@@ -904,7 +917,7 @@
         ),
         cost_estimate=cost_of(115),
         name="ffn_forward",
-    )(act_ffn, w_parts)
+    )(act_ffn, w_parts, middle, cotangent, gains)
 
 
 FILL_COLUMNS = 256
@@ -1109,11 +1122,14 @@
     ).astype(jnp.float32)
 
 
-def ffn_forward_wide(act_ffn, w_parts):
+def ffn_forward_wide(act_ffn, w_parts, middle, cotangent, gains):
     acts = lax.all_gather(act_ffn, "blk", axis=0, tiled=True)
     hidden = ffn_hidden(acts, w_parts)[2]
     partial = jnp.dot(hidden, w_parts[2], preferred_element_type=jnp.float32)
-    return (scatter_tokens(partial), acts)
+    normed, inverse = norm_parts(scatter_tokens(partial))
+    result = (middle + normed * gains[3]).astype(jnp.bfloat16)
+    grad_v, gain_row = norm_back(cotangent.astype(jnp.float32), normed, inverse, gains[3])
+    return (result, grad_v.astype(jnp.bfloat16), gain_row[None], acts)
 
 
 def ffn_back_wide(grad_ffn, kept, w_parts, owners):
@@ -1169,9 +1185,9 @@
     pl.semaphore_wait(barrier, groups - 1)
 
 
-def gather_project_kernel(x_ref, w_ref, full_ref, out_ref, w, w_done, own_done, sent, landed):
+def gather_rows(x, w_ref, full_ref, w, w_done, own_done, sent, landed, prepare, project):
     me = lax.axis_index("sp")
-    size = x_ref.shape[0]
+    size = x.shape[0]
     units = w.shape[0]
     mate = me + 1 - 2 * (me % 2)
     across = (me + 2) % 4
@@ -1183,57 +1199,152 @@
         w_ref.at[pl.ds(pl.multiple_of(me * units, units), units), :], w, w_done
     )
     load.start()
+    prepare()
     greet_sp(me, 4)
-    over = push_sp(x_ref, spot(me), sent.at[0], landed.at[0], across)
+    over = push_sp(x, spot(me), sent.at[0], landed.at[0], across)
     over.start()
-    beside = push_sp(x_ref, spot(me), sent.at[1], landed.at[1], mate)
+    beside = push_sp(x, spot(me), sent.at[1], landed.at[1], mate)
     beside.start()
-    keep = pltpu.make_async_copy(x_ref, spot(me), own_done)
+    keep = pltpu.make_async_copy(x, spot(me), own_done)
     keep.start()
     keep.wait()
     load.wait()
 
-    def project(chip):
+    def project_chip(chip):
         rows = pl.ds(pl.multiple_of(chip * 2 * size, 2 * size), 2 * size)
-        out_ref[rows, :] = contract_last(full_ref[rows, :], w[...]).astype(jnp.bfloat16)
+        project(rows, contract_last(full_ref[rows, :], w[...]).astype(jnp.bfloat16))
 
     beside.wait_recv()
-    project(me // 2)
+    project_chip(me // 2)
     over.wait_recv()
     onward = push_sp(spot(across), spot(across), sent.at[2], landed.at[2], mate)
     onward.start()
     onward.wait_recv()
-    project(across // 2)
+    project_chip(across // 2)
     over.wait_send()
     beside.wait_send()
     onward.wait_send()
 
 
-def gather_project(rows, weights, identity):
-    size, width = rows.shape
+def project_in_kernel(tokens_ref, gains_ref, w_ref, full_ref, out_ref, x, *scratch):
+    def prepare():
+        normed = norm_parts(tokens_ref[...].astype(jnp.float32))[0]
+        x[...] = (normed * gains_ref[0:1, :]).astype(jnp.bfloat16)
+
+    def project(rows, value):
+        out_ref[rows, :] = value
+
+    gather_rows(x, w_ref, full_ref, *scratch, prepare, project)
+
+
+def gather_scratch(size, width, units):
+    dma = pltpu.SemaphoreType.DMA
+    return [
+        pltpu.VMEM((size, width), jnp.bfloat16),
+        pltpu.VMEM((units, width), jnp.bfloat16),
+        dma,
+        dma,
+        dma((3,)),
+        dma((3,)),
+    ]
+
+
+def project_in(tokens, gains, weights):
+    size, width = tokens.shape
     units = weights.shape[0] // 4
     whole = pl.BlockSpec(memory_space=pltpu.VMEM)
     return pl.pallas_call(
-        gather_project_kernel,
+        project_in_kernel,
         out_shape=(
             jax.ShapeDtypeStruct((4 * size, width), jnp.bfloat16),
             jax.ShapeDtypeStruct((4 * size, units), jnp.bfloat16),
         ),
-        in_specs=[whole, pl.BlockSpec(memory_space=pl.ANY)],
+        in_specs=[whole, whole, pl.BlockSpec(memory_space=pl.ANY)],
         out_specs=(whole, whole),
-        scratch_shapes=[
-            pltpu.VMEM((units, width), jnp.bfloat16),
-            pltpu.SemaphoreType.DMA,
-            pltpu.SemaphoreType.DMA,
-            pltpu.SemaphoreType.DMA((3,)),
-            pltpu.SemaphoreType.DMA((3,)),
-        ],
+        scratch_shapes=gather_scratch(size, width, units),
         compiler_params=pltpu.CompilerParams(
-            collective_id=identity, has_side_effects=True, vmem_limit_bytes=VMEM_BYTES
+            collective_id=4, has_side_effects=True, vmem_limit_bytes=VMEM_BYTES
         ),
         cost_estimate=cost_of(18),
-        name="gather_project",
-    )(rows, weights)
+        name="project_in",
+    )(tokens, gains, weights)
+
+
+def project_back_kernel(
+    grad_ref,
+    middle_ref,
+    attn_ref,
+    cotangent_ref,
+    gains_ref,
+    attended_ref,
+    by_row_ref,
+    totals_ref,
+    w_ref,
+    full_ref,
+    scaled_ref,
+    delta_ref,
+    grad_middle_ref,
+    rows_ref,
+    x,
+    *scratch,
+):
+    def prepare():
+        grad_v, row_two = norm_back(
+            grad_ref[...], *norm_parts(middle_ref[...]), gains_ref[2:3, :]
+        )
+        grad_middle = cotangent_ref[...].astype(jnp.float32) + grad_v
+        grad_middle_ref[...] = grad_middle
+        grad_v, row_one = norm_back(grad_middle, *norm_parts(attn_ref[...]), gains_ref[1:2, :])
+        x[...] = grad_v.astype(jnp.bfloat16)
+        rows_ref[...] = jnp.zeros_like(rows_ref)
+        rows_ref[1:2, :] = row_one[None, :]
+        rows_ref[2:3, :] = row_two[None, :]
+
+    def project(rows, value):
+        for head in range(value.shape[1] // HEAD):
+            columns = slice(head * HEAD, (head + 1) * HEAD)
+            grad = value[:, columns].astype(jnp.float32)
+            scaled_ref[rows, columns] = (grad / by_row_ref[head, rows, :1]).astype(jnp.bfloat16)
+            product = grad * attended_ref[rows, columns]
+            delta_ref[head, :, rows] = (
+                jnp.sum(product.T, axis=0, keepdims=True) / totals_ref[head, :, rows]
+            )
+
+    gather_rows(x, w_ref, full_ref, *scratch, prepare, project)
+
+
+def project_back(
+    grad_act, middle, attn, cotangent, gains, attended, by_row, totals, weights
+):
+    size, width = attn.shape
+    units = weights.shape[0] // 4
+    whole = pl.BlockSpec(memory_space=pltpu.VMEM)
+    return pl.pallas_call(
+        project_back_kernel,
+        out_shape=(
+            jax.ShapeDtypeStruct((4 * size, width), jnp.bfloat16),
+            jax.ShapeDtypeStruct((4 * size, units), jnp.bfloat16),
+            jax.ShapeDtypeStruct(totals.shape, jnp.float32),
+            jax.ShapeDtypeStruct((size, width), jnp.float32),
+            jax.ShapeDtypeStruct((8, width), jnp.float32),
+        ),
+        in_specs=[whole] * 8 + [pl.BlockSpec(memory_space=pl.ANY)],
+        out_specs=(whole,) * 5,
+        scratch_shapes=gather_scratch(size, width, units),
+        compiler_params=pltpu.CompilerParams(
+            collective_id=6, has_side_effects=True, vmem_limit_bytes=VMEM_BYTES
+        ),
+        cost_estimate=cost_of(20),
+        name="project_back",
+    )(grad_act, middle, attn, cotangent, gains, attended, by_row, totals, weights)
+
+
+def exchange_norm_kernel(x_ref, w_ref, tokens_ref, gains_ref, out_ref, middle_ref, act_ref, *scratch):
+    exchange_project_kernel(x_ref, w_ref, out_ref, *scratch)
+    normed = norm_parts(out_ref[...])[0]
+    middle = tokens_ref[...].astype(jnp.float32) + normed * gains_ref[1:2, :]
+    middle_ref[...] = middle
+    act_ref[...] = (norm_parts(middle)[0] * gains_ref[2:3, :]).astype(jnp.bfloat16)
 
 
 def exchange_project_kernel(x_ref, w_ref, out_ref, w, got, w_done, own_done, sent, landed):
@@ -1275,14 +1386,17 @@
         send(step).wait_send()
 
 
-def exchange_project(columns, weights, identity):
+def exchange_project(columns, weights, identity, norm_inputs=()):
     size = columns.shape[0] // 4
     whole = pl.BlockSpec(memory_space=pltpu.VMEM)
+    total = jax.ShapeDtypeStruct((size, weights.shape[1]), jnp.float32)
+    low = jax.ShapeDtypeStruct(total.shape, jnp.bfloat16)
+    shapes = [total, total, low] if norm_inputs else [total]
     return pl.pallas_call(
-        exchange_project_kernel,
-        out_shape=jax.ShapeDtypeStruct((size, weights.shape[1]), jnp.float32),
-        in_specs=[whole, pl.BlockSpec(memory_space=pl.ANY)],
-        out_specs=whole,
+        exchange_norm_kernel if norm_inputs else exchange_project_kernel,
+        out_shape=shapes,
+        in_specs=[whole, pl.BlockSpec(memory_space=pl.ANY)] + [whole] * len(norm_inputs),
+        out_specs=[whole] * len(shapes),
         scratch_shapes=[
             pltpu.VMEM(weights.shape, jnp.bfloat16),
             pltpu.VMEM((4, size, columns.shape[1]), jnp.bfloat16),
@@ -1296,7 +1410,7 @@
         ),
         cost_estimate=cost_of(16),
         name="exchange_project",
-    )(columns, weights)
+    )(columns, weights, *norm_inputs)
 
 
 def finish_kernel(
@@ -1307,8 +1421,9 @@
     w_ref,
     tokens_ref,
     middle_ref,
-    gain_ref,
+    gains_in_ref,
     rows_ref,
+    row_three_ref,
     cross_ref,
     qkv_ref,
     out_ref,
@@ -1436,10 +1551,11 @@
             else:
                 grad_in[...] += term
         normed, inverse = norm_parts(tokens_ref[...].astype(jnp.float32))
-        grad_v, gain_row = norm_back(grad_in[...], normed, inverse, gain_ref[...])
+        grad_v, gain_row = norm_back(grad_in[...], normed, inverse, gains_in_ref[0:1, :])
         tokens_grad_ref[...] = (middle_ref[...] + grad_v).astype(jnp.bfloat16)
         mine[...] = rows_ref[...]
         mine[0:1, :] = gain_row[None, :]
+        mine[3:4, :] = row_three_ref[...]
         for step in range(1, 4):
             sp_gains(step).start()
 
@@ -1480,16 +1596,16 @@
 
 
 def finish(
-    cols, act_block, attended, grad_block, w_qkv, tokens, grad_middle, gain, gain_rows, cross
+    cols, act_block, attended, grad_block, w_qkv, tokens, grad_middle, gains, rows, row_three, cross
 ):
     blocks = lax.axis_size("blk")
-    rows = blocks // 2
+    lines = blocks // 2
     size, width = tokens.shape
     block = (cols.shape[1] + attended.shape[1]) // blocks
     whole = pl.BlockSpec(memory_space=pltpu.VMEM)
     any_space = pl.BlockSpec(memory_space=pl.ANY)
     dma = pltpu.SemaphoreType.DMA
-    small = gain_rows.shape
+    small = rows.shape
     return pl.pallas_call(
         finish_kernel,
         out_shape=(
@@ -1499,18 +1615,18 @@
             jax.ShapeDtypeStruct(small, jnp.float32),
             half_of(cross),
         ),
-        in_specs=[whole] * 4 + [any_space] + [whole] * 4 + [any_space],
+        in_specs=[whole] * 4 + [any_space] + [whole] * 5 + [any_space],
         out_specs=(whole, whole, whole, whole, any_space),
         scratch_shapes=[
             pltpu.VMEM(w_qkv.shape, jnp.bfloat16),
             pltpu.VMEM((4, size, cols.shape[1]), jnp.bfloat16),
             pltpu.VMEM((size, width), jnp.float32),
             pltpu.VMEM((block, width), jnp.float32),
-            *lane_buffers(rows, block, width),
+            *lane_buffers(lines, block, width),
             pltpu.VMEM(small, jnp.float32),
             pltpu.VMEM((4, *small), jnp.float32),
             pltpu.VMEM(small, jnp.float32),
-            pltpu.VMEM((rows, *small), jnp.float32),
+            pltpu.VMEM((lines, *small), jnp.float32),
             dma((4,)),
             dma,
             dma((4,)),
@@ -1518,18 +1634,30 @@
             dma((4,)),
             dma((4,)),
             dma((2,)),
-            dma((rows,)),
-            dma((rows,)),
+            dma((lines,)),
+            dma((lines,)),
             dma,
             dma,
-            *lane_sems(rows),
+            *lane_sems(lines),
         ],
         compiler_params=pltpu.CompilerParams(
             collective_id=8, has_side_effects=True, vmem_limit_bytes=VMEM_BYTES
         ),
         cost_estimate=cost_of(85),
         name="finish",
-    )(cols, act_block, attended, grad_block, w_qkv, tokens, grad_middle, gain, gain_rows, cross)
+    )(
+        cols,
+        act_block,
+        attended,
+        grad_block,
+        w_qkv,
+        tokens,
+        grad_middle,
+        gains,
+        rows,
+        row_three,
+        cross,
+    )
 
 
 def weight_sums_wide(left, right):
@@ -1538,12 +1666,14 @@
 
 
 def finish_wide(
-    cols, act_block, attended, grad_block, w_qkv, tokens, grad_middle, gain, gain_rows, cross
+    cols, act_block, attended, grad_block, w_qkv, tokens, grad_middle, gains, rows, row_three, cross
 ):
-    grad_act_in = exchange_project(cols, w_qkv, 7)
+    (grad_act_in,) = exchange_project(cols, w_qkv, 7)
     normed, inverse = norm_parts(tokens.astype(jnp.float32))
-    grad_v, gain_row = norm_back(grad_act_in, normed, inverse, gain)
-    gains_all = lax.psum(jnp.concatenate([gain_row[None], gain_rows[1:]]), ("blk", "sp"))
+    grad_v, gain_row = norm_back(grad_act_in, normed, inverse, gains[0])
+    gains_all = lax.psum(
+        jnp.concatenate([gain_row[None], rows[1:3], row_three, rows[4:]]), ("blk", "sp")
+    )
     return (
         weight_sums_wide(cols, act_block),
         weight_sums_wide(attended, grad_block),
@@ -1555,61 +1685,32 @@
 
 def body(tokens, w_qkv, w_out, gains, w_ffn, cotangent):
     groups = lax.axis_size("sp")
-    heads_here = HEADS // groups
-    source = tokens.astype(jnp.float32)
-    normed_in, inverse_in = norm_parts(source)
-    act_in = (normed_in * gains[0]).astype(jnp.bfloat16)
-    act_block, projected = gather_project(act_in, w_qkv, 4)
-    block_rows = projected.shape[0]
-    attended_cols, attended, totals, kv_all = attend(projected, heads_here)
-    attn = exchange_project(attended_cols, w_out, 5)
-    normed_attn, inverse_attn = norm_parts(attn)
-    middle = source + normed_attn * gains[1]
-    normed_mid, inverse_mid = norm_parts(middle)
-    act_ffn = (normed_mid * gains[2]).astype(jnp.bfloat16)
     wide = lax.axis_size("blk") > 8
+    act_block, projected = project_in(tokens, gains, w_qkv)
+    attended_low, attended, totals, by_row, kv_all = attend(projected, HEADS // groups)
+    attn, middle, act_ffn = exchange_project(attended_low, w_out, 5, (tokens, gains))
     w_parts = jnp.transpose(w_ffn, (1, 0, 2))
-    ffn_out, *kept = (ffn_forward_wide if wide else ffn_forward)(act_ffn, w_parts)
-    normed_ffn, inverse_ffn = norm_parts(ffn_out)
-    result = middle + normed_ffn * gains[3]
-    grad_out = cotangent.astype(jnp.float32)
-    grad_ffn_f, gain_grad3 = norm_back(grad_out, normed_ffn, inverse_ffn, gains[3])
-    grad_ffn = grad_ffn_f.astype(jnp.bfloat16)
+    result, grad_ffn, row_three, *kept = (ffn_forward_wide if wide else ffn_forward)(
+        act_ffn, w_parts, middle, cotangent, gains
+    )
     grad_act_ffn, ffn_part, cross = (ffn_back_wide if wide else ffn_back)(
         grad_ffn, kept, w_parts, groups
     )
-    grad_norm_mid, gain_grad2 = norm_back(grad_act_ffn, normed_mid, inverse_mid, gains[2])
-    grad_middle = grad_out + grad_norm_mid
-    grad_attn_f, gain_grad1 = norm_back(grad_middle, normed_attn, inverse_attn, gains[1])
-    grad_attn = grad_attn_f.astype(jnp.bfloat16)
-    grad_block, grad_attended = gather_project(grad_attn, w_out, 6)
-    grad_heads = grad_attended.astype(jnp.float32).reshape(block_rows, heads_here, HEAD)
-    totals_rows = jnp.transpose(totals.reshape(heads_here, block_rows))
-    scaled = (grad_heads / totals_rows[..., None]).astype(jnp.bfloat16)
-    row_delta = (
-        jnp.sum(grad_heads * attended.reshape(block_rows, heads_here, HEAD), axis=-1) / totals_rows
-    )
-    grad_cols, *far_first = attend_back(
-        projected,
-        scaled.reshape(block_rows, heads_here * HEAD),
-        jnp.transpose(row_delta).reshape(heads_here, 1, block_rows),
-        kv_all,
-        cross,
-    )
-    gain_rows = jnp.stack(
-        [jnp.zeros_like(gain_grad1), gain_grad1, gain_grad2, gain_grad3]
-        + [jnp.zeros_like(gain_grad1)] * 4
-    )
+    grad_block, scaled, delta, grad_middle, rows = project_back(
+        grad_act_ffn, middle, attn, cotangent, gains, attended, by_row, totals, w_out
+    )
+    grad_cols, *far_first = attend_back(projected, scaled, delta, kv_all, cross)
     qkv_grad, out_grad, tokens_grad, gains_all, far_last = (finish_wide if wide else finish)(
         grad_cols,
         act_block,
-        attended_cols,
+        attended_low,
         grad_block,
         w_qkv,
         tokens,
         grad_middle,
-        gains[0][None],
-        gain_rows,
+        gains,
+        rows,
+        row_three,
         cross,
     )
     ffn_sum = ffn_part.astype(jnp.float32)
@@ -1619,7 +1720,7 @@
     share = gains_all.shape[1] // (groups * lax.axis_size("blk"))
     place = lax.axis_index("sp") * lax.axis_size("blk") + lax.axis_index("blk")
     gains_grad = lax.dynamic_slice_in_dim(gains_all[:4], place * share, share, 1)
-    return (result.astype(jnp.bfloat16), tokens_grad, qkv_grad, out_grad, gains_grad, ffn_grad)
+    return (result, tokens_grad, qkv_grad, out_grad, gains_grad, ffn_grad)
 
 
 def solution(mesh):

time: 529 us -> 507 us (0.958); the launches traced: 523 us -> 507 us
  other arithmetic: 21.2 us -> 5.55 us
  Pallas kernels: 487 us -> 494 us
  local copies, waits for them, and re-layouts: 13.1 us -> 6.34 us
    reduce_sum x8 -> x0, other arithmetic: 8.88 us -> none  [the longest x4 4.72 us: norm_parts(): jnp.mean(values * values, axis=-1, keepdims=True) + NORM_EPSILON]
    convert_element_type x4 -> x0, other arithmetic: 5.63 us -> none  [the longest x1 2.09 us: body(): act_in = (normed_in * gains[0]).astype(jnp.bfloat16)]
where the time goes in v9:
time: 507 us
  Pallas kernels  494 us (97%)
  local copies, waits for them, and re-layouts  6.34 us (1%)
  other arithmetic  5.55 us (1%)
    pallas_call x1, Pallas kernels, ffn_back(): pl.pallas_call(functools.partial(ffn_back_kernel, owners), out_shape=(jax...  118 us
    pallas_call x1, Pallas kernels, ffn_forward(): pl.pallas_call(ffn_kernel, out_shape=(jax.ShapeDtypeStruct((size, width),...  112 us
    pallas_call x1, Pallas kernels, finish(): pl.pallas_call(finish_kernel, out_shape=(jax.ShapeDtypeStruct((cols.shape...  97.3 us
    pallas_call x1, Pallas kernels, attend(): pl.pallas_call(functools.partial(attend_kernel, heads), out_shape=(jax.Sh...  56.3 us
    pallas_call x1, Pallas kernels, attend_back(): pl.pallas_call(functools.partial(attend_back_kernel, heads, carried), out...  53.9 us
    pallas_call x1, Pallas kernels, project_back(): pl.pallas_call(project_back_kernel, out_shape=(jax.ShapeDtypeStruct((4 *...  23.6 us
    pallas_call x1, Pallas kernels, project_in(): pl.pallas_call(project_in_kernel, out_shape=(jax.ShapeDtypeStruct((4 * si...  21.2 us
    pallas_call x1, Pallas kernels, exchange_project(): pl.pallas_call(exchange_norm_kernel if norm_inputs else exchange_project_...  11.9 us

profile of v9, /device:TPU:26, one launch (start us, length us, event | category | flops | bytes accessed | tf_op | source)
XLA Modules:
  0.0 507.0 jit_solution(16788388119115768347)
XLA Ops:
  0.6 21.2 %project_in.1 = (bf16[512,2304]{1,0:T(8,128)(2,1)}, bf16[512,1024]{1,0:T(8,128)(2,1)}) custom-call(bf16[128,2304]{1,0:T(8,128)(2,1)} %tokens_ref.5, f32[4,2304]{1,0:T(4,128)} %gains_in_ref.1, bf16[4096,2304]{1,0:T(8,128)(2,1)} %w_ref.7), custom_call_target="tpu_custom_call" | custom-call | flops 17999998976 | bytes 54000000 | tf_op jit(solution)/shard_map/project_in/pallas_call | solution.py:1256
  21.9 56.3 %attend.1 = (bf16[512,512]{1,0:T(8,128)(2,1)}, f32[512,512]{1,0:T(8,128)}, f32[2,1,512]{2,1,0:T(1,128)}, f32[2,512,128]{2,1,0:T(8,128)}, bf16[8,512,512]{2,1,0:T(8,128)(2,1)}) custom-call(bf16[512,1024]{1,0:T(8,128)(2,1)} %get-tuple-element.36.x_ref.refs_0_), custom_call_target="tpu_custom_call" | custom-call | flops 49999998976 | bytes 150000000 | tf_op jit(solution)/shard_map/attend/pallas_call | solution.py:215
  78.2 11.9 %exchange_project.1 = (f32[128,2304]{1,0:T(8,128)}, f32[128,2304]{1,0:T(8,128)}, bf16[128,2304]{1,0:T(8,128)(2,1)}) custom-call(bf16[512,512]{1,0:T(8,128)(2,1)} %get-tuple-element.37.x_ref.att_ref, bf16[2048,2304]{1,0:T(8,128)(2,1)} %w_ref.6, bf16[128,2304]{1,0:T(8,128)(2,1)} %tokens_ref.5, f32[4,2304]{1,0:T(4,128)} %gains_in_ref.1), custom_call_target="tpu_custom_call" | custom-call | flops 16000000000 | bytes 48000000 | tf_op jit(solution)/shard_map/exchange_project/pallas_call | solution.py:1395
  90.1 112.5 %ffn_forward.1 = (bf16[128,2304]{1,0:T(8,128)(2,1)}, bf16[128,2304]{1,0:T(8,128)(2,1)}, f32[1,2304]{1,0:T(1,128)}, bf16[1024,2304]{1,0:T(8,128)(2,1)}, bf16[3,1152,1024]{2,1,0:T(8,128)(2,1)}) custom-call(bf16[128,2304]{1,0:T(8,128)(2,1)} %get-tuple-element.38.act_ref, bf16[3,1152,2304]{2,1,0:T(8,128)(2,1)} %bitcast.3, ...), custom_call_target="tpu_custom_call" | custom-call | flops 115000000512 | bytes 345000000 | tf_op jit(solution)/shard_map/ffn_forward/pallas_call | solution.py:891
  202.6 117.7 %ffn_back.1 = (f32[128,2304]{1,0:T(8,128)}, bf16[3,288,2304]{2,1,0:T(8,128)(2,1)}, bf16[3,288,2304]{2,1,0:T(8,128)(2,1)}) custom-call(bf16[128,2304]{1,0:T(8,128)(2,1)} %get-tuple-element.41.grad_ref, bf16[1024,2304]{1,0:T(8,128)(2,1)} %get-tuple-element.42.acts_ref, bf16[3,1152,1024]{2,1,0:T(8,128)(2,1)} %get-tuple-element.43.factors_ref, ...), custom_call_target="tpu_custom_call" | custom-call | flops 115000000512 | bytes 345000000 | tf_op jit(solution)/shard_map/ffn_back/pallas_call | solution.py:1079
  320.3 23.6 %project_back.1 = (bf16[512,2304]{1,0:T(8,128)(2,1)}, bf16[512,512]{1,0:T(8,128)(2,1)}, f32[2,1,512]{2,1,0:T(1,128)}, f32[128,2304]{1,0:T(8,128)}, f32[8,2304]{1,0:T(8,128)}) custom-call(f32[128,2304]{1,0:T(8,128)} %get-tuple-element.44.grad_ref, f32[128,2304]{1,0:T(8,128)} %get-tuple-element.39.middle_ref, f32[128,2304]{1,0:T(8,128)} %get-tuple-element.45.attn_ref, ...), custom_call_target="tpu_custom_call" | custom-call | flops 20000000000 | bytes 60000000 | tf_op jit(solution)/shard_map/project_back/pallas_call | solution.py:1322
  343.9 53.9 %attend_back.1 = (bf16[512,1024]{1,0:T(8,128)(2,1)}, bf16[3,144,2304]{2,1,0:T(8,128)(2,1)}) custom-call(bf16[512,1024]{1,0:T(8,128)(2,1)} %get-tuple-element.36.x_ref.refs_0_, bf16[512,512]{1,0:T(8,128)(2,1)} %get-tuple-element.49.refs_1_, f32[2,1,512]{2,1,0:T(1,128)} %get-tuple-element.50.refs_2_, bf16[8,512,512]{2,1,0:T(8,128)(2,1)} %get-tuple-element.51.refs_3_, ...), custom_call_target="tpu_custom_call" | custom-call | flops 49999998976 | bytes 150000000 | tf_op jit(solution)/shard_map/attend_back/pallas_call | solution.py:439
  397.8 0.0 copy-start
  397.8 97.3 %finish.1 = (f32[128,2304]{1,0:T(8,128)}, f32[64,2304]{1,0:T(8,128)}, bf16[128,2304]{1,0:T(8,128)(2,1)}, f32[8,2304]{1,0:T(8,128)}, bf16[3,144,2304]{2,1,0:T(8,128)(2,1)}) custom-call(bf16[512,1024]{1,0:T(8,128)(2,1)} %get-tuple-element.53.cols_ref, bf16[512,2304]{1,0:T(8,128)(2,1)} %get-tuple-element.54.act_ref, ...), custom_call_target="tpu_custom_call" | custom-call | flops 85000003584 | bytes 255000000 | tf_op jit(solution)/shard_map/finish/pallas_call | solution.py:1609
  495.1 0.0 copy-done
  495.1 0.0 copy-start.3
  495.1 0.0 copy-start.1
  495.1 5.6 %add_bitcast_fusion = f32[288,3,2304]{2,0,1:T(8,128)} fusion(bf16[3,288,2304]{2,1,0:T(8,128)(2,1)} %get-tuple-element.63, bf16[3,144,2304]{2,1,0:T(8,128)(2,1)} %get-tuple-element.65, bf16[3,144,2304]{2,1,0:T(8,128)(2,1)S(1)} %copy-done), kind=kLoop, calls=%fused_computation | loop fusion | flops 11943936 | bytes 15925248 | tf_op jit(solution)/shard_map/transpose | solution.py:1719
  500.7 0.0 copy-start.2
  500.7 0.0 copy-done.3
  500.7 0.7 constant_dynamic-slice_fusion
  501.3 1.9 copy.16
  503.3 1.9 copy.17
  505.2 0.0 copy-done.1
  505.2 1.0 copy.18
  506.2 0.0 copy-done.2
  506.2 0.8 copy.19
  (1 shorter events, 0.0 us)
Async XLA Ops:
  397.8 97.3 %copy-start = (bf16[3,144,2304]{2,1,0:T(8,128)(2,1)S(1)}, bf16[3,144,2304]{2,1,0:T(8,128)(2,1)}, u32[]{:S(2)}) copy-start(bf16[3,144,2304]{2,1,0:T(8,128)(2,1)} %get-tuple-element.64) | copy-start | bytes 5971972
  495.1 5.6 %copy-start.3 = (f32[8,2304]{1,0:T(8,128)S(1)}, f32[8,2304]{1,0:T(8,128)}, u32[]{:S(2)}) copy-start(f32[8,2304]{1,0:T(8,128)} %get-tuple-element.62) | copy-start | bytes 221188
  495.1 10.1 %copy-start.1 = (f32[128,2304]{1,0:T(8,128)S(1)}, f32[128,2304]{1,0:T(8,128)}, u32[]{:S(2)}) copy-start(f32[128,2304]{1,0:T(8,128)} %get-tuple-element.74) | copy-start | bytes 3538948
  500.7 5.5 %copy-start.2 = (f32[64,2304]{1,0:T(8,128)S(1)}, f32[64,2304]{1,0:T(8,128)}, u32[]{:S(2)}) copy-start(f32[64,2304]{1,0:T(8,128)} %get-tuple-element.75) | copy-start | bytes 1769476

commit v10 on v9

--- a/solution.py
+++ b/solution.py
@@ -13,6 +13,7 @@
 
 
 VMEM_BYTES = 62 * 1024 * 1024
+PIECES = 2
 NORM_EPSILON = 1e-06
 CAP_VALUE = 50.0
 GELU_SCALE = 0.7978845608028654
@@ -104,6 +105,8 @@
     up_landed,
     side_sent,
     side_landed,
+    extra_sent,
+    extra_landed,
     own_done,
     save_done,
 ):
@@ -117,24 +120,62 @@
     own = x_ref.at[:, pl.ds(first, 2 * HEAD)]
     greet(at, line, rows)
 
-    def up_copy(index, source):
-        return push(source, kv.at[index], up_sent.at[index // 2], up_landed.at[index // 2], at + 2)
-
-    def side_copy(index, source):
+    def halves(act):
+        pl.loop(0, PIECES)(act)
+
+    def span(piece):
+        count = size // PIECES
+        return pl.ds(pl.multiple_of(piece * count, count), count)
+
+    def source_of(index, piece, is_own):
+        if is_own:
+            return x_ref.at[span(piece), pl.ds(first, 2 * HEAD)]
+        return kv.at[index, span(piece)]
+
+    def up_copy(index, piece, is_own=False):
         return push(
-            source, kv.at[index], side_sent.at[index // 2], side_landed.at[index // 2], partner
-        )
+            source_of(index, piece, is_own),
+            kv.at[index, span(piece)],
+            up_sent.at[index // 2, piece],
+            up_landed.at[index // 2, piece],
+            at + 2,
+        )
+
+    def side_copy(index, piece, is_own=False):
+        return push(
+            source_of(index, piece, is_own),
+            kv.at[index, span(piece)],
+            side_sent.at[index // 2, piece],
+            side_landed.at[index // 2, piece],
+            partner,
+        )
+
+    def extra_copy():
+        rows_now = kv.at[0, span(PIECES - 1)]
+        return push(rows_now, rows_now, extra_sent.at[0], extra_landed.at[0], at + 2)
+
+    def crossing(index):
+        return jnp.where(both(index == 0, at > 0), PIECES - 1, PIECES)
 
     def save(index):
         return pltpu.make_async_copy(kv.at[index], kv_ref.at[index], save_done.at[index])
 
-    pl.when(line < rows - 1)(lambda: up_copy(at, own).start())
-    pl.when(column == 0)(lambda: side_copy(at, own).start())
+    @pl.loop(0, PIECES)
+    def _(piece):
+        pl.when(line < rows - 1)(lambda: up_copy(at, piece, True).start())
+        pl.when(column == 0)(lambda: side_copy(at, PIECES - 1 - piece, True).start())
+
     keep = pltpu.make_async_copy(own, kv.at[at], own_done)
     keep.start()
     acc[...] = jnp.zeros_like(acc)
     part[...] = jnp.zeros_like(part)
     keep.wait()
+
+    @pl.when(at == 1)
+    def _():
+        side_copy(0, PIECES - 1).wait_recv()
+        extra_copy().start()
+
     ahead = lax.broadcasted_iota(jnp.int32, (size, size), 1) - lax.broadcasted_iota(
         jnp.int32, (size, size), 0
     )
@@ -168,9 +209,16 @@
 
         @pl.when(both(step > 0, source >= 0))
         def _():
-            up_copy(index, kv.at[index]).wait_recv()
-            pl.when(line < rows - 1)(lambda: up_copy(index, kv.at[index]).start())
-            side_copy(index, kv.at[index]).start()
+            @pl.loop(0, PIECES)
+            def _(piece):
+                up_copy(index, piece).wait_recv()
+                pl.when(line < rows - 1)(lambda: up_copy(index, piece).start())
+                pl.when(piece < crossing(index))(lambda: side_copy(index, piece).start())
+
+        @pl.when(both(step > 0, source == 0, column == 1))
+        def _():
+            extra_copy().wait_recv()
+            pl.when(line < rows - 1)(lambda: extra_copy().start())
 
         @pl.loop(0, 2)
         def _(way):
@@ -180,7 +228,11 @@
 
             @pl.when(both(found >= 0, due))
             def _():
-                pl.when(way == 1)(lambda: side_copy(here, kv.at[here]).wait_recv())
+                pl.when(way == 1)(
+                    lambda: pl.loop(0, crossing(here))(
+                        lambda piece: side_copy(here, piece).wait_recv()
+                    )
+                )
                 compute(here)
 
     for head in range(heads):
@@ -198,10 +250,16 @@
 
         @pl.when(source <= line)
         def _():
-            pl.when(line < rows - 1)(lambda: up_copy(index, kv.at[index]).wait_send())
+            pl.when(line < rows - 1)(
+                lambda: halves(lambda piece: up_copy(index, piece).wait_send())
+            )
             pl.when(jnp.logical_or(source < line, column == 0))(
-                lambda: side_copy(index, kv.at[index]).wait_send()
+                lambda: pl.loop(0, crossing(index))(
+                    lambda piece: side_copy(index, piece).wait_send()
+                )
             )
+
+    pl.when(both(column == 1, line < rows - 1))(lambda: extra_copy().wait_send())
 
     @pl.loop(0, blocks)
     def _(index):
@@ -227,10 +285,12 @@
             pltpu.VMEM((blocks, size, 2 * HEAD), jnp.bfloat16),
             pltpu.VMEM((size, heads * HEAD), jnp.float32),
             pltpu.VMEM((heads, size, 128), jnp.float32),
-            pltpu.SemaphoreType.DMA((blocks // 2,)),
-            pltpu.SemaphoreType.DMA((blocks // 2,)),
-            pltpu.SemaphoreType.DMA((blocks // 2,)),
-            pltpu.SemaphoreType.DMA((blocks // 2,)),
+            pltpu.SemaphoreType.DMA((blocks // 2, PIECES)),
+            pltpu.SemaphoreType.DMA((blocks // 2, PIECES)),
+            pltpu.SemaphoreType.DMA((blocks // 2, PIECES)),
+            pltpu.SemaphoreType.DMA((blocks // 2, PIECES)),
+            pltpu.SemaphoreType.DMA((1,)),
+            pltpu.SemaphoreType.DMA((1,)),
             pltpu.SemaphoreType.DMA,
             pltpu.SemaphoreType.DMA((blocks,)),
         ],
@@ -304,21 +364,28 @@
     greet(at, line, rows, across)
     after_greeting()
 
-    def side_copy(target):
+    def halves(act):
+        pl.loop(0, PIECES)(act)
+
+    def span(piece):
+        count = size // PIECES
+        return pl.ds(pl.multiple_of(piece * count, count), count)
+
+    def side_copy(target, piece):
         return push(
-            part.at[target, 1 - column],
-            side.at[target],
-            side_sent.at[target],
-            side_landed.at[target],
+            part.at[target, 1 - column, span(piece)],
+            side.at[target, span(piece)],
+            side_sent.at[target, piece],
+            side_landed.at[target, piece],
             partner,
         )
 
-    def down_copy(target):
+    def down_copy(target, piece):
         return push(
-            part.at[target, column],
-            down.at[target],
-            down_sent.at[target],
-            down_landed.at[target],
+            part.at[target, column, span(piece)],
+            down.at[target, span(piece)],
+            down_sent.at[target, piece],
+            down_landed.at[target, piece],
             at - 2,
         )
 
@@ -368,25 +435,27 @@
         part[target, half, :, HEAD:] = dv[...].astype(jnp.bfloat16)
 
     def merge(target):
-        last = target == line
-
-        @pl.when(jnp.logical_or(target < line, column == 0))
-        def _():
-            side_copy(target).wait_recv()
-            part[target, column] = (
-                part[target, column].astype(jnp.float32) + side[target].astype(jnp.float32)
+        def add(piece, more):
+            part[target, column, span(piece)] = (
+                part[target, column, span(piece)].astype(jnp.float32) + more.astype(jnp.float32)
             ).astype(jnp.bfloat16)
 
-        @pl.when(line < rows - 1)
-        def _():
-            down_copy(target).wait_recv()
-            part[target, column] = (
-                part[target, column].astype(jnp.float32) + down[target].astype(jnp.float32)
-            ).astype(jnp.bfloat16)
-
-        pl.when(target < line)(lambda: down_copy(target).start())
-
-        @pl.when(last)
+        def merge_piece(piece):
+            @pl.when(jnp.logical_or(target < line, column == 0))
+            def _():
+                side_copy(target, piece).wait_recv()
+                add(piece, side[target, span(piece)])
+
+            @pl.when(line < rows - 1)
+            def _():
+                down_copy(target, piece).wait_recv()
+                add(piece, down[target, span(piece)])
+
+            pl.when(target < line)(lambda: down_copy(target, piece).start())
+
+        halves(merge_piece)
+
+        @pl.when(target == line)
         def _():
             out_ref[:, heads * HEAD :] = part[target, column]
 
@@ -399,9 +468,10 @@
             @pl.when(jnp.logical_or(both(way == 0, away), both(way == 1, target <= line)))
             def _():
                 compute(target, jnp.where(way == 0, 1 - column, column))
-                pl.when(way == 0)(lambda: side_copy(target).start())
-
-        pl.when(both(line == rows - 1, target > 0))(lambda: merge(target - 1))
+                pl.when(way == 0)(lambda: halves(lambda piece: side_copy(target, piece).start()))
+
+            pl.when(both(way == 0, line == rows - 1, target > 0))(lambda: merge(target - 1))
+
 
     out_ref[:, : heads * HEAD] = (dq[...] * HEAD ** (-0.5)).astype(jnp.bfloat16)
 
@@ -414,9 +484,9 @@
     @pl.loop(0, rows)
     def _(target):
         pl.when(jnp.logical_or(target < line, both(target == line, column == 1)))(
-            lambda: side_copy(target).wait_send()
-        )
-        pl.when(target < line)(lambda: down_copy(target).wait_send())
+            lambda: halves(lambda piece: side_copy(target, piece).wait_send())
+        )
+        pl.when(target < line)(lambda: halves(lambda piece: down_copy(target, piece).wait_send()))
 
 
 def half_of(cross):
@@ -450,10 +520,10 @@
             pltpu.VMEM((size, HEAD), jnp.float32),
             pltpu.VMEM((size, HEAD), jnp.float32),
             pltpu.SemaphoreType.DMA((blocks,)),
-            pltpu.SemaphoreType.DMA((rows,)),
-            pltpu.SemaphoreType.DMA((rows,)),
-            pltpu.SemaphoreType.DMA((rows,)),
-            pltpu.SemaphoreType.DMA((rows,)),
+            pltpu.SemaphoreType.DMA((rows, PIECES)),
+            pltpu.SemaphoreType.DMA((rows, PIECES)),
+            pltpu.SemaphoreType.DMA((rows, PIECES)),
+            pltpu.SemaphoreType.DMA((rows, PIECES)),
         ]
         + [pltpu.SemaphoreType.DMA, pltpu.SemaphoreType.DMA] * carried,
         compiler_params=pltpu.CompilerParams(
@@ -920,7 +990,7 @@
     )(act_ffn, w_parts, middle, cotangent, gains)
 
 
-FILL_COLUMNS = 256
+FILL_COLUMNS = 768
 FILL_FIRST = 0
 
 
@@ -942,7 +1012,6 @@
     tail,
     stage,
     mate_part,
-    summed,
     w_done,
     acts_done,
     factors_done,
@@ -1004,18 +1073,18 @@
 
     def mate_copy(item):
         return push_sp(
-            stage.at[item % 3, :, 1 - core],
+            stage.at[item % 2, :, 1 - core],
             mate_part.at[item],
-            mate_sent.at[item % 3],
+            mate_sent.at[item % 2],
             mate_landed.at[item],
             mate,
         )
 
     def put(item, side_chip, target):
         return pltpu.make_async_copy(
-            summed.at[item % 2, side_chip],
+            mate_part.at[item, side_chip],
             target.at[item // pieces, :, piece_columns(item)],
-            summed_done.at[item % 2, side_chip],
+            summed_done.at[item, side_chip],
         )
 
     def put_wait(item):
@@ -1023,10 +1092,9 @@
         put(item, 1 - chip, cross_ref).wait()
 
     def sum_one(item):
-        pl.when(item > 1)(lambda: put_wait(item - 2))
         mate_copy(item).wait_recv()
-        summed[item % 2] = (
-            stage[item % 3, :, core].astype(jnp.float32) + mate_part[item].astype(jnp.float32)
+        mate_part[item] = (
+            stage[item % 2, :, core].astype(jnp.float32) + mate_part[item].astype(jnp.float32)
         ).astype(jnp.bfloat16)
         put(item, chip, keep_ref).start()
         put(item, 1 - chip, cross_ref).start()
@@ -1038,8 +1106,8 @@
             rights[which // 2, :, piece_columns(item)],
             preferred_element_type=jnp.float32,
         )
-        pl.when(item > 2)(lambda: mate_copy(item - 3).wait_send())
-        stage[item % 3] = total.astype(jnp.bfloat16).reshape(
+        pl.when(item > 1)(lambda: mate_copy(item - 2).wait_send())
+        stage[item % 2] = total.astype(jnp.bfloat16).reshape(
             2, 2, units // owners, FILL_COLUMNS
         )
         mate_copy(item).start()
@@ -1061,9 +1129,8 @@
     acts_copy.wait()
     line_scatter(part, side, lane, tail, out_ref, *sems[8:], reduce, fill)
     sum_one(total_pieces - 1)
-    put_wait(total_pieces - 2)
-    put_wait(total_pieces - 1)
-    for item in range(total_pieces - 3, total_pieces):
+    pl.loop(0, total_pieces)(put_wait)
+    for item in range(total_pieces - 2, total_pieces):
         mate_copy(item).wait_send()
 
 
@@ -1090,15 +1157,14 @@
             pltpu.VMEM((2, tokens, width), jnp.bfloat16),
             pltpu.VMEM((3, units, tokens), jnp.bfloat16),
             *lane_buffers(rows, size, width),
-            pltpu.VMEM((3, 2, 2, units // owners, FILL_COLUMNS), jnp.bfloat16),
+            pltpu.VMEM((2, 2, 2, units // owners, FILL_COLUMNS), jnp.bfloat16),
             pltpu.VMEM((items, 2, units // owners, FILL_COLUMNS), jnp.bfloat16),
-            pltpu.VMEM((2, 2, units // owners, FILL_COLUMNS), jnp.bfloat16),
             pltpu.SemaphoreType.DMA((3,)),
             pltpu.SemaphoreType.DMA,
             pltpu.SemaphoreType.DMA,
-            pltpu.SemaphoreType.DMA((3,)),
+            pltpu.SemaphoreType.DMA((2,)),
             pltpu.SemaphoreType.DMA((items,)),
-            pltpu.SemaphoreType.DMA((2, 2)),
+            pltpu.SemaphoreType.DMA((items, 2)),
             *line_sems(rows),
             *lane_sems(rows),
         ],

time: 507 us -> 489 us (0.964)
  Pallas kernels: 494 us -> 475 us
    pallas_call x1, Pallas kernels: 118 us -> 110 us  [ffn_back(): pl.pallas_call(functools.partial(ffn_back_kernel, owners), out_shape=(jax...]
    pallas_call x1, Pallas kernels: 56.3 us -> 49.9 us  [attend(): pl.pallas_call(functools.partial(attend_kernel, heads), out_shape=(jax.Sh...]
    pallas_call x1, Pallas kernels: 97.3 us -> 91.9 us  [finish(): pl.pallas_call(finish_kernel, out_shape=(jax.ShapeDtypeStruct((cols.shape...]
where the time goes in v10:
time: 489 us; the launch traced here: 488 us
  Pallas kernels  475 us (97%)
  local copies, waits for them, and re-layouts  6.34 us (1%)
  other arithmetic  5.55 us (1%)
    pallas_call x1, Pallas kernels, ffn_forward(): pl.pallas_call(ffn_kernel, out_shape=(jax.ShapeDtypeStruct((size, width),...  114 us
    pallas_call x1, Pallas kernels, ffn_back(): pl.pallas_call(functools.partial(ffn_back_kernel, owners), out_shape=(jax...  110 us
    pallas_call x1, Pallas kernels, finish(): pl.pallas_call(finish_kernel, out_shape=(jax.ShapeDtypeStruct((cols.shape...  91.9 us
    pallas_call x1, Pallas kernels, attend_back(): pl.pallas_call(functools.partial(attend_back_kernel, heads, carried), out...  53.3 us
    pallas_call x1, Pallas kernels, attend(): pl.pallas_call(functools.partial(attend_kernel, heads), out_shape=(jax.Sh...  49.9 us
    pallas_call x1, Pallas kernels, project_back(): pl.pallas_call(project_back_kernel, out_shape=(jax.ShapeDtypeStruct((4 *...  23.6 us
    pallas_call x1, Pallas kernels, project_in(): pl.pallas_call(project_in_kernel, out_shape=(jax.ShapeDtypeStruct((4 * si...  21.2 us
    pallas_call x1, Pallas kernels, exchange_project(): pl.pallas_call(exchange_norm_kernel if norm_inputs else exchange_project_...  11.9 us

profile of v10, /device:TPU:26, one launch (start us, length us, event | category | flops | bytes accessed | tf_op | source)
XLA Modules:
  0.0 488.0 jit_solution(10958103749861691019)
XLA Ops:
  0.6 21.2 %project_in.1 = (bf16[512,2304]{1,0:T(8,128)(2,1)}, bf16[512,1024]{1,0:T(8,128)(2,1)}) custom-call(bf16[128,2304]{1,0:T(8,128)(2,1)} %tokens_ref.5, f32[4,2304]{1,0:T(4,128)} %gains_in_ref.1, bf16[4096,2304]{1,0:T(8,128)(2,1)} %w_ref.7), custom_call_target="tpu_custom_call" | custom-call | flops 17999998976 | bytes 54000000 | tf_op jit(solution)/shard_map/project_in/pallas_call | solution.py:1322
  21.9 49.9 %attend.1 = (bf16[512,512]{1,0:T(8,128)(2,1)}, f32[512,512]{1,0:T(8,128)}, f32[2,1,512]{2,1,0:T(1,128)}, f32[2,512,128]{2,1,0:T(8,128)}, bf16[8,512,512]{2,1,0:T(8,128)(2,1)}) custom-call(bf16[512,1024]{1,0:T(8,128)(2,1)} %get-tuple-element.36.x_ref.refs_0_), custom_call_target="tpu_custom_call" | custom-call | flops 49999998976 | bytes 150000000 | tf_op jit(solution)/shard_map/attend/pallas_call | solution.py:273
  71.8 11.9 %exchange_project.1 = (f32[128,2304]{1,0:T(8,128)}, f32[128,2304]{1,0:T(8,128)}, bf16[128,2304]{1,0:T(8,128)(2,1)}) custom-call(bf16[512,512]{1,0:T(8,128)(2,1)} %get-tuple-element.37.x_ref.att_ref, bf16[2048,2304]{1,0:T(8,128)(2,1)} %w_ref.6, bf16[128,2304]{1,0:T(8,128)(2,1)} %tokens_ref.5, f32[4,2304]{1,0:T(4,128)} %gains_in_ref.1), custom_call_target="tpu_custom_call" | custom-call | flops 16000000000 | bytes 48000000 | tf_op jit(solution)/shard_map/exchange_project/pallas_call | solution.py:1461
  83.6 113.5 %ffn_forward.1 = (bf16[128,2304]{1,0:T(8,128)(2,1)}, bf16[128,2304]{1,0:T(8,128)(2,1)}, f32[1,2304]{1,0:T(1,128)}, bf16[1024,2304]{1,0:T(8,128)(2,1)}, bf16[3,1152,1024]{2,1,0:T(8,128)(2,1)}) custom-call(bf16[128,2304]{1,0:T(8,128)(2,1)} %get-tuple-element.38.act_ref, bf16[3,1152,2304]{2,1,0:T(8,128)(2,1)} %bitcast.3, ...), custom_call_target="tpu_custom_call" | custom-call | flops 115000000512 | bytes 345000000 | tf_op jit(solution)/shard_map/ffn_forward/pallas_call | solution.py:961
  197.2 110.0 %ffn_back.1 = (f32[128,2304]{1,0:T(8,128)}, bf16[3,288,2304]{2,1,0:T(8,128)(2,1)}, bf16[3,288,2304]{2,1,0:T(8,128)(2,1)}) custom-call(bf16[128,2304]{1,0:T(8,128)(2,1)} %get-tuple-element.41.grad_ref, bf16[1024,2304]{1,0:T(8,128)(2,1)} %get-tuple-element.42.acts_ref, bf16[3,1152,1024]{2,1,0:T(8,128)(2,1)} %get-tuple-element.43.factors_ref, ...), custom_call_target="tpu_custom_call" | custom-call | flops 115000000512 | bytes 345000000 | tf_op jit(solution)/shard_map/ffn_back/pallas_call | solution.py:1146
  307.2 23.6 %project_back.1 = (bf16[512,2304]{1,0:T(8,128)(2,1)}, bf16[512,512]{1,0:T(8,128)(2,1)}, f32[2,1,512]{2,1,0:T(1,128)}, f32[128,2304]{1,0:T(8,128)}, f32[8,2304]{1,0:T(8,128)}) custom-call(f32[128,2304]{1,0:T(8,128)} %get-tuple-element.44.grad_ref, f32[128,2304]{1,0:T(8,128)} %get-tuple-element.39.middle_ref, f32[128,2304]{1,0:T(8,128)} %get-tuple-element.45.attn_ref, ...), custom_call_target="tpu_custom_call" | custom-call | flops 20000000000 | bytes 60000000 | tf_op jit(solution)/shard_map/project_back/pallas_call | solution.py:1388
  330.8 53.3 %attend_back.1 = (bf16[512,1024]{1,0:T(8,128)(2,1)}, bf16[3,144,2304]{2,1,0:T(8,128)(2,1)}) custom-call(bf16[512,1024]{1,0:T(8,128)(2,1)} %get-tuple-element.36.x_ref.refs_0_, bf16[512,512]{1,0:T(8,128)(2,1)} %get-tuple-element.49.refs_1_, f32[2,1,512]{2,1,0:T(1,128)} %get-tuple-element.50.refs_2_, bf16[8,512,512]{2,1,0:T(8,128)(2,1)} %get-tuple-element.51.refs_3_, ...), custom_call_target="tpu_custom_call" | custom-call | flops 49999998976 | bytes 150000000 | tf_op jit(solution)/shard_map/attend_back/pallas_call | solution.py:509
  384.1 0.0 copy-start
  384.1 91.9 %finish.1 = (f32[128,2304]{1,0:T(8,128)}, f32[64,2304]{1,0:T(8,128)}, bf16[128,2304]{1,0:T(8,128)(2,1)}, f32[8,2304]{1,0:T(8,128)}, bf16[3,144,2304]{2,1,0:T(8,128)(2,1)}) custom-call(bf16[512,1024]{1,0:T(8,128)(2,1)} %get-tuple-element.53.cols_ref, bf16[512,2304]{1,0:T(8,128)(2,1)} %get-tuple-element.54.act_ref, ...), custom_call_target="tpu_custom_call" | custom-call | flops 85000003584 | bytes 255000000 | tf_op jit(solution)/shard_map/finish/pallas_call | solution.py:1675
  476.0 0.0 copy-done
  476.0 0.0 copy-start.3
  476.1 0.0 copy-start.1
  476.1 5.6 %add_bitcast_fusion = f32[288,3,2304]{2,0,1:T(8,128)} fusion(bf16[3,288,2304]{2,1,0:T(8,128)(2,1)} %get-tuple-element.63, bf16[3,144,2304]{2,1,0:T(8,128)(2,1)} %get-tuple-element.65, bf16[3,144,2304]{2,1,0:T(8,128)(2,1)S(1)} %copy-done), kind=kLoop, calls=%fused_computation | loop fusion | flops 11943936 | bytes 15925248 | tf_op jit(solution)/shard_map/transpose | solution.py:1785
  481.6 0.0 copy-start.2
  481.6 0.0 copy-done.3
  481.6 0.7 constant_dynamic-slice_fusion
  482.3 1.9 copy.16
  484.2 1.9 copy.17
  486.1 0.0 copy-done.1
  486.1 1.0 copy.18
  487.1 0.0 copy-done.2
  487.1 0.8 copy.19
  (1 shorter events, 0.0 us)
Async XLA Ops:
  384.1 91.9 %copy-start = (bf16[3,144,2304]{2,1,0:T(8,128)(2,1)S(1)}, bf16[3,144,2304]{2,1,0:T(8,128)(2,1)}, u32[]{:S(2)}) copy-start(bf16[3,144,2304]{2,1,0:T(8,128)(2,1)} %get-tuple-element.64) | copy-start | bytes 5971972
  476.0 5.6 %copy-start.3 = (f32[8,2304]{1,0:T(8,128)S(1)}, f32[8,2304]{1,0:T(8,128)}, u32[]{:S(2)}) copy-start(f32[8,2304]{1,0:T(8,128)} %get-tuple-element.62) | copy-start | bytes 221188
  476.1 10.1 %copy-start.1 = (f32[128,2304]{1,0:T(8,128)S(1)}, f32[128,2304]{1,0:T(8,128)}, u32[]{:S(2)}) copy-start(f32[128,2304]{1,0:T(8,128)} %get-tuple-element.74) | copy-start | bytes 3538948
  481.6 5.5 %copy-start.2 = (f32[64,2304]{1,0:T(8,128)S(1)}, f32[64,2304]{1,0:T(8,128)}, u32[]{:S(2)}) copy-start(f32[64,2304]{1,0:T(8,128)} %get-tuple-element.75) | copy-start | bytes 1769476

commit v11 on v10

--- a/solution.py
+++ b/solution.py
@@ -346,6 +346,8 @@
     side_landed,
     down_sent,
     down_landed,
+    extra,
+    extra_done,
 ):
     at = lax.axis_index("blk")
     blocks = lax.axis_size("blk")
@@ -388,6 +390,26 @@
             down_landed.at[target, piece],
             at - 2,
         )
+
+    def extra_copy():
+        return push(
+            part.at[0, 0, span(PIECES - 1)], extra, extra_done.at[0], extra_done.at[1], at - 2
+        )
+
+    def crossing(target, receives):
+        fewer = both(target == 0, line > 0, column == (0 if receives else 1))
+        return jnp.where(fewer, PIECES - 1, PIECES)
+
+    def extra_step():
+        @pl.when(line < rows - 1)
+        def _():
+            extra_copy().wait_recv()
+            part[0, 0, span(PIECES - 1)] = (
+                part[0, 0, span(PIECES - 1)].astype(jnp.float32) + extra[...].astype(jnp.float32)
+            ).astype(jnp.bfloat16)
+
+        pl.when(line > 0)(lambda: extra_copy().start())
+        pl.when(line == 0)(lambda: side_copy(0, PIECES - 1).start())
 
     dq[...] = jnp.zeros_like(dq)
     ahead = lax.broadcasted_iota(jnp.int32, (size, size), 0) - lax.broadcasted_iota(
@@ -441,7 +463,9 @@
             ).astype(jnp.bfloat16)
 
         def merge_piece(piece):
-            @pl.when(jnp.logical_or(target < line, column == 0))
+            meets = jnp.logical_or(target < line, column == 0)
+
+            @pl.when(both(meets, piece < crossing(target, True)))
             def _():
                 side_copy(target, piece).wait_recv()
                 add(piece, side[target, span(piece)])
@@ -453,6 +477,7 @@
 
             pl.when(target < line)(lambda: down_copy(target, piece).start())
 
+        pl.when(both(column == 1, target == 0, line == 0))(extra_step)
         halves(merge_piece)
 
         @pl.when(target == line)
@@ -468,7 +493,13 @@
             @pl.when(jnp.logical_or(both(way == 0, away), both(way == 1, target <= line)))
             def _():
                 compute(target, jnp.where(way == 0, 1 - column, column))
-                pl.when(way == 0)(lambda: halves(lambda piece: side_copy(target, piece).start()))
+
+                @pl.when(way == 0)
+                def _():
+                    now = jnp.where(at == 1, PIECES - 1, crossing(target, False))
+                    pl.loop(0, now)(lambda piece: side_copy(target, piece).start())
+                    due = jnp.where(line == rows - 1, target == 0, both(target == 1, line > 0))
+                    pl.when(both(column == 1, due))(extra_step)
 
             pl.when(both(way == 0, line == rows - 1, target > 0))(lambda: merge(target - 1))
 
@@ -484,9 +515,13 @@
     @pl.loop(0, rows)
     def _(target):
         pl.when(jnp.logical_or(target < line, both(target == line, column == 1)))(
-            lambda: halves(lambda piece: side_copy(target, piece).wait_send())
+            lambda: pl.loop(0, crossing(target, False))(
+                lambda piece: side_copy(target, piece).wait_send()
+            )
         )
         pl.when(target < line)(lambda: halves(lambda piece: down_copy(target, piece).wait_send()))
+
+    pl.when(both(column == 1, line > 0))(lambda: extra_copy().wait_send())
 
 
 def half_of(cross):
@@ -524,6 +559,8 @@
             pltpu.SemaphoreType.DMA((rows, PIECES)),
             pltpu.SemaphoreType.DMA((rows, PIECES)),
             pltpu.SemaphoreType.DMA((rows, PIECES)),
+            pltpu.VMEM((size // PIECES, 2 * HEAD), jnp.bfloat16),
+            pltpu.SemaphoreType.DMA((2,)),
         ]
         + [pltpu.SemaphoreType.DMA, pltpu.SemaphoreType.DMA] * carried,
         compiler_params=pltpu.CompilerParams(
@@ -1267,9 +1304,28 @@
     load.start()
     prepare()
     greet_sp(me, 4)
-    over = push_sp(x, spot(me), sent.at[0], landed.at[0], across)
-    over.start()
-    beside = push_sp(x, spot(me), sent.at[1], landed.at[1], mate)
+    half = size // 2
+
+    def half_spot(member, piece):
+        start = pl.multiple_of(member * size + piece * half, half)
+        return full_ref.at[pl.ds(start, half), :]
+
+    def over(piece):
+        return push_sp(
+            x.at[pl.ds(piece * half, half)],
+            half_spot(me, piece),
+            sent.at[piece],
+            landed.at[piece],
+            across,
+        )
+
+    def onward(piece):
+        rows_now = half_spot(across, piece)
+        return push_sp(rows_now, rows_now, sent.at[3 + piece], landed.at[3 + piece], mate)
+
+    over(0).start()
+    over(1).start()
+    beside = push_sp(x, spot(me), sent.at[2], landed.at[2], mate)
     beside.start()
     keep = pltpu.make_async_copy(x, spot(me), own_done)
     keep.start()
@@ -1282,14 +1338,16 @@
 
     beside.wait_recv()
     project_chip(me // 2)
-    over.wait_recv()
-    onward = push_sp(spot(across), spot(across), sent.at[2], landed.at[2], mate)
-    onward.start()
-    onward.wait_recv()
+    for piece in range(2):
+        over(piece).wait_recv()
+        onward(piece).start()
+    for piece in range(2):
+        onward(piece).wait_recv()
     project_chip(across // 2)
-    over.wait_send()
     beside.wait_send()
-    onward.wait_send()
+    for piece in range(2):
+        over(piece).wait_send()
+        onward(piece).wait_send()
 
 
 def project_in_kernel(tokens_ref, gains_ref, w_ref, full_ref, out_ref, x, *scratch):
@@ -1310,8 +1368,8 @@
         pltpu.VMEM((units, width), jnp.bfloat16),
         dma,
         dma,
-        dma((3,)),
-        dma((3,)),
+        dma((5,)),
+        dma((5,)),
     ]
 
 
@@ -1749,6 +1807,40 @@
     )
 
 
+def deliver_kernel(*refs):
+    keep_ref, first_ref, last_ref, *others = refs
+    ins, sum_ref, outs = others[:4], others[4], others[5:]
+    half = first_ref.shape[1]
+    for start, far_ref in ((0, first_ref), (half, last_ref)):
+        rows = slice(start, start + half)
+        sum_ref[:, rows] = keep_ref[:, rows].astype(jnp.float32) + far_ref[...].astype(
+            jnp.float32
+        )
+    for source, target in zip(ins, outs):
+        target[...] = source[...]
+
+
+def deliver(keep, first, last, *results):
+    kinds, units, width = keep.shape
+    copies = [
+        pl.BlockSpec((result.shape[0] // 2, width), lambda i: (jnp.minimum(i, 1), 0))
+        for result in results
+    ]
+    sums = pl.BlockSpec((1, units, width), lambda i: (i, 0, 0))
+    halves = pl.BlockSpec((1, units // 2, width), lambda i: (i, 0, 0))
+    return pl.pallas_call(
+        deliver_kernel,
+        grid=(kinds,),
+        out_shape=[jax.ShapeDtypeStruct(keep.shape, jnp.float32)]
+        + [jax.ShapeDtypeStruct(result.shape, result.dtype) for result in results],
+        in_specs=[sums, halves, halves] + copies,
+        out_specs=[sums] + copies,
+        compiler_params=pltpu.CompilerParams(vmem_limit_bytes=VMEM_BYTES),
+        cost_estimate=cost_of(8),
+        name="deliver",
+    )(keep, first, last, *results)
+
+
 def body(tokens, w_qkv, w_out, gains, w_ffn, cotangent):
     groups = lax.axis_size("sp")
     wide = lax.axis_size("blk") > 8
@@ -1779,9 +1871,12 @@
         row_three,
         cross,
     )
-    ffn_sum = ffn_part.astype(jnp.float32)
-    if not wide:
-        ffn_sum = ffn_sum + jnp.concatenate([*far_first, far_last], axis=1).astype(jnp.float32)
+    if wide:
+        ffn_sum = ffn_part.astype(jnp.float32)
+    else:
+        ffn_sum, result, tokens_grad, qkv_grad, out_grad = deliver(
+            ffn_part, *far_first, far_last, result, tokens_grad, qkv_grad, out_grad
+        )
     ffn_grad = jnp.transpose(ffn_sum, (1, 0, 2))
     share = gains_all.shape[1] // (groups * lax.axis_size("blk"))
     place = lax.axis_index("sp") * lax.axis_size("blk") + lax.axis_index("blk")

time: 489 us -> 482 us (0.986)
  local copies, waits for them, and re-layouts: 6.34 us -> 0.67 us
  other arithmetic: 5.55 us -> 0 us
  Pallas kernels: 475 us -> 480 us
    pallas_call x0 -> x1, Pallas kernels: none -> 8.69 us  [deliver(): pl.pallas_call(deliver_kernel, grid=(kinds,), out_shape=[jax.ShapeDtypeSt...]
    unnamed x12 -> x2, local copies, waits for them, and re-layouts: 5.68 us -> 0.01 us
    transpose x1 -> x0, other arithmetic: 5.55 us -> none  [body(): ffn_grad = jnp.transpose(ffn_sum, (1, 0, 2))]
where the time goes in v11:
time: 482 us; the launch traced here: 481 us
  Pallas kernels  480 us (100%)
    pallas_call x1, Pallas kernels, ffn_forward(): pl.pallas_call(ffn_kernel, out_shape=(jax.ShapeDtypeStruct((size, width),...  114 us
    pallas_call x1, Pallas kernels, ffn_back(): pl.pallas_call(functools.partial(ffn_back_kernel, owners), out_shape=(jax...  110 us
    pallas_call x1, Pallas kernels, finish(): pl.pallas_call(finish_kernel, out_shape=(jax.ShapeDtypeStruct((cols.shape...  92.4 us
    pallas_call x1, Pallas kernels, attend(): pl.pallas_call(functools.partial(attend_kernel, heads), out_shape=(jax.Sh...  49.9 us
    pallas_call x1, Pallas kernels, attend_back(): pl.pallas_call(functools.partial(attend_back_kernel, heads, carried), out...  49.4 us
    pallas_call x1, Pallas kernels, project_back(): pl.pallas_call(project_back_kernel, out_shape=(jax.ShapeDtypeStruct((4 *...  23.3 us
    pallas_call x1, Pallas kernels, project_in(): pl.pallas_call(project_in_kernel, out_shape=(jax.ShapeDtypeStruct((4 * si...  20.8 us
    pallas_call x1, Pallas kernels, exchange_project(): pl.pallas_call(exchange_norm_kernel if norm_inputs else exchange_project_...  11.9 us

profile of v11, /device:TPU:26, one launch (start us, length us, event | category | flops | bytes accessed | tf_op | source)
XLA Modules:
  0.0 481.3 jit_solution(2076714949705901949)
XLA Ops:
  0.6 20.8 %project_in.1 = (bf16[512,2304]{1,0:T(8,128)(2,1)}, bf16[512,1024]{1,0:T(8,128)(2,1)}) custom-call(bf16[128,2304]{1,0:T(8,128)(2,1)} %tokens_ref.5, f32[4,2304]{1,0:T(4,128)} %gains_in_ref.1, bf16[4096,2304]{1,0:T(8,128)(2,1)} %w_ref.7), custom_call_target="tpu_custom_call" | custom-call | flops 17999998976 | bytes 54000000 | tf_op jit(solution)/shard_map/project_in/pallas_call | solution.py:1380
  21.5 49.9 %attend.1 = (bf16[512,512]{1,0:T(8,128)(2,1)}, f32[512,512]{1,0:T(8,128)}, f32[2,1,512]{2,1,0:T(1,128)}, f32[2,512,128]{2,1,0:T(8,128)}, bf16[8,512,512]{2,1,0:T(8,128)(2,1)}) custom-call(bf16[512,1024]{1,0:T(8,128)(2,1)} %get-tuple-element.41.x_ref.refs_0_), custom_call_target="tpu_custom_call" | custom-call | flops 49999998976 | bytes 150000000 | tf_op jit(solution)/shard_map/attend/pallas_call | solution.py:273
  71.4 11.9 %exchange_project.1 = (f32[128,2304]{1,0:T(8,128)}, f32[128,2304]{1,0:T(8,128)}, bf16[128,2304]{1,0:T(8,128)(2,1)}) custom-call(bf16[512,512]{1,0:T(8,128)(2,1)} %get-tuple-element.42.x_ref.att_ref, bf16[2048,2304]{1,0:T(8,128)(2,1)} %w_ref.6, bf16[128,2304]{1,0:T(8,128)(2,1)} %tokens_ref.5, f32[4,2304]{1,0:T(4,128)} %gains_in_ref.1), custom_call_target="tpu_custom_call" | custom-call | flops 16000000000 | bytes 48000000 | tf_op jit(solution)/shard_map/exchange_project/pallas_call | solution.py:1519
  83.3 113.6 %ffn_forward.1 = (bf16[128,2304]{1,0:T(8,128)(2,1)}, bf16[128,2304]{1,0:T(8,128)(2,1)}, f32[1,2304]{1,0:T(1,128)}, bf16[1024,2304]{1,0:T(8,128)(2,1)}, bf16[3,1152,1024]{2,1,0:T(8,128)(2,1)}) custom-call(bf16[128,2304]{1,0:T(8,128)(2,1)} %get-tuple-element.43.act_ref, bf16[3,1152,2304]{2,1,0:T(8,128)(2,1)} %bitcast.2, ...), custom_call_target="tpu_custom_call" | custom-call | flops 115000000512 | bytes 345000000 | tf_op jit(solution)/shard_map/ffn_forward/pallas_call | solution.py:998
  196.8 110.0 %ffn_back.1 = (f32[128,2304]{1,0:T(8,128)}, bf16[3,288,2304]{2,1,0:T(8,128)(2,1)}, bf16[3,288,2304]{2,1,0:T(8,128)(2,1)}) custom-call(bf16[128,2304]{1,0:T(8,128)(2,1)} %get-tuple-element.45.grad_ref, bf16[1024,2304]{1,0:T(8,128)(2,1)} %get-tuple-element.46.acts_ref, bf16[3,1152,1024]{2,1,0:T(8,128)(2,1)} %get-tuple-element.47.factors_ref, ...), custom_call_target="tpu_custom_call" | custom-call | flops 115000000512 | bytes 345000000 | tf_op jit(solution)/shard_map/ffn_back/pallas_call | solution.py:1183
  306.9 23.3 %project_back.1 = (bf16[512,2304]{1,0:T(8,128)(2,1)}, bf16[512,512]{1,0:T(8,128)(2,1)}, f32[2,1,512]{2,1,0:T(1,128)}, f32[128,2304]{1,0:T(8,128)}, f32[8,2304]{1,0:T(8,128)}) custom-call(f32[128,2304]{1,0:T(8,128)} %get-tuple-element.49.grad_ref, f32[128,2304]{1,0:T(8,128)} %get-tuple-element.44.middle_ref, f32[128,2304]{1,0:T(8,128)} %get-tuple-element.50.attn_ref, ...), custom_call_target="tpu_custom_call" | custom-call | flops 20000000000 | bytes 60000000 | tf_op jit(solution)/shard_map/project_back/pallas_call | solution.py:1446
  330.2 49.4 %attend_back.1 = (bf16[512,1024]{1,0:T(8,128)(2,1)}, bf16[3,144,2304]{2,1,0:T(8,128)(2,1)}) custom-call(bf16[512,1024]{1,0:T(8,128)(2,1)} %get-tuple-element.41.x_ref.refs_0_, bf16[512,512]{1,0:T(8,128)(2,1)} %get-tuple-element.54.refs_1_, f32[2,1,512]{2,1,0:T(1,128)} %get-tuple-element.55.refs_2_, bf16[8,512,512]{2,1,0:T(8,128)(2,1)} %get-tuple-element.56.refs_3_, ...), custom_call_target="tpu_custom_call" | custom-call | flops 49999998976 | bytes 150000000 | tf_op jit(solution)/shard_map/attend_back/pallas_call | solution.py:544
  379.5 92.4 %finish.1 = (f32[128,2304]{1,0:T(8,128)}, f32[64,2304]{1,0:T(8,128)}, bf16[128,2304]{1,0:T(8,128)(2,1)}, f32[8,2304]{1,0:T(8,128)}, bf16[3,144,2304]{2,1,0:T(8,128)(2,1)}) custom-call(bf16[512,1024]{1,0:T(8,128)(2,1)} %get-tuple-element.59.cols_ref, bf16[512,2304]{1,0:T(8,128)(2,1)} %get-tuple-element.60.act_ref, ...), custom_call_target="tpu_custom_call" | custom-call | flops 85000003584 | bytes 255000000 | tf_op jit(solution)/shard_map/finish/pallas_call | solution.py:1733
  471.9 0.0 copy-start
  471.9 8.7 %deliver.1 = (f32[3,288,2304]{2,1,0:T(8,128)}, bf16[128,2304]{1,0:T(8,128)(2,1)}, bf16[128,2304]{1,0:T(8,128)(2,1)}, f32[128,2304]{1,0:T(8,128)}, f32[64,2304]{1,0:T(8,128)}) custom-call(bf16[3,288,2304]{2,1,0:T(8,128)(2,1)} %get-tuple-element.48.refs_0_, bf16[3,144,2304]{2,1,0:T(8,128)(2,1)} %get-tuple-element.58.refs_1_, ...), custom_call_target="tpu_custom_call" | custom-call | flops 8000000000 | bytes 24000000 | tf_op jit(solution)/shard_map/deliver/pallas_call | solution.py:1831
  480.6 0.0 copy-done
  480.7 0.7 constant_dynamic-slice_fusion
  (1 shorter events, 0.0 us)
Async XLA Ops:
  471.9 8.7 %copy-start = (f32[8,2304]{1,0:T(8,128)S(1)}, f32[8,2304]{1,0:T(8,128)}, u32[]{:S(2)}) copy-start(f32[8,2304]{1,0:T(8,128)} %get-tuple-element.74) | copy-start | bytes 221188

commit v12 on v11

--- a/solution.py
+++ b/solution.py
@@ -722,6 +722,7 @@
     tail_done,
     work,
     fill,
+    split=False,
 ):
     at = lax.axis_index("blk")
     rows = lax.axis_size("blk") // 2
@@ -737,12 +738,13 @@
         member = jnp.where(which == 2, 1 - column, column)
         return span(target, member * size + jnp.where(which == 0, 0, half), half)
 
-    def side_copy(target, count):
+    def side_copy(target, which, count):
+        start = which * half
         return push(
-            part.at[span(target, (1 - column) * size, count), :],
-            side.at[target, :count],
-            side_sent.at[target],
-            side_landed.at[target],
+            part.at[span(target, (1 - column) * size + start, count), :],
+            side.at[target, pl.ds(start, count)],
+            side_sent.at[target, which],
+            side_landed.at[target, which],
             partner,
         )
 
@@ -776,9 +778,15 @@
     def end(row):
         return jnp.logical_or(row == 0, row == rows - 1)
 
-    def by_end(target, act):
-        pl.when(end(target))(lambda: act(half))
-        pl.when(jnp.logical_not(end(target)))(lambda: act(size))
+    def sides(target, act):
+        pl.when(end(target))(lambda: act(side_copy(target, 0, half)))
+
+        @pl.when(jnp.logical_not(end(target)))
+        def _():
+            if split:
+                pl.loop(0, 2)(lambda which: act(side_copy(target, which, half)))
+            else:
+                act(side_copy(target, 0, size))
 
     def add(where, more):
         part[where, :] = (
@@ -808,7 +816,7 @@
             @pl.when(both(step < rows - way, inside(target)))
             def _():
                 work(target)
-                by_end(target, lambda count: side_copy(target, count).start())
+                sides(target, lambda copy: copy.start())
 
                 pl.when(early(target))(lambda: pl.loop(1, 3)(lambda which: hop(target, which)))
 
@@ -832,12 +840,15 @@
             gather_lanes(2)
             tail_copy().start()
 
-        by_end(target, lambda count: side_copy(target, count).wait_recv())
+        if not split:
+            sides(target, lambda copy: copy.wait_recv())
 
         @pl.loop(0, 2)
         def _(which):
             @pl.when(jnp.logical_or(which == 0, jnp.logical_not(end(target))))
             def _():
+                if split:
+                    side_copy(target, which, half).wait_recv()
                 add(piece(target, which), side[target, pl.ds(which * half, half)])
                 pl.when(target != line)(lambda: hop(target, which))
 
@@ -861,7 +872,7 @@
 
     @pl.loop(0, rows)
     def _(target):
-        by_end(target, lambda count: side_copy(target, count).wait_send())
+        sides(target, lambda copy: copy.wait_send())
 
         def sent(sign):
             pl.loop(0, jnp.where(end(target), 3, 2))(
@@ -880,7 +891,7 @@
 
 def lane_sems(rows):
     dma = pltpu.SemaphoreType.DMA
-    return [dma((rows,)), dma((rows,)), dma((rows, 3)), dma((rows + 1, 3)), dma((2,))]
+    return [dma((rows, 2)), dma((rows, 2)), dma((rows, 3)), dma((rows + 1, 3)), dma((2,))]
 
 
 def lane_buffers(rows, size, width):
@@ -1276,7 +1287,7 @@
     )
 
 
-def greet_sp(me, groups):
+def greet_sp(me, groups, before_wait=lambda: None):
     barrier = pltpu.get_barrier_semaphore()
     for step in range(1, groups):
         pl.semaphore_signal(
@@ -1285,6 +1296,7 @@
             device_id={"sp": (me + step) % groups},
             device_id_type=pl.DeviceIdType.MESH,
         )
+    before_wait()
     pl.semaphore_wait(barrier, groups - 1)
 
 
@@ -1302,8 +1314,7 @@
         w_ref.at[pl.ds(pl.multiple_of(me * units, units), units), :], w, w_done
     )
     load.start()
-    prepare()
-    greet_sp(me, 4)
+    greet_sp(me, 4, prepare)
     half = size // 2
 
     def half_spot(member, piece):
@@ -1702,7 +1713,7 @@
             for other in range(1, rows):
                 line_gains(other).start()
 
-    line_scatter(part, side, lane, tail, total, *sems, reduce, fill)
+    line_scatter(part, side, lane, tail, total, *sems, reduce, fill, split=True)
     qkv_ref[...] = total[:size]
     out_ref[...] = total[size:]
     gains = from_line[0]

time: 482 us -> 480 us (level)
  no operation moved by 1% of the time
where the time goes in v12:
time: 480 us
  Pallas kernels  479 us (100%)
    pallas_call x1, Pallas kernels, ffn_forward(): pl.pallas_call(ffn_kernel, out_shape=(jax.ShapeDtypeStruct((size, width),...  114 us
    pallas_call x1, Pallas kernels, ffn_back(): pl.pallas_call(functools.partial(ffn_back_kernel, owners), out_shape=(jax...  110 us
    pallas_call x1, Pallas kernels, finish(): pl.pallas_call(finish_kernel, out_shape=(jax.ShapeDtypeStruct((cols.shape...  92.4 us
    pallas_call x1, Pallas kernels, attend(): pl.pallas_call(functools.partial(attend_kernel, heads), out_shape=(jax.Sh...  49.9 us
    pallas_call x1, Pallas kernels, attend_back(): pl.pallas_call(functools.partial(attend_back_kernel, heads, carried), out...  49.4 us
    pallas_call x1, Pallas kernels, project_back(): pl.pallas_call(project_back_kernel, out_shape=(jax.ShapeDtypeStruct((4 *...  21.9 us
    pallas_call x1, Pallas kernels, project_in(): pl.pallas_call(project_in_kernel, out_shape=(jax.ShapeDtypeStruct((4 * si...  20.6 us
    pallas_call x1, Pallas kernels, exchange_project(): pl.pallas_call(exchange_norm_kernel if norm_inputs else exchange_project_...  11.9 us

profile of v12, /device:TPU:26, one launch (start us, length us, event | category | flops | bytes accessed | tf_op | source)
XLA Modules:
  0.0 479.9 jit_solution(3124599790906825450)
XLA Ops:
  0.6 20.6 %project_in.1 = (bf16[512,2304]{1,0:T(8,128)(2,1)}, bf16[512,1024]{1,0:T(8,128)(2,1)}) custom-call(bf16[128,2304]{1,0:T(8,128)(2,1)} %tokens_ref.5, f32[4,2304]{1,0:T(4,128)} %gains_in_ref.1, bf16[4096,2304]{1,0:T(8,128)(2,1)} %w_ref.7), custom_call_target="tpu_custom_call" | custom-call | flops 17999998976 | bytes 54000000 | tf_op jit(solution)/shard_map/project_in/pallas_call | solution.py:1391
  21.2 49.9 %attend.1 = (bf16[512,512]{1,0:T(8,128)(2,1)}, f32[512,512]{1,0:T(8,128)}, f32[2,1,512]{2,1,0:T(1,128)}, f32[2,512,128]{2,1,0:T(8,128)}, bf16[8,512,512]{2,1,0:T(8,128)(2,1)}) custom-call(bf16[512,1024]{1,0:T(8,128)(2,1)} %get-tuple-element.41.x_ref.refs_0_), custom_call_target="tpu_custom_call" | custom-call | flops 49999998976 | bytes 150000000 | tf_op jit(solution)/shard_map/attend/pallas_call | solution.py:273
  71.2 11.9 %exchange_project.1 = (f32[128,2304]{1,0:T(8,128)}, f32[128,2304]{1,0:T(8,128)}, bf16[128,2304]{1,0:T(8,128)(2,1)}) custom-call(bf16[512,512]{1,0:T(8,128)(2,1)} %get-tuple-element.42.x_ref.att_ref, bf16[2048,2304]{1,0:T(8,128)(2,1)} %w_ref.6, bf16[128,2304]{1,0:T(8,128)(2,1)} %tokens_ref.5, f32[4,2304]{1,0:T(4,128)} %gains_in_ref.1), custom_call_target="tpu_custom_call" | custom-call | flops 16000000000 | bytes 48000000 | tf_op jit(solution)/shard_map/exchange_project/pallas_call | solution.py:1530
  83.0 113.6 %ffn_forward.1 = (bf16[128,2304]{1,0:T(8,128)(2,1)}, bf16[128,2304]{1,0:T(8,128)(2,1)}, f32[1,2304]{1,0:T(1,128)}, bf16[1024,2304]{1,0:T(8,128)(2,1)}, bf16[3,1152,1024]{2,1,0:T(8,128)(2,1)}) custom-call(bf16[128,2304]{1,0:T(8,128)(2,1)} %get-tuple-element.43.act_ref, bf16[3,1152,2304]{2,1,0:T(8,128)(2,1)} %bitcast.2, ...), custom_call_target="tpu_custom_call" | custom-call | flops 115000000512 | bytes 345000000 | tf_op jit(solution)/shard_map/ffn_forward/pallas_call | solution.py:1009
  196.6 110.2 %ffn_back.1 = (f32[128,2304]{1,0:T(8,128)}, bf16[3,288,2304]{2,1,0:T(8,128)(2,1)}, bf16[3,288,2304]{2,1,0:T(8,128)(2,1)}) custom-call(bf16[128,2304]{1,0:T(8,128)(2,1)} %get-tuple-element.45.grad_ref, bf16[1024,2304]{1,0:T(8,128)(2,1)} %get-tuple-element.46.acts_ref, bf16[3,1152,1024]{2,1,0:T(8,128)(2,1)} %get-tuple-element.47.factors_ref, ...), custom_call_target="tpu_custom_call" | custom-call | flops 115000000512 | bytes 345000000 | tf_op jit(solution)/shard_map/ffn_back/pallas_call | solution.py:1194
  306.8 21.9 %project_back.1 = (bf16[512,2304]{1,0:T(8,128)(2,1)}, bf16[512,512]{1,0:T(8,128)(2,1)}, f32[2,1,512]{2,1,0:T(1,128)}, f32[128,2304]{1,0:T(8,128)}, f32[8,2304]{1,0:T(8,128)}) custom-call(f32[128,2304]{1,0:T(8,128)} %get-tuple-element.49.grad_ref, f32[128,2304]{1,0:T(8,128)} %get-tuple-element.44.middle_ref, f32[128,2304]{1,0:T(8,128)} %get-tuple-element.50.attn_ref, ...), custom_call_target="tpu_custom_call" | custom-call | flops 20000000000 | bytes 60000000 | tf_op jit(solution)/shard_map/project_back/pallas_call | solution.py:1457
  328.7 49.4 %attend_back.1 = (bf16[512,1024]{1,0:T(8,128)(2,1)}, bf16[3,144,2304]{2,1,0:T(8,128)(2,1)}) custom-call(bf16[512,1024]{1,0:T(8,128)(2,1)} %get-tuple-element.41.x_ref.refs_0_, bf16[512,512]{1,0:T(8,128)(2,1)} %get-tuple-element.54.refs_1_, f32[2,1,512]{2,1,0:T(1,128)} %get-tuple-element.55.refs_2_, bf16[8,512,512]{2,1,0:T(8,128)(2,1)} %get-tuple-element.56.refs_3_, ...), custom_call_target="tpu_custom_call" | custom-call | flops 49999998976 | bytes 150000000 | tf_op jit(solution)/shard_map/attend_back/pallas_call | solution.py:544
  378.1 92.4 %finish.1 = (f32[128,2304]{1,0:T(8,128)}, f32[64,2304]{1,0:T(8,128)}, bf16[128,2304]{1,0:T(8,128)(2,1)}, f32[8,2304]{1,0:T(8,128)}, bf16[3,144,2304]{2,1,0:T(8,128)(2,1)}) custom-call(bf16[512,1024]{1,0:T(8,128)(2,1)} %get-tuple-element.59.cols_ref, bf16[512,2304]{1,0:T(8,128)(2,1)} %get-tuple-element.60.act_ref, ...), custom_call_target="tpu_custom_call" | custom-call | flops 85000003584 | bytes 255000000 | tf_op jit(solution)/shard_map/finish/pallas_call | solution.py:1744
  470.5 0.0 copy-start
  470.5 8.7 %deliver.1 = (f32[3,288,2304]{2,1,0:T(8,128)}, bf16[128,2304]{1,0:T(8,128)(2,1)}, bf16[128,2304]{1,0:T(8,128)(2,1)}, f32[128,2304]{1,0:T(8,128)}, f32[64,2304]{1,0:T(8,128)}) custom-call(bf16[3,288,2304]{2,1,0:T(8,128)(2,1)} %get-tuple-element.48.refs_0_, bf16[3,144,2304]{2,1,0:T(8,128)(2,1)} %get-tuple-element.58.refs_1_, ...), custom_call_target="tpu_custom_call" | custom-call | flops 8000000000 | bytes 24000000 | tf_op jit(solution)/shard_map/deliver/pallas_call | solution.py:1842
  479.2 0.0 copy-done
  479.2 0.7 constant_dynamic-slice_fusion
  (1 shorter events, 0.0 us)
Async XLA Ops:
  470.5 8.7 %copy-start = (f32[8,2304]{1,0:T(8,128)S(1)}, f32[8,2304]{1,0:T(8,128)}, u32[]{:S(2)}) copy-start(f32[8,2304]{1,0:T(8,128)} %get-tuple-element.74) | copy-start | bytes 221188

commit v13 on v12

--- a/solution.py
+++ b/solution.py
@@ -1506,14 +1506,15 @@
     for step in range(4):
         load((me + step) % 4).start()
     keep.wait()
-    for step in (0, 1, 3, 2):
+    core = me % 2
+    for place, step in enumerate((0, 1 + 2 * core, 2, 3 - 2 * core)):
         member = (me + step) % 4
         load(member).wait()
-        if step > 0:
+        if place > 0:
             send(4 - step).wait_recv()
         rows = pl.ds(pl.multiple_of(member * units, units), units)
         term = jnp.dot(got[step], w[rows, :], preferred_element_type=jnp.float32)
-        if step == 0:
+        if place == 0:
             out_ref[...] = term
         else:
             out_ref[...] += term

time: 480 us -> 477 us (level)
  no operation moved by 1% of the time
where the time goes in v13:
time: 477 us
  Pallas kernels  475 us (100%)
    pallas_call x1, Pallas kernels, ffn_forward(): pl.pallas_call(ffn_kernel, out_shape=(jax.ShapeDtypeStruct((size, width),...  111 us
    pallas_call x1, Pallas kernels, ffn_back(): pl.pallas_call(functools.partial(ffn_back_kernel, owners), out_shape=(jax...  110 us
    pallas_call x1, Pallas kernels, finish(): pl.pallas_call(finish_kernel, out_shape=(jax.ShapeDtypeStruct((cols.shape...  92.4 us
    pallas_call x1, Pallas kernels, attend(): pl.pallas_call(functools.partial(attend_kernel, heads), out_shape=(jax.Sh...  49.9 us
    pallas_call x1, Pallas kernels, attend_back(): pl.pallas_call(functools.partial(attend_back_kernel, heads, carried), out...  49.4 us
    pallas_call x1, Pallas kernels, project_back(): pl.pallas_call(project_back_kernel, out_shape=(jax.ShapeDtypeStruct((4 *...  21.9 us
    pallas_call x1, Pallas kernels, project_in(): pl.pallas_call(project_in_kernel, out_shape=(jax.ShapeDtypeStruct((4 * si...  20.6 us
    pallas_call x1, Pallas kernels, exchange_project(): pl.pallas_call(exchange_norm_kernel if norm_inputs else exchange_project_...  11.5 us

profile of v13, /device:TPU:26, one launch (start us, length us, event | category | flops | bytes accessed | tf_op | source)
XLA Modules:
  0.0 476.6 jit_solution(1834870458500090849)
XLA Ops:
  0.6 20.6 %project_in.1 = (bf16[512,2304]{1,0:T(8,128)(2,1)}, bf16[512,1024]{1,0:T(8,128)(2,1)}) custom-call(bf16[128,2304]{1,0:T(8,128)(2,1)} %tokens_ref.5, f32[4,2304]{1,0:T(4,128)} %gains_in_ref.1, bf16[4096,2304]{1,0:T(8,128)(2,1)} %w_ref.7), custom_call_target="tpu_custom_call" | custom-call | flops 17999998976 | bytes 54000000 | tf_op jit(solution)/shard_map/project_in/pallas_call | solution.py:1391
  21.2 49.9 %attend.1 = (bf16[512,512]{1,0:T(8,128)(2,1)}, f32[512,512]{1,0:T(8,128)}, f32[2,1,512]{2,1,0:T(1,128)}, f32[2,512,128]{2,1,0:T(8,128)}, bf16[8,512,512]{2,1,0:T(8,128)(2,1)}) custom-call(bf16[512,1024]{1,0:T(8,128)(2,1)} %get-tuple-element.41.x_ref.refs_0_), custom_call_target="tpu_custom_call" | custom-call | flops 49999998976 | bytes 150000000 | tf_op jit(solution)/shard_map/attend/pallas_call | solution.py:273
  71.2 11.5 %exchange_project.1 = (f32[128,2304]{1,0:T(8,128)}, f32[128,2304]{1,0:T(8,128)}, bf16[128,2304]{1,0:T(8,128)(2,1)}) custom-call(bf16[512,512]{1,0:T(8,128)(2,1)} %get-tuple-element.42.x_ref.att_ref, bf16[2048,2304]{1,0:T(8,128)(2,1)} %w_ref.6, bf16[128,2304]{1,0:T(8,128)(2,1)} %tokens_ref.5, f32[4,2304]{1,0:T(4,128)} %gains_in_ref.1), custom_call_target="tpu_custom_call" | custom-call | flops 16000000000 | bytes 48000000 | tf_op jit(solution)/shard_map/exchange_project/pallas_call | solution.py:1531
  82.6 110.8 %ffn_forward.1 = (bf16[128,2304]{1,0:T(8,128)(2,1)}, bf16[128,2304]{1,0:T(8,128)(2,1)}, f32[1,2304]{1,0:T(1,128)}, bf16[1024,2304]{1,0:T(8,128)(2,1)}, bf16[3,1152,1024]{2,1,0:T(8,128)(2,1)}) custom-call(bf16[128,2304]{1,0:T(8,128)(2,1)} %get-tuple-element.43.act_ref, bf16[3,1152,2304]{2,1,0:T(8,128)(2,1)} %bitcast.2, ...), custom_call_target="tpu_custom_call" | custom-call | flops 115000000512 | bytes 345000000 | tf_op jit(solution)/shard_map/ffn_forward/pallas_call | solution.py:1009
  193.5 110.1 %ffn_back.1 = (f32[128,2304]{1,0:T(8,128)}, bf16[3,288,2304]{2,1,0:T(8,128)(2,1)}, bf16[3,288,2304]{2,1,0:T(8,128)(2,1)}) custom-call(bf16[128,2304]{1,0:T(8,128)(2,1)} %get-tuple-element.45.grad_ref, bf16[1024,2304]{1,0:T(8,128)(2,1)} %get-tuple-element.46.acts_ref, bf16[3,1152,1024]{2,1,0:T(8,128)(2,1)} %get-tuple-element.47.factors_ref, ...), custom_call_target="tpu_custom_call" | custom-call | flops 115000000512 | bytes 345000000 | tf_op jit(solution)/shard_map/ffn_back/pallas_call | solution.py:1194
  303.5 21.9 %project_back.1 = (bf16[512,2304]{1,0:T(8,128)(2,1)}, bf16[512,512]{1,0:T(8,128)(2,1)}, f32[2,1,512]{2,1,0:T(1,128)}, f32[128,2304]{1,0:T(8,128)}, f32[8,2304]{1,0:T(8,128)}) custom-call(f32[128,2304]{1,0:T(8,128)} %get-tuple-element.49.grad_ref, f32[128,2304]{1,0:T(8,128)} %get-tuple-element.44.middle_ref, f32[128,2304]{1,0:T(8,128)} %get-tuple-element.50.attn_ref, ...), custom_call_target="tpu_custom_call" | custom-call | flops 20000000000 | bytes 60000000 | tf_op jit(solution)/shard_map/project_back/pallas_call | solution.py:1457
  325.4 49.4 %attend_back.1 = (bf16[512,1024]{1,0:T(8,128)(2,1)}, bf16[3,144,2304]{2,1,0:T(8,128)(2,1)}) custom-call(bf16[512,1024]{1,0:T(8,128)(2,1)} %get-tuple-element.41.x_ref.refs_0_, bf16[512,512]{1,0:T(8,128)(2,1)} %get-tuple-element.54.refs_1_, f32[2,1,512]{2,1,0:T(1,128)} %get-tuple-element.55.refs_2_, bf16[8,512,512]{2,1,0:T(8,128)(2,1)} %get-tuple-element.56.refs_3_, ...), custom_call_target="tpu_custom_call" | custom-call | flops 49999998976 | bytes 150000000 | tf_op jit(solution)/shard_map/attend_back/pallas_call | solution.py:544
  374.8 92.4 %finish.1 = (f32[128,2304]{1,0:T(8,128)}, f32[64,2304]{1,0:T(8,128)}, bf16[128,2304]{1,0:T(8,128)(2,1)}, f32[8,2304]{1,0:T(8,128)}, bf16[3,144,2304]{2,1,0:T(8,128)(2,1)}) custom-call(bf16[512,1024]{1,0:T(8,128)(2,1)} %get-tuple-element.59.cols_ref, bf16[512,2304]{1,0:T(8,128)(2,1)} %get-tuple-element.60.act_ref, ...), custom_call_target="tpu_custom_call" | custom-call | flops 85000003584 | bytes 255000000 | tf_op jit(solution)/shard_map/finish/pallas_call | solution.py:1745
  467.2 0.0 copy-start
  467.2 8.7 %deliver.1 = (f32[3,288,2304]{2,1,0:T(8,128)}, bf16[128,2304]{1,0:T(8,128)(2,1)}, bf16[128,2304]{1,0:T(8,128)(2,1)}, f32[128,2304]{1,0:T(8,128)}, f32[64,2304]{1,0:T(8,128)}) custom-call(bf16[3,288,2304]{2,1,0:T(8,128)(2,1)} %get-tuple-element.48.refs_0_, bf16[3,144,2304]{2,1,0:T(8,128)(2,1)} %get-tuple-element.58.refs_1_, ...), custom_call_target="tpu_custom_call" | custom-call | flops 8000000000 | bytes 24000000 | tf_op jit(solution)/shard_map/deliver/pallas_call | solution.py:1843
  475.9 0.0 copy-done
  475.9 0.7 constant_dynamic-slice_fusion
  (1 shorter events, 0.0 us)
Async XLA Ops:
  467.2 8.7 %copy-start = (f32[8,2304]{1,0:T(8,128)S(1)}, f32[8,2304]{1,0:T(8,128)}, u32[]{:S(2)}) copy-start(f32[8,2304]{1,0:T(8,128)} %get-tuple-element.74) | copy-start | bytes 221188
